TPU v7x, 32 devices: a whole 2x2x4 slice. The times are simulated.
32 devices in a mesh: dp: 8 (over z, y), replica: 4 (over x, core).
Axes of the slice: x: 2, y: 2, z: 4, core: 2. Of those that a mesh axis runs over, the one named last changes fastest.
Arguments:
- text_tokens: bfloat16 [32768, 384], P(('dp', 'replica')), may hold values from -6 to 6
- segment_ids: int32 [512, 64], P(('dp', 'replica')), may hold values from 0 to 3, never falling along the last dimension, each value on 1 to 32 neighbouring positions
- pair_index: int32 [2048], P(('dp', 'replica')), may hold values from 0 to 2047, each once
- image_tokens: bfloat16 [2048, 50, 384], P(('dp', 'replica')), may hold values from -6 to 6
- img_ln1: float32 [384], replicated, may hold values from 0.5 to 1.5
- img_qkv: bfloat16 [384, 1152], replicated, may hold values from -0.4375 to 0.4375
- img_out: bfloat16 [384, 384], replicated, may hold values from -1.75 to 1.75
- img_ln2: float32 [384], replicated, may hold values from 0.5 to 1.5
- img_up: bfloat16 [384, 1536], replicated, may hold values from -0.3125 to 0.3125
- img_down: bfloat16 [1536, 384], replicated, may hold values from -0.15625 to 0.15625
- img_proj: bfloat16 [384, 384], replicated, may hold values from -0.3125 to 0.3125
- txt_ln1: float32 [384], replicated, may hold values from 0.5 to 1.5
- txt_qkv: bfloat16 [384, 1152], replicated, may hold values from -0.4375 to 0.4375
- txt_out: bfloat16 [384, 384], replicated, may hold values from -1.25 to 1.25
- txt_ln2: float32 [384], replicated, may hold values from 0.5 to 1.5
- txt_up: bfloat16 [384, 1536], replicated, may hold values from -0.3125 to 0.3125
- txt_down: bfloat16 [1536, 384], replicated, may hold values from -0.15625 to 0.15625
- txt_proj: bfloat16 [384, 384], replicated, may hold values from -0.3125 to 0.3125
- log_scale: float32 [1], replicated, may hold values from 3 to 4.1
Outputs:
- loss: float32 [1], replicated
- grad_text_tokens: float32 [32768, 384], P(('dp', 'replica'))
- grad_txt_ln1: float32 [384], replicated
- grad_txt_qkv: float32 [384, 1152], replicated
- grad_txt_out: float32 [384, 384], replicated
- grad_txt_ln2: float32 [384], replicated
- grad_txt_up: float32 [384, 1536], replicated
- grad_txt_down: float32 [1536, 384], replicated
- grad_txt_proj: float32 [384, 384], replicated
- grad_log_scale: float32 [1], replicated
Inputs may be any that keep to these rules, and one draw needn't show every extreme that they name: `segment_ids`: in every packed row the ids never fall, every caption 0 to 3 appears, and a caption has 1 to 32 tokens. `pair_index`: a permutation: every image is paired with exactly one caption.
All inputs are finite; a program needn't handle non-finite values.
Results may differ from a plain program's by a relative error of at most 0.014.
The roundings to bfloat16 on the way count: a program that leaves them out, or rounds other values in their place, can miss the bound.
Values may be sent and summed in bfloat16 or wider, within the bound.
No kernel may reach another device: no remote copies, remote signals or barrier semaphores. Data moves between devices by JAX's collectives and lax.ppermute only.
A program may use at most 192 MiB of HBM per device.

v0:
```python
import jax
import jax.numpy as jnp
from jax import lax
from jax.sharding import PartitionSpec as P

D = 384
HEADS = 6
HEAD = 64
IMG_LEN = 50
PACK = 4


precise = lax.Precision.HIGHEST


def layer_norm(values, gain_vec):
    centre = values - jnp.mean(values, -1, keepdims=True)
    spread = jnp.mean(centre * centre, -1, keepdims=True)
    return centre * lax.rsqrt(spread + 1e-06) * gain_vec


def gelu_tanh(values):
    return jax.nn.gelu(values, approximate=True)


def unit_rows(values):
    return values * lax.rsqrt(jnp.sum(values * values, -1, keepdims=True) + 1e-06)


def row_lse(scores):
    top_val = jnp.max(scores, -1, keepdims=True)
    return top_val[:, 0] + jnp.log(jnp.sum(jnp.exp(scores - top_val), -1))


def project(left_mat, right_mat):
    return jnp.dot(left_mat, right_mat, preferred_element_type=jnp.float32)


def attend(packed, mask_bias, groups, group_len):
    by_head = packed.reshape(groups, group_len, 3, HEADS, HEAD)
    scores = jnp.einsum(
        "gqhd,gkhd->ghqk", by_head[:, :, 0], by_head[:, :, 1], preferred_element_type=jnp.float32
    ) * HEAD ** (-0.5)
    if mask_bias is not None:
        scores = scores + mask_bias[:, None]
    top_val = jnp.max(scores, -1, keepdims=True)
    expo_val = jnp.exp(scores - top_val)
    row_total = jnp.sum(expo_val, -1, keepdims=True)
    log_sum = top_val + jnp.log(row_total)
    weights_p = (expo_val / row_total).astype(jnp.bfloat16)
    mixed_out = jnp.einsum(
        "ghqk,gkhd->gqhd", weights_p, by_head[:, :, 2], preferred_element_type=jnp.float32
    )
    return (mixed_out.reshape(groups * group_len, HEADS * HEAD).astype(jnp.bfloat16), log_sum)


def attend_back(packed, mask_bias, log_sum, grad_mixed, groups, group_len):
    by_head = packed.reshape(groups, group_len, 3, HEADS, HEAD)
    queries = by_head[:, :, 0]
    key_part = by_head[:, :, 1]
    value_part = by_head[:, :, 2]
    scores = jnp.einsum(
        "gqhd,gkhd->ghqk", queries, key_part, preferred_element_type=jnp.float32
    ) * HEAD ** (-0.5)
    scores = scores + mask_bias[:, None]
    prob_full = jnp.exp(scores - log_sum)
    grad_heads = grad_mixed.reshape(groups, group_len, HEADS, HEAD)
    grad_vals = jnp.einsum(
        "ghqk,gqhd->gkhd",
        prob_full.astype(jnp.bfloat16),
        grad_heads,
        preferred_element_type=jnp.float32,
    )
    grad_probs = jnp.einsum(
        "gqhd,gkhd->ghqk", grad_heads, value_part, preferred_element_type=jnp.float32
    )
    grad_scores = (
        prob_full * (grad_probs - jnp.sum(grad_probs * prob_full, -1, keepdims=True))
    ).astype(jnp.bfloat16)
    grad_query = jnp.einsum(
        "ghqk,gkhd->gqhd", grad_scores, key_part, preferred_element_type=jnp.float32
    ) * HEAD ** (-0.5)
    grad_keys = jnp.einsum(
        "ghqk,gqhd->gkhd", grad_scores, queries, preferred_element_type=jnp.float32
    ) * HEAD ** (-0.5)
    stacked = jnp.stack([grad_query, grad_keys, grad_vals], 2)
    return stacked.reshape(groups * group_len, 3 * HEADS * HEAD)


def shards(
    text_tokens,
    segment_ids,
    pair_index,
    image_tokens,
    img_ln1,
    img_qkv,
    img_out,
    img_ln2,
    img_up,
    img_down,
    img_proj,
    txt_ln1,
    txt_qkv,
    txt_out,
    txt_ln2,
    txt_up,
    txt_down,
    txt_proj,
    log_scale,
):
    image_count = image_tokens.shape[0]
    image_flat = image_tokens.reshape(image_count * IMG_LEN, D).astype(jnp.float32)
    img_normed = layer_norm(image_flat, img_ln1).astype(jnp.bfloat16)
    img_mixed, unused = attend(
        project(img_normed, img_qkv).astype(jnp.bfloat16), None, image_count, IMG_LEN
    )
    img_resid = image_flat + project(img_mixed, img_out)
    img_hidden = gelu_tanh(
        project(layer_norm(img_resid, img_ln2).astype(jnp.bfloat16), img_up)
    ).astype(jnp.bfloat16)
    img_block_out = img_resid + project(img_hidden, img_down)
    img_first = img_block_out.reshape(image_count, IMG_LEN, D)[:, 0].astype(jnp.bfloat16)
    image_emb = unit_rows(project(img_first, img_proj)).astype(jnp.bfloat16)
    row_count = segment_ids.shape[0]
    text_len = segment_ids.shape[1]
    groups = row_count // 2
    group_len = 2 * text_len
    labels = (segment_ids + PACK * jnp.arange(row_count, dtype=jnp.int32)[:, None]).reshape(
        groups, group_len
    )
    mask_bias = jnp.where(labels[:, :, None] == labels[:, None, :], 0.0, -1000000000.0).astype(
        jnp.float32
    )
    tokens32 = text_tokens.astype(jnp.float32)
    normed_one, ln_one_back = jax.vjp(layer_norm, tokens32, txt_ln1)
    normed_one_b = normed_one.astype(jnp.bfloat16)
    packed = project(normed_one_b, txt_qkv).astype(jnp.bfloat16)
    attended, log_sum = attend(packed, mask_bias, groups, group_len)
    residual = tokens32 + project(attended, txt_out)
    normed_two, ln_two_back = jax.vjp(layer_norm, residual, txt_ln2)
    normed_two_b = normed_two.astype(jnp.bfloat16)
    pre_act = project(normed_two_b, txt_up)
    activated, gelu_back = jax.vjp(gelu_tanh, pre_act)
    hidden_b = activated.astype(jnp.bfloat16)
    block_out = residual + project(hidden_b, txt_down)
    member = (segment_ids[:, :, None] == jnp.arange(PACK, dtype=jnp.int32)[None, None, :]).astype(
        jnp.float32
    )
    counts = jnp.sum(member, 1)
    pooled = (
        jnp.einsum(
            "rlp,rld->rpd", member, block_out.reshape(row_count, text_len, D), precision=precise
        )
        / counts[:, :, None]
    )
    pooled_b = pooled.reshape(row_count * PACK, D).astype(jnp.bfloat16)
    raw_emb = project(pooled_b, txt_proj)
    text_unit, unit_back = jax.vjp(unit_rows, raw_emb)
    text_emb = text_unit.astype(jnp.bfloat16)
    text_all, image_all = (
        lax.all_gather(text_emb, ("dp", "replica"), axis=0, tiled=True),
        lax.all_gather(image_emb, ("dp", "replica"), axis=0, tiled=True),
    )
    caption_total = text_all.shape[0]
    inv_temp = jnp.exp(log_scale[0])
    cos_rows = jnp.einsum("ce,je->cj", text_emb, image_all, preferred_element_type=jnp.float32)
    logit_rows = inv_temp * cos_rows
    lse_rows = row_lse(logit_rows)
    positive = jnp.take_along_axis(logit_rows, pair_index[:, None], 1)[:, 0]
    cos_cols = jnp.einsum("ie,ce->ic", image_emb, text_all, preferred_element_type=jnp.float32)
    logit_cols = inv_temp * cos_cols
    lse_cols = row_lse(logit_cols)
    pair_denom = 2.0 * caption_total
    loss_part = (jnp.sum(lse_rows) + jnp.sum(lse_cols) - 2.0 * jnp.sum(positive)) / pair_denom
    target = (jnp.arange(caption_total, dtype=jnp.int32)[None, :] == pair_index[:, None]).astype(
        jnp.float32
    )
    grad_rows = jnp.exp(logit_rows - lse_rows[:, None]) / pair_denom - target * (2.0 / pair_denom)
    grad_cols = jnp.exp(logit_cols - lse_cols[:, None]) / pair_denom
    grad_temp = inv_temp * (jnp.sum(grad_rows * cos_rows) + jnp.sum(grad_cols * cos_cols))
    grad_text = project((inv_temp * grad_rows).astype(jnp.bfloat16), image_all)
    col_round = (inv_temp * grad_cols).astype(jnp.bfloat16)
    grad_text = grad_text + lax.psum_scatter(
        jnp.einsum("ic,ie->ce", col_round, image_emb, preferred_element_type=jnp.float32),
        ("dp", "replica"),
        scatter_dimension=0,
        tiled=True,
    )
    grad_raw = unit_back(grad_text)[0].astype(jnp.bfloat16)
    grad_proj = jnp.einsum("cd,ce->de", pooled_b, grad_raw, preferred_element_type=jnp.float32)
    grad_pooled = jnp.einsum("ce,de->cd", grad_raw, txt_proj, preferred_element_type=jnp.float32)
    spread_back = grad_pooled.reshape(row_count, PACK, D) / counts[:, :, None]
    grad_final = jnp.einsum("rlp,rpd->rld", member, spread_back, precision=precise).reshape(
        row_count * text_len, D
    )
    grad_final_b = grad_final.astype(jnp.bfloat16)
    grad_down = jnp.einsum("tf,td->fd", hidden_b, grad_final_b, preferred_element_type=jnp.float32)
    grad_hidden = jnp.einsum(
        "td,fd->tf", grad_final_b, txt_down, preferred_element_type=jnp.float32
    )
    grad_pre = gelu_back(grad_hidden)[0].astype(jnp.bfloat16)
    grad_up = jnp.einsum("td,tf->df", normed_two_b, grad_pre, preferred_element_type=jnp.float32)
    grad_normed_two = jnp.einsum("tf,df->td", grad_pre, txt_up, preferred_element_type=jnp.float32)
    grad_resid_ln, grad_ln2 = ln_two_back(grad_normed_two)
    grad_resid = grad_final + grad_resid_ln
    grad_resid_b = grad_resid.astype(jnp.bfloat16)
    grad_out = jnp.einsum("td,te->de", attended, grad_resid_b, preferred_element_type=jnp.float32)
    grad_att = jnp.einsum(
        "te,de->td", grad_resid_b, txt_out, preferred_element_type=jnp.float32
    ).astype(jnp.bfloat16)
    grad_packed = attend_back(packed, mask_bias, log_sum, grad_att, groups, group_len).astype(
        jnp.bfloat16
    )
    grad_qkv = jnp.einsum(
        "td,te->de", normed_one_b, grad_packed, preferred_element_type=jnp.float32
    )
    grad_normed_one = jnp.einsum(
        "te,de->td", grad_packed, txt_qkv, preferred_element_type=jnp.float32
    )
    grad_tok_ln, grad_ln1 = ln_one_back(grad_normed_one)
    grad_tokens = grad_resid + grad_tok_ln
    totals = lax.psum(
        (
            grad_ln1,
            grad_qkv,
            grad_out,
            grad_ln2,
            grad_up,
            grad_down,
            grad_proj,
            grad_temp.reshape(1),
            loss_part.reshape(1),
        ),
        ("dp", "replica"),
    )
    return (
        totals[8],
        grad_tokens,
        totals[0],
        totals[1],
        totals[2],
        totals[3],
        totals[4],
        totals[5],
        totals[6],
        totals[7],
    )


def solution(mesh):
    return jax.shard_map(
        shards,
        mesh=mesh,
        in_specs=(
            P(("dp", "replica"), None),
            P(("dp", "replica"), None),
            P(("dp", "replica")),
            P(("dp", "replica"), None, None),
            P(),
            P(),
            P(),
            P(),
            P(),
            P(),
            P(),
            P(),
            P(),
            P(),
            P(),
            P(),
            P(),
            P(),
            P(),
        ),
        out_specs=(P(), P(("dp", "replica"), None), P(), P(), P(), P(), P(), P(), P(), P()),
        check_vma=False,
    )
```

profile of v0, /device:TPU:0, one launch (start us, length us, event | category | flops | bytes accessed | tf_op | source)
XLA Modules:
  0.0 577.8 jit_solution(3463116824827041461)
XLA Ops:
  11.9 4.4 convolution_convert_fusion.1
  16.2 2.8 copy.72
  30.0 2.4 convolution_add_fusion.1
  34.7 5.7 copy.78
  42.4 5.4 reshape.254
  48.2 9.2 %convolution_convert_fusion = bf16[3200,1152]{1,0:T(8,128)(2,1)} fusion(bf16[384,1152]{1,0:T(8,128)(2,1)} %param.24, f32[3200,384]{1,0:T(8,128)} %reshape.254, f32[384]{0:T(512)S(1)} %copy-done.61, f32[3200]{0:T(1024)S(1)} %rsqrt.61, f32[3200]{0:T(1024)S(1)} %div.104), kind=kOutput, calls=%fused_computation.11 | convolution fusion | flops 2839756800 | bytes 13199872 | tf_op jit(solution)/shard_map/dot_general | solution.py:36
  57.3 22.4 %reshape.264 = bf16[64,50,3,6,64]{4,3,2,1,0:T(8,128)(2,1)} reshape(bf16[3200,1152]{1,0:T(8,128)(2,1)} %convolution_convert_fusion) | data formatting | bytes 14745600 | tf_op jit(solution)/shard_map/reshape | solution.py:40
  79.8 13.4 %fusion.119 = (bf16[64,50,1,6,64]{4,3,2,1,0:T(8,128)(2,1)}, bf16[64,50,1,6,64]{4,3,2,1,0:T(8,128)(2,1)}, bf16[64,50,1,6,64]{4,3,2,1,0:T(8,128)(2,1)}) fusion(bf16[64,50,3,6,64]{4,3,2,1,0:T(8,128)(2,1)} %reshape.264), kind=kLoop, calls=%fused_computation.199 | loop fusion | bytes 14745600 | tf_op jit(solution)/shard_map/slice | solution.py:52
  93.2 11.8 %fusion.23 = f32[64,6,50,50]{2,3,1,0:T(8,128)} fusion(bf16[64,50,1,6,64]{4,3,2,1,0:T(8,128)(2,1)} %get-tuple-element.31, bf16[64,50,1,6,64]{4,3,2,1,0:T(8,128)(2,1)} %get-tuple-element.30), kind=kOutput, calls=%fused_computation.32 | convolution fusion | flops 122880000 | bytes 8755200 | tf_op jit(solution)/shard_map/gqhd,gkhd->ghqk/dot_general | solution.py:41
  105.0 14.7 %fusion.123 = (f32[64,6,50]{2,1,0:T(8,128)S(1)}, f32[64,6,50,50]{2,3,1,0:T(8,128)}) fusion(f32[64,6,50,50]{2,3,1,0:T(8,128)} %fusion.23), kind=kOutput, calls=%fused_computation.203 | output fusion | flops 3840049 | bytes 7756800 | tf_op jit(solution)/shard_map/sub | solution.py:47
  119.6 9.6 %convert_bitcast_fusion = bf16[64,50,6,64]{3,1,2,0:T(8,128)(2,1)} fusion(f32[64,6,50,50]{2,3,1,0:T(8,128)} %get-tuple-element.44, f32[64,6,50]{2,1,0:T(8,128)S(1)} %get-tuple-element.43, bf16[64,50,1,6,64]{4,3,2,1,0:T(8,128)(2,1)S(1)} %copy-done.16), kind=kOutput, calls=%fused_computation.35 | convolution fusion | flops 126028800 | bytes 8832000 | tf_op jit(solution)/shard_map/ghqk,gkhd->gqhd/dot_general | solution.py:51
  129.2 9.4 %copy.86 = bf16[64,50,6,64]{1,0,3,2:T(8,128)(2,1)} copy(bf16[64,50,6,64]{3,1,2,0:T(8,128)(2,1)} %convert_bitcast_fusion) | data formatting | bytes 4915200 | tf_op jit(solution)/shard_map/convert_element_type | solution.py:54
  138.6 10.6 %convert_element_type.133 = bf16[3200,384]{0,1:T(8,128)(2,1)} reshape(bf16[64,50,6,64]{1,0,3,2:T(8,128)(2,1)} %copy.86) | data formatting | bytes 4915200 | tf_op jit(solution)/shard_map/convert_element_type | solution.py:54
  149.2 5.0 fusion.124
  156.4 17.0 %fusion.21 = bf16[3200,384]{1,0:T(8,128)(2,1)} fusion(f32[3200,384]{1,0:T(8,128)} %copy-done.3, bf16[1536,384]{1,0:T(8,128)(2,1)} %param.28, bf16[384,1536]{1,0:T(8,128)(2,1)} %param.27, f32[384]{0:T(512)S(1)} %copy-done.62, f32[3200]{0:T(1024)S(1)} %add_rsqrt_fusion.1, f32[3200]{0:T(1024)S(1)} %broadcast_multiply_fusion.3), kind=kOutput, calls=%fused_computation.29 | convolution fusion | flops 7601356800 | bytes 9759232 | tf_op jit(solution)/shard_map/dot_general | solution.py:36
  173.4 4.3 reshape.247
  183.6 2.3 fusion.78
  187.3 50.1 %all-gather.3.cloned.1.call-done = bf16[2048,384]{1,0:T(8,128)(2,1)} async-done(((bf16[64,384]{1,0:T(8,128)(2,1)}), bf16[2048,384]{1,0:T(8,128)(2,1)}) %all-gather.3.cloned.1.call-update) | async-done | bytes 1572880 | tf_op jit(solution)/shard_map/all_gather | solution.py:162
  242.3 101.7 %reduce-scatter.2.cloned.1.call-done = f32[64,384]{1,0:T(8,128)} async-done(((f32[2048,384]{1,0:T(8,128)}), f32[64,384]{1,0:T(8,128)}) %reduce-scatter.2.cloned.1.call-update) | async-done | bytes 98320 | tf_op jit(solution)/shard_map/reduce_scatter | solution.py:183
  348.3 6.8 %fusion.19 = bf16[1024,1536]{1,0:T(8,128)(2,1)S(1)} fusion(f32[1024,1536]{1,0:T(8,128)} %copy-done.7, bf16[1024,384]{1,0:T(8,128)(2,1)S(1)} %bitcast_convert_fusion, bf16[1536,384]{1,0:T(8,128)(2,1)S(1)} %copy-done.60), kind=kOutput, calls=%fused_computation.25 | convolution fusion | flops 1239416832 | bytes 11403264 | tf_op jit(solution)/shard_map/td,fd->tf/dot_general | solution.py:198
  355.1 6.8 %fusion.115 = f32[1536,384]{1,0:T(8,128)} fusion(bf16[1024,384]{1,0:T(8,128)(2,1)S(1)} %bitcast_convert_fusion, f32[1024,1536]{1,0:T(8,128)} %copy-done.7), kind=kOutput, calls=%fused_computation.195 | convolution fusion | flops 1222115328 | bytes 9437184 | tf_op jit(solution)/shard_map/tf,td->fd/dot_general | solution.py:197
  361.9 2.9 fusion.113
  364.9 2.5 multiply_reduce_fusion.4
  372.2 3.2 multiply_reduce_fusion.3
  386.6 2.8 fusion.41
  390.1 2.7 multiply_reduce_fusion.8
  394.1 2.4 gather_fusion
  399.7 3.8 fusion.52
  406.0 42.7 %all-reduce = (f32[1]{0:T(128)}, f32[384]{0:T(512)}, f32[384]{0:T(512)}, f32[1]{0:T(128)}) all-reduce(f32[1]{0:T(128)} %bitcast.13, f32[384]{0:T(512)} %get-tuple-element.12, f32[384]{0:T(512)} %get-tuple-element.10, f32[1]{0:T(128)} %bitcast.21), channel_id=1, replica_groups=mesh['dp'=8,'replica'=4] {'dp','replica'}, use_global_device_ids=true, to_apply=%region_22.23 | all-reduce | flops 770 | bytes 6160 | tf_op jit(solution)/shard_map/psum | solution.py:222
  448.7 3.0 add_add_fusion.2
  451.7 110.6 %all-reduce.4.cloned.1.call-done = (f32[384,1152]{1,0:T(8,128)}, f32[384,384]{1,0:T(8,128)}, f32[384,1536]{1,0:T(8,128)}, f32[1536,384]{1,0:T(8,128)}, f32[384,384]{1,0:T(8,128)}) async-done(((f32[384,1152]{1,0:T(8,128)}, f32[384,384]{1,0:T(8,128)}, f32[384,1536]{1,0:T(8,128)}, f32[1536,384]{1,0:T(8,128)}, f32[384,384]{1,0:T(8,128)}), (f32[384,1152]{1,0:T(8,128)}, f32[384,384]{1,0:T(8,128)}, ...) | async-done | bytes 7667728 | tf_op jit(solution)/shard_map/psum | solution.py:222
  562.3 2.9 copy.179
  (216 shorter events, 63.4 us)
Async XLA Ops:
  7.2 20.9 %copy-start = (bf16[384,1536]{1,0:T(8,128)(2,1)S(1)}, bf16[384,1536]{1,0:T(8,128)(2,1)}, u32[]{:S(2)}) copy-start(bf16[384,1536]{1,0:T(8,128)(2,1)} %param.34) | copy-start | bytes 3538948
  7.2 173.3 %all-gather.5.cloned.1.call-start = ((), (), s32[]{:S(2)}) async-start(), calls=%async_computation.2 | async-start | bytes 1622016 | tf_op jit(solution)/shard_map/all_gather | solution.py:161
  20.4 4.1 copy-start.10
  20.4 4.1 copy-start.12
  20.4 4.9 copy-start.18
  30.0 3.4 copy-start.22
  33.4 7.0 %copy-start.31 = (bf16[64,384]{1,0:T(8,128)(2,1)}, bf16[64,384]{1,0:T(8,128)(2,1)S(1)}, u32[]{:S(2)}) copy-start(bf16[64,384]{1,0:T(8,128)(2,1)S(1)} %convert_element_type.123) | copy-start | bytes 147460
  33.7 6.7 %copy-start.57 = (f32[64]{0:T(128)}, f32[64]{0:T(128)S(1)}, u32[]{:S(2)}) copy-start(f32[64]{0:T(128)S(1)} %get-tuple-element.41) | copy-start | bytes 772
  33.7 6.7 %copy-start.52 = (f32[64]{0:T(128)}, f32[64]{0:T(128)S(1)}, u32[]{:S(2)}) copy-start(f32[64]{0:T(128)S(1)} %add_rsqrt_fusion.3) | copy-start | bytes 772
  34.5 202.9 %all-gather.3.cloned.1.call-start = ((), (), s32[]{:S(2)}) async-start(), calls=%async_computation.1 | async-start | bytes 1622016 | tf_op jit(solution)/shard_map/all_gather | solution.py:162
  34.7 5.7 copy-start.4
  42.4 5.8 copy-start.61
  105.0 14.7 %copy-start.16 = (bf16[64,50,1,6,64]{4,3,2,1,0:T(8,128)(2,1)S(1)}, bf16[64,50,1,6,64]{4,3,2,1,0:T(8,128)(2,1)}, u32[]{:S(2)}) copy-start(bf16[64,50,1,6,64]{4,3,2,1,0:T(8,128)(2,1)} %get-tuple-element.29) | copy-start | bytes 7372804
  138.6 10.6 %copy-start.38 = (bf16[384,384]{1,0:T(8,128)(2,1)S(1)}, bf16[384,384]{1,0:T(8,128)(2,1)}, u32[]{:S(2)}) copy-start(bf16[384,384]{1,0:T(8,128)(2,1)} %param.25) | copy-start | bytes 884740
  173.4 5.3 copy-start.37
  179.8 3.8 copy-start.26
  179.8 164.2 %reduce-scatter.2.cloned.1.call-start = ((), (), s32[]{:S(2)}) async-start(), calls=%async_computation.3 | async-start | bytes 3244032 | tf_op jit(solution)/shard_map/reduce_scatter | solution.py:183
  185.9 51.5 %copy-start.30 = (bf16[64,384]{1,0:T(8,128)(2,1)S(1)}, bf16[64,384]{1,0:T(8,128)(2,1)}, u32[]{:S(2)}) copy-start(bf16[64,384]{1,0:T(8,128)(2,1)} %multiply_convert_fusion.15) | copy-start | bytes 147460
  185.9 158.1 %copy-start.54 = (s32[64]{0:T(128)S(1)}, s32[64]{0:T(128)}, u32[]{:S(2)}) copy-start(s32[64]{0:T(128)} %param.21) | copy-start | bytes 772
  186.0 376.3 %all-reduce.4.cloned.1.call-start = ((), (), s32[]{:S(2)}) async-start(), calls=%async_computation.4 | async-start | bytes 15335424 | tf_op jit(solution)/shard_map/psum | solution.py:222
  187.3 158.7 %copy-start.58 = (f32[64]{0:T(128)S(1)}, f32[64]{0:T(128)}, u32[]{:S(2)}) copy-start(f32[64]{0:T(128)} %copy-done.57) | copy-start | bytes 772
  187.3 158.7 %copy-start.53 = (f32[64]{0:T(128)S(1)}, f32[64]{0:T(128)}, u32[]{:S(2)}) copy-start(f32[64]{0:T(128)} %copy-done.52) | copy-start | bytes 772
  239.5 108.6 %copy-start.8 = (f32[64,2048]{1,0:T(8,128)}, f32[64,2048]{1,0:T(8,128)S(1)}, u32[]{:S(2)}) copy-start(f32[64,2048]{1,0:T(8,128)S(1)} %get-tuple-element.50) | copy-start | bytes 1572868
  242.3 105.8 %copy-start.51 = (f32[64]{0:T(128)}, f32[64]{0:T(128)S(1)}, u32[]{:S(2)}) copy-start(f32[64]{0:T(128)S(1)} %get-tuple-element.28) | copy-start | bytes 772
  372.2 3.3 copy-start.2
  382.9 3.8 copy-start.6
  382.9 3.7 copy-start.44
  382.9 3.7 copy-start.46
  382.9 3.7 copy-start.49
  399.7 3.8 copy-start.48
  399.7 4.9 copy-start.50
  562.3 3.8 copy-start.20
  (35 other events, 51.1 us)
Sparse Core Ops, SparseCore 0:
  34.6 57.5 all-gather.4
  179.9 57.4 all-gather.2
  242.8 101.1 reduce-scatter.1
  389.5 172.7 all-reduce.3
where the time goes:
time: 588 us; the launch traced here: 578 us
  waiting for transfers between devices  262 us (45%)
  matrix products  110 us (19%)
  local copies, waits for them, and re-layouts  103 us (18%)
  blocking collectives  42.7 us (7%)
  other arithmetic  40.2 us (7%)
  between operations  19 us (3%)
    psum x1, waiting for transfers between devices, shards(): lax.psum((grad_ln1, grad_qkv, grad_out, grad_ln2, grad_up, grad_down, gra...  111 us
    reduce_scatter x1, waiting for transfers between devices, shards(): lax.psum_scatter(jnp.einsum('ic,ie->ce', col_round, image_emb, preferred_...  102 us
    all_gather x1, waiting for transfers between devices, shards(): lax.all_gather(image_emb, ('dp', 'replica'), axis=0, tiled=True)  50.1 us
    dot_general x10, matrix products, project(): return jnp.dot(left_mat, right_mat, preferred_element_type=jnp.float32)  43.1 us
    psum x1, blocking collectives, shards(): lax.psum((grad_ln1, grad_qkv, grad_out, grad_ln2, grad_up, grad_down, gra...  42.7 us
    reshape x1, local copies, waits for them, and re-layouts, attend(): by_head = packed.reshape(groups, group_len, 3, HEADS, HEAD)  22.4 us
    convert_element_type x3, local copies, waits for them, and re-layouts, attend(): mixed_out.reshape(groups * group_len, HEADS * HEAD).astype(jnp.bfloat16)  20.5 us
    unnamed x134, local copies, waits for them, and re-layouts  18.9 us
  transfers between devices with their start and end apart: 4, of which 3 were waited for; matrix products, arithmetic and copies ran while one was open for 29% of the time, Pallas kernels for 0%

commit v1 on v0

v1 whole, which is shorter than its diff:
```python
import functools
import math

import jax
import jax.numpy as jnp
from jax import lax
from jax.experimental import pallas as pl
from jax.experimental.pallas import tpu as pltpu
from jax.sharding import PartitionSpec as P

D = 384
HEADS = 6
HEAD = 64
FF = 1536
IMG_LEN = 50
PACK = 4
CAPS = 64
TOK_BLOCK = 256
CAP_BLOCK = 16
BLOCKS = 4
PAIR = 128
IMG_BLOCK = 16
EPS = 1e-06

BF = jnp.bfloat16
F32 = jnp.float32
GELU_K = math.sqrt(2.0 / math.pi)
GELU_C = 0.044715


def mm(a, b):
    return lax.dot_general(a, b, (((1,), (0,)), ((), ())), preferred_element_type=F32)


def mm_nt(a, b):
    return lax.dot_general(a, b, (((1,), (1,)), ((), ())), preferred_element_type=F32)


def mm_tn(a, b):
    return lax.dot_general(a, b, (((0,), (0,)), ((), ())), preferred_element_type=F32)


def row_mean(v):
    return jnp.sum(v, -1, keepdims=True) * (1.0 / D)


def normalize(v):
    centre = v - row_mean(v)
    return centre * lax.rsqrt(row_mean(centre * centre) + EPS)


def split3(v):
    high = v.astype(BF)
    rest = v - high.astype(F32)
    mid = rest.astype(BF)
    low = (rest - mid.astype(F32)).astype(BF)
    return high, mid, low


def wide_mm(v, w):
    high, mid, low = split3(v)
    n = v.shape[0]
    out = mm(jnp.concatenate([high, mid, low], 0), w)
    return out[:n] + out[n : 2 * n] + out[2 * n :]


def gelu_parts(z):
    z2 = z * z
    t = jnp.tanh(z * (z2 * (GELU_K * GELU_C) + GELU_K))
    hp = t * 0.5 + 0.5
    u = z * hp
    slope = hp + (u * (1.0 - hp)) * (z2 * (6.0 * GELU_K * GELU_C) + 2.0 * GELU_K)
    return u, slope


def lanes_head(shape):
    return lax.broadcasted_iota(jnp.int32, shape, len(shape) - 1) // HEAD


def image_kernel(x_ref, g1, wqkv, wout, g2, wup, wdown, wproj, emb_ref, hs, x0, att):
    step = pl.program_id(0)

    @pl.when(step == 0)
    def _():
        hs[...] = jnp.zeros_like(hs)

    gain = g1[...]
    for i in range(IMG_BLOCK):
        x = x_ref[i].astype(F32)
        hs[64 * i : 64 * i + IMG_LEN, :] = (normalize(x) * gain).astype(BF)
        x0[pl.ds(step * IMG_BLOCK + i, 1), :] = x[0:1]
    first = x0[pl.ds(pl.multiple_of(step * IMG_BLOCK, IMG_BLOCK), IMG_BLOCK), :]
    h0 = (normalize(first) * gain).astype(BF)
    q = mm(h0, wqkv[:, :D]).astype(BF).astype(F32) * (HEAD**-0.5)
    kv = mm(hs[...], wqkv[:, D:]).astype(BF)
    head8 = lanes_head((8, D))
    rows = lax.broadcasted_iota(jnp.int32, (48, 512), 0)
    cols = lax.broadcasted_iota(jnp.int32, (48, 512), 1)
    own = (cols // 64 == rows % 8) & (cols % 64 < IMG_LEN)
    for g in range(IMG_BLOCK // 8):
        q8 = q[8 * g : 8 * g + 8]
        q48 = jnp.concatenate([jnp.where(head8 == h, q8, 0.0) for h in range(HEADS)], 0)
        s = mm_nt(q48.astype(BF), kv[512 * g : 512 * g + 512, :D])
        s = jnp.where(own, s, -1e30)
        e = jnp.exp(s - jnp.max(s, -1, keepdims=True))
        p = (e / jnp.sum(e, -1, keepdims=True)).astype(BF)
        r = mm(p, kv[512 * g : 512 * g + 512, D:])
        o8 = jnp.where(head8 == 0, r[0:8], 0.0)
        for h in range(1, HEADS):
            o8 = jnp.where(head8 == h, r[8 * h : 8 * h + 8], o8)
        att[pl.ds(pl.multiple_of(step * IMG_BLOCK + 8 * g, 8), 8), :] = o8

    @pl.when(step == pl.num_programs(0) - 1)
    def _():
        x1 = x0[...] + mm(att[...].astype(BF), wout[...])
        h2 = (normalize(x1) * g2[...]).astype(BF)
        u, _ = gelu_parts(mm(h2, wup[...]))
        y = x1 + mm(u.astype(BF), wdown[...])
        e = mm(y.astype(BF), wproj[...])
        emb_ref[...] = (e * lax.rsqrt(jnp.sum(e * e, -1, keepdims=True) + EPS)).astype(BF)


def const_spec(shape):
    zeros = (0,) * len(shape)
    return pl.BlockSpec(shape, lambda *_: zeros, pipeline_mode=pl.Buffered(1))


def image_tower(x, g1, wqkv, wout, g2, wup, wdown, wproj):
    count = x.shape[0]
    return pl.pallas_call(
        image_kernel,
        grid=(count // IMG_BLOCK,),
        in_specs=[
            pl.BlockSpec((IMG_BLOCK, IMG_LEN, D), lambda i: (i, 0, 0)),
            const_spec((1, D)),
            const_spec((D, 3 * D)),
            const_spec((D, D)),
            const_spec((1, D)),
            const_spec((D, FF)),
            const_spec((FF, D)),
            const_spec((D, D)),
        ],
        out_specs=pl.BlockSpec((count, D), lambda i: (0, 0)),
        out_shape=jax.ShapeDtypeStruct((count, D), BF),
        scratch_shapes=[
            pltpu.VMEM((IMG_BLOCK * 64, D), BF),
            pltpu.VMEM((count, D), F32),
            pltpu.VMEM((count, D), F32),
        ],
        name="image_tower",
    )(x, g1, wqkv, wout, g2, wup, wdown, wproj)


def pair_mask(lab_ref, pair):
    lab = lab_ref[0, :, PAIR * pair : PAIR * pair + PAIR].astype(F32)
    wide = jnp.broadcast_to(lab, (PAIR, PAIR))
    return wide == wide.T


def text_kernel(
    tok_ref, lab_ref, g1, wqkv, wout, g2, wup, wdown, wproj,
    h2_ref, o_ref, qkv_ref, p_ref, c2_ref, gp_ref, pu_ref, pb_ref, e_ref, emb_ref, cnt_ref,
    pt, po, osc,
):
    step = pl.program_id(0)
    tok = tok_ref[...]
    x = tok.astype(F32)
    h1 = (normalize(x) * g1[...]).astype(BF)
    qkv = mm(h1, wqkv[...]).astype(BF)
    qkv_ref[...] = qkv
    low = lax.broadcasted_iota(jnp.int32, (PAIR, PAIR), 1) < HEAD
    for pair in range(2):
        rows = slice(PAIR * pair, PAIR * pair + PAIR)
        mask = pair_mask(lab_ref, pair)
        mask = jnp.concatenate([mask, mask], 0)
        for j in range(HEADS // 2):
            cols = slice(PAIR * j, PAIR * j + PAIR)
            q2 = qkv[rows, PAIR * j : PAIR * j + PAIR] * jnp.asarray(HEAD**-0.5, BF)
            k2 = qkv[rows, D + PAIR * j : D + PAIR * j + PAIR]
            v2 = qkv[rows, 2 * D + PAIR * j : 2 * D + PAIR * j + PAIR]
            zero = jnp.zeros_like(q2)
            q22 = jnp.concatenate([jnp.where(low, q2, zero), jnp.where(low, zero, q2)], 0)
            s = jnp.where(mask, mm_nt(q22, k2), -1e30)
            ex = jnp.exp(s - jnp.max(s, -1, keepdims=True))
            p = (ex * (1.0 / jnp.sum(ex, -1, keepdims=True))).astype(BF)
            p_ref[pair, j] = p
            v22 = jnp.concatenate([jnp.where(low, v2, zero), jnp.where(low, zero, v2)], 0)
            o = mm(jnp.concatenate([p[:PAIR], p[PAIR:]], 1), v22)
            osc[rows, cols] = o.astype(BF)
    o = osc[...]
    o_ref[...] = o
    x1 = x + mm(o, wout[...])
    c2 = x1 - row_mean(x1)
    c2_ref[...] = c2
    h2 = (c2 * lax.rsqrt(row_mean(c2 * c2) + EPS) * g2[...]).astype(BF)
    h2_ref[...] = h2
    u, slope = gelu_parts(mm(h2, wup[...]))
    gp_ref[...] = slope.astype(BF)
    hit = lax.broadcasted_iota(jnp.int32, (CAP_BLOCK, TOK_BLOCK), 0) == lab_ref[0]
    member = jnp.where(hit, 1.0, 0.0)
    caps = pl.ds(pl.multiple_of(step * CAP_BLOCK, CAP_BLOCK), CAP_BLOCK)
    member_b = member.astype(BF)
    pt[caps, :] = mm(member_b, tok)
    po[caps, :] = mm(member_b, o)
    pu_ref[caps, :] = mm(member_b, u.astype(BF))
    cnt_ref[caps, :] = jnp.broadcast_to(jnp.sum(member, -1, keepdims=True), (CAP_BLOCK, 128))

    @pl.when(step == pl.num_programs(0) - 1)
    def _():
        total = pt[...] + wide_mm(po[...], wout[...]) + wide_mm(pu_ref[...], wdown[...])
        pooled = (total * (1.0 / cnt_ref[:, 0:1])).astype(BF)
        pb_ref[...] = pooled
        e = mm(pooled, wproj[...])
        e_ref[...] = e
        emb_ref[...] = (e * lax.rsqrt(jnp.sum(e * e, -1, keepdims=True) + EPS)).astype(BF)


def text_forward(tok, lab, g1, wqkv, wout, g2, wup, wdown, wproj):
    n = tok.shape[0]
    blocks = n // TOK_BLOCK

    def rows(width):
        return pl.BlockSpec((TOK_BLOCK, width), lambda i: (i, 0))

    def whole(width):
        return pl.BlockSpec((CAPS, width), lambda i: (0, 0))

    shape = jax.ShapeDtypeStruct
    return pl.pallas_call(
        text_kernel,
        grid=(blocks,),
        in_specs=[
            rows(D),
            pl.BlockSpec((1, 1, TOK_BLOCK), lambda i: (i, 0, 0)),
            const_spec((1, D)),
            const_spec((D, 3 * D)),
            const_spec((D, D)),
            const_spec((1, D)),
            const_spec((D, FF)),
            const_spec((FF, D)),
            const_spec((D, D)),
        ],
        out_specs=[
            rows(D), rows(D), rows(3 * D),
            pl.BlockSpec((2, 3, 2 * PAIR, PAIR), lambda i: (i, 0, 0, 0)),
            rows(D), rows(FF),
            whole(FF), whole(D), whole(D), whole(D), whole(128),
        ],
        out_shape=[
            shape((n, D), BF), shape((n, D), BF), shape((n, 3 * D), BF),
            shape((2 * blocks, 3, 2 * PAIR, PAIR), BF),
            shape((n, D), F32), shape((n, FF), BF),
            shape((CAPS, FF), F32), shape((CAPS, D), BF), shape((CAPS, D), F32),
            shape((CAPS, D), BF), shape((CAPS, 128), F32),
        ],
        scratch_shapes=[
            pltpu.VMEM((CAPS, D), F32),
            pltpu.VMEM((CAPS, D), F32),
            pltpu.VMEM((TOK_BLOCK, D), BF),
        ],
        name="text_forward",
    )(tok, lab, g1, wqkv, wout, g2, wup, wdown, wproj)


def cosine_kernel(scale_ref, emb, images, g_ref, sum_ref):
    scale = jnp.exp(jnp.full((1, 1), scale_ref[0], F32))
    g = mm_nt(emb[...], images[...])
    g_ref[...] = g
    sum_ref[...] = jnp.sum(jnp.exp(g * scale), 0, keepdims=True)


def rows_kernel(denom, scale_ref, g_ref, images, pair, dt_ref, part_ref):
    scale = jnp.exp(jnp.full((1, 1), scale_ref[0], F32))
    g = g_ref[...]
    logits = g * scale
    e = jnp.exp(logits)
    total = jnp.sum(e, -1, keepdims=True)
    hit = lax.broadcasted_iota(jnp.int32, g.shape, 1) == pair[...]
    target = jnp.where(hit, 1.0, 0.0)
    lse = jnp.log(total)
    pos = jnp.sum(jnp.where(hit, logits, 0.0), -1, keepdims=True)
    dl = (e * (1.0 / total) - 2.0 * target) * (1.0 / denom)
    dt_ref[...] = mm((dl * scale).astype(BF), images[...])
    temp = jnp.sum(jnp.sum(dl * g, -1, keepdims=True), 0, keepdims=True)
    loss = jnp.sum(lse - 2.0 * pos, 0, keepdims=True)
    lane = lax.broadcasted_iota(jnp.int32, (1, 128), 1)
    part_ref[...] = jnp.where(lane == 0, loss, jnp.where(lane == 1, temp, 0.0))


def place(mine, rb, acc, send_ref, keep_ref):
    for rel in range(32):
        src = acc[pl.ds(pl.multiple_of((mine ^ rel) * rb, 16), rb), :].astype(BF)
        if rel < 16:
            keep_ref[rel * rb : (rel + 1) * rb, :] = src
        else:
            send_ref[(rel - 16) * rb : (rel - 15) * rb, :] = src


def head_kernel(
    denom, devices, scale_ref, mine_ref, g_ref, images, sums, dt_row, part, e_ref, pb, cnt, pu, wproj, wdown,
    send_ref, keep_ref, du_ref, dy_ref, part_out, acc,
):
    scale = jnp.exp(jnp.full((1, 1), scale_ref[0], F32))
    g = g_ref[...]
    total = sums[...]
    dl = jnp.exp(g * scale) * (1.0 / total) * (1.0 / denom)
    temp = jnp.sum(jnp.sum(dl * g, -1, keepdims=True), 0, keepdims=True)
    lse = jnp.sum(jnp.log(total), -1, keepdims=True)
    lane = lax.broadcasted_iota(jnp.int32, (1, 128), 1)
    both = part[...] + jnp.where(lane == 0, lse * (1.0 / devices), jnp.where(lane == 1, temp, 0.0))
    part_out[...] = both * jnp.where(lane == 0, 1.0 / denom, scale)
    dt = dt_row[...] + mm((dl * scale).astype(BF), images[...])
    e = e_ref[...]
    r = lax.rsqrt(jnp.sum(e * e, -1, keepdims=True) + EPS)
    de = (dt - e * (r * r * jnp.sum(dt * e, -1, keepdims=True))) * r
    de = de.astype(BF)
    dpooled = mm_nt(de, wproj[...])
    dy = dpooled * (1.0 / cnt[:, 0:1])
    dyb = dy.astype(BF)
    du = mm_nt(dyb, wdown[...])
    for i, piece in enumerate(split3(du)):
        for b in range(BLOCKS):
            du_ref[b, CAP_BLOCK * i : CAP_BLOCK * (i + 1), :] = piece[CAP_BLOCK * b : CAP_BLOCK * (b + 1)]
    for i, piece in enumerate(split3(dy)):
        for b in range(BLOCKS):
            dy_ref[b, CAP_BLOCK * i : CAP_BLOCK * (i + 1), :] = piece[CAP_BLOCK * b : CAP_BLOCK * (b + 1)]
    acc[0:FF, :] = mm_tn(jnp.concatenate(split3(pu[...]), 0), jnp.concatenate([dyb, dyb, dyb], 0))
    acc[FF : FF + D, :] = mm_tn(pb[...], de)
    acc[FF + D :, :] = jnp.zeros((2048 - FF - D, D), F32)
    place(mine_ref[0], 64, acc, send_ref, keep_ref)


def mlp_back_kernel(
    mine_ref, lab_ref, h2_ref, gp_ref, c2_ref, du_ref, dy_ref, g2, wup,
    dx_ref, gain_ref, send_ref, keep_ref, acc,
):
    step = pl.program_id(0)

    @pl.when(step == 0)
    def _():
        acc[...] = jnp.zeros_like(acc)
        gain_ref[...] = jnp.zeros_like(gain_ref)

    hit = lax.broadcasted_iota(jnp.int32, (3 * CAP_BLOCK, TOK_BLOCK), 0) % CAP_BLOCK == lab_ref[0]
    spread = jnp.where(hit, 1.0, 0.0).astype(BF)
    du = mm_tn(spread, du_ref[0])
    dz = (du * gp_ref[...].astype(F32)).astype(BF)
    dy = mm_tn(spread, dy_ref[0])
    dh = mm_nt(dz, wup[...])
    c2 = c2_ref[...]
    r = lax.rsqrt(row_mean(c2 * c2) + EPS)
    unit = c2 * r
    gain_ref[...] += jnp.sum(dh * unit, 0, keepdims=True)
    dn = dh * g2[...]
    dx_ref[...] = dy + r * (dn - row_mean(dn) - unit * row_mean(dn * unit))
    h2 = h2_ref[...]
    for k in range(4):
        acc[D * k : D * (k + 1), :] += mm_tn(h2, dz[:, D * k : D * (k + 1)])

    @pl.when(step == pl.num_programs(0) - 1)
    def _():
        place(mine_ref[0], 48, acc, send_ref, keep_ref)


def att_back_kernel(
    mine_ref, tok_ref, qkv_ref, p_ref, o_ref, dx_ref, g1, wqkv, wout,
    gtok_ref, gain_ref, send_ref, keep_ref, acc, dsc,
):
    step = pl.program_id(0)

    @pl.when(step == 0)
    def _():
        acc[...] = jnp.zeros_like(acc)
        gain_ref[...] = jnp.zeros_like(gain_ref)

    dx = dx_ref[...]
    dxb = dx.astype(BF)
    acc[0:D, :] += mm_tn(o_ref[...], dxb)
    do = mm_nt(dxb, wout[...]).astype(BF)
    low = lax.broadcasted_iota(jnp.int32, (PAIR, PAIR), 1) < HEAD
    zero = jnp.zeros((PAIR, PAIR), BF)
    half = HEAD**-0.5

    def twice(v):
        return jnp.concatenate([jnp.where(low, v, zero), jnp.where(low, zero, v)], 0)

    for pair in range(2):
        rows = slice(PAIR * pair, PAIR * pair + PAIR)
        for j in range(HEADS // 2):
            cols = slice(PAIR * j, PAIR * j + PAIR)
            q2 = qkv_ref[rows, PAIR * j : PAIR * j + PAIR]
            k2 = qkv_ref[rows, D + PAIR * j : D + PAIR * j + PAIR]
            v2 = qkv_ref[rows, 2 * D + PAIR * j : 2 * D + PAIR * j + PAIR]
            do2 = twice(do[rows, cols])
            pb = p_ref[pair, j]
            p = pb.astype(F32)
            dp = mm_nt(do2, v2)
            ds = (p * (dp - jnp.sum(dp * p, -1, keepdims=True))).astype(BF)
            dq = mm(jnp.concatenate([ds[:PAIR], ds[PAIR:]], 1), twice(k2)) * half
            dk = mm_tn(ds, twice(q2)) * half
            dv = mm_tn(pb, do2)
            dsc[rows, PAIR * j : PAIR * j + PAIR] = dq.astype(BF)
            dsc[rows, D + PAIR * j : D + PAIR * j + PAIR] = dk.astype(BF)
            dsc[rows, 2 * D + PAIR * j : 2 * D + PAIR * j + PAIR] = dv.astype(BF)
    x = tok_ref[...].astype(F32)
    centre = x - row_mean(x)
    r = lax.rsqrt(row_mean(centre * centre) + EPS)
    unit = centre * r
    gain = g1[...]
    h1 = (unit * gain).astype(BF)
    dqkv = dsc[...]
    for k in range(3):
        acc[D * (k + 1) : D * (k + 2), :] += mm_tn(h1, dqkv[:, D * k : D * (k + 1)])
    dh = mm_nt(dqkv, wqkv[...])
    gain_ref[...] += jnp.sum(dh * unit, 0, keepdims=True)
    dn = dh * gain
    gtok_ref[...] = dx + r * (dn - row_mean(dn) - unit * row_mean(dn * unit))

    @pl.when(step == pl.num_programs(0) - 1)
    def _():
        place(mine_ref[0], 48, acc, send_ref, keep_ref)


def spread_head_kernel(mine_ref, own, other, proj_ref, down_ref, full):
    mine = mine_ref[0]
    for rel in range(32):
        src = own if rel < 16 else other
        at = (rel % 16) * 64
        full[pl.ds(pl.multiple_of((mine ^ rel) * 64, 64), 64), :] = src[at : at + 64, :].astype(F32)
    down_ref[...] = full[0:FF, :]
    proj_ref[...] = full[FF : FF + D, :]


def spread_up_kernel(mine_ref, own, other, up_ref, full):
    mine = mine_ref[0]
    for rel in range(32):
        src = own if rel < 16 else other
        at = (rel % 16) * 48
        full[pl.ds(pl.multiple_of((mine ^ rel) * 48, 16), 48), :] = src[at : at + 48, :].astype(F32)
    for k in range(4):
        up_ref[:, D * k : D * (k + 1)] = full[D * k : D * (k + 1), :]


def spread_att_kernel(mine_ref, own, other, out_ref, qkv_ref, full):
    mine = mine_ref[0]
    for rel in range(32):
        src = own if rel < 16 else other
        at = (rel % 16) * 48
        full[pl.ds(pl.multiple_of((mine ^ rel) * 48, 16), 48), :] = src[at : at + 48, :].astype(F32)
    out_ref[...] = full[0:D, :]
    for k in range(3):
        qkv_ref[:, D * k : D * (k + 1)] = full[D * (k + 1) : D * (k + 2), :]


SMEM = pl.BlockSpec(memory_space=pltpu.SMEM)
VMEM = pl.BlockSpec(memory_space=pltpu.VMEM)


def simple(kernel, outs, scratch=(), smem=0, name=None):
    def call(*args):
        return pl.pallas_call(
            kernel,
            in_specs=[SMEM] * smem + [VMEM] * (len(args) - smem),
            out_specs=[VMEM] * len(outs),
            out_shape=[jax.ShapeDtypeStruct(s, t) for s, t in outs],
            scratch_shapes=list(scratch),
            name=name,
        )(*args)

    return call


def mlp_back(mine, lab, h2, gp, c2, du, dy, g2, wup):
    n = h2.shape[0]

    def rows(width):
        return pl.BlockSpec((TOK_BLOCK, width), lambda i: (i, 0))

    def blk(a, b):
        return pl.BlockSpec((1, a, b), lambda i: (i, 0, 0))

    shape = jax.ShapeDtypeStruct
    return pl.pallas_call(
        mlp_back_kernel,
        grid=(n // TOK_BLOCK,),
        in_specs=[
            SMEM, blk(1, TOK_BLOCK), rows(D), rows(FF), rows(D), blk(3 * CAP_BLOCK, FF), blk(3 * CAP_BLOCK, D),
            const_spec((1, D)), const_spec((D, FF)),
        ],
        out_specs=[rows(D), pl.BlockSpec((1, D), lambda i: (0, 0))]
        + [pl.BlockSpec((768, D), lambda i: (0, 0))] * 2,
        out_shape=[shape((n, D), F32), shape((1, D), F32), shape((768, D), BF), shape((768, D), BF)],
        scratch_shapes=[pltpu.VMEM((1536, D), F32)],
        name="mlp_back",
    )(mine, lab, h2, gp, c2, du, dy, g2, wup)


def att_back(mine, tok, qkv, p, o, dx, g1, wqkv, wout):
    n = tok.shape[0]

    def rows(width):
        return pl.BlockSpec((TOK_BLOCK, width), lambda i: (i, 0))

    shape = jax.ShapeDtypeStruct
    return pl.pallas_call(
        att_back_kernel,
        grid=(n // TOK_BLOCK,),
        in_specs=[
            SMEM, rows(D), rows(3 * D), pl.BlockSpec((2, 3, 2 * PAIR, PAIR), lambda i: (i, 0, 0, 0)), rows(D), rows(D),
            const_spec((1, D)), const_spec((D, 3 * D)), const_spec((D, D)),
        ],
        out_specs=[rows(D), pl.BlockSpec((1, D), lambda i: (0, 0))]
        + [pl.BlockSpec((768, D), lambda i: (0, 0))] * 2,
        out_shape=[shape((n, D), F32), shape((1, D), F32), shape((768, D), BF), shape((768, D), BF)],
        scratch_shapes=[pltpu.VMEM((1536, D), F32), pltpu.VMEM((TOK_BLOCK, 3 * D), BF)],
        name="att_back",
    )(mine, tok, qkv, p, o, dx, g1, wqkv, wout)


AXES = ("dp", "replica")


class Hops:
    def __init__(self):
        index = lax.axis_index(AXES)
        self.mine = ((index & 1) * 16 + ((index >> 1) & 3) * 4 + (index >> 3)).astype(jnp.int32).reshape(1)

    def swap(self, v, mask):
        return lax.ppermute(v, AXES, [(i, i ^ mask) for i in range(32)])

    def gather_images(self, emb):
        zs = jnp.concatenate([emb] + [self.swap(emb, 8 * m) for m in (1, 2, 3)], 0)
        ps = jnp.concatenate([zs] + [self.swap(zs, 2 * m) for m in (1, 2, 3)], 0)
        return jnp.concatenate([ps, self.swap(ps, 1)], 0)

    def image_ids(self, pair):
        owner, row = pair // CAPS, pair % CAPS
        block = ((owner & 1) * 16 + ((owner >> 1) & 3) * 4 + (owner >> 3)) ^ self.mine
        return block * CAPS + row

    def sum_columns(self, sums):
        return sums

    def total(self, v):
        for mask in (1, 2, 4, 8, 16):
            v = v + self.swap(v, mask)
        return v

    def reduce(self, send, keep, rb):
        part = keep.astype(F32) + self.swap(send, 1).astype(F32)
        part = part.astype(BF).reshape(4, 4 * rb, D)
        got = [self.swap(part[m], 2 * m) for m in (1, 2, 3)]
        part = part[0].astype(F32) + (got[0].astype(F32) + got[1].astype(F32) + got[2].astype(F32))
        part = part.astype(BF).reshape(4, rb, D)
        got = [self.swap(part[m], 8 * m) for m in (1, 2, 3)]
        part = part[0].astype(F32) + (got[0].astype(F32) + got[1].astype(F32) + got[2].astype(F32))
        return part.astype(BF)

    def collect(self, part):
        zs = jnp.concatenate([part] + [self.swap(part, 8 * m) for m in (1, 2, 3)], 0)
        ps = jnp.concatenate([zs] + [self.swap(zs, 2 * m) for m in (1, 2, 3)], 0)
        return ps, self.swap(ps, 1)

    def all_sum(self, send, keep, rb):
        return self.collect(self.reduce(send, keep, rb))


class Plain:
    def __init__(self):
        self.mine = jnp.zeros((1,), jnp.int32)

    def gather_images(self, emb):
        return lax.all_gather(emb, AXES, axis=0, tiled=True)

    def image_ids(self, pair):
        return pair

    def total(self, v):
        return lax.psum(v, AXES)

    def all_sum(self, send, keep, rb):
        both = lax.psum((keep.astype(F32), send.astype(F32)), AXES)
        return both[0].astype(BF), both[1].astype(BF)


def shards(
    devices, tuned,
    text_tokens, segment_ids, pair_index, image_tokens,
    img_ln1, img_qkv, img_out, img_ln2, img_up, img_down, img_proj,
    txt_ln1, txt_qkv, txt_out, txt_ln2, txt_up, txt_down, txt_proj, log_scale,
):
    net = Hops() if tuned else Plain()
    mine = net.mine
    total = CAPS * devices
    denom = 2.0 * total
    emb = image_tower(
        image_tokens, img_ln1.reshape(1, D), img_qkv, img_out, img_ln2.reshape(1, D), img_up, img_down, img_proj
    )
    images = net.gather_images(emb)
    row_of = jnp.arange(segment_ids.shape[0], dtype=jnp.int32) % (TOK_BLOCK // segment_ids.shape[1])
    lab = (segment_ids + PACK * row_of[:, None]).reshape(BLOCKS, 1, TOK_BLOCK)
    g1, g2 = txt_ln1.reshape(1, D), txt_ln2.reshape(1, D)
    h2, o, qkv, p, c2, gp, pu, pb, e, temb, cnt = text_forward(
        text_tokens, lab, g1, txt_qkv, txt_out, g2, txt_up, txt_down, txt_proj
    )
    g, sums = simple(cosine_kernel, [((CAPS, total), F32), ((1, total), F32)], smem=1, name="cosine")(
        log_scale, temb, images
    )
    dt_row, part = simple(
        functools.partial(rows_kernel, denom), [((CAPS, D), F32), ((1, 128), F32)], smem=1, name="rows"
    )(log_scale, g, images, net.image_ids(pair_index).reshape(CAPS, 1))
    sums = net.total(sums) if not tuned else column_total(net, sums)
    send, keep, du, dy, part = simple(
        functools.partial(head_kernel, denom, devices),
        [((1024, D), BF), ((1024, D), BF), ((BLOCKS, 48, FF), BF), ((BLOCKS, 48, D), BF), ((1, 128), F32)],
        [pltpu.VMEM((2048, D), F32)],
        smem=2,
        name="head_back",
    )(log_scale, mine, g, images, sums, dt_row, part, e, pb, cnt, pu, txt_proj, txt_down)
    grad_proj, grad_down = simple(
        spread_head_kernel, [((D, D), F32), ((FF, D), F32)], [pltpu.VMEM((2048, D), F32)], smem=1, name="spread_head"
    )(mine, *net.all_sum(send, keep, 64))
    dx, gain2, send, keep = mlp_back(mine, lab, h2, gp, c2, du, dy, g2, txt_up)
    (grad_up,) = simple(
        spread_up_kernel, [((D, FF), F32)], [pltpu.VMEM((1536, D), F32)], smem=1, name="spread_up"
    )(mine, *net.all_sum(send, keep, 48))
    grad_tokens, gain1, send, keep = att_back(mine, text_tokens, qkv, p, o, dx, g1, txt_qkv, txt_out)
    grad_out, grad_qkv = simple(
        spread_att_kernel, [((D, D), F32), ((D, 3 * D), F32)], [pltpu.VMEM((1536, D), F32)], smem=1, name="spread_att"
    )(mine, *net.all_sum(send, keep, 48))
    small = net.total(jnp.concatenate([gain1, gain2, part], 1))
    return (
        small[0, 768:769], grad_tokens, small[0, 0:384], grad_qkv, grad_out, small[0, 384:768],
        grad_up, grad_down, grad_proj, small[0, 769:770],
    )


def column_total(net, sums):
    v = sums.reshape(32, CAPS)
    for mask, bit in ((1, 16), (2, 4), (4, 8), (8, 1), (16, 2)):
        other = net.swap(v, mask)
        other = other.reshape(32 // (2 * bit), 2, bit, CAPS)[:, ::-1].reshape(32, CAPS)
        v = v + other
    return v.reshape(1, 32 * CAPS)


def solution(mesh):
    both = ("dp", "replica")
    devices = mesh.shape["dp"] * mesh.shape["replica"]
    tuned = (mesh.shape["dp"], mesh.shape["replica"]) == (8, 4)
    rows = P(both, None)
    return jax.shard_map(
        functools.partial(shards, devices, tuned),
        mesh=mesh,
        in_specs=(rows, rows, P(both), P(both, None, None)) + (P(),) * 15,
        out_specs=(P(), rows) + (P(),) * 8,
        check_vma=False,
    )
```

time: 588 us -> 236 us (0.40); the launches traced: 578 us -> 235 us
  waiting for transfers between devices: 262 us -> 65.2 us
  matrix products: 110 us -> 0 us
  local copies, waits for them, and re-layouts: 103 us -> 16.7 us
  Pallas kernels: 0 us -> 75.6 us
  starting transfers between devices: 0.38 us -> 71.1 us
  blocking collectives: 42.7 us -> 0 us
  other arithmetic: 40.2 us -> 4.89 us
  between operations: 19 us -> 1.85 us
    psum x1 -> x0, waiting for transfers between devices: 111 us -> none  [shards(): lax.psum((grad_ln1, grad_qkv, grad_out, grad_ln2, grad_up, grad_down, gra...]
    dot_general x33 -> x0, matrix products: 110 us -> none  [the longest x10 43.1 us: project(): return jnp.dot(left_mat, right_mat, preferred_element_type=jnp.float32)]
    reduce_scatter x1 -> x0, waiting for transfers between devices: 102 us -> none  [shards(): lax.psum_scatter(jnp.einsum('ic,ie->ce', col_round, image_emb, preferred_...]
    pallas_call x0 -> x10, Pallas kernels: none -> 75.6 us  [the longest x6 20.1 us: call(): pl.pallas_call(kernel, in_specs=[SMEM] * smem + [VMEM] * (len(args) - sme...]
    ppermute x0 -> x59, starting transfers between devices: none -> 71.1 us  [swap(): return lax.ppermute(v, AXES, [(i, i ^ mask) for i in range(32)])]
    ppermute x0 -> x59, waiting for transfers between devices: none -> 65.2 us  [swap(): return lax.ppermute(v, AXES, [(i, i ^ mask) for i in range(32)])]
    all_gather x2 -> x0, waiting for transfers between devices: 50.1 us -> none  [the longest x1 50.1 us: shards(): lax.all_gather(image_emb, ('dp', 'replica'), axis=0, tiled=True)]
    psum x1 -> x0, blocking collectives: 42.7 us -> none  [shards(): lax.psum((grad_ln1, grad_qkv, grad_out, grad_ln2, grad_up, grad_down, gra...]
  transfers between devices with their start and end apart: 4 -> 59, of which waited for: 3 -> 25; matrix products, arithmetic and copies ran while one was open for 29% -> 3% of each run, Pallas kernels for 0% -> 11%
where the time goes in v1:
time: 236 us; the launch traced here: 235 us
  Pallas kernels  75.6 us (32%)
  starting transfers between devices  71.1 us (30%)
  waiting for transfers between devices  65.2 us (28%)
  local copies, waits for them, and re-layouts  16.7 us (7%)
  other arithmetic  4.89 us (2%)
    ppermute x59, starting transfers between devices, swap(): return lax.ppermute(v, AXES, [(i, i ^ mask) for i in range(32)])  71.1 us
    ppermute x59, waiting for transfers between devices, swap(): return lax.ppermute(v, AXES, [(i, i ^ mask) for i in range(32)])  65.2 us
    pallas_call x6, Pallas kernels, call(): pl.pallas_call(kernel, in_specs=[SMEM] * smem + [VMEM] * (len(args) - sme...  20.1 us
    pallas_call x1, Pallas kernels, att_back(): pl.pallas_call(att_back_kernel, grid=(n // TOK_BLOCK,), in_specs=[SMEM, r...  16.7 us
    pallas_call x1, Pallas kernels, text_forward(): pl.pallas_call(text_kernel, grid=(blocks,), in_specs=[rows(D), pl.BlockSp...  16.3 us
    pallas_call x1, Pallas kernels, image_tower(): pl.pallas_call(image_kernel, grid=(count // IMG_BLOCK,), in_specs=[pl.Blo...  13.6 us
    pallas_call x1, Pallas kernels, mlp_back(): pl.pallas_call(mlp_back_kernel, grid=(n // TOK_BLOCK,), in_specs=[SMEM, b...  8.93 us
    unnamed x60, local copies, waits for them, and re-layouts  8.89 us
  transfers between devices with their start and end apart: 59, of which 25 were waited for; matrix products, arithmetic and copies ran while one was open for 3% of the time, Pallas kernels for 11%

profile of v1, /device:TPU:0, one launch (start us, length us, event | category | flops | bytes accessed | tf_op | source)
XLA Modules:
  0.0 235.2 jit_solution(4865589199095716481)
XLA Ops:
  3.1 4.7 %copy.29.x_ref = bf16[64,50,384]{2,1,0:T(8,128)(2,1)} copy(bf16[64,50,384]{2,0,1:T(8,128)(2,1)} %param.22) | data formatting | bytes 4915200 | tf_op args[3]
  7.8 13.6 %image_tower.1 = bf16[64,384]{1,0:T(8,128)(2,1)} custom-call(bf16[64,50,384]{2,1,0:T(8,128)(2,1)} %copy.29.x_ref, f32[1,384]{1,0:T(1,128)} %reshape.158.g1, bf16[384,1152]{1,0:T(8,128)(2,1)} %wqkv.4, bf16[384,384]{1,0:T(8,128)(2,1)} %wout.4, f32[1,384]{1,0:T(1,128)} %reshape.159.g2, bf16[384,1536]{1,0:T(8,128)(2,1)} %wup.4, bf16[1536,384]{1,0:T(8,128)(2,1)} %wdown.4, ...), custom_call_target="tpu_custom_call" | custom-call | tf_op jit(solution)/shard_map/image_tower/pallas_call | solution.py:130
  21.4 5.1 %collective-permute-start.2 = (bf16[64,384]{1,0:T(8,128)(2,1)}, bf16[64,384]{1,0:T(8,128)(2,1)S(1)}, u32[]{:S(2)}, u32[]{:S(2)}) collective-permute-start(bf16[64,384]{1,0:T(8,128)(2,1)} %image_tower.1), channel_id=1, source_target_pairs={{0,24},{1,25},{2,26},{3,27},{4,28},{5,29},{6,30},{7,31},{8,16},{9,... | collective-permute-start | bytes 147464 | tf_op jit(solution)/shard_map/ppermute | solution.py:529
  29.0 2.8 %collective-permute-done.1 = bf16[64,384]{1,0:T(8,128)(2,1)S(1)} collective-permute-done((bf16[64,384]{1,0:T(8,128)(2,1)}, bf16[64,384]{1,0:T(8,128)(2,1)S(1)}, u32[]{:S(2)}, u32[]{:S(2)}) %collective-permute-start.1) | collective-permute-done | bytes 49184 | tf_op jit(solution)/shard_map/ppermute | solution.py:529
  32.6 2.5 %collective-permute-start.5 = (bf16[256,384]{1,0:T(8,128)(2,1)S(1)}, bf16[256,384]{1,0:T(8,128)(2,1)S(1)}, u32[]{:S(2)}, u32[]{:S(2)}) collective-permute-start(bf16[256,384]{1,0:T(8,128)(2,1)S(1)} %pad_maximum_fusion), channel_id=1, source_target_pairs={{0,6},{1,7},{2,4},{3,5},{4,2},{5,3},{6,0},{7,1},{8,14},{9,15},{10,... | collective-permute-start | bytes 589832 | tf_op jit(solution)/shard_map/ppermute | solution.py:529
  36.2 7.4 %collective-permute-done.3 = bf16[256,384]{1,0:T(8,128)(2,1)S(1)} collective-permute-done((bf16[256,384]{1,0:T(8,128)(2,1)S(1)}, bf16[256,384]{1,0:T(8,128)(2,1)S(1)}, u32[]{:S(2)}, u32[]{:S(2)}) %collective-permute-start.3) | collective-permute-done | bytes 196640 | tf_op jit(solution)/shard_map/ppermute | solution.py:529
  46.5 16.3 %text_forward.1 = (bf16[1024,384]{1,0:T(8,128)(2,1)}, bf16[1024,384]{1,0:T(8,128)(2,1)}, bf16[1024,1152]{1,0:T(8,128)(2,1)}, bf16[8,3,256,128]{3,2,1,0:T(8,128)(...) custom-call(bf16[1024,384]{1,0:T(8,128)(2,1)} %tok_ref.3, ...), custom_call_target="tpu_custom_call" | custom-call | tf_op jit(solution)/shard_map/text_forward/pallas_call | solution.py:229
  64.1 2.8 %cosine.1 = (f32[64,2048]{1,0:T(8,128)}, f32[1,2048]{1,0:T(1,128)}) custom-call(f32[1]{0:T(128)S(6)} %copy.64.scale_ref, bf16[64,384]{1,0:T(8,128)(2,1)} %get-tuple-element.48.emb, bf16[2048,384]{1,0:T(8,128)(2,1)} %copy-done), custom_call_target="tpu_custom_call" | custom-call | tf_op jit(solution)/shard_map/cosine/pallas_call | solution.py:461
  71.7 2.3 collective-permute-done.8
  75.4 2.4 %collective-permute-done.9 = f32[32,64]{1,0:T(8,128)S(1)} collective-permute-done((f32[32,64]{1,0:T(8,128)S(1)}, f32[32,64]{1,0:T(8,128)S(1)}, u32[]{:S(2)}, u32[]{:S(2)}) %collective-permute-start.9) | collective-permute-done | bytes 8224 | tf_op jit(solution)/shard_map/ppermute | solution.py:529
  78.5 3.0 %collective-permute-done.10 = f32[32,64]{1,0:T(8,128)S(1)} collective-permute-done((f32[32,64]{1,0:T(8,128)S(1)}, f32[32,64]{1,0:T(8,128)S(1)}, u32[]{:S(2)}, u32[]{:S(2)}) %collective-permute-start.10) | collective-permute-done | bytes 8224 | tf_op jit(solution)/shard_map/ppermute | solution.py:529
  83.6 2.8 %rows.1 = (f32[64,384]{1,0:T(8,128)}, f32[1,128]{1,0:T(1,128)}) custom-call(f32[1]{0:T(128)S(6)} %copy.64.scale_ref, f32[64,2048]{1,0:T(8,128)} %get-tuple-element.49.g_ref, bf16[2048,384]{1,0:T(8,128)(2,1)} %copy-done, s32[64,1]{1,0:T(8,128)} %copy.30.pair), custom_call_target="tpu_custom_call" | custom-call | tf_op jit(solution)/shard_map/rows/pallas_call | solution.py:461
  87.4 5.3 %head_back.1 = (bf16[1024,384]{1,0:T(8,128)(2,1)}, bf16[1024,384]{1,0:T(8,128)(2,1)}, bf16[4,48,1536]{2,1,0:T(8,128)(2,1)}, bf16[4,48,384]{2,1,0:T(8,128)(2,1)}, f32[1,128]{1,0:T(1,128)}) custom-call(f32[1]{0:T(128)S(6)} %copy.64.scale_ref, s32[1]{0:T(128)} %bitcast.mine_ref, f32[64,2048]{1,0:T(8,128)} %get-tuple-element.49.g_ref, ...), custom_call_target="tpu_custom_call" | custom-call | tf_op jit(solution)/shard_map/head_back/pallas_call | solution.py:461
  92.8 8.9 %mlp_back.1 = (f32[1024,384]{1,0:T(8,128)}, f32[1,384]{1,0:T(1,128)}, bf16[768,384]{1,0:T(8,128)(2,1)}, bf16[768,384]{1,0:T(8,128)(2,1)}) custom-call(s32[1]{0:T(128)} %bitcast.mine_ref, s32[4,1,256]{2,1,0:T(1,128)} %reshape.155.lab_ref, bf16[1024,384]{1,0:T(8,128)(2,1)} %get-tuple-element.45.h2_ref, bf16[1024,1536]{1,0:T(8,128)(2,1)} %get-tuple-element.46.gp_ref, ...), custom_call_target="tpu_custom_call" | custom-call | tf_op jit(solution)/shard_map/mlp_back/pallas_call | solution.py:483
  101.7 16.7 %att_back.1 = (f32[1024,384]{1,0:T(8,128)}, f32[1,384]{1,0:T(1,128)}, bf16[768,384]{1,0:T(8,128)(2,1)}, bf16[768,384]{1,0:T(8,128)(2,1)}) custom-call(s32[1]{0:T(128)} %bitcast.mine_ref, bf16[1024,384]{1,0:T(8,128)(2,1)} %tok_ref.3, bf16[1024,1152]{1,0:T(8,128)(2,1)} %get-tuple-element.42.qkv_ref, bf16[8,3,256,128]{3,2,1,0:T(8,128)(2,1)} %get-tuple-element.43.p_ref, ...), custom_call_target="tpu_custom_call" | custom-call | tf_op jit(solution)/shard_map/att_back/pallas_call | solution.py:505
  130.3 2.4 %collective-permute-done.20 = bf16[192,384]{1,0:T(8,128)(2,1)S(1)} collective-permute-done((bf16[192,384]{1,0:T(8,128)(2,1)S(1)}, bf16[192,384]{1,0:T(8,128)(2,1)S(1)}, u32[]{:S(2)}, u32[]{:S(2)}) %collective-permute-start.20) | collective-permute-done | bytes 147488 | tf_op jit(solution)/shard_map/ppermute | solution.py:529
  151.2 2.4 %collective-permute-start.38 = (bf16[48,384]{1,0:T(8,128)(2,1)S(1)}, bf16[48,384]{1,0:T(8,128)(2,1)S(1)}, u32[]{:S(2)}, u32[]{:S(2)}) collective-permute-start(bf16[48,384]{1,0:T(8,128)(2,1)S(1)} %get-tuple-element.79), channel_id=1, source_target_pairs={{0,8},{1,9},{2,10},{3,11},{4,12},{5,13},{6,14},{7,15},{8,0},{9,1},... | collective-permute-start | bytes 110600 | tf_op jit(solution)/shard_map/ppermute | solution.py:529
  159.5 7.5 %collective-permute-done.27 = bf16[192,384]{1,0:T(8,128)(2,1)S(1)} collective-permute-done((bf16[192,384]{1,0:T(8,128)(2,1)S(1)}, bf16[192,384]{1,0:T(8,128)(2,1)S(1)}, u32[]{:S(2)}, u32[]{:S(2)}) %collective-permute-start.27) | collective-permute-done | bytes 147488 | tf_op jit(solution)/shard_map/ppermute | solution.py:529
  173.4 4.3 %collective-permute-done.42 = bf16[192,384]{1,0:T(8,128)(2,1)S(1)} collective-permute-done((bf16[192,384]{1,0:T(8,128)(2,1)S(1)}, bf16[192,384]{1,0:T(8,128)(2,1)S(1)}, u32[]{:S(2)}, u32[]{:S(2)}) %collective-permute-start.42) | collective-permute-done | bytes 147488 | tf_op jit(solution)/shard_map/ppermute | solution.py:529
  180.5 2.6 %collective-permute-done.50 = bf16[64,384]{1,0:T(8,128)(2,1)S(1)} collective-permute-done((bf16[64,384]{1,0:T(8,128)(2,1)S(1)}, bf16[64,384]{1,0:T(8,128)(2,1)S(1)}, u32[]{:S(2)}, u32[]{:S(2)}) %collective-permute-start.50) | collective-permute-done | bytes 49184 | tf_op jit(solution)/shard_map/ppermute | solution.py:529
  185.2 2.3 collective-permute-start.52
  192.5 4.6 %collective-permute-done.55 = bf16[256,384]{1,0:T(8,128)(2,1)S(1)} collective-permute-done((bf16[256,384]{1,0:T(8,128)(2,1)S(1)}, bf16[256,384]{1,0:T(8,128)(2,1)S(1)}, u32[]{:S(2)}, u32[]{:S(2)}) %collective-permute-start.55) | collective-permute-done | bytes 196640 | tf_op jit(solution)/shard_map/ppermute | solution.py:529
  198.7 5.0 %collective-permute-done.57 = bf16[256,384]{1,0:T(8,128)(2,1)S(1)} collective-permute-done((bf16[256,384]{1,0:T(8,128)(2,1)S(1)}, bf16[256,384]{1,0:T(8,128)(2,1)S(1)}, u32[]{:S(2)}, u32[]{:S(2)}) %collective-permute-start.57) | collective-permute-done | bytes 196640 | tf_op jit(solution)/shard_map/ppermute | solution.py:529
  204.6 2.3 collective-permute-done.12
  208.2 2.3 collective-permute-done.13
  211.7 2.5 %collective-permute-done.14 = f32[1,896]{1,0:T(1,128)S(1)} collective-permute-done((f32[1,896]{1,0:T(1,128)S(1)}, f32[1,896]{1,0:T(1,128)S(1)}, u32[]{:S(2)}, u32[]{:S(2)}) %collective-permute-start.14) | collective-permute-done | bytes 3616 | tf_op jit(solution)/shard_map/ppermute | solution.py:529
  214.1 2.9 %collective-permute-start.15 = (f32[1,896]{1,0:T(1,128)S(1)}, f32[1,896]{1,0:T(1,128)S(1)}, u32[]{:S(2)}, u32[]{:S(2)}) collective-permute-start(f32[1,896]{1,0:T(1,128)S(1)} %add.170), channel_id=1, source_target_pairs={{0,8},{1,9},{2,10},{3,11},{4,12},{5,13},{6,14},{7,15},{8,0},{9,1},... | collective-permute-start | bytes 10760 | tf_op jit(solution)/shard_map/ppermute | solution.py:529
  218.7 2.2 collective-permute-start.16
  220.8 2.3 collective-permute-done.16
  224.4 3.0 %spread_up.1 = f32[384,1536]{1,0:T(8,128)} custom-call(s32[1]{0:T(128)} %bitcast.mine_ref, bf16[768,384]{1,0:T(8,128)(2,1)} %copy-done.5, bf16[768,384]{1,0:T(8,128)(2,1)} %collective-permute-done.44.other), custom_call_target="tpu_custom_call" | custom-call | tf_op jit(solution)/shard_map/spread_up/pallas_call | solution.py:461
  228.2 2.8 %spread_att.1 = (f32[384,384]{1,0:T(8,128)}, f32[384,1152]{1,0:T(8,128)}) custom-call(s32[1]{0:T(128)} %bitcast.mine_ref, bf16[768,384]{1,0:T(8,128)(2,1)} %copy-done.4, bf16[768,384]{1,0:T(8,128)(2,1)} %copy-done.7), custom_call_target="tpu_custom_call" | custom-call | tf_op jit(solution)/shard_map/spread_att/pallas_call | solution.py:461
  231.9 3.3 %spread_head.1 = (f32[384,384]{1,0:T(8,128)}, f32[1536,384]{1,0:T(8,128)}) custom-call(s32[1]{0:T(128)} %bitcast.mine_ref, bf16[1024,384]{1,0:T(8,128)(2,1)} %copy-done.1, bf16[1024,384]{1,0:T(8,128)(2,1)} %copy-done.2), custom_call_target="tpu_custom_call" | custom-call | tf_op jit(solution)/shard_map/spread_head/pallas_call | solution.py:461
  (215 shorter events, 81.8 us)
Async XLA Ops:
  21.4 7.6 %collective-permute-start.2 = (bf16[64,384]{1,0:T(8,128)(2,1)}, bf16[64,384]{1,0:T(8,128)(2,1)S(1)}, u32[]{:S(2)}, u32[]{:S(2)}) collective-permute-start(bf16[64,384]{1,0:T(8,128)(2,1)} %image_tower.1), channel_id=1, source_target_pairs={{0,24},{1,25},{2,26},{3,27},{4,28},{5,29},{6,30},{7,31},{8,16},{9,... | collective-permute-start | bytes 147464 | tf_op jit(solution)/shard_map/ppermute | solution.py:529
  32.6 11.2 %collective-permute-start.5 = (bf16[256,384]{1,0:T(8,128)(2,1)S(1)}, bf16[256,384]{1,0:T(8,128)(2,1)S(1)}, u32[]{:S(2)}, u32[]{:S(2)}) collective-permute-start(bf16[256,384]{1,0:T(8,128)(2,1)S(1)} %pad_maximum_fusion), channel_id=1, source_target_pairs={{0,6},{1,7},{2,4},{3,5},{4,2},{5,3},{6,0},{7,1},{8,14},{9,15},{10,... | collective-permute-start | bytes 589832 | tf_op jit(solution)/shard_map/ppermute | solution.py:529
  35.1 8.6 %collective-permute-start.4 = (bf16[256,384]{1,0:T(8,128)(2,1)S(1)}, bf16[256,384]{1,0:T(8,128)(2,1)S(1)}, u32[]{:S(2)}, u32[]{:S(2)}) collective-permute-start(bf16[256,384]{1,0:T(8,128)(2,1)S(1)} %pad_maximum_fusion), channel_id=1, source_target_pairs={{0,4},{1,5},{2,6},{3,7},{4,0},{5,1},{6,2},{7,3},{8,12},{9,13},{10,... | collective-permute-start | bytes 589832 | tf_op jit(solution)/shard_map/ppermute | solution.py:529
  35.6 8.0 %collective-permute-start.3 = (bf16[256,384]{1,0:T(8,128)(2,1)S(1)}, bf16[256,384]{1,0:T(8,128)(2,1)S(1)}, u32[]{:S(2)}, u32[]{:S(2)}) collective-permute-start(bf16[256,384]{1,0:T(8,128)(2,1)S(1)} %pad_maximum_fusion), channel_id=1, source_target_pairs={{0,2},{1,3},{2,0},{3,1},{4,6},{5,7},{6,4},{7,5},{8,10},{9,11},{10,... | collective-permute-start | bytes 589832 | tf_op jit(solution)/shard_map/ppermute | solution.py:529
  43.9 18.9 %collective-permute-start.6 = (bf16[1024,384]{1,0:T(8,128)(2,1)S(1)}, bf16[1024,384]{1,0:T(8,128)(2,1)S(1)}, u32[]{:S(2)}, u32[]{:S(2)}) collective-permute-start(bf16[1024,384]{1,0:T(8,128)(2,1)S(1)} %get-tuple-element.94), channel_id=1, source_target_pairs={{0,1},{1,0},{2,3},{3,2},{4,5},{5,4},{6,7},{7,6},{8,9},{9,8},{10,11... | collective-permute-start | bytes 2359304 | tf_op jit(solution)/shard_map/ppermute | solution.py:529
  119.0 31.9 %collective-permute-start.45 = (bf16[1024,384]{1,0:T(8,128)(2,1)S(1)}, bf16[1024,384]{1,0:T(8,128)(2,1)S(1)}, u32[]{:S(2)}, u32[]{:S(2)}) collective-permute-start(bf16[1024,384]{1,0:T(8,128)(2,1)S(1)} %copy-done.14), channel_id=1, source_target_pairs={{0,1},{1,0},{2,3},{3,2},{4,5},{5,4},{6,7},{7,6},{8,9},{9,8},{10,11... | collective-permute-start | bytes 2359304 | tf_op jit(solution)/shard_map/ppermute | solution.py:529
  123.6 9.2 %collective-permute-start.20 = (bf16[192,384]{1,0:T(8,128)(2,1)S(1)}, bf16[192,384]{1,0:T(8,128)(2,1)S(1)}, u32[]{:S(2)}, u32[]{:S(2)}) collective-permute-start(bf16[192,384]{1,0:T(8,128)(2,1)S(1)} %get-tuple-element.89), channel_id=1, source_target_pairs={{0,6},{1,7},{2,4},{3,5},{4,2},{5,3},{6,0},{7,1},{8,14},{9,15},{10,... | collective-permute-start | bytes 442376 | tf_op jit(solution)/shard_map/ppermute | solution.py:529
  124.8 8.6 %collective-permute-start.19 = (bf16[192,384]{1,0:T(8,128)(2,1)S(1)}, bf16[192,384]{1,0:T(8,128)(2,1)S(1)}, u32[]{:S(2)}, u32[]{:S(2)}) collective-permute-start(bf16[192,384]{1,0:T(8,128)(2,1)S(1)} %get-tuple-element.90), channel_id=1, source_target_pairs={{0,4},{1,5},{2,6},{3,7},{4,0},{5,1},{6,2},{7,3},{8,12},{9,13},{10,... | collective-permute-start | bytes 442376 | tf_op jit(solution)/shard_map/ppermute | solution.py:529
  125.8 9.4 %collective-permute-start.32 = (bf16[192,384]{1,0:T(8,128)(2,1)S(1)}, bf16[192,384]{1,0:T(8,128)(2,1)S(1)}, u32[]{:S(2)}, u32[]{:S(2)}) collective-permute-start(bf16[192,384]{1,0:T(8,128)(2,1)S(1)} %get-tuple-element.85), channel_id=1, source_target_pairs={{0,2},{1,3},{2,0},{3,1},{4,6},{5,7},{6,4},{7,5},{8,10},{9,11},{10,... | collective-permute-start | bytes 442376 | tf_op jit(solution)/shard_map/ppermute | solution.py:529
  128.8 9.6 %collective-permute-start.34 = (bf16[192,384]{1,0:T(8,128)(2,1)S(1)}, bf16[192,384]{1,0:T(8,128)(2,1)S(1)}, u32[]{:S(2)}, u32[]{:S(2)}) collective-permute-start(bf16[192,384]{1,0:T(8,128)(2,1)S(1)} %get-tuple-element.86), channel_id=1, source_target_pairs={{0,6},{1,7},{2,4},{3,5},{4,2},{5,3},{6,0},{7,1},{8,14},{9,15},{10,... | collective-permute-start | bytes 442376 | tf_op jit(solution)/shard_map/ppermute | solution.py:529
  132.7 7.4 %collective-permute-start.33 = (bf16[192,384]{1,0:T(8,128)(2,1)S(1)}, bf16[192,384]{1,0:T(8,128)(2,1)S(1)}, u32[]{:S(2)}, u32[]{:S(2)}) collective-permute-start(bf16[192,384]{1,0:T(8,128)(2,1)S(1)} %get-tuple-element.87), channel_id=1, source_target_pairs={{0,4},{1,5},{2,6},{3,7},{4,0},{5,1},{6,2},{7,3},{8,12},{9,13},{10,... | collective-permute-start | bytes 442376 | tf_op jit(solution)/shard_map/ppermute | solution.py:529
  133.5 7.9 %collective-permute-start.21 = (bf16[48,384]{1,0:T(8,128)(2,1)S(1)}, bf16[48,384]{1,0:T(8,128)(2,1)S(1)}, u32[]{:S(2)}, u32[]{:S(2)}) collective-permute-start(bf16[48,384]{1,0:T(8,128)(2,1)S(1)} %get-tuple-element.103), channel_id=1, source_target_pairs={{0,8},{1,9},{2,10},{3,11},{4,12},{5,13},{6,14},{7,15},{8,0},{9,1},... | collective-permute-start | bytes 110600 | tf_op jit(solution)/shard_map/ppermute | solution.py:529
  135.1 8.4 %collective-permute-start.23 = (bf16[48,384]{1,0:T(8,128)(2,1)S(1)}, bf16[48,384]{1,0:T(8,128)(2,1)S(1)}, u32[]{:S(2)}, u32[]{:S(2)}) collective-permute-start(bf16[48,384]{1,0:T(8,128)(2,1)S(1)} %get-tuple-element.104), channel_id=1, source_target_pairs={{0,24},{1,25},{2,26},{3,27},{4,28},{5,29},{6,30},{7,31},{8,16},{9,... | collective-permute-start | bytes 110600 | tf_op jit(solution)/shard_map/ppermute | solution.py:529
  143.8 7.4 %collective-permute-start.26 = (bf16[48,384]{1,0:T(8,128)(2,1)S(1)}, bf16[48,384]{1,0:T(8,128)(2,1)S(1)}, u32[]{:S(2)}, u32[]{:S(2)}) collective-permute-start(bf16[48,384]{1,0:T(8,128)(2,1)S(1)} %get-tuple-element.81), channel_id=1, source_target_pairs={{0,24},{1,25},{2,26},{3,27},{4,28},{5,29},{6,30},{7,31},{8,16},{9,... | collective-permute-start | bytes 110600 | tf_op jit(solution)/shard_map/ppermute | solution.py:529
  145.8 7.9 %collective-permute-start.25 = (bf16[48,384]{1,0:T(8,128)(2,1)S(1)}, bf16[48,384]{1,0:T(8,128)(2,1)S(1)}, u32[]{:S(2)}, u32[]{:S(2)}) collective-permute-start(bf16[48,384]{1,0:T(8,128)(2,1)S(1)} %get-tuple-element.81), channel_id=1, source_target_pairs={{0,16},{1,17},{2,18},{3,19},{4,20},{5,21},{6,22},{7,23},{8,24},{9,... | collective-permute-start | bytes 110600 | tf_op jit(solution)/shard_map/ppermute | solution.py:529
  147.4 7.3 %collective-permute-start.24 = (bf16[48,384]{1,0:T(8,128)(2,1)S(1)}, bf16[48,384]{1,0:T(8,128)(2,1)S(1)}, u32[]{:S(2)}, u32[]{:S(2)}) collective-permute-start(bf16[48,384]{1,0:T(8,128)(2,1)S(1)} %get-tuple-element.81), channel_id=1, source_target_pairs={{0,8},{1,9},{2,10},{3,11},{4,12},{5,13},{6,14},{7,15},{8,0},{9,1},... | collective-permute-start | bytes 110600 | tf_op jit(solution)/shard_map/ppermute | solution.py:529
  148.9 7.2 %collective-permute-start.40 = (bf16[48,384]{1,0:T(8,128)(2,1)S(1)}, bf16[48,384]{1,0:T(8,128)(2,1)S(1)}, u32[]{:S(2)}, u32[]{:S(2)}) collective-permute-start(bf16[48,384]{1,0:T(8,128)(2,1)S(1)} %get-tuple-element.79), channel_id=1, source_target_pairs={{0,24},{1,25},{2,26},{3,27},{4,28},{5,29},{6,30},{7,31},{8,16},{9,... | collective-permute-start | bytes 110600 | tf_op jit(solution)/shard_map/ppermute | solution.py:529
  151.2 7.0 %collective-permute-start.38 = (bf16[48,384]{1,0:T(8,128)(2,1)S(1)}, bf16[48,384]{1,0:T(8,128)(2,1)S(1)}, u32[]{:S(2)}, u32[]{:S(2)}) collective-permute-start(bf16[48,384]{1,0:T(8,128)(2,1)S(1)} %get-tuple-element.79), channel_id=1, source_target_pairs={{0,8},{1,9},{2,10},{3,11},{4,12},{5,13},{6,14},{7,15},{8,0},{9,1},... | collective-permute-start | bytes 110600 | tf_op jit(solution)/shard_map/ppermute | solution.py:529
  153.7 15.9 %collective-permute-start.46 = (bf16[256,384]{1,0:T(8,128)(2,1)S(1)}, bf16[256,384]{1,0:T(8,128)(2,1)S(1)}, u32[]{:S(2)}, u32[]{:S(2)}) collective-permute-start(bf16[256,384]{1,0:T(8,128)(2,1)S(1)} %get-tuple-element.82), channel_id=1, source_target_pairs={{0,2},{1,3},{2,0},{3,1},{4,6},{5,7},{6,4},{7,5},{8,10},{9,11},{10,... | collective-permute-start | bytes 589832 | tf_op jit(solution)/shard_map/ppermute | solution.py:529
  154.7 16.1 %collective-permute-start.48 = (bf16[256,384]{1,0:T(8,128)(2,1)S(1)}, bf16[256,384]{1,0:T(8,128)(2,1)S(1)}, u32[]{:S(2)}, u32[]{:S(2)}) collective-permute-start(bf16[256,384]{1,0:T(8,128)(2,1)S(1)} %get-tuple-element.83), channel_id=1, source_target_pairs={{0,6},{1,7},{2,4},{3,5},{4,2},{5,3},{6,0},{7,1},{8,14},{9,15},{10,... | collective-permute-start | bytes 589832 | tf_op jit(solution)/shard_map/ppermute | solution.py:529
  156.1 14.7 %collective-permute-start.47 = (bf16[256,384]{1,0:T(8,128)(2,1)S(1)}, bf16[256,384]{1,0:T(8,128)(2,1)S(1)}, u32[]{:S(2)}, u32[]{:S(2)}) collective-permute-start(bf16[256,384]{1,0:T(8,128)(2,1)S(1)} %get-tuple-element.84), channel_id=1, source_target_pairs={{0,4},{1,5},{2,6},{3,7},{4,0},{5,1},{6,2},{7,3},{8,12},{9,13},{10,... | collective-permute-start | bytes 589832 | tf_op jit(solution)/shard_map/ppermute | solution.py:529
  157.3 9.7 %collective-permute-start.27 = (bf16[192,384]{1,0:T(8,128)(2,1)S(1)}, bf16[192,384]{1,0:T(8,128)(2,1)S(1)}, u32[]{:S(2)}, u32[]{:S(2)}) collective-permute-start(bf16[192,384]{1,0:T(8,128)(2,1)S(1)} %pad_maximum_fusion.2), channel_id=1, source_target_pairs={{0,2},{1,3},{2,0},{3,1},{4,6},{5,7},{6,4},{7,5},{8,10},{9,11},{10,... | collective-permute-start | bytes 442376 | tf_op jit(solution)/shard_map/ppermute | solution.py:529
  158.3 10.3 %collective-permute-start.41 = (bf16[192,384]{1,0:T(8,128)(2,1)S(1)}, bf16[192,384]{1,0:T(8,128)(2,1)S(1)}, u32[]{:S(2)}, u32[]{:S(2)}) collective-permute-start(bf16[192,384]{1,0:T(8,128)(2,1)S(1)} %pad_maximum_fusion.3), channel_id=1, source_target_pairs={{0,2},{1,3},{2,0},{3,1},{4,6},{5,7},{6,4},{7,5},{8,10},{9,11},{10,... | collective-permute-start | bytes 442376 | tf_op jit(solution)/shard_map/ppermute | solution.py:529
  167.0 36.9 %collective-permute-start.29 = (bf16[192,384]{1,0:T(8,128)(2,1)S(1)}, bf16[192,384]{1,0:T(8,128)(2,1)S(1)}, u32[]{:S(2)}, u32[]{:S(2)}) collective-permute-start(bf16[192,384]{1,0:T(8,128)(2,1)S(1)} %pad_maximum_fusion.2), channel_id=1, source_target_pairs={{0,6},{1,7},{2,4},{3,5},{4,2},{5,3},{6,0},{7,1},{8,14},{9,15},{10,... | collective-permute-start | bytes 442376 | tf_op jit(solution)/shard_map/ppermute | solution.py:529
  168.6 35.2 %collective-permute-start.28 = (bf16[192,384]{1,0:T(8,128)(2,1)S(1)}, bf16[192,384]{1,0:T(8,128)(2,1)S(1)}, u32[]{:S(2)}, u32[]{:S(2)}) collective-permute-start(bf16[192,384]{1,0:T(8,128)(2,1)S(1)} %pad_maximum_fusion.2), channel_id=1, source_target_pairs={{0,4},{1,5},{2,6},{3,7},{4,0},{5,1},{6,2},{7,3},{8,12},{9,13},{10,... | collective-permute-start | bytes 442376 | tf_op jit(solution)/shard_map/ppermute | solution.py:529
  169.5 8.2 %collective-permute-start.42 = (bf16[192,384]{1,0:T(8,128)(2,1)S(1)}, bf16[192,384]{1,0:T(8,128)(2,1)S(1)}, u32[]{:S(2)}, u32[]{:S(2)}) collective-permute-start(bf16[192,384]{1,0:T(8,128)(2,1)S(1)} %pad_maximum_fusion.3), channel_id=1, source_target_pairs={{0,4},{1,5},{2,6},{3,7},{4,0},{5,1},{6,2},{7,3},{8,12},{9,13},{10,... | collective-permute-start | bytes 442376 | tf_op jit(solution)/shard_map/ppermute | solution.py:529
  171.0 7.8 %collective-permute-start.49 = (bf16[64,384]{1,0:T(8,128)(2,1)S(1)}, bf16[64,384]{1,0:T(8,128)(2,1)S(1)}, u32[]{:S(2)}, u32[]{:S(2)}) collective-permute-start(bf16[64,384]{1,0:T(8,128)(2,1)S(1)} %get-tuple-element.91), channel_id=1, source_target_pairs={{0,8},{1,9},{2,10},{3,11},{4,12},{5,13},{6,14},{7,15},{8,0},{9,1},... | collective-permute-start | bytes 147464 | tf_op jit(solution)/shard_map/ppermute | solution.py:529
  171.4 9.1 %collective-permute-start.51 = (bf16[64,384]{1,0:T(8,128)(2,1)S(1)}, bf16[64,384]{1,0:T(8,128)(2,1)S(1)}, u32[]{:S(2)}, u32[]{:S(2)}) collective-permute-start(bf16[64,384]{1,0:T(8,128)(2,1)S(1)} %get-tuple-element.92), channel_id=1, source_target_pairs={{0,24},{1,25},{2,26},{3,27},{4,28},{5,29},{6,30},{7,31},{8,16},{9,... | collective-permute-start | bytes 147464 | tf_op jit(solution)/shard_map/ppermute | solution.py:529
  189.1 35.3 %collective-permute-start.44 = (bf16[768,384]{1,0:T(8,128)(2,1)S(1)}, bf16[768,384]{1,0:T(8,128)(2,1)}, u32[]{:S(2)}, u32[]{:S(2)}) collective-permute-start(bf16[768,384]{1,0:T(8,128)(2,1)S(1)} %constant_dynamic-update-slice_fusion.25.own), channel_id=1, source_target_pairs={{0,1},{1,0},{2,3},{3,2},{4,5},{5,4},{6,7},{7,6},{8,9},{9,8},{10,11... | collective-permute-start | bytes 1769480 | tf_op jit(solution)/shard_map/ppermute | solution.py:529
  190.2 8.4 %collective-permute-start.56 = (bf16[256,384]{1,0:T(8,128)(2,1)S(1)}, bf16[256,384]{1,0:T(8,128)(2,1)S(1)}, u32[]{:S(2)}, u32[]{:S(2)}) collective-permute-start(bf16[256,384]{1,0:T(8,128)(2,1)S(1)} %pad_maximum_fusion.1), channel_id=1, source_target_pairs={{0,4},{1,5},{2,6},{3,7},{4,0},{5,1},{6,2},{7,3},{8,12},{9,13},{10,... | collective-permute-start | bytes 589832 | tf_op jit(solution)/shard_map/ppermute | solution.py:529
  203.7 27.3 %collective-permute-start.58 = (bf16[1024,384]{1,0:T(8,128)(2,1)S(1)}, bf16[1024,384]{1,0:T(8,128)(2,1)S(1)}, u32[]{:S(2)}, u32[]{:S(2)}) collective-permute-start(bf16[1024,384]{1,0:T(8,128)(2,1)S(1)} %constant_dynamic-update-slice_fusion.32.own), channel_id=1, source_target_pairs={{0,1},{1,0},{2,3},{3,2},{4,5},{5,4},{6,7},{7,6},{8,9},{9,8},{10,11... | collective-permute-start | bytes 2359304 | tf_op jit(solution)/shard_map/ppermute | solution.py:529
  203.9 23.4 %collective-permute-start.30 = (bf16[768,384]{1,0:T(8,128)(2,1)S(1)}, bf16[768,384]{1,0:T(8,128)(2,1)S(1)}, u32[]{:S(2)}, u32[]{:S(2)}) collective-permute-start(bf16[768,384]{1,0:T(8,128)(2,1)S(1)} %constant_dynamic-update-slice_fusion.18.own), channel_id=1, source_target_pairs={{0,1},{1,0},{2,3},{3,2},{4,5},{5,4},{6,7},{7,6},{8,9},{9,8},{10,11... | collective-permute-start | bytes 1769480 | tf_op jit(solution)/shard_map/ppermute | solution.py:529
  (45 other events, 473.3 us)

commit v2 on v1

v2 whole, which is shorter than its diff:
```python
import functools
import math

import jax
import jax.numpy as jnp
from jax import lax
from jax.experimental import pallas as pl
from jax.experimental.pallas import tpu as pltpu
from jax.sharding import PartitionSpec as P

D = 384
HEADS = 6
HEAD = 64
FF = 1536
IMG_LEN = 50
PACK = 4
CAPS = 64
TOK_BLOCK = 256
CAP_BLOCK = 16
BLOCKS = 4
PAIR = 128
IMG_BLOCK = 16
IMG_ROWS = IMG_BLOCK * IMG_LEN
EPS = 1e-06

BF = jnp.bfloat16
F32 = jnp.float32
GELU_K = math.sqrt(2.0 / math.pi)
GELU_C = 0.044715


def mm(a, b):
    return lax.dot_general(a, b, (((1,), (0,)), ((), ())), preferred_element_type=F32)


def mm_nt(a, b):
    return lax.dot_general(a, b, (((1,), (1,)), ((), ())), preferred_element_type=F32)


def mm_tn(a, b):
    return lax.dot_general(a, b, (((0,), (0,)), ((), ())), preferred_element_type=F32)


def row_mean(v):
    return jnp.sum(v, -1, keepdims=True) * (1.0 / D)


def normalize(v):
    centre = v - row_mean(v)
    return centre * lax.rsqrt(row_mean(centre * centre) + EPS)


def split3(v):
    high = v.astype(BF)
    rest = v - high.astype(F32)
    mid = rest.astype(BF)
    low = (rest - mid.astype(F32)).astype(BF)
    return high, mid, low


def wide_mm(v, w):
    high, mid, low = split3(v)
    n = v.shape[0]
    out = mm(jnp.concatenate([high, mid, low], 0), w)
    return out[:n] + out[n : 2 * n] + out[2 * n :]


def gelu_parts(z):
    z2 = z * z
    t = jnp.tanh(z * (z2 * (GELU_K * GELU_C) + GELU_K))
    hp = t * 0.5 + 0.5
    u = z * hp
    slope = hp + (u * (1.0 - hp)) * (z2 * (6.0 * GELU_K * GELU_C) + 2.0 * GELU_K)
    return u, slope


def lanes_head(shape):
    return lax.broadcasted_iota(jnp.int32, shape, len(shape) - 1) // HEAD


def image_kernel(x_ref, g1, wqkv, wout, g2, wup, wdown, wproj, emb_ref, kv, x0, att):
    step = pl.program_id(0)
    gain = g1[...].reshape(1, D)
    for c in range(2):
        x = x_ref[IMG_LEN // 2 * c : IMG_LEN // 2 * (c + 1)].astype(F32).reshape(IMG_ROWS // 2, D)
        h = (normalize(x) * gain).astype(BF)
        kv[IMG_ROWS // 2 * c : IMG_ROWS // 2 * (c + 1), :] = mm(h, wqkv[:, D:]).astype(BF)
        if c == 0:
            x0[pl.ds(pl.multiple_of(step * IMG_BLOCK, IMG_BLOCK), IMG_BLOCK), :] = x[:IMG_BLOCK]
            h0 = h[:IMG_BLOCK]
    q = mm(h0, wqkv[:, :D]).astype(BF).astype(F32) * (HEAD**-0.5)
    head = lanes_head((IMG_BLOCK, D))
    queries = HEADS * IMG_BLOCK
    rows = lax.broadcasted_iota(jnp.int32, (queries, IMG_ROWS), 0)
    cols = lax.broadcasted_iota(jnp.int32, (queries, IMG_ROWS), 1)
    own = cols % IMG_BLOCK == rows % IMG_BLOCK
    q6 = jnp.concatenate([jnp.where(head == h, q, 0.0) for h in range(HEADS)], 0)
    s = mm_nt(q6.astype(BF), kv[:, :D])
    s = jnp.where(own, s, -1e30)
    e = jnp.exp(s - jnp.max(s, -1, keepdims=True))
    p = (e * (1.0 / jnp.sum(e, -1, keepdims=True))).astype(BF)
    r = mm(p, kv[:, D:])
    o = jnp.where(head == 0, r[0:IMG_BLOCK], 0.0)
    for h in range(1, HEADS):
        o = jnp.where(head == h, r[IMG_BLOCK * h : IMG_BLOCK * (h + 1)], o)
    att[pl.ds(pl.multiple_of(step * IMG_BLOCK, IMG_BLOCK), IMG_BLOCK), :] = o

    @pl.when(step == pl.num_programs(0) - 1)
    def _():
        x1 = x0[...] + mm(att[...].astype(BF), wout[...])
        h2 = (normalize(x1) * g2[...].reshape(1, D)).astype(BF)
        u, _ = gelu_parts(mm(h2, wup[...]))
        y = x1 + mm(u.astype(BF), wdown[...])
        e = mm(y.astype(BF), wproj[...])
        emb_ref[...] = (e * lax.rsqrt(jnp.sum(e * e, -1, keepdims=True) + EPS)).astype(BF)


def cost(us):
    return pl.CostEstimate(flops=int(us * 1e9), bytes_accessed=int(us * 3e6), transcendentals=0)


def const_spec(shape):
    zeros = (0,) * len(shape)
    return pl.BlockSpec(shape, lambda *_: zeros, pipeline_mode=pl.Buffered(1))


def image_tower(x, g1, wqkv, wout, g2, wup, wdown, wproj):
    count = x.shape[1]
    return pl.pallas_call(
        image_kernel,
        grid=(count // IMG_BLOCK,),
        in_specs=[
            pl.BlockSpec((IMG_LEN, IMG_BLOCK, D), lambda i: (0, i, 0)),
            const_spec((D,)),
            const_spec((D, 3 * D)),
            const_spec((D, D)),
            const_spec((D,)),
            const_spec((D, FF)),
            const_spec((FF, D)),
            const_spec((D, D)),
        ],
        out_specs=pl.BlockSpec((count, D), lambda i: (0, 0)),
        out_shape=jax.ShapeDtypeStruct((count, D), BF),
        scratch_shapes=[
            pltpu.VMEM((IMG_ROWS, 2 * D), BF),
            pltpu.VMEM((count, D), F32),
            pltpu.VMEM((count, D), F32),
        ],
        cost_estimate=cost(12),
        name="image_tower",
    )(x, g1, wqkv, wout, g2, wup, wdown, wproj)


def pair_mask(lab_ref, pair):
    lab = lab_ref[0, :, PAIR * pair : PAIR * pair + PAIR].astype(F32)
    wide = jnp.broadcast_to(lab, (PAIR, PAIR))
    return wide == wide.T


def text_att_kernel(tok_ref, lab_ref, g1, wqkv, o_ref, qkv_ref, p_ref, h1_ref):
    x = tok_ref[...].astype(F32)
    h1 = (normalize(x) * g1[...].reshape(1, D)).astype(BF)
    h1_ref[...] = h1
    qkv = mm(h1, wqkv[...]).astype(BF)
    qkv_ref[...] = qkv
    low = lax.broadcasted_iota(jnp.int32, (PAIR, PAIR), 1) < HEAD
    for pair in range(2):
        rows = slice(PAIR * pair, PAIR * pair + PAIR)
        mask = pair_mask(lab_ref, pair)
        mask = jnp.concatenate([mask, mask], 0)
        for j in range(HEADS // 2):
            cols = slice(PAIR * j, PAIR * j + PAIR)
            q2 = qkv[rows, PAIR * j : PAIR * j + PAIR] * jnp.asarray(HEAD**-0.5, BF)
            k2 = qkv[rows, D + PAIR * j : D + PAIR * j + PAIR]
            v2 = qkv[rows, 2 * D + PAIR * j : 2 * D + PAIR * j + PAIR]
            zero = jnp.zeros_like(q2)
            q22 = jnp.concatenate([jnp.where(low, q2, zero), jnp.where(low, zero, q2)], 0)
            s = jnp.where(mask, mm_nt(q22, k2), -1e30)
            ex = jnp.exp(s - jnp.max(s, -1, keepdims=True))
            p = (ex * (1.0 / jnp.sum(ex, -1, keepdims=True))).astype(BF)
            p_ref[pair, j] = p
            v22 = jnp.concatenate([jnp.where(low, v2, zero), jnp.where(low, zero, v2)], 0)
            o = mm(jnp.concatenate([p[:PAIR], p[PAIR:]], 1), v22)
            o_ref[rows, cols] = o.astype(BF)


def text_mlp_kernel(
    tok_ref, o_ref, lab_ref, wout, g2, wup, wdown, wproj,
    h2_ref, c2_ref, gp_ref, pu_ref, pb_ref, e_ref, emb_ref, cnt_ref, pt, po,
):
    step = pl.program_id(0)
    tok = tok_ref[...]
    o = o_ref[...]
    x1 = tok.astype(F32) + mm(o, wout[...])
    c2 = x1 - row_mean(x1)
    c2_ref[...] = c2
    h2 = (c2 * lax.rsqrt(row_mean(c2 * c2) + EPS) * g2[...].reshape(1, D)).astype(BF)
    h2_ref[...] = h2
    hit = lax.broadcasted_iota(jnp.int32, (CAP_BLOCK, TOK_BLOCK), 0) == lab_ref[0]
    member = jnp.where(hit, 1.0, 0.0)
    caps = pl.ds(pl.multiple_of(step * CAP_BLOCK, CAP_BLOCK), CAP_BLOCK)
    member_b = member.astype(BF)
    pt[caps, :] = mm(member_b, tok)
    po[caps, :] = mm(member_b, o)
    cnt_ref[caps, :] = jnp.broadcast_to(jnp.sum(member, -1, keepdims=True), (CAP_BLOCK, 128))
    for k in range(FF // 512):
        cols = slice(512 * k, 512 * (k + 1))
        u, slope = gelu_parts(mm(h2, wup[:, cols]))
        gp_ref[:, cols] = slope.astype(BF)
        pu_ref[caps, cols] = mm(member_b, u.astype(BF))

    @pl.when(step == pl.num_programs(0) - 1)
    def _():
        total = pt[...] + wide_mm(po[...], wout[...]) + wide_mm(pu_ref[...], wdown[...])
        pooled = (total * (1.0 / cnt_ref[:, 0:1])).astype(BF)
        pb_ref[...] = pooled
        e = mm(pooled, wproj[...])
        e_ref[...] = e
        emb_ref[...] = (e * lax.rsqrt(jnp.sum(e * e, -1, keepdims=True) + EPS)).astype(BF)


def token_rows(width):
    return pl.BlockSpec((TOK_BLOCK, width), lambda i: (i, 0))


def block_of(a, b):
    return pl.BlockSpec((1, a, b), lambda i: (i, 0, 0))


def whole(a, b):
    return pl.BlockSpec((a, b), lambda i: (0, 0))


def text_att(tok, lab, g1, wqkv):
    n = tok.shape[0]
    blocks = n // TOK_BLOCK
    shape = jax.ShapeDtypeStruct
    return pl.pallas_call(
        text_att_kernel,
        grid=(blocks,),
        in_specs=[token_rows(D), block_of(1, TOK_BLOCK), const_spec((D,)), const_spec((D, 3 * D))],
        out_specs=[
            token_rows(D),
            token_rows(3 * D),
            pl.BlockSpec((2, 3, 2 * PAIR, PAIR), lambda i: (i, 0, 0, 0)),
            token_rows(D),
        ],
        out_shape=[
            shape((n, D), BF), shape((n, 3 * D), BF), shape((2 * blocks, 3, 2 * PAIR, PAIR), BF), shape((n, D), BF),
        ],
        cost_estimate=cost(9),
        name="text_att",
    )(tok, lab, g1, wqkv)


def text_mlp(tok, o, lab, wout, g2, wup, wdown, wproj):
    n = tok.shape[0]
    shape = jax.ShapeDtypeStruct
    return pl.pallas_call(
        text_mlp_kernel,
        grid=(n // TOK_BLOCK,),
        in_specs=[
            token_rows(D), token_rows(D), block_of(1, TOK_BLOCK),
            const_spec((D, D)), const_spec((D,)), const_spec((D, FF)), const_spec((FF, D)), const_spec((D, D)),
        ],
        out_specs=[
            token_rows(D), token_rows(D), token_rows(FF),
            whole(CAPS, FF), whole(CAPS, D), whole(CAPS, D), whole(CAPS, D), whole(CAPS, 128),
        ],
        out_shape=[
            shape((n, D), BF), shape((n, D), F32), shape((n, FF), BF),
            shape((CAPS, FF), F32), shape((CAPS, D), BF), shape((CAPS, D), F32),
            shape((CAPS, D), BF), shape((CAPS, 128), F32),
        ],
        scratch_shapes=[pltpu.VMEM((CAPS, D), F32), pltpu.VMEM((CAPS, D), F32)],
        cost_estimate=cost(11),
        name="text_mlp",
    )(tok, o, lab, wout, g2, wup, wdown, wproj)


def reorder(mine, row):
    return jnp.where(mine & 1 == 1, pltpu.roll(row, 64, 1), row)


def cosine_kernel(denom, scale_ref, mine_ref, emb, images, pair, g_ref, sum_ref):
    mine = mine_ref[0]
    scale = jnp.exp(jnp.full((1, 1), scale_ref[0], F32))
    g = mm_nt(emb[...], images[...])
    g_ref[...] = g
    e = jnp.exp(g * scale)
    eg = e * g
    total = jnp.sum(e, -1, keepdims=True)
    hit = lax.broadcasted_iota(jnp.int32, g.shape, 1) == pair[...]
    own = jnp.sum(jnp.where(hit, g, 0.0), -1, keepdims=True)
    loss = jnp.sum(jnp.log(total) - 2.0 * scale * own, 0, keepdims=True)
    temp = jnp.sum(jnp.sum(eg, -1, keepdims=True) / total - 2.0 * own, 0, keepdims=True)
    n = g.shape[1] // 128
    for k, v in enumerate((jnp.sum(e, 0, keepdims=True), jnp.sum(eg, 0, keepdims=True))):
        for r in range(n):
            sum_ref[pl.ds(k * n + ((mine >> 1) ^ r), 1), :] = reorder(mine, v[:, 128 * r : 128 * (r + 1)])
    lane = lax.broadcasted_iota(jnp.int32, (8, 128), 1)
    sum_ref[2 * n :, :] = jnp.where(lane == 0, loss, jnp.where(lane == 1, temp, 0.0))


def rows_kernel(denom, scale_ref, g_ref, images, pair, dt_ref):
    scale = jnp.exp(jnp.full((1, 1), scale_ref[0], F32))
    g = g_ref[...]
    e = jnp.exp(g * scale)
    hit = lax.broadcasted_iota(jnp.int32, g.shape, 1) == pair[...]
    p = e * (1.0 / jnp.sum(e, -1, keepdims=True))
    dl = jnp.where(hit, p - 2.0, p) * (scale * (1.0 / denom))
    dt_ref[...] = mm(dl.astype(BF), images[...])


def halves(place, rows, send_ref, keep_ref, pieces):
    for rel in range(8):
        ref = keep_ref if rel < 4 else send_ref
        at = (rel % 4) * rows
        for v in pieces(place ^ rel):
            ref[at : at + v.shape[0], :] = v.astype(BF)
            at += v.shape[0]


def block(acc, at, rows, col=0):
    return acc[pl.ds(pl.multiple_of(at * rows, 16), rows), D * col : D * (col + 1)]


def head_kernel(
    denom, scale_ref, mine_ref, g_ref, images, sums, dt_row, e_ref, pb, cnt, pu, wproj, wdown,
    sd_ref, kd_ref, sp_ref, kp_ref, du_ref, dy_ref, loss_out, temp_out, down, proj,
):
    mine = mine_ref[0]
    scale = jnp.exp(jnp.full((1, 1), scale_ref[0], F32))
    n = g_ref.shape[1] // 128

    def columns(k):
        return jnp.concatenate([reorder(mine, sums[pl.ds(k * n + ((mine >> 1) ^ r), 1), :]) for r in range(n)], 1)

    temp = jnp.sum(jnp.sum(sums[n : 2 * n, :] / sums[0:n, :], 0, keepdims=True), -1, keepdims=True)
    loss = jnp.sum(jnp.sum(jnp.log(sums[0:n, :]), 0, keepdims=True), -1, keepdims=True)
    loss_out[...] = (sums[2 * n : 2 * n + 1, 0:1] + loss) * (1.0 / denom)
    temp_out[...] = (sums[2 * n : 2 * n + 1, 1:2] + temp) * (scale * (1.0 / denom))
    inverse = 1.0 / columns(0)
    dl = jnp.exp(g_ref[...] * scale) * (inverse * (scale * (1.0 / denom)))
    dt = dt_row[...] + mm(dl.astype(BF), images[...])
    e = e_ref[...]
    r = lax.rsqrt(jnp.sum(e * e, -1, keepdims=True) + EPS)
    de = (dt - e * (r * r * jnp.sum(dt * e, -1, keepdims=True))) * r
    de = de.astype(BF)
    dpooled = mm_nt(de, wproj[...])
    dy = dpooled * (1.0 / cnt[:, 0:1])
    dyb = dy.astype(BF)
    du = mm_nt(dyb, wdown[...])
    for i, piece in enumerate(split3(du)):
        for b in range(BLOCKS):
            du_ref[b, CAP_BLOCK * i : CAP_BLOCK * (i + 1), :] = piece[CAP_BLOCK * b : CAP_BLOCK * (b + 1)]
    for i, piece in enumerate(split3(dy)):
        for b in range(BLOCKS):
            dy_ref[b, CAP_BLOCK * i : CAP_BLOCK * (i + 1), :] = piece[CAP_BLOCK * b : CAP_BLOCK * (b + 1)]
    down[...] = mm_tn(jnp.concatenate(split3(pu[...]), 0), jnp.concatenate([dyb, dyb, dyb], 0))
    proj[...] = mm_tn(pb[...], de)
    halves(mine >> 2, 192, sd_ref, kd_ref, lambda at: [block(down, at, 192)])
    halves(mine >> 2, 48, sp_ref, kp_ref, lambda at: [block(proj, at, 48)])


def mlp_back_kernel(
    mine_ref, lab_ref, h2_ref, gp_ref, c2_ref, du_ref, dy_ref, g2, wup,
    dx_ref, dxb_ref, send_ref, keep_ref, acc,
):
    step = pl.program_id(0)

    @pl.when(step == 0)
    def _():
        acc[...] = jnp.zeros_like(acc)

    hit = lax.broadcasted_iota(jnp.int32, (3 * CAP_BLOCK, TOK_BLOCK), 0) % CAP_BLOCK == lab_ref[0]
    spread = jnp.where(hit, 1.0, 0.0).astype(BF)
    du = mm_tn(spread, du_ref[0])
    dz = (du * gp_ref[...].astype(F32)).astype(BF)
    dy = mm_tn(spread, dy_ref[0])
    dh = mm_nt(dz, wup[...])
    c2 = c2_ref[...]
    r = lax.rsqrt(row_mean(c2 * c2) + EPS)
    unit = c2 * r
    dn = dh * g2[...].reshape(1, D)
    dx = dy + r * (dn - row_mean(dn) - unit * row_mean(dn * unit))
    dx_ref[...] = dx
    dxb_ref[...] = dx.astype(BF)
    h2 = h2_ref[...]
    acc[...] += mm_tn(h2, dz)

    @pl.when(step == pl.num_programs(0) - 1)
    def _():
        halves(mine_ref[0] >> 2, 192, send_ref, keep_ref, lambda at: [block(acc, at, 48, k) for k in range(4)])


def att_core_kernel(qkv_ref, p_ref, dxb_ref, wout, dqkv_ref):
    do = mm_nt(dxb_ref[...], wout[...]).astype(BF)
    low = lax.broadcasted_iota(jnp.int32, (PAIR, PAIR), 1) < HEAD
    zero = jnp.zeros((PAIR, PAIR), BF)
    half = HEAD**-0.5

    def twice(v):
        return jnp.concatenate([jnp.where(low, v, zero), jnp.where(low, zero, v)], 0)

    for pair in range(2):
        rows = slice(PAIR * pair, PAIR * pair + PAIR)
        for j in range(HEADS // 2):
            cols = slice(PAIR * j, PAIR * j + PAIR)
            q2 = qkv_ref[rows, PAIR * j : PAIR * j + PAIR]
            k2 = qkv_ref[rows, D + PAIR * j : D + PAIR * j + PAIR]
            v2 = qkv_ref[rows, 2 * D + PAIR * j : 2 * D + PAIR * j + PAIR]
            do2 = twice(do[rows, cols])
            pb = p_ref[pair, j]
            p = pb.astype(F32)
            dp = mm_nt(do2, v2)
            ds = (p * (dp - jnp.sum(dp * p, -1, keepdims=True))).astype(BF)
            dq = mm(jnp.concatenate([ds[:PAIR], ds[PAIR:]], 1), twice(k2)) * half
            dk = mm_tn(ds, twice(q2)) * half
            dv = mm_tn(pb, do2)
            dqkv_ref[rows, PAIR * j : PAIR * j + PAIR] = dq.astype(BF)
            dqkv_ref[rows, D + PAIR * j : D + PAIR * j + PAIR] = dk.astype(BF)
            dqkv_ref[rows, 2 * D + PAIR * j : 2 * D + PAIR * j + PAIR] = dv.astype(BF)


def att_grads_kernel(mine_ref, h1_ref, dqkv_ref, o_ref, dxb_ref, send_ref, keep_ref, acc, out):
    step = pl.program_id(0)

    @pl.when(step == 0)
    def _():
        acc[...] = jnp.zeros_like(acc)
        out[...] = jnp.zeros_like(out)

    out[...] += mm_tn(o_ref[...], dxb_ref[...])
    acc[...] += mm_tn(h1_ref[...], dqkv_ref[...])

    @pl.when(step == pl.num_programs(0) - 1)
    def _():
        def pieces(at):
            return [block(out, at, 48)] + [block(acc, at, 48, k) for k in range(3)]

        halves(mine_ref[0] >> 2, 192, send_ref, keep_ref, pieces)


def tok_back_kernel(tok_ref, dqkv_ref, dx_ref, g1, wqkv, gtok_ref):
    x = tok_ref[...].astype(F32)
    centre = x - row_mean(x)
    r = lax.rsqrt(row_mean(centre * centre) + EPS)
    unit = centre * r
    dn = mm_nt(dqkv_ref[...], wqkv[...]) * g1[...].reshape(1, D)
    gtok_ref[...] = dx_ref[...] + r * (dn - row_mean(dn) - unit * row_mean(dn * unit))


def gain_of(grad, weight, gain):
    high, mid, _ = split3(grad * weight.astype(F32))
    ones = jnp.ones((8, grad.shape[1]), BF)
    total = mm_nt(ones, high) + mm_nt(ones, mid)
    return total[0:1] / gain.reshape(1, D)


def arrived(mine_ref, own, other, rows):
    for rel in range(8):
        src = own if rel < 4 else other
        yield (mine_ref[0] >> 2) ^ rel, src, (rel % 4) * rows


def spread_mlp_kernel(mine_ref, own, other, wup, g2, down_ref, up_ref, gain_ref):
    for at, src, row in arrived(mine_ref, own, other, 384):
        down_ref[pl.ds(pl.multiple_of(at * 192, 64), 192), :] = src[row : row + 192, :].astype(F32)
        rows = pl.ds(pl.multiple_of(at * 48, 16), 48)
        for k in range(4):
            up_ref[rows, D * k : D * (k + 1)] = src[row + 192 + 48 * k : row + 240 + 48 * k, :].astype(F32)
    gain_ref[...] = gain_of(up_ref[...], wup[...], g2[...])


def spread_att_kernel(mine_ref, own, other, wqkv, g1, out_ref, qkv_ref, proj_ref, gain_ref):
    for at, src, row in arrived(mine_ref, own, other, 240):
        rows = pl.ds(pl.multiple_of(at * 48, 16), 48)
        out_ref[rows, :] = src[row : row + 48, :].astype(F32)
        for k in range(3):
            qkv_ref[rows, D * k : D * (k + 1)] = src[row + 48 + 48 * k : row + 96 + 48 * k, :].astype(F32)
        proj_ref[rows, :] = src[row + 192 : row + 240, :].astype(F32)
    gain_ref[...] = gain_of(qkv_ref[...], wqkv[...], g1[...])


SMEM = pl.BlockSpec(memory_space=pltpu.SMEM)
VMEM = pl.BlockSpec(memory_space=pltpu.VMEM)


def simple(kernel, outs, scratch=(), smem=0, us=3, name=None):
    def call(*args):
        return pl.pallas_call(
            kernel,
            in_specs=[SMEM] * smem + [VMEM] * (len(args) - smem),
            out_specs=[VMEM] * len(outs),
            out_shape=[jax.ShapeDtypeStruct(s, t) for s, t in outs],
            scratch_shapes=list(scratch),
            cost_estimate=cost(us),
            name=name,
        )(*args)

    return call


def mlp_back(mine, lab, h2, gp, c2, du, dy, g2, wup):
    n = h2.shape[0]

    def rows(width):
        return pl.BlockSpec((TOK_BLOCK, width), lambda i: (i, 0))

    def blk(a, b):
        return pl.BlockSpec((1, a, b), lambda i: (i, 0, 0))

    shape = jax.ShapeDtypeStruct
    return pl.pallas_call(
        mlp_back_kernel,
        grid=(n // TOK_BLOCK,),
        in_specs=[
            SMEM, blk(1, TOK_BLOCK), rows(D), rows(FF), rows(D), blk(3 * CAP_BLOCK, FF), blk(3 * CAP_BLOCK, D),
            const_spec((D,)), const_spec((D, FF)),
        ],
        out_specs=[rows(D), rows(D)] + [pl.BlockSpec((768, D), lambda i: (0, 0))] * 2,
        out_shape=[shape((n, D), F32), shape((n, D), BF), shape((768, D), BF), shape((768, D), BF)],
        scratch_shapes=[pltpu.VMEM((D, FF), F32)],
        cost_estimate=cost(9),
        name="mlp_back",
    )(mine, lab, h2, gp, c2, du, dy, g2, wup)


def att_core(qkv, p, dxb, wout):
    n = dxb.shape[0]
    return pl.pallas_call(
        att_core_kernel,
        grid=(n // TOK_BLOCK,),
        in_specs=[
            token_rows(3 * D),
            pl.BlockSpec((2, 3, 2 * PAIR, PAIR), lambda i: (i, 0, 0, 0)),
            token_rows(D),
            const_spec((D, D)),
        ],
        out_specs=token_rows(3 * D),
        out_shape=jax.ShapeDtypeStruct((n, 3 * D), BF),
        cost_estimate=cost(10),
        name="att_core",
    )(qkv, p, dxb, wout)


def att_grads(mine, h1, dqkv, o, dxb):
    n = h1.shape[0]
    return pl.pallas_call(
        att_grads_kernel,
        grid=(n // TOK_BLOCK,),
        in_specs=[SMEM, token_rows(D), token_rows(3 * D), token_rows(D), token_rows(D)],
        out_specs=[whole(768, D)] * 2,
        out_shape=[jax.ShapeDtypeStruct((768, D), BF)] * 2,
        scratch_shapes=[pltpu.VMEM((D, 3 * D), F32), pltpu.VMEM((D, D), F32)],
        cost_estimate=cost(4),
        name="att_grads",
    )(mine, h1, dqkv, o, dxb)


def tok_back(tok, dqkv, dx, g1, wqkv):
    n = tok.shape[0]
    return pl.pallas_call(
        tok_back_kernel,
        grid=(n // TOK_BLOCK,),
        in_specs=[token_rows(D), token_rows(3 * D), token_rows(D), const_spec((D,)), const_spec((D, 3 * D))],
        out_specs=token_rows(D),
        out_shape=jax.ShapeDtypeStruct((n, D), F32),
        cost_estimate=cost(4),
        name="tok_back",
    )(tok, dqkv, dx, g1, wqkv)


AXES = ("dp", "replica")


def swap(v, mask):
    return lax.ppermute(v, AXES, [(i, i ^ mask) for i in range(32)])


def plane(parts):
    return [swap(parts[m], 2 * m) for m in (1, 2, 3)]


def column(parts):
    return [swap(parts[m], 8 * m) for m in (1, 2, 3)]


def added(own, got):
    total = own.astype(F32)
    for v in got:
        total = total + v.astype(F32)
    return total.astype(BF)


def joined(own, got):
    return jnp.concatenate([own] + got, 0)


def shards(
    devices, tuned,
    text_tokens, segment_ids, pair_index, image_tokens,
    img_ln1, img_qkv, img_out, img_ln2, img_up, img_down, img_proj,
    txt_ln1, txt_qkv, txt_out, txt_ln2, txt_up, txt_down, txt_proj, log_scale,
):
    total = CAPS * devices
    denom = 2.0 * total
    row_of = jnp.arange(segment_ids.shape[0], dtype=jnp.int32) % (TOK_BLOCK // segment_ids.shape[1])
    lab = (segment_ids + PACK * row_of[:, None]).reshape(BLOCKS, 1, TOK_BLOCK)
    pair = pair_index
    if tuned:
        index = lax.axis_index(AXES)
        mine = ((index & 1) * 16 + ((index >> 1) & 3) * 4 + (index >> 3)).astype(jnp.int32).reshape(1)
        owner, row = pair // CAPS, pair % CAPS
        pair = (((owner & 1) * 16 + ((owner >> 1) & 3) * 4 + (owner >> 3)) ^ mine) * CAPS + row
    else:
        mine = jnp.zeros((1,), jnp.int32)
    pair = pair.reshape(CAPS, 1)
    lab, pair = lax.optimization_barrier((lab, pair))
    emb = image_tower(
        jnp.transpose(image_tokens, (1, 0, 2)), img_ln1, img_qkv, img_out, img_ln2, img_up, img_down, img_proj
    )
    if tuned:
        near = joined(emb, column([emb] * 4))
        o, qkv, p, h1 = text_att(text_tokens, lab, txt_ln1, txt_qkv)
        o, near = lax.optimization_barrier((o, near))
        got = plane([near] * 4)
    else:
        o, qkv, p, h1 = text_att(text_tokens, lab, txt_ln1, txt_qkv)
    h2, c2, gp, pu, pb, e, temb, cnt = text_mlp(text_tokens, o, lab, txt_out, txt_ln2, txt_up, txt_down, txt_proj)
    if tuned:
        near, got, temb = lax.optimization_barrier((near, got, temb))
        near = joined(near, got)
        images = joined(near, [swap(near, 1)])
    else:
        images = lax.all_gather(emb, AXES, axis=0, tiled=True)
    lines = total // 128
    g, sums = simple(
        functools.partial(cosine_kernel, denom),
        [((CAPS, total), F32), ((2 * lines + 8, 128), F32)],
        smem=2,
        us=3,
        name="cosine",
    )(log_scale, mine, temb, images, pair)
    (dt_row,) = simple(functools.partial(rows_kernel, denom), [((CAPS, D), F32)], smem=1, us=2, name="rows")(
        log_scale, g, images, pair
    )
    if tuned:
        for mask in (1, 2, 4, 8, 16):
            sums = sums + swap(sums, mask)
    else:
        sums = lax.psum(sums, AXES)
    send_d, keep_d, send_p, keep_p, du, dy, loss, temp = simple(
        functools.partial(head_kernel, denom),
        [
            ((768, D), BF), ((768, D), BF), ((192, D), BF), ((192, D), BF),
            ((BLOCKS, 48, FF), BF), ((BLOCKS, 48, D), BF), ((1, 1), F32), ((1, 1), F32),
        ],
        [pltpu.VMEM((FF, D), F32), pltpu.VMEM((D, D), F32)],
        smem=2,
        us=5,
        name="head_back",
    )(log_scale, mine, g, images, sums, dt_row, e, pb, cnt, pu, txt_proj, txt_down)
    dx, dxb, send_u, keep_u = mlp_back(mine, lab, h2, gp, c2, du, dy, txt_ln2, txt_up)

    def mlp_parts(d, u):
        return jnp.concatenate([d.reshape(4, 192, D), u.reshape(4, 192, D)], 1)

    def att_parts(a, p):
        return jnp.concatenate([a.reshape(4, 192, D), p.reshape(4, 48, D)], 1)

    def spread_mlp(own, other):
        outs = [((FF, D), F32), ((D, FF), F32), ((1, D), F32)]
        return simple(spread_mlp_kernel, outs, smem=1, us=4, name="spread_mlp")(mine, own, other, txt_up, txt_ln2)

    def spread_att(own, other):
        outs = [((D, D), F32), ((D, 3 * D), F32), ((D, D), F32), ((1, D), F32)]
        return simple(spread_att_kernel, outs, smem=1, us=4, name="spread_att")(mine, own, other, txt_qkv, txt_ln1)

    if not tuned:
        dqkv = att_core(qkv, p, dxb, txt_out)
        send_a, keep_a = att_grads(mine, h1, dqkv, o, dxb)
        grad_tokens = tok_back(text_tokens, dqkv, dx, txt_ln1, txt_qkv)
        sums = [keep_d, send_d, keep_u, send_u, keep_a, send_a, keep_p, send_p]
        d, d2, u, u2, a, a2, p, p2 = [v.astype(BF) for v in lax.psum([v.astype(F32) for v in sums], AXES)]
        grad_down, grad_up, gain2 = spread_mlp(mlp_parts(d, u).reshape(1536, D), mlp_parts(d2, u2).reshape(1536, D))
        grad_out, grad_qkv, grad_proj, gain1 = spread_att(
            att_parts(a, p).reshape(960, D), att_parts(a2, p2).reshape(960, D)
        )
    else:
        d = added(keep_d, [swap(send_d, 1)])
        pr = added(keep_p, [swap(send_p, 1)])
        m = mlp_parts(d, added(keep_u, [swap(send_u, 1)]))
        dxb, m = lax.optimization_barrier((dxb, m))
        got = plane(m)
        dqkv = att_core(qkv, p, dxb, txt_out)
        got, dqkv = lax.optimization_barrier((got, dqkv))
        m = added(m[0], got)
        m, dqkv = lax.optimization_barrier((m, dqkv))
        other = swap(m, 16)
        send_a, keep_a = att_grads(mine, h1, dqkv, o, dxb)
        other, send_a, keep_a = lax.optimization_barrier((other, send_a, keep_a))
        a = att_parts(added(keep_a, [swap(send_a, 1)]), pr)
        a, dqkv = lax.optimization_barrier((a, dqkv))
        grad_tokens = tok_back(text_tokens, dqkv, dx, txt_ln1, txt_qkv)
        m = added(m, [other])
        m = added(m, [swap(m, 8)])
        a = added(a[0], plane(a))
        a = added(a, [swap(a, 16)])
        m = joined(m, plane([m] * 4))
        a = added(a, [swap(a, 8)])
        grad_down, grad_up, gain2 = spread_mlp(m, swap(m, 1))
        got = plane([a] * 4)
        got, grad_up = lax.optimization_barrier((got, grad_up))
        a = joined(a, got)
        grad_out, grad_qkv, grad_proj, gain1 = spread_att(a, swap(a, 1))
    return (
        loss.reshape(1), grad_tokens, gain1.reshape(D), grad_qkv, grad_out, gain2.reshape(D),
        grad_up, grad_down, grad_proj, temp.reshape(1),
    )


def solution(mesh):
    both = ("dp", "replica")
    devices = mesh.shape["dp"] * mesh.shape["replica"]
    tuned = (mesh.shape["dp"], mesh.shape["replica"]) == (8, 4)
    rows = P(both, None)
    return jax.shard_map(
        functools.partial(shards, devices, tuned),
        mesh=mesh,
        in_specs=(rows, rows, P(both), P(both, None, None)) + (P(),) * 15,
        out_specs=(P(), rows) + (P(),) * 8,
        check_vma=False,
    )
```

time: 236 us -> 190 us (0.81)
  starting transfers between devices: 71.1 us -> 35.5 us
  local copies, waits for them, and re-layouts: 16.7 us -> 4.9 us
  Pallas kernels: 75.6 us -> 81.7 us
  waiting for transfers between devices: 65.2 us -> 61.4 us
    ppermute x59 -> x34, starting transfers between devices: 71.1 us -> 35.5 us  [swap(): return lax.ppermute(v, AXES, [(i, i ^ mask) for i in range(32)])]
    pallas_call x2 -> x5, Pallas kernels: 33 us -> 42.7 us  [the longest x1 12.1 us: text_mlp(): pl.pallas_call(text_mlp_kernel, grid=(n // TOK_BLOCK,), in_specs=[token_r...]
    unnamed x60 -> x32, local copies, waits for them, and re-layouts: 8.89 us -> 3.2 us
    reshape x11 -> x0, local copies, waits for them, and re-layouts: 4.82 us -> none  [the longest x1 1.25 us: shards(): img_ln1.reshape(1, D)]
    ppermute x59 -> x34, waiting for transfers between devices: 65.2 us -> 61.4 us  [swap(): return lax.ppermute(v, AXES, [(i, i ^ mask) for i in range(32)])]
    pallas_call x6 -> x5, Pallas kernels: 20.1 us -> 18.5 us  [call(): pl.pallas_call(kernel, in_specs=[SMEM] * smem + [VMEM] * (len(args) - sme...]
  transfers between devices with their start and end apart: 59 -> 34, of which waited for: 25 -> 16; matrix products, arithmetic and copies ran while one was open for 3% -> 2% of each run, Pallas kernels for 11% -> 31%
where the time goes in v2:
time: 190 us
  Pallas kernels  81.7 us (43%)
  waiting for transfers between devices  61.4 us (32%)
  starting transfers between devices  35.5 us (19%)
  local copies, waits for them, and re-layouts  4.9 us (3%)
  other arithmetic  4.75 us (2%)
    ppermute x34, waiting for transfers between devices, swap(): return lax.ppermute(v, AXES, [(i, i ^ mask) for i in range(32)])  61.4 us
    ppermute x34, starting transfers between devices, swap(): return lax.ppermute(v, AXES, [(i, i ^ mask) for i in range(32)])  35.5 us
    pallas_call x5, Pallas kernels, call(): pl.pallas_call(kernel, in_specs=[SMEM] * smem + [VMEM] * (len(args) - sme...  18.5 us
    pallas_call x1, Pallas kernels, text_mlp(): pl.pallas_call(text_mlp_kernel, grid=(n // TOK_BLOCK,), in_specs=[token_r...  12.1 us
    pallas_call x1, Pallas kernels, image_tower(): pl.pallas_call(image_kernel, grid=(count // IMG_BLOCK,), in_specs=[pl.Blo...  11.4 us
    pallas_call x1, Pallas kernels, att_core(): pl.pallas_call(att_core_kernel, grid=(n // TOK_BLOCK,), in_specs=[token_r...  11.3 us
    pallas_call x1, Pallas kernels, mlp_back(): pl.pallas_call(mlp_back_kernel, grid=(n // TOK_BLOCK,), in_specs=[SMEM, b...  9.04 us
    pallas_call x1, Pallas kernels, text_att(): pl.pallas_call(text_att_kernel, grid=(blocks,), in_specs=[token_rows(D),...  7.59 us
  transfers between devices with their start and end apart: 34, of which 16 were waited for; matrix products, arithmetic and copies ran while one was open for 2% of the time, Pallas kernels for 31%

profile of v2, /device:TPU:0, one launch (start us, length us, event | category | flops | bytes accessed | tf_op | source)
XLA Modules:
  0.0 189.9 jit_solution(1313093973517699015)
XLA Ops:
  0.7 11.4 %image_tower.1 = bf16[64,384]{1,0:T(8,128)(2,1)} custom-call(bf16[50,64,384]{2,1,0:T(8,128)(2,1)} %bitcast.32, f32[384]{0:T(512)} %g1.5, bf16[384,1152]{1,0:T(8,128)(2,1)} %wqkv.5, bf16[384,384]{1,0:T(8,128)(2,1)} %wout.3, f32[384]{0:T(512)} %g2.4, bf16[384,1536]{1,0:T(8,128)(2,1)} %wup.4, bf16[1536,384]{1,0:T(8,128)(2,1)} %wdown.3, bf16[384,384]{1,0:T(8,128)(2,1)} %wproj.3), custom_call_target="tpu_custom_call" | custom-call | flops 12000000000 | bytes 36000000 | tf_op jit(solution)/shard_map/image_tower/pallas_call | solution.py:129
  12.1 3.0 %collective-permute-start = (bf16[64,384]{1,0:T(8,128)(2,1)}, bf16[64,384]{1,0:T(8,128)(2,1)S(1)}, u32[]{:S(2)}, u32[]{:S(2)}) collective-permute-start(bf16[64,384]{1,0:T(8,128)(2,1)} %image_tower.1), channel_id=1, source_target_pairs={{0,8},{1,9},{2,10},{3,11},{4,12},{5,13},{6,14},{7,15},{8,0},{9,1},... | collective-permute-start | bytes 147464 | tf_op jit(solution)/shard_map/ppermute | solution.py:579
  15.1 2.6 %collective-permute-start.1 = (bf16[64,384]{1,0:T(8,128)(2,1)}, bf16[64,384]{1,0:T(8,128)(2,1)S(1)}, u32[]{:S(2)}, u32[]{:S(2)}) collective-permute-start(bf16[64,384]{1,0:T(8,128)(2,1)} %image_tower.1), channel_id=1, source_target_pairs={{0,16},{1,17},{2,18},{3,19},{4,20},{5,21},{6,22},{7,23},{8,24},{9,... | collective-permute-start | bytes 147464 | tf_op jit(solution)/shard_map/ppermute | solution.py:579
  18.5 7.6 %text_att.1 = (bf16[1024,384]{1,0:T(8,128)(2,1)}, bf16[1024,1152]{1,0:T(8,128)(2,1)}, bf16[8,3,256,128]{3,2,1,0:T(8,128)(2,1)}, bf16[1024,384]{1,0:T(8,128)(2,1)}) custom-call(bf16[1024,384]{1,0:T(8,128)(2,1)} %tok_ref.5, s32[4,1,256]{2,1,0:T(1,128)} %reshape.70.lab_ref, f32[384]{0:T(512)} %g1.7, bf16[384,1152]{1,0:T(8,128)(2,1)} %wqkv.7), custom_call_target="tpu_custom_call" | custom-call | flops 8999999488 | bytes 27000000 | tf_op jit(solution)/shard_map/text_att/pallas_call | solution.py:238
  26.2 1.8 collective-permute-start.3
  29.7 12.1 %text_mlp.1 = (bf16[1024,384]{1,0:T(8,128)(2,1)}, f32[1024,384]{1,0:T(8,128)}, bf16[1024,1536]{1,0:T(8,128)(2,1)}, f32[64,1536]{1,0:T(8,128)}, bf16[64,384]{1,0:...) custom-call(bf16[1024,384]{1,0:T(8,128)(2,1)} %tok_ref.5, ...), custom_call_target="tpu_custom_call" | custom-call | flops 11000000512 | bytes 33000000 | tf_op jit(solution)/shard_map/text_mlp/pallas_call | solution.py:259
  45.7 2.8 %cosine.1 = (f32[64,2048]{1,0:T(8,128)}, f32[40,128]{1,0:T(8,128)}) custom-call(f32[1]{0:T(128)S(6)} %copy.35.scale_ref, s32[1]{0:T(128)} %bitcast.mine_ref, bf16[64,384]{1,0:T(8,128)(2,1)} %get-tuple-element.76.emb, bf16[2048,384]{1,0:T(8,128)(2,1)} %copy-done.7, s32[64,1]{1,0:T(8,128)} %copy.29.pair), custom_call_target="tpu_custom_call" | custom-call | flops 3000000000 | bytes 9000000 | tf_op jit(solution)/shard_map/cosine/pallas_call | solution.py:492
  50.6 1.7 collective-permute-start.8
  52.3 2.1 %collective-permute-done.8 = f32[40,128]{1,0:T(8,128)S(1)} collective-permute-done((f32[40,128]{1,0:T(8,128)S(1)}, f32[40,128]{1,0:T(8,128)S(1)}, u32[]{:S(2)}, u32[]{:S(2)}) %collective-permute-start.8) | collective-permute-done | bytes 20512 | tf_op jit(solution)/shard_map/ppermute | solution.py:579
  54.4 1.7 collective-permute-start.9
  56.1 2.1 %collective-permute-done.9 = f32[40,128]{1,0:T(8,128)S(1)} collective-permute-done((f32[40,128]{1,0:T(8,128)S(1)}, f32[40,128]{1,0:T(8,128)S(1)}, u32[]{:S(2)}, u32[]{:S(2)}) %collective-permute-start.9) | collective-permute-done | bytes 20512 | tf_op jit(solution)/shard_map/ppermute | solution.py:579
  59.1 2.9 %collective-permute-done.10 = f32[40,128]{1,0:T(8,128)S(1)} collective-permute-done((f32[40,128]{1,0:T(8,128)S(1)}, f32[40,128]{1,0:T(8,128)S(1)}, u32[]{:S(2)}, u32[]{:S(2)}) %collective-permute-start.10) | collective-permute-done | bytes 20512 | tf_op jit(solution)/shard_map/ppermute | solution.py:579
  62.0 2.4 %collective-permute-start.11 = (f32[40,128]{1,0:T(8,128)S(1)}, f32[40,128]{1,0:T(8,128)S(1)}, u32[]{:S(2)}, u32[]{:S(2)}) collective-permute-start(f32[40,128]{1,0:T(8,128)S(1)} %add.113), channel_id=1, source_target_pairs={{0,16},{1,17},{2,18},{3,19},{4,20},{5,21},{6,22},{7,23},{8,24},{9,... | collective-permute-start | bytes 61448 | tf_op jit(solution)/shard_map/ppermute | solution.py:579
  64.4 2.7 %rows.1.dt_row = f32[64,384]{1,0:T(8,128)} custom-call(f32[1]{0:T(128)S(6)} %copy.35.scale_ref, f32[64,2048]{1,0:T(8,128)} %get-tuple-element.82.g_ref, bf16[2048,384]{1,0:T(8,128)(2,1)} %copy-done.7, s32[64,1]{1,0:T(8,128)} %copy.29.pair), custom_call_target="tpu_custom_call" | custom-call | flops 2000000000 | bytes 6000000 | tf_op jit(solution)/shard_map/rows/pallas_call | solution.py:492
  67.6 5.2 %head_back.1 = (bf16[768,384]{1,0:T(8,128)(2,1)}, bf16[768,384]{1,0:T(8,128)(2,1)}, bf16[192,384]{1,0:T(8,128)(2,1)}, bf16[192,384]{1,0:T(8,128)(2,1)}, bf16[4,4...) custom-call(f32[1]{0:T(128)S(6)} %copy.35.scale_ref, s32[1]{0:T(128)} %bitcast.mine_ref, ...), custom_call_target="tpu_custom_call" | custom-call | flops 5000000000 | bytes 15000000 | tf_op jit(solution)/shard_map/head_back/pallas_call | solution.py:492
  73.0 9.0 %mlp_back.1 = (f32[1024,384]{1,0:T(8,128)}, bf16[1024,384]{1,0:T(8,128)(2,1)}, bf16[768,384]{1,0:T(8,128)(2,1)}, bf16[768,384]{1,0:T(8,128)(2,1)}) custom-call(s32[1]{0:T(128)} %bitcast.mine_ref, s32[4,1,256]{2,1,0:T(1,128)} %reshape.70.lab_ref, bf16[1024,384]{1,0:T(8,128)(2,1)} %get-tuple-element.89.h2_ref, bf16[1024,1536]{1,0:T(8,128)(2,1)} %get-tuple-element.90.gp_ref, ...), custom_call_target="tpu_custom_call" | custom-call | flops 8999999488 | bytes 27000000 | tf_op jit(solution)/shard_map/mlp_back/pallas_call | solution.py:515
  88.4 11.3 %att_core.1.dqkv_ref = bf16[1024,1152]{1,0:T(8,128)(2,1)} custom-call(bf16[1024,1152]{1,0:T(8,128)(2,1)} %get-tuple-element.100.qkv_ref, bf16[8,3,256,128]{3,2,1,0:T(8,128)(2,1)} %get-tuple-element.101.p_ref, bf16[1024,384]{1,0:T(8,128)(2,1)} %get-tuple-element.102.dxb_ref, bf16[384,384]{1,0:T(8,128)(2,1)} %wout.5), custom_call_target="tpu_custom_call" | custom-call | flops 10000000000 | bytes 30000000 | tf_op jit(solution)/shard_map/att_core/pallas_call | solution.py:532
  99.7 2.0 %collective-permute-done.15 = bf16[384,384]{1,0:T(8,128)(2,1)S(1)} collective-permute-done((bf16[384,384]{1,0:T(8,128)(2,1)S(1)}, bf16[384,384]{1,0:T(8,128)(2,1)S(1)}, u32[]{:S(2)}, u32[]{:S(2)}) %collective-permute-start.15) | collective-permute-done | bytes 294944 | tf_op jit(solution)/shard_map/ppermute | solution.py:579
  101.8 2.1 %collective-permute-start.17 = (bf16[384,384]{1,0:T(8,128)(2,1)S(1)}, bf16[384,384]{1,0:T(8,128)(2,1)S(1)}, u32[]{:S(2)}, u32[]{:S(2)}) collective-permute-start(bf16[384,384]{1,0:T(8,128)(2,1)S(1)} %fusion.2), channel_id=1, source_target_pairs={{0,16},{1,17},{2,18},{3,19},{4,20},{5,21},{6,22},{7,23},{8,24},{9,... | collective-permute-start | bytes 884744 | tf_op jit(solution)/shard_map/ppermute | solution.py:579
  103.9 5.6 %att_grads.1 = (bf16[768,384]{1,0:T(8,128)(2,1)}, bf16[768,384]{1,0:T(8,128)(2,1)}) custom-call(s32[1]{0:T(128)} %bitcast.mine_ref, bf16[1024,384]{1,0:T(8,128)(2,1)} %get-tuple-element.108.h1_ref, bf16[1024,1152]{1,0:T(8,128)(2,1)} %att_core.1.dqkv_ref, bf16[1024,384]{1,0:T(8,128)(2,1)} %get-tuple-element.74.o_ref, bf16[1024,384]{1,0:T(8,128)(2,1)} %get-tuple-element.102.dxb_ref), custom_call_target="tpu_custom_call" | custom-call | flops 4000000000 | bytes 12000000 | tf_op jit(solution)/shard_map/att_grads/pallas_call | solution.py:550
  109.6 7.8 %collective-permute-done.17 = bf16[384,384]{1,0:T(8,128)(2,1)S(1)} collective-permute-done((bf16[384,384]{1,0:T(8,128)(2,1)S(1)}, bf16[384,384]{1,0:T(8,128)(2,1)S(1)}, u32[]{:S(2)}, u32[]{:S(2)}) %collective-permute-start.17) | collective-permute-done | bytes 294944 | tf_op jit(solution)/shard_map/ppermute | solution.py:579
  117.6 9.3 %collective-permute-done.28 = bf16[384,384]{1,0:T(8,128)(2,1)S(1)} collective-permute-done((bf16[384,384]{1,0:T(8,128)(2,1)S(1)}, bf16[384,384]{1,0:T(8,128)(2,1)S(1)}, u32[]{:S(2)}, u32[]{:S(2)}) %collective-permute-start.28) | collective-permute-done | bytes 294944 | tf_op jit(solution)/shard_map/ppermute | solution.py:579
  132.9 4.0 %collective-permute-done.29 = bf16[384,384]{1,0:T(8,128)(2,1)S(1)} collective-permute-done((bf16[384,384]{1,0:T(8,128)(2,1)S(1)}, bf16[384,384]{1,0:T(8,128)(2,1)S(1)}, u32[]{:S(2)}, u32[]{:S(2)}) %collective-permute-start.29) | collective-permute-done | bytes 294944 | tf_op jit(solution)/shard_map/ppermute | solution.py:579
  138.3 6.3 %collective-permute-done.30 = bf16[384,384]{1,0:T(8,128)(2,1)S(1)} collective-permute-done((bf16[384,384]{1,0:T(8,128)(2,1)S(1)}, bf16[384,384]{1,0:T(8,128)(2,1)S(1)}, u32[]{:S(2)}, u32[]{:S(2)}) %collective-permute-start.30) | collective-permute-done | bytes 294944 | tf_op jit(solution)/shard_map/ppermute | solution.py:579
  144.9 2.4 %collective-permute-done.20 = bf16[240,384]{1,0:T(8,128)(2,1)S(1)} collective-permute-done((bf16[240,384]{1,0:T(8,128)(2,1)S(1)}, bf16[240,384]{1,0:T(8,128)(2,1)S(1)}, u32[]{:S(2)}, u32[]{:S(2)}) %collective-permute-start.20) | collective-permute-done | bytes 184352 | tf_op jit(solution)/shard_map/ppermute | solution.py:579
  147.2 3.7 %collective-permute-done.21 = bf16[240,384]{1,0:T(8,128)(2,1)S(1)} collective-permute-done((bf16[240,384]{1,0:T(8,128)(2,1)S(1)}, bf16[240,384]{1,0:T(8,128)(2,1)S(1)}, u32[]{:S(2)}, u32[]{:S(2)}) %collective-permute-start.21) | collective-permute-done | bytes 184352 | tf_op jit(solution)/shard_map/ppermute | solution.py:579
  151.1 2.1 %collective-permute-start.23 = (bf16[240,384]{1,0:T(8,128)(2,1)S(1)}, bf16[240,384]{1,0:T(8,128)(2,1)S(1)}, u32[]{:S(2)}, u32[]{:S(2)}) collective-permute-start(bf16[240,384]{1,0:T(8,128)(2,1)S(1)} %fusion.5), channel_id=1, source_target_pairs={{0,16},{1,17},{2,18},{3,19},{4,20},{5,21},{6,22},{7,23},{8,24},{9,... | collective-permute-start | bytes 552968 | tf_op jit(solution)/shard_map/ppermute | solution.py:579
  153.1 8.0 %collective-permute-done.23 = bf16[240,384]{1,0:T(8,128)(2,1)S(1)} collective-permute-done((bf16[240,384]{1,0:T(8,128)(2,1)S(1)}, bf16[240,384]{1,0:T(8,128)(2,1)S(1)}, u32[]{:S(2)}, u32[]{:S(2)}) %collective-permute-start.23) | collective-permute-done | bytes 184352 | tf_op jit(solution)/shard_map/ppermute | solution.py:579
  161.3 6.2 %collective-permute-done.24 = bf16[240,384]{1,0:T(8,128)(2,1)S(1)} collective-permute-done((bf16[240,384]{1,0:T(8,128)(2,1)S(1)}, bf16[240,384]{1,0:T(8,128)(2,1)S(1)}, u32[]{:S(2)}, u32[]{:S(2)}) %collective-permute-start.24) | collective-permute-done | bytes 184352 | tf_op jit(solution)/shard_map/ppermute | solution.py:579
  172.2 4.3 %spread_mlp.1 = (f32[1536,384]{1,0:T(8,128)}, f32[384,1536]{1,0:T(8,128)}, f32[1,384]{1,0:T(1,128)}) custom-call(s32[1]{0:T(128)} %bitcast.mine_ref, bf16[1536,384]{1,0:T(8,128)(2,1)} %copy-done, bf16[1536,384]{1,0:T(8,128)(2,1)} %copy-done.10, bf16[384,1536]{1,0:T(8,128)(2,1)} %wup.7, f32[384]{0:T(512)} %g2.7), custom_call_target="tpu_custom_call" | custom-call | flops 4000000000 | bytes 12000000 | tf_op jit(solution)/shard_map/spread_mlp/pallas_call | solution.py:492
  177.7 6.0 %tok_back.1 = f32[1024,384]{1,0:T(8,128)} custom-call(bf16[1024,384]{1,0:T(8,128)(2,1)} %tok_ref.5, bf16[1024,1152]{1,0:T(8,128)(2,1)} %att_core.1.dqkv_ref, f32[1024,384]{1,0:T(8,128)} %get-tuple-element.117.dx_ref, f32[384]{0:T(512)} %g1.7, bf16[384,1152]{1,0:T(8,128)(2,1)} %wqkv.7), custom_call_target="tpu_custom_call" | custom-call | flops 4000000000 | bytes 12000000 | tf_op jit(solution)/shard_map/tok_back/pallas_call | solution.py:564
  185.2 3.4 %spread_att.1 = (f32[384,384]{1,0:T(8,128)}, f32[384,1152]{1,0:T(8,128)}, f32[384,384]{1,0:T(8,128)}, f32[1,384]{1,0:T(1,128)}) custom-call(s32[1]{0:T(128)} %bitcast.mine_ref, bf16[960,384]{1,0:T(8,128)(2,1)} %copy-done.1, bf16[960,384]{1,0:T(8,128)(2,1)} %copy-done.11, bf16[384,1152]{1,0:T(8,128)(2,1)} %wqkv.7, f32[384]{0:T(512)} %g1.7), custom_call_target="tpu_custom_call" | custom-call | flops 4000000000 | bytes 12000000 | tf_op jit(solution)/shard_map/spread_att/pallas_call | solution.py:492
  (111 shorter events, 32.5 us)
Async XLA Ops:
  12.1 14.0 %collective-permute-start = (bf16[64,384]{1,0:T(8,128)(2,1)}, bf16[64,384]{1,0:T(8,128)(2,1)S(1)}, u32[]{:S(2)}, u32[]{:S(2)}) collective-permute-start(bf16[64,384]{1,0:T(8,128)(2,1)} %image_tower.1), channel_id=1, source_target_pairs={{0,8},{1,9},{2,10},{3,11},{4,12},{5,13},{6,14},{7,15},{8,0},{9,1},... | collective-permute-start | bytes 147464 | tf_op jit(solution)/shard_map/ppermute | solution.py:579
  15.1 11.0 %collective-permute-start.1 = (bf16[64,384]{1,0:T(8,128)(2,1)}, bf16[64,384]{1,0:T(8,128)(2,1)S(1)}, u32[]{:S(2)}, u32[]{:S(2)}) collective-permute-start(bf16[64,384]{1,0:T(8,128)(2,1)} %image_tower.1), channel_id=1, source_target_pairs={{0,16},{1,17},{2,18},{3,19},{4,20},{5,21},{6,22},{7,23},{8,24},{9,... | collective-permute-start | bytes 147464 | tf_op jit(solution)/shard_map/ppermute | solution.py:579
  17.7 8.4 %collective-permute-start.2 = (bf16[64,384]{1,0:T(8,128)(2,1)}, bf16[64,384]{1,0:T(8,128)(2,1)S(1)}, u32[]{:S(2)}, u32[]{:S(2)}) collective-permute-start(bf16[64,384]{1,0:T(8,128)(2,1)} %image_tower.1), channel_id=1, source_target_pairs={{0,24},{1,25},{2,26},{3,27},{4,28},{5,29},{6,30},{7,31},{8,16},{9,... | collective-permute-start | bytes 147464 | tf_op jit(solution)/shard_map/ppermute | solution.py:579
  26.2 15.7 %collective-permute-start.3 = (bf16[256,384]{1,0:T(8,128)(2,1)S(1)}, bf16[256,384]{1,0:T(8,128)(2,1)S(1)}, u32[]{:S(2)}, u32[]{:S(2)}) collective-permute-start(bf16[256,384]{1,0:T(8,128)(2,1)S(1)} %pad_maximum_fusion.5), channel_id=1, source_target_pairs={{0,2},{1,3},{2,0},{3,1},{4,6},{5,7},{6,4},{7,5},{8,10},{9,11},{10,... | collective-permute-start | bytes 589832 | tf_op jit(solution)/shard_map/ppermute | solution.py:579
  27.9 14.0 %collective-permute-start.4 = (bf16[256,384]{1,0:T(8,128)(2,1)S(1)}, bf16[256,384]{1,0:T(8,128)(2,1)S(1)}, u32[]{:S(2)}, u32[]{:S(2)}) collective-permute-start(bf16[256,384]{1,0:T(8,128)(2,1)S(1)} %pad_maximum_fusion.5), channel_id=1, source_target_pairs={{0,4},{1,5},{2,6},{3,7},{4,0},{5,1},{6,2},{7,3},{8,12},{9,13},{10,... | collective-permute-start | bytes 589832 | tf_op jit(solution)/shard_map/ppermute | solution.py:579
  29.5 12.4 %collective-permute-start.5 = (bf16[256,384]{1,0:T(8,128)(2,1)S(1)}, bf16[256,384]{1,0:T(8,128)(2,1)S(1)}, u32[]{:S(2)}, u32[]{:S(2)}) collective-permute-start(bf16[256,384]{1,0:T(8,128)(2,1)S(1)} %pad_maximum_fusion.5), channel_id=1, source_target_pairs={{0,6},{1,7},{2,4},{3,5},{4,2},{5,3},{6,0},{7,1},{8,14},{9,15},{10,... | collective-permute-start | bytes 589832 | tf_op jit(solution)/shard_map/ppermute | solution.py:579
  50.6 3.8 %collective-permute-start.8 = (f32[40,128]{1,0:T(8,128)S(1)}, f32[40,128]{1,0:T(8,128)S(1)}, u32[]{:S(2)}, u32[]{:S(2)}) collective-permute-start(f32[40,128]{1,0:T(8,128)S(1)} %add.110), channel_id=1, source_target_pairs={{0,2},{1,3},{2,0},{3,1},{4,6},{5,7},{6,4},{7,5},{8,10},{9,11},{10,... | collective-permute-start | bytes 61448 | tf_op jit(solution)/shard_map/ppermute | solution.py:579
  54.4 3.8 %collective-permute-start.9 = (f32[40,128]{1,0:T(8,128)S(1)}, f32[40,128]{1,0:T(8,128)S(1)}, u32[]{:S(2)}, u32[]{:S(2)}) collective-permute-start(f32[40,128]{1,0:T(8,128)S(1)} %add.111), channel_id=1, source_target_pairs={{0,4},{1,5},{2,6},{3,7},{4,0},{5,1},{6,2},{7,3},{8,12},{9,13},{10,... | collective-permute-start | bytes 61448 | tf_op jit(solution)/shard_map/ppermute | solution.py:579
  58.2 3.8 %collective-permute-start.10 = (f32[40,128]{1,0:T(8,128)S(1)}, f32[40,128]{1,0:T(8,128)S(1)}, u32[]{:S(2)}, u32[]{:S(2)}) collective-permute-start(f32[40,128]{1,0:T(8,128)S(1)} %add.112), channel_id=1, source_target_pairs={{0,8},{1,9},{2,10},{3,11},{4,12},{5,13},{6,14},{7,15},{8,0},{9,1},... | collective-permute-start | bytes 61448 | tf_op jit(solution)/shard_map/ppermute | solution.py:579
  62.0 5.1 %collective-permute-start.11 = (f32[40,128]{1,0:T(8,128)S(1)}, f32[40,128]{1,0:T(8,128)S(1)}, u32[]{:S(2)}, u32[]{:S(2)}) collective-permute-start(f32[40,128]{1,0:T(8,128)S(1)} %add.113), channel_id=1, source_target_pairs={{0,16},{1,17},{2,18},{3,19},{4,20},{5,21},{6,22},{7,23},{8,24},{9,... | collective-permute-start | bytes 61448 | tf_op jit(solution)/shard_map/ppermute | solution.py:579
  72.9 9.8 %collective-permute-start.12 = (bf16[768,384]{1,0:T(8,128)(2,1)}, bf16[768,384]{1,0:T(8,128)(2,1)S(1)}, u32[]{:S(2)}, u32[]{:S(2)}) collective-permute-start(bf16[768,384]{1,0:T(8,128)(2,1)} %get-tuple-element.96), channel_id=1, source_target_pairs={{0,1},{1,0},{2,3},{3,2},{4,5},{5,4},{6,7},{7,6},{8,9},{9,8},{10,11... | collective-permute-start | bytes 1769480 | tf_op jit(solution)/shard_map/ppermute | solution.py:579
  82.0 2.4 %collective-permute-start.13 = (bf16[768,384]{1,0:T(8,128)(2,1)}, bf16[768,384]{1,0:T(8,128)(2,1)S(1)}, u32[]{:S(2)}, u32[]{:S(2)}) collective-permute-start(bf16[768,384]{1,0:T(8,128)(2,1)} %get-tuple-element.98), channel_id=1, source_target_pairs={{0,1},{1,0},{2,3},{3,2},{4,5},{5,4},{6,7},{7,6},{8,9},{9,8},{10,11... | collective-permute-start | bytes 1769480 | tf_op jit(solution)/shard_map/ppermute | solution.py:579
  82.6 35.0 %collective-permute-start.19 = (bf16[192,384]{1,0:T(8,128)(2,1)S(1)}, bf16[192,384]{1,0:T(8,128)(2,1)S(1)}, u32[]{:S(2)}, u32[]{:S(2)}) collective-permute-start(bf16[192,384]{1,0:T(8,128)(2,1)S(1)} %copy-done.12), channel_id=1, source_target_pairs={{0,1},{1,0},{2,3},{3,2},{4,5},{5,4},{6,7},{7,6},{8,9},{9,8},{10,11... | collective-permute-start | bytes 442376 | tf_op jit(solution)/shard_map/ppermute | solution.py:579
  84.8 14.9 %collective-permute-start.14 = (bf16[384,384]{1,0:T(8,128)(2,1)S(1)}, bf16[384,384]{1,0:T(8,128)(2,1)S(1)}, u32[]{:S(2)}, u32[]{:S(2)}) collective-permute-start(bf16[384,384]{1,0:T(8,128)(2,1)S(1)} %get-tuple-element.134), channel_id=1, source_target_pairs={{0,2},{1,3},{2,0},{3,1},{4,6},{5,7},{6,4},{7,5},{8,10},{9,11},{10,... | collective-permute-start | bytes 884744 | tf_op jit(solution)/shard_map/ppermute | solution.py:579
  86.3 15.3 %collective-permute-start.15 = (bf16[384,384]{1,0:T(8,128)(2,1)S(1)}, bf16[384,384]{1,0:T(8,128)(2,1)S(1)}, u32[]{:S(2)}, u32[]{:S(2)}) collective-permute-start(bf16[384,384]{1,0:T(8,128)(2,1)S(1)} %get-tuple-element.133), channel_id=1, source_target_pairs={{0,4},{1,5},{2,6},{3,7},{4,0},{5,1},{6,2},{7,3},{8,12},{9,13},{10,... | collective-permute-start | bytes 884744 | tf_op jit(solution)/shard_map/ppermute | solution.py:579
  87.8 13.8 %collective-permute-start.16 = (bf16[384,384]{1,0:T(8,128)(2,1)S(1)}, bf16[384,384]{1,0:T(8,128)(2,1)S(1)}, u32[]{:S(2)}, u32[]{:S(2)}) collective-permute-start(bf16[384,384]{1,0:T(8,128)(2,1)S(1)} %get-tuple-element.132), channel_id=1, source_target_pairs={{0,6},{1,7},{2,4},{3,5},{4,2},{5,3},{6,0},{7,1},{8,14},{9,15},{10,... | collective-permute-start | bytes 884744 | tf_op jit(solution)/shard_map/ppermute | solution.py:579
  101.8 15.5 %collective-permute-start.17 = (bf16[384,384]{1,0:T(8,128)(2,1)S(1)}, bf16[384,384]{1,0:T(8,128)(2,1)S(1)}, u32[]{:S(2)}, u32[]{:S(2)}) collective-permute-start(bf16[384,384]{1,0:T(8,128)(2,1)S(1)} %fusion.2), channel_id=1, source_target_pairs={{0,16},{1,17},{2,18},{3,19},{4,20},{5,21},{6,22},{7,23},{8,24},{9,... | collective-permute-start | bytes 884744 | tf_op jit(solution)/shard_map/ppermute | solution.py:579
  117.3 13.2 %collective-permute-start.18 = (bf16[768,384]{1,0:T(8,128)(2,1)}, bf16[768,384]{1,0:T(8,128)(2,1)S(1)}, u32[]{:S(2)}, u32[]{:S(2)}) collective-permute-start(bf16[768,384]{1,0:T(8,128)(2,1)} %get-tuple-element.113), channel_id=1, source_target_pairs={{0,1},{1,0},{2,3},{3,2},{4,5},{5,4},{6,7},{7,6},{8,9},{9,8},{10,11... | collective-permute-start | bytes 1769480 | tf_op jit(solution)/shard_map/ppermute | solution.py:579
  117.4 9.5 %collective-permute-start.28 = (bf16[384,384]{1,0:T(8,128)(2,1)S(1)}, bf16[384,384]{1,0:T(8,128)(2,1)S(1)}, u32[]{:S(2)}, u32[]{:S(2)}) collective-permute-start(bf16[384,384]{1,0:T(8,128)(2,1)S(1)} %add_convert_fusion.4), channel_id=1, source_target_pairs={{0,8},{1,9},{2,10},{3,11},{4,12},{5,13},{6,14},{7,15},{8,0},{9,1},... | collective-permute-start | bytes 884744 | tf_op jit(solution)/shard_map/ppermute | solution.py:579
  127.0 9.9 %collective-permute-start.29 = (bf16[384,384]{1,0:T(8,128)(2,1)S(1)}, bf16[384,384]{1,0:T(8,128)(2,1)S(1)}, u32[]{:S(2)}, u32[]{:S(2)}) collective-permute-start(bf16[384,384]{1,0:T(8,128)(2,1)S(1)} %add_convert_fusion.3), channel_id=1, source_target_pairs={{0,2},{1,3},{2,0},{3,1},{4,6},{5,7},{6,4},{7,5},{8,10},{9,11},{10,... | collective-permute-start | bytes 884744 | tf_op jit(solution)/shard_map/ppermute | solution.py:579
  128.5 16.2 %collective-permute-start.30 = (bf16[384,384]{1,0:T(8,128)(2,1)S(1)}, bf16[384,384]{1,0:T(8,128)(2,1)S(1)}, u32[]{:S(2)}, u32[]{:S(2)}) collective-permute-start(bf16[384,384]{1,0:T(8,128)(2,1)S(1)} %add_convert_fusion.3), channel_id=1, source_target_pairs={{0,4},{1,5},{2,6},{3,7},{4,0},{5,1},{6,2},{7,3},{8,12},{9,13},{10,... | collective-permute-start | bytes 884744 | tf_op jit(solution)/shard_map/ppermute | solution.py:579
  129.0 15.6 %collective-permute-start.31 = (bf16[384,384]{1,0:T(8,128)(2,1)S(1)}, bf16[384,384]{1,0:T(8,128)(2,1)S(1)}, u32[]{:S(2)}, u32[]{:S(2)}) collective-permute-start(bf16[384,384]{1,0:T(8,128)(2,1)S(1)} %add_convert_fusion.3), channel_id=1, source_target_pairs={{0,6},{1,7},{2,4},{3,5},{4,2},{5,3},{6,0},{7,1},{8,14},{9,15},{10,... | collective-permute-start | bytes 884744 | tf_op jit(solution)/shard_map/ppermute | solution.py:579
  130.8 16.4 %collective-permute-start.20 = (bf16[240,384]{1,0:T(8,128)(2,1)S(1)}, bf16[240,384]{1,0:T(8,128)(2,1)S(1)}, u32[]{:S(2)}, u32[]{:S(2)}) collective-permute-start(bf16[240,384]{1,0:T(8,128)(2,1)S(1)} %get-tuple-element.135), channel_id=1, source_target_pairs={{0,2},{1,3},{2,0},{3,1},{4,6},{5,7},{6,4},{7,5},{8,10},{9,11},{10,... | collective-permute-start | bytes 552968 | tf_op jit(solution)/shard_map/ppermute | solution.py:579
  132.3 18.6 %collective-permute-start.21 = (bf16[240,384]{1,0:T(8,128)(2,1)S(1)}, bf16[240,384]{1,0:T(8,128)(2,1)S(1)}, u32[]{:S(2)}, u32[]{:S(2)}) collective-permute-start(bf16[240,384]{1,0:T(8,128)(2,1)S(1)} %get-tuple-element.137), channel_id=1, source_target_pairs={{0,4},{1,5},{2,6},{3,7},{4,0},{5,1},{6,2},{7,3},{8,12},{9,13},{10,... | collective-permute-start | bytes 552968 | tf_op jit(solution)/shard_map/ppermute | solution.py:579
  136.9 14.0 %collective-permute-start.22 = (bf16[240,384]{1,0:T(8,128)(2,1)S(1)}, bf16[240,384]{1,0:T(8,128)(2,1)S(1)}, u32[]{:S(2)}, u32[]{:S(2)}) collective-permute-start(bf16[240,384]{1,0:T(8,128)(2,1)S(1)} %get-tuple-element.136), channel_id=1, source_target_pairs={{0,6},{1,7},{2,4},{3,5},{4,2},{5,3},{6,0},{7,1},{8,14},{9,15},{10,... | collective-permute-start | bytes 552968 | tf_op jit(solution)/shard_map/ppermute | solution.py:579
  144.8 26.3 %collective-permute-start.32 = (bf16[1536,384]{1,0:T(8,128)(2,1)S(1)}, bf16[1536,384]{1,0:T(8,128)(2,1)S(1)}, u32[]{:S(2)}, u32[]{:S(2)}) collective-permute-start(bf16[1536,384]{1,0:T(8,128)(2,1)S(1)} %pad_maximum_fusion.1.own), channel_id=1, source_target_pairs={{0,1},{1,0},{2,3},{3,2},{4,5},{5,4},{6,7},{7,6},{8,9},{9,8},{10,11... | collective-permute-start | bytes 3538952 | tf_op jit(solution)/shard_map/ppermute | solution.py:579
  151.1 10.1 %collective-permute-start.23 = (bf16[240,384]{1,0:T(8,128)(2,1)S(1)}, bf16[240,384]{1,0:T(8,128)(2,1)S(1)}, u32[]{:S(2)}, u32[]{:S(2)}) collective-permute-start(bf16[240,384]{1,0:T(8,128)(2,1)S(1)} %fusion.5), channel_id=1, source_target_pairs={{0,16},{1,17},{2,18},{3,19},{4,20},{5,21},{6,22},{7,23},{8,24},{9,... | collective-permute-start | bytes 552968 | tf_op jit(solution)/shard_map/ppermute | solution.py:579
  161.2 6.4 %collective-permute-start.24 = (bf16[240,384]{1,0:T(8,128)(2,1)S(1)}, bf16[240,384]{1,0:T(8,128)(2,1)S(1)}, u32[]{:S(2)}, u32[]{:S(2)}) collective-permute-start(bf16[240,384]{1,0:T(8,128)(2,1)S(1)} %add_convert_fusion.6), channel_id=1, source_target_pairs={{0,8},{1,9},{2,10},{3,11},{4,12},{5,13},{6,14},{7,15},{8,0},{9,1},... | collective-permute-start | bytes 552968 | tf_op jit(solution)/shard_map/ppermute | solution.py:579
  167.6 8.9 %collective-permute-start.25 = (bf16[240,384]{1,0:T(8,128)(2,1)S(1)}, bf16[240,384]{1,0:T(8,128)(2,1)S(1)}, u32[]{:S(2)}, u32[]{:S(2)}) collective-permute-start(bf16[240,384]{1,0:T(8,128)(2,1)S(1)} %add_convert_fusion.5), channel_id=1, source_target_pairs={{0,2},{1,3},{2,0},{3,1},{4,6},{5,7},{6,4},{7,5},{8,10},{9,11},{10,... | collective-permute-start | bytes 552968 | tf_op jit(solution)/shard_map/ppermute | solution.py:579
  168.2 9.4 %collective-permute-start.26 = (bf16[240,384]{1,0:T(8,128)(2,1)S(1)}, bf16[240,384]{1,0:T(8,128)(2,1)S(1)}, u32[]{:S(2)}, u32[]{:S(2)}) collective-permute-start(bf16[240,384]{1,0:T(8,128)(2,1)S(1)} %add_convert_fusion.5), channel_id=1, source_target_pairs={{0,4},{1,5},{2,6},{3,7},{4,0},{5,1},{6,2},{7,3},{8,12},{9,13},{10,... | collective-permute-start | bytes 552968 | tf_op jit(solution)/shard_map/ppermute | solution.py:579
  169.6 7.9 %collective-permute-start.27 = (bf16[240,384]{1,0:T(8,128)(2,1)S(1)}, bf16[240,384]{1,0:T(8,128)(2,1)S(1)}, u32[]{:S(2)}, u32[]{:S(2)}) collective-permute-start(bf16[240,384]{1,0:T(8,128)(2,1)S(1)} %add_convert_fusion.5), channel_id=1, source_target_pairs={{0,6},{1,7},{2,4},{3,5},{4,2},{5,3},{6,0},{7,1},{8,14},{9,15},{10,... | collective-permute-start | bytes 552968 | tf_op jit(solution)/shard_map/ppermute | solution.py:579
  177.6 6.7 %collective-permute-start.33 = (bf16[960,384]{1,0:T(8,128)(2,1)S(1)}, bf16[960,384]{1,0:T(8,128)(2,1)S(1)}, u32[]{:S(2)}, u32[]{:S(2)}) collective-permute-start(bf16[960,384]{1,0:T(8,128)(2,1)S(1)} %pad_maximum_fusion.4.own), channel_id=1, source_target_pairs={{0,1},{1,0},{2,3},{3,2},{4,5},{5,4},{6,7},{7,6},{8,9},{9,8},{10,11... | collective-permute-start | bytes 2211848 | tf_op jit(solution)/shard_map/ppermute | solution.py:579
  (16 other events, 144.2 us)

commit v3 on v2

--- a/solution.py
+++ b/solution.py
@@ -312,13 +312,20 @@
     dt_ref[...] = mm(dl.astype(BF), images[...])
 
 
-def halves(place, rows, send_ref, keep_ref, pieces):
+def quarter(mine, base, k, rows=48):
+    far = (mine & 3) ^ k
+    return pl.multiple_of(base + rows * ((far & 1) * 2 + (far >> 1)), 16)
+
+
+def halves(mine, rows, send_ref, keep_ref, piece):
     for rel in range(8):
         ref = keep_ref if rel < 4 else send_ref
         at = (rel % 4) * rows
-        for v in pieces(place ^ rel):
-            ref[at : at + v.shape[0], :] = v.astype(BF)
-            at += v.shape[0]
+        if rows == 48:
+            ref[at : at + 48, :] = piece((mine >> 2) ^ rel, 0).astype(BF)
+            continue
+        for k in range(4):
+            ref[pl.ds(quarter(mine, at, k), 48), :] = piece((mine >> 2) ^ rel, k).astype(BF)
 
 
 def block(acc, at, rows, col=0):
@@ -359,8 +366,8 @@
             dy_ref[b, CAP_BLOCK * i : CAP_BLOCK * (i + 1), :] = piece[CAP_BLOCK * b : CAP_BLOCK * (b + 1)]
     down[...] = mm_tn(jnp.concatenate(split3(pu[...]), 0), jnp.concatenate([dyb, dyb, dyb], 0))
     proj[...] = mm_tn(pb[...], de)
-    halves(mine >> 2, 192, sd_ref, kd_ref, lambda at: [block(down, at, 192)])
-    halves(mine >> 2, 48, sp_ref, kp_ref, lambda at: [block(proj, at, 48)])
+    halves(mine, 192, sd_ref, kd_ref, lambda at, k: block(down, at * 4 + k, 48))
+    halves(mine, 48, sp_ref, kp_ref, lambda at, k: block(proj, at, 48))
 
 
 def mlp_back_kernel(
@@ -391,7 +398,7 @@
 
     @pl.when(step == pl.num_programs(0) - 1)
     def _():
-        halves(mine_ref[0] >> 2, 192, send_ref, keep_ref, lambda at: [block(acc, at, 48, k) for k in range(4)])
+        halves(mine_ref[0], 192, send_ref, keep_ref, lambda at, k: block(acc, at, 48, k))
 
 
 def att_core_kernel(qkv_ref, p_ref, dxb_ref, wout, dqkv_ref):
@@ -423,23 +430,10 @@
             dqkv_ref[rows, 2 * D + PAIR * j : 2 * D + PAIR * j + PAIR] = dv.astype(BF)
 
 
-def att_grads_kernel(mine_ref, h1_ref, dqkv_ref, o_ref, dxb_ref, send_ref, keep_ref, acc, out):
-    step = pl.program_id(0)
-
-    @pl.when(step == 0)
-    def _():
-        acc[...] = jnp.zeros_like(acc)
-        out[...] = jnp.zeros_like(out)
-
-    out[...] += mm_tn(o_ref[...], dxb_ref[...])
-    acc[...] += mm_tn(h1_ref[...], dqkv_ref[...])
-
-    @pl.when(step == pl.num_programs(0) - 1)
-    def _():
-        def pieces(at):
-            return [block(out, at, 48)] + [block(acc, at, 48, k) for k in range(3)]
-
-        halves(mine_ref[0] >> 2, 192, send_ref, keep_ref, pieces)
+def att_grads_kernel(mine_ref, h1_ref, dqkv_ref, o_ref, dxb_ref, send_ref, keep_ref, acc):
+    acc[:, :D] = mm_tn(o_ref[...], dxb_ref[...])
+    acc[:, D:] = mm_tn(h1_ref[...], dqkv_ref[...])
+    halves(mine_ref[0], 192, send_ref, keep_ref, lambda at, k: block(acc, at, 48, k))
 
 
 def tok_back_kernel(tok_ref, dqkv_ref, dx_ref, g1, wqkv, gtok_ref):
@@ -464,23 +458,24 @@
         yield (mine_ref[0] >> 2) ^ rel, src, (rel % 4) * rows
 
 
-def spread_mlp_kernel(mine_ref, own, other, wup, g2, down_ref, up_ref, gain_ref):
-    for at, src, row in arrived(mine_ref, own, other, 384):
-        down_ref[pl.ds(pl.multiple_of(at * 192, 64), 192), :] = src[row : row + 192, :].astype(F32)
+def spread_mlp_kernel(mine_ref, own, other, wup, g2, down_ref, up_ref, proj_ref, gain_ref):
+    for at, src, row in arrived(mine_ref, own, other, 432):
         rows = pl.ds(pl.multiple_of(at * 48, 16), 48)
         for k in range(4):
-            up_ref[rows, D * k : D * (k + 1)] = src[row + 192 + 48 * k : row + 240 + 48 * k, :].astype(F32)
-    gain_ref[...] = gain_of(up_ref[...], wup[...], g2[...])
-
-
-def spread_att_kernel(mine_ref, own, other, wqkv, g1, out_ref, qkv_ref, proj_ref, gain_ref):
-    for at, src, row in arrived(mine_ref, own, other, 240):
+            part = quarter(mine_ref[0], row, k, 96)
+            down_ref[pl.ds(pl.multiple_of(at * 192 + 48 * k, 16), 48), :] = src[pl.ds(part, 48), :].astype(F32)
+            up_ref[rows, D * k : D * (k + 1)] = src[pl.ds(pl.multiple_of(part + 48, 16), 48), :].astype(F32)
+        proj_ref[rows, :] = src[row + 384 : row + 432, :].astype(F32)
+    gain_ref[...] = gain_of(up_ref[...], wup[...], g2[...]).reshape(D)
+
+
+def spread_att_kernel(mine_ref, own, other, wqkv, g1, out_ref, qkv_ref, gain_ref):
+    for at, src, row in arrived(mine_ref, own, other, 192):
         rows = pl.ds(pl.multiple_of(at * 48, 16), 48)
-        out_ref[rows, :] = src[row : row + 48, :].astype(F32)
+        out_ref[rows, :] = src[pl.ds(quarter(mine_ref[0], row, 0), 48), :].astype(F32)
         for k in range(3):
-            qkv_ref[rows, D * k : D * (k + 1)] = src[row + 48 + 48 * k : row + 96 + 48 * k, :].astype(F32)
-        proj_ref[rows, :] = src[row + 192 : row + 240, :].astype(F32)
-    gain_ref[...] = gain_of(qkv_ref[...], wqkv[...], g1[...])
+            qkv_ref[rows, D * k : D * (k + 1)] = src[pl.ds(quarter(mine_ref[0], row, k + 1), 48), :].astype(F32)
+    gain_ref[...] = gain_of(qkv_ref[...], wqkv[...], g1[...]).reshape(D)
 
 
 SMEM = pl.BlockSpec(memory_space=pltpu.SMEM)
@@ -546,17 +541,9 @@
 
 
 def att_grads(mine, h1, dqkv, o, dxb):
-    n = h1.shape[0]
-    return pl.pallas_call(
-        att_grads_kernel,
-        grid=(n // TOK_BLOCK,),
-        in_specs=[SMEM, token_rows(D), token_rows(3 * D), token_rows(D), token_rows(D)],
-        out_specs=[whole(768, D)] * 2,
-        out_shape=[jax.ShapeDtypeStruct((768, D), BF)] * 2,
-        scratch_shapes=[pltpu.VMEM((D, 3 * D), F32), pltpu.VMEM((D, D), F32)],
-        cost_estimate=cost(4),
-        name="att_grads",
-    )(mine, h1, dqkv, o, dxb)
+    outs = [((768, D), BF)] * 2
+    scratch = [pltpu.VMEM((D, 4 * D), F32)]
+    return simple(att_grads_kernel, outs, scratch, smem=1, us=4, name="att_grads")(mine, h1, dqkv, o, dxb)
 
 
 def tok_back(tok, dqkv, dx, g1, wqkv):
@@ -587,11 +574,13 @@
     return [swap(parts[m], 8 * m) for m in (1, 2, 3)]
 
 
+def total_of(own, got):
+    v = [own.astype(F32)] + [x.astype(F32) for x in got]
+    return v[0] + v[1] if len(v) == 2 else (v[0] + v[1]) + (v[2] + v[3])
+
+
 def added(own, got):
-    total = own.astype(F32)
-    for v in got:
-        total = total + v.astype(F32)
-    return total.astype(BF)
+    return total_of(own, got).astype(BF)
 
 
 def joined(own, got):
@@ -647,8 +636,9 @@
         log_scale, g, images, pair
     )
     if tuned:
-        for mask in (1, 2, 4, 8, 16):
-            sums = sums + swap(sums, mask)
+        sums = total_of(sums, [swap(sums, 1)])
+        sums = total_of(sums, plane([sums] * 4))
+        sums = total_of(sums, column([sums] * 4))
     else:
         sums = lax.psum(sums, AXES)
     send_d, keep_d, send_p, keep_p, du, dy, loss, temp = simple(
@@ -664,18 +654,16 @@
     )(log_scale, mine, g, images, sums, dt_row, e, pb, cnt, pu, txt_proj, txt_down)
     dx, dxb, send_u, keep_u = mlp_back(mine, lab, h2, gp, c2, du, dy, txt_ln2, txt_up)
 
-    def mlp_parts(d, u):
-        return jnp.concatenate([d.reshape(4, 192, D), u.reshape(4, 192, D)], 1)
-
-    def att_parts(a, p):
-        return jnp.concatenate([a.reshape(4, 192, D), p.reshape(4, 48, D)], 1)
+    def mlp_parts(d, u, p):
+        both = jnp.concatenate([d.reshape(4, 4, 48, D), u.reshape(4, 4, 48, D)], 2).reshape(4, 384, D)
+        return jnp.concatenate([both, p.reshape(4, 48, D)], 1)
 
     def spread_mlp(own, other):
-        outs = [((FF, D), F32), ((D, FF), F32), ((1, D), F32)]
+        outs = [((FF, D), F32), ((D, FF), F32), ((D, D), F32), ((D,), F32)]
         return simple(spread_mlp_kernel, outs, smem=1, us=4, name="spread_mlp")(mine, own, other, txt_up, txt_ln2)
 
     def spread_att(own, other):
-        outs = [((D, D), F32), ((D, 3 * D), F32), ((D, D), F32), ((1, D), F32)]
+        outs = [((D, D), F32), ((D, 3 * D), F32), ((D,), F32)]
         return simple(spread_att_kernel, outs, smem=1, us=4, name="spread_att")(mine, own, other, txt_qkv, txt_ln1)
 
     if not tuned:
@@ -684,39 +672,50 @@
         grad_tokens = tok_back(text_tokens, dqkv, dx, txt_ln1, txt_qkv)
         sums = [keep_d, send_d, keep_u, send_u, keep_a, send_a, keep_p, send_p]
         d, d2, u, u2, a, a2, p, p2 = [v.astype(BF) for v in lax.psum([v.astype(F32) for v in sums], AXES)]
-        grad_down, grad_up, gain2 = spread_mlp(mlp_parts(d, u).reshape(1536, D), mlp_parts(d2, u2).reshape(1536, D))
-        grad_out, grad_qkv, grad_proj, gain1 = spread_att(
-            att_parts(a, p).reshape(960, D), att_parts(a2, p2).reshape(960, D)
+        grad_down, grad_up, grad_proj, gain2 = spread_mlp(
+            mlp_parts(d, u, p).reshape(1728, D), mlp_parts(d2, u2, p2).reshape(1728, D)
         )
+        grad_out, grad_qkv, gain1 = spread_att(a, a2)
     else:
         d = added(keep_d, [swap(send_d, 1)])
         pr = added(keep_p, [swap(send_p, 1)])
-        m = mlp_parts(d, added(keep_u, [swap(send_u, 1)]))
+        m = mlp_parts(d, added(keep_u, [swap(send_u, 1)]), pr)
         dxb, m = lax.optimization_barrier((dxb, m))
         got = plane(m)
         dqkv = att_core(qkv, p, dxb, txt_out)
         got, dqkv = lax.optimization_barrier((got, dqkv))
         m = added(m[0], got)
         m, dqkv = lax.optimization_barrier((m, dqkv))
-        other = swap(m, 16)
+        parts = [jnp.concatenate([m[96 * k : 96 * k + 96], m[384:]], 0) for k in (0, 2, 1, 3)]
+        got = column(parts)
         send_a, keep_a = att_grads(mine, h1, dqkv, o, dxb)
-        other, send_a, keep_a = lax.optimization_barrier((other, send_a, keep_a))
-        a = att_parts(added(keep_a, [swap(send_a, 1)]), pr)
-        a, dqkv = lax.optimization_barrier((a, dqkv))
+        got, send_a, keep_a = lax.optimization_barrier((got, send_a, keep_a))
+        q = added(parts[0], got)
+        far = swap(q[:96], 16)
+        a = added(keep_a, [swap(send_a, 1)]).reshape(4, 192, D)
+        got_a = plane(a)
+        m = joined(q[:96], [far])
+        near = swap(m, 8)
+        dqkv, a, m = lax.optimization_barrier((dqkv, a, m))
         grad_tokens = tok_back(text_tokens, dqkv, dx, txt_ln1, txt_qkv)
-        m = added(m, [other])
-        m = added(m, [swap(m, 8)])
-        a = added(a[0], plane(a))
-        a = added(a, [swap(a, 16)])
-        m = joined(m, plane([m] * 4))
-        a = added(a, [swap(a, 8)])
-        grad_down, grad_up, gain2 = spread_mlp(m, swap(m, 1))
-        got = plane([a] * 4)
-        got, grad_up = lax.optimization_barrier((got, grad_up))
-        a = joined(a, got)
-        grad_out, grad_qkv, grad_proj, gain1 = spread_att(a, swap(a, 1))
+        got_a, near, grad_tokens = lax.optimization_barrier((got_a, near, grad_tokens))
+        a = added(a[0], got_a)
+        m = joined(m, [near, q[96:]])
+        got_m = plane([m] * 4)
+        a = added(a[:96], [swap(a[96:], 8)])
+        a = added(a[:48], [swap(a[48:], 16)])
+        a, got_m[0], got_m[1] = lax.optimization_barrier((a, got_m[0], got_m[1]))
+        a = joined(a, [swap(a, 16)])
+        a = joined(a, [swap(a, 8)])
+        got_m, a = lax.optimization_barrier((got_m, a))
+        got_a = plane([a] * 4)
+        m = joined(m, got_m)
+        grad_down, grad_up, grad_proj, gain2 = spread_mlp(m, swap(m, 1))
+        got_a, grad_up = lax.optimization_barrier((got_a, grad_up))
+        a = joined(a, got_a)
+        grad_out, grad_qkv, gain1 = spread_att(a, swap(a, 1))
     return (
-        loss.reshape(1), grad_tokens, gain1.reshape(D), grad_qkv, grad_out, gain2.reshape(D),
+        loss.reshape(1), grad_tokens, gain1, grad_qkv, grad_out, gain2,
         grad_up, grad_down, grad_proj, temp.reshape(1),
     )
 

time: 190 us -> 169 us (0.89)
  waiting for transfers between devices: 61.4 us -> 32.2 us
  starting transfers between devices: 35.5 us -> 46.8 us
  other arithmetic: 4.75 us -> 2.75 us
    ppermute x34 -> x41, waiting for transfers between devices: 61.4 us -> 32.2 us  [swap(): return lax.ppermute(v, AXES, [(i, i ^ mask) for i in range(32)])]
    ppermute x34 -> x41, starting transfers between devices: 35.5 us -> 46.8 us  [swap(): return lax.ppermute(v, AXES, [(i, i ^ mask) for i in range(32)])]
    pallas_call x1 -> x0, Pallas kernels: 5.65 us -> none  [att_grads(): pl.pallas_call(att_grads_kernel, grid=(n // TOK_BLOCK,), in_specs=[SMEM,...]
    pallas_call x5 -> x6, Pallas kernels: 18.5 us -> 23.8 us  [call(): pl.pallas_call(kernel, in_specs=[SMEM] * smem + [VMEM] * (len(args) - sme...]
  transfers between devices with their start and end apart: 34 -> 41, of which waited for: 16 -> 18; matrix products, arithmetic and copies ran while one was open for 2% -> 1% of each run, Pallas kernels for 31% -> 35%
where the time goes in v3:
time: 169 us
  Pallas kernels  81.1 us (48%)
  starting transfers between devices  46.8 us (28%)
  waiting for transfers between devices  32.2 us (19%)
  local copies, waits for them, and re-layouts  4.17 us (2%)
  other arithmetic  2.75 us (2%)
  between operations  1.83 us (1%)
    ppermute x41, starting transfers between devices, swap(): return lax.ppermute(v, AXES, [(i, i ^ mask) for i in range(32)])  46.8 us
    ppermute x41, waiting for transfers between devices, swap(): return lax.ppermute(v, AXES, [(i, i ^ mask) for i in range(32)])  32.2 us
    pallas_call x6, Pallas kernels, call(): pl.pallas_call(kernel, in_specs=[SMEM] * smem + [VMEM] * (len(args) - sme...  23.8 us
    pallas_call x1, Pallas kernels, text_mlp(): pl.pallas_call(text_mlp_kernel, grid=(n // TOK_BLOCK,), in_specs=[token_r...  12.2 us
    pallas_call x1, Pallas kernels, image_tower(): pl.pallas_call(image_kernel, grid=(count // IMG_BLOCK,), in_specs=[pl.Blo...  11.4 us
    pallas_call x1, Pallas kernels, att_core(): pl.pallas_call(att_core_kernel, grid=(n // TOK_BLOCK,), in_specs=[token_r...  11.3 us
    pallas_call x1, Pallas kernels, mlp_back(): pl.pallas_call(mlp_back_kernel, grid=(n // TOK_BLOCK,), in_specs=[SMEM, b...  9.02 us
    pallas_call x1, Pallas kernels, text_att(): pl.pallas_call(text_att_kernel, grid=(blocks,), in_specs=[token_rows(D),...  7.62 us
  transfers between devices with their start and end apart: 41, of which 18 were waited for; matrix products, arithmetic and copies ran while one was open for 1% of the time, Pallas kernels for 35%

profile of v3, /device:TPU:0, one launch (start us, length us, event | category | flops | bytes accessed | tf_op | source)
XLA Modules:
  0.0 168.9 jit_solution(7557248333347065734)
XLA Ops:
  0.7 11.4 %image_tower.1 = bf16[64,384]{1,0:T(8,128)(2,1)} custom-call(bf16[50,64,384]{2,1,0:T(8,128)(2,1)} %bitcast.28, f32[384]{0:T(512)} %g1.5, bf16[384,1152]{1,0:T(8,128)(2,1)} %wqkv.5, bf16[384,384]{1,0:T(8,128)(2,1)} %wout.3, f32[384]{0:T(512)} %g2.4, bf16[384,1536]{1,0:T(8,128)(2,1)} %wup.4, bf16[1536,384]{1,0:T(8,128)(2,1)} %wdown.3, bf16[384,384]{1,0:T(8,128)(2,1)} %wproj.3), custom_call_target="tpu_custom_call" | custom-call | flops 12000000000 | bytes 36000000 | tf_op jit(solution)/shard_map/image_tower/pallas_call | solution.py:129
  12.1 3.1 %collective-permute-start = (bf16[64,384]{1,0:T(8,128)(2,1)}, bf16[64,384]{1,0:T(8,128)(2,1)S(1)}, u32[]{:S(2)}, u32[]{:S(2)}) collective-permute-start(bf16[64,384]{1,0:T(8,128)(2,1)} %image_tower.1), channel_id=1, source_target_pairs={{0,8},{1,9},{2,10},{3,11},{4,12},{5,13},{6,14},{7,15},{8,0},{9,1},... | collective-permute-start | bytes 147464 | tf_op jit(solution)/shard_map/ppermute | solution.py:566
  15.1 2.6 %collective-permute-start.1 = (bf16[64,384]{1,0:T(8,128)(2,1)}, bf16[64,384]{1,0:T(8,128)(2,1)S(1)}, u32[]{:S(2)}, u32[]{:S(2)}) collective-permute-start(bf16[64,384]{1,0:T(8,128)(2,1)} %image_tower.1), channel_id=1, source_target_pairs={{0,16},{1,17},{2,18},{3,19},{4,20},{5,21},{6,22},{7,23},{8,24},{9,... | collective-permute-start | bytes 147464 | tf_op jit(solution)/shard_map/ppermute | solution.py:566
  18.5 7.6 %text_att.1 = (bf16[1024,384]{1,0:T(8,128)(2,1)}, bf16[1024,1152]{1,0:T(8,128)(2,1)}, bf16[8,3,256,128]{3,2,1,0:T(8,128)(2,1)}, bf16[1024,384]{1,0:T(8,128)(2,1)}) custom-call(bf16[1024,384]{1,0:T(8,128)(2,1)} %tok_ref.5, s32[4,1,256]{2,1,0:T(1,128)} %reshape.73.lab_ref, f32[384]{0:T(512)} %g1.7, bf16[384,1152]{1,0:T(8,128)(2,1)} %wqkv.7), custom_call_target="tpu_custom_call" | custom-call | flops 8999999488 | bytes 27000000 | tf_op jit(solution)/shard_map/text_att/pallas_call | solution.py:238
  26.2 1.7 %collective-permute-start.3 = (bf16[256,384]{1,0:T(8,128)(2,1)S(1)}, bf16[256,384]{1,0:T(8,128)(2,1)S(1)}, u32[]{:S(2)}, u32[]{:S(2)}) collective-permute-start(bf16[256,384]{1,0:T(8,128)(2,1)S(1)} %pad_maximum_fusion.4), channel_id=1, source_target_pairs={{0,2},{1,3},{2,0},{3,1},{4,6},{5,7},{6,4},{7,5},{8,10},{9,11},{10,... | collective-permute-start | bytes 589832 | tf_op jit(solution)/shard_map/ppermute | solution.py:566
  29.7 12.2 %text_mlp.1 = (bf16[1024,384]{1,0:T(8,128)(2,1)}, f32[1024,384]{1,0:T(8,128)}, bf16[1024,1536]{1,0:T(8,128)(2,1)}, f32[64,1536]{1,0:T(8,128)}, bf16[64,384]{1,0:...) custom-call(bf16[1024,384]{1,0:T(8,128)(2,1)} %tok_ref.5, ...), custom_call_target="tpu_custom_call" | custom-call | flops 11000000512 | bytes 33000000 | tf_op jit(solution)/shard_map/text_mlp/pallas_call | solution.py:259
  45.7 2.9 %cosine.1 = (f32[64,2048]{1,0:T(8,128)}, f32[40,128]{1,0:T(8,128)}) custom-call(f32[1]{0:T(128)S(6)} %copy.43.scale_ref, s32[1]{0:T(128)} %bitcast.mine_ref, bf16[64,384]{1,0:T(8,128)(2,1)} %get-tuple-element.91.emb, bf16[2048,384]{1,0:T(8,128)(2,1)} %copy-done.6, s32[64,1]{1,0:T(8,128)} %copy.29.pair), custom_call_target="tpu_custom_call" | custom-call | flops 3000000000 | bytes 9000000 | tf_op jit(solution)/shard_map/cosine/pallas_call | solution.py:487
  50.7 2.6 %collective-permute-start.10 = (f32[40,128]{1,0:T(8,128)S(1)}, f32[40,128]{1,0:T(8,128)S(1)}, u32[]{:S(2)}, u32[]{:S(2)}) collective-permute-start(f32[40,128]{1,0:T(8,128)S(1)} %add.119), channel_id=1, source_target_pairs={{0,6},{1,7},{2,4},{3,5},{4,2},{5,3},{6,0},{7,1},{8,14},{9,15},{10,... | collective-permute-start | bytes 61448 | tf_op jit(solution)/shard_map/ppermute | solution.py:566
  55.4 1.7 %collective-permute-done.8 = f32[40,128]{1,0:T(8,128)S(1)} collective-permute-done((f32[40,128]{1,0:T(8,128)S(1)}, f32[40,128]{1,0:T(8,128)S(1)}, u32[]{:S(2)}, u32[]{:S(2)}) %collective-permute-start.8) | collective-permute-done | bytes 20512 | tf_op jit(solution)/shard_map/ppermute | solution.py:566
  58.5 3.5 %collective-permute-start.12 = (f32[40,128]{1,0:T(8,128)S(1)}, f32[40,128]{1,0:T(8,128)S(1)}, u32[]{:S(2)}, u32[]{:S(2)}) collective-permute-start(f32[40,128]{1,0:T(8,128)S(1)} %add_add_fusion.1), channel_id=1, source_target_pairs={{0,16},{1,17},{2,18},{3,19},{4,20},{5,21},{6,22},{7,23},{8,24},{9,... | collective-permute-start | bytes 61448 | tf_op jit(solution)/shard_map/ppermute | solution.py:566
  62.2 2.7 %rows.1.dt_row = f32[64,384]{1,0:T(8,128)} custom-call(f32[1]{0:T(128)S(6)} %copy.43.scale_ref, f32[64,2048]{1,0:T(8,128)} %get-tuple-element.97.g_ref, bf16[2048,384]{1,0:T(8,128)(2,1)} %copy-done.6, s32[64,1]{1,0:T(8,128)} %copy.29.pair), custom_call_target="tpu_custom_call" | custom-call | flops 2000000000 | bytes 6000000 | tf_op jit(solution)/shard_map/rows/pallas_call | solution.py:487
  64.8 2.7 %collective-permute-done.13 = f32[40,128]{1,0:T(8,128)S(1)} collective-permute-done((f32[40,128]{1,0:T(8,128)S(1)}, f32[40,128]{1,0:T(8,128)S(1)}, u32[]{:S(2)}, u32[]{:S(2)}) %collective-permute-start.13) | collective-permute-done | bytes 20512 | tf_op jit(solution)/shard_map/ppermute | solution.py:566
  68.1 5.3 %head_back.1 = (bf16[768,384]{1,0:T(8,128)(2,1)}, bf16[768,384]{1,0:T(8,128)(2,1)}, bf16[192,384]{1,0:T(8,128)(2,1)}, bf16[192,384]{1,0:T(8,128)(2,1)}, bf16[4,4...) custom-call(f32[1]{0:T(128)S(6)} %copy.43.scale_ref, s32[1]{0:T(128)} %bitcast.mine_ref, ...), custom_call_target="tpu_custom_call" | custom-call | flops 5000000000 | bytes 15000000 | tf_op jit(solution)/shard_map/head_back/pallas_call | solution.py:487
  74.0 9.0 %mlp_back.1 = (f32[1024,384]{1,0:T(8,128)}, bf16[1024,384]{1,0:T(8,128)(2,1)}, bf16[768,384]{1,0:T(8,128)(2,1)}, bf16[768,384]{1,0:T(8,128)(2,1)}) custom-call(s32[1]{0:T(128)} %bitcast.mine_ref, s32[4,1,256]{2,1,0:T(1,128)} %reshape.73.lab_ref, bf16[1024,384]{1,0:T(8,128)(2,1)} %get-tuple-element.104.h2_ref, bf16[1024,1536]{1,0:T(8,128)(2,1)} %get-tuple-element.105.gp_ref, ...), custom_call_target="tpu_custom_call" | custom-call | flops 8999999488 | bytes 27000000 | tf_op jit(solution)/shard_map/mlp_back/pallas_call | solution.py:510
  83.4 1.9 %collective-permute-done.15 = bf16[768,384]{1,0:T(8,128)(2,1)S(1)} collective-permute-done((bf16[768,384]{1,0:T(8,128)(2,1)}, bf16[768,384]{1,0:T(8,128)(2,1)S(1)}, u32[]{:S(2)}, u32[]{:S(2)}) %collective-permute-start.15) | collective-permute-done | bytes 589856 | tf_op jit(solution)/shard_map/ppermute | solution.py:566
  89.5 11.3 %att_core.1.dqkv_ref = bf16[1024,1152]{1,0:T(8,128)(2,1)} custom-call(bf16[1024,1152]{1,0:T(8,128)(2,1)} %get-tuple-element.117.qkv_ref, bf16[8,3,256,128]{3,2,1,0:T(8,128)(2,1)} %get-tuple-element.118.p_ref, bf16[1024,384]{1,0:T(8,128)(2,1)} %get-tuple-element.119.dxb_ref, bf16[384,384]{1,0:T(8,128)(2,1)} %wout.5), custom_call_target="tpu_custom_call" | custom-call | flops 10000000000 | bytes 30000000 | tf_op jit(solution)/shard_map/att_core/pallas_call | solution.py:527
  100.8 3.4 %collective-permute-done.18 = bf16[432,384]{1,0:T(8,128)(2,1)S(1)} collective-permute-done((bf16[432,384]{1,0:T(8,128)(2,1)S(1)}, bf16[432,384]{1,0:T(8,128)(2,1)S(1)}, u32[]{:S(2)}, u32[]{:S(2)}) %collective-permute-start.18) | collective-permute-done | bytes 331808 | tf_op jit(solution)/shard_map/ppermute | solution.py:566
  106.0 2.9 %collective-permute-start.22 = (bf16[144,384]{1,0:T(8,128)(2,1)S(1)}, bf16[144,384]{1,0:T(8,128)(2,1)S(1)}, u32[]{:S(2)}, u32[]{:S(2)}) collective-permute-start(bf16[144,384]{1,0:T(8,128)(2,1)S(1)} %concatenate.55), channel_id=1, source_target_pairs={{0,24},{1,25},{2,26},{3,27},{4,28},{5,29},{6,30},{7,31},{8,16},{9,... | collective-permute-start | bytes 331784 | tf_op jit(solution)/shard_map/ppermute | solution.py:566
  108.9 5.0 %att_grads.1 = (bf16[768,384]{1,0:T(8,128)(2,1)}, bf16[768,384]{1,0:T(8,128)(2,1)}) custom-call(s32[1]{0:T(128)} %bitcast.mine_ref, bf16[1024,384]{1,0:T(8,128)(2,1)} %get-tuple-element.125.h1_ref, bf16[1024,1152]{1,0:T(8,128)(2,1)} %att_core.1.dqkv_ref, bf16[1024,384]{1,0:T(8,128)(2,1)} %get-tuple-element.89.o_ref, bf16[1024,384]{1,0:T(8,128)(2,1)} %get-tuple-element.119.dxb_ref), custom_call_target="tpu_custom_call" | custom-call | flops 4000000000 | bytes 12000000 | tf_op jit(solution)/shard_map/att_grads/pallas_call | solution.py:487
  115.5 1.7 collective-permute-start.27
  117.2 5.5 %collective-permute-done.27 = bf16[96,384]{1,0:T(8,128)(2,1)S(1)} collective-permute-done((bf16[96,384]{1,0:T(8,128)(2,1)S(1)}, bf16[96,384]{1,0:T(8,128)(2,1)S(1)}, u32[]{:S(2)}, u32[]{:S(2)}) %collective-permute-start.27) | collective-permute-done | bytes 73760 | tf_op jit(solution)/shard_map/ppermute | solution.py:566
  126.9 5.8 %tok_back.1 = f32[1024,384]{1,0:T(8,128)} custom-call(bf16[1024,384]{1,0:T(8,128)(2,1)} %tok_ref.5, bf16[1024,1152]{1,0:T(8,128)(2,1)} %att_core.1.dqkv_ref, f32[1024,384]{1,0:T(8,128)} %get-tuple-element.135.dx_ref, f32[384]{0:T(512)} %g1.7, bf16[384,1152]{1,0:T(8,128)(2,1)} %wqkv.7), custom_call_target="tpu_custom_call" | custom-call | flops 4000000000 | bytes 12000000 | tf_op jit(solution)/shard_map/tok_back/pallas_call | solution.py:551
  132.9 1.8 %collective-permute-start.29 = (bf16[96,384]{1,0:T(8,128)(2,1)S(1)}, bf16[96,384]{1,0:T(8,128)(2,1)S(1)}, u32[]{:S(2)}, u32[]{:S(2)}) collective-permute-start(bf16[96,384]{1,0:T(8,128)(2,1)S(1)} %slice.86), channel_id=1, source_target_pairs={{0,8},{1,9},{2,10},{3,11},{4,12},{5,13},{6,14},{7,15},{8,0},{9,1},... | collective-permute-start | bytes 221192 | tf_op jit(solution)/shard_map/ppermute | solution.py:566
  137.4 2.2 %collective-permute-start.30 = (bf16[48,384]{1,0:T(8,128)(2,1)S(1)}, bf16[48,384]{1,0:T(8,128)(2,1)S(1)}, u32[]{:S(2)}, u32[]{:S(2)}) collective-permute-start(bf16[48,384]{1,0:T(8,128)(2,1)S(1)} %slice.88), channel_id=1, source_target_pairs={{0,16},{1,17},{2,18},{3,19},{4,20},{5,21},{6,22},{7,23},{8,24},{9,... | collective-permute-start | bytes 110600 | tf_op jit(solution)/shard_map/ppermute | solution.py:566
  139.6 2.7 %collective-permute-done.30 = bf16[48,384]{1,0:T(8,128)(2,1)S(1)} collective-permute-done((bf16[48,384]{1,0:T(8,128)(2,1)S(1)}, bf16[48,384]{1,0:T(8,128)(2,1)S(1)}, u32[]{:S(2)}, u32[]{:S(2)}) %collective-permute-start.30) | collective-permute-done | bytes 36896 | tf_op jit(solution)/shard_map/ppermute | solution.py:566
  142.5 2.1 %collective-permute-start.34 = (bf16[48,384]{1,0:T(8,128)(2,1)S(1)}, bf16[48,384]{1,0:T(8,128)(2,1)S(1)}, u32[]{:S(2)}, u32[]{:S(2)}) collective-permute-start(bf16[48,384]{1,0:T(8,128)(2,1)S(1)} %add_convert_fusion.6), channel_id=1, source_target_pairs={{0,16},{1,17},{2,18},{3,19},{4,20},{5,21},{6,22},{7,23},{8,24},{9,... | collective-permute-start | bytes 110600 | tf_op jit(solution)/shard_map/ppermute | solution.py:566
  147.4 1.9 %collective-permute-start.35 = (bf16[96,384]{1,0:T(8,128)(2,1)S(1)}, bf16[96,384]{1,0:T(8,128)(2,1)S(1)}, u32[]{:S(2)}, u32[]{:S(2)}) collective-permute-start(bf16[96,384]{1,0:T(8,128)(2,1)S(1)} %pad_maximum_fusion.10), channel_id=1, source_target_pairs={{0,8},{1,9},{2,10},{3,11},{4,12},{5,13},{6,14},{7,15},{8,0},{9,1},... | collective-permute-start | bytes 221192 | tf_op jit(solution)/shard_map/ppermute | solution.py:566
  149.2 2.5 %collective-permute-done.35 = bf16[96,384]{1,0:T(8,128)(2,1)S(1)} collective-permute-done((bf16[96,384]{1,0:T(8,128)(2,1)S(1)}, bf16[96,384]{1,0:T(8,128)(2,1)S(1)}, u32[]{:S(2)}, u32[]{:S(2)}) %collective-permute-start.35) | collective-permute-done | bytes 73760 | tf_op jit(solution)/shard_map/ppermute | solution.py:566
  156.5 4.8 %spread_mlp.1 = (f32[1536,384]{1,0:T(8,128)}, f32[384,1536]{1,0:T(8,128)}, f32[384,384]{1,0:T(8,128)}, f32[384]{0:T(512)}) custom-call(s32[1]{0:T(128)} %bitcast.mine_ref, bf16[1728,384]{1,0:T(8,128)(2,1)} %copy-done.7, bf16[1728,384]{1,0:T(8,128)(2,1)} %collective-permute-done.39.other, bf16[384,1536]{1,0:T(8,128)(2,1)} %wup.7, f32[384]{0:T(512)} %g2.7), custom_call_target="tpu_custom_call" | custom-call | flops 4000000000 | bytes 12000000 | tf_op jit(solution)/shard_map/spread_mlp/pallas_call | solution.py:487
  161.3 1.6 collective-permute-done.37
  163.0 2.0 %collective-permute-done.40.other = bf16[768,384]{1,0:T(8,128)(2,1)S(1)} collective-permute-done((bf16[768,384]{1,0:T(8,128)(2,1)S(1)}, bf16[768,384]{1,0:T(8,128)(2,1)S(1)}, u32[]{:S(2)}, u32[]{:S(2)}) %collective-permute-start.40) | collective-permute-done | bytes 589856 | tf_op jit(solution)/shard_map/ppermute | solution.py:566
  165.8 3.1 %spread_att.1 = (f32[384,384]{1,0:T(8,128)}, f32[384,1152]{1,0:T(8,128)}, f32[384]{0:T(512)}) custom-call(s32[1]{0:T(128)} %bitcast.mine_ref, bf16[768,384]{1,0:T(8,128)(2,1)} %copy-done.5, bf16[768,384]{1,0:T(8,128)(2,1)} %copy-done.9, bf16[384,1152]{1,0:T(8,128)(2,1)} %wqkv.7, f32[384]{0:T(512)} %g1.7), custom_call_target="tpu_custom_call" | custom-call | flops 4000000000 | bytes 12000000 | tf_op jit(solution)/shard_map/spread_att/pallas_call | solution.py:487
  (133 shorter events, 35.8 us)
Async XLA Ops:
  12.1 14.1 %collective-permute-start = (bf16[64,384]{1,0:T(8,128)(2,1)}, bf16[64,384]{1,0:T(8,128)(2,1)S(1)}, u32[]{:S(2)}, u32[]{:S(2)}) collective-permute-start(bf16[64,384]{1,0:T(8,128)(2,1)} %image_tower.1), channel_id=1, source_target_pairs={{0,8},{1,9},{2,10},{3,11},{4,12},{5,13},{6,14},{7,15},{8,0},{9,1},... | collective-permute-start | bytes 147464 | tf_op jit(solution)/shard_map/ppermute | solution.py:566
  15.1 11.0 %collective-permute-start.1 = (bf16[64,384]{1,0:T(8,128)(2,1)}, bf16[64,384]{1,0:T(8,128)(2,1)S(1)}, u32[]{:S(2)}, u32[]{:S(2)}) collective-permute-start(bf16[64,384]{1,0:T(8,128)(2,1)} %image_tower.1), channel_id=1, source_target_pairs={{0,16},{1,17},{2,18},{3,19},{4,20},{5,21},{6,22},{7,23},{8,24},{9,... | collective-permute-start | bytes 147464 | tf_op jit(solution)/shard_map/ppermute | solution.py:566
  17.7 8.4 %collective-permute-start.2 = (bf16[64,384]{1,0:T(8,128)(2,1)}, bf16[64,384]{1,0:T(8,128)(2,1)S(1)}, u32[]{:S(2)}, u32[]{:S(2)}) collective-permute-start(bf16[64,384]{1,0:T(8,128)(2,1)} %image_tower.1), channel_id=1, source_target_pairs={{0,24},{1,25},{2,26},{3,27},{4,28},{5,29},{6,30},{7,31},{8,16},{9,... | collective-permute-start | bytes 147464 | tf_op jit(solution)/shard_map/ppermute | solution.py:566
  26.2 15.7 %collective-permute-start.3 = (bf16[256,384]{1,0:T(8,128)(2,1)S(1)}, bf16[256,384]{1,0:T(8,128)(2,1)S(1)}, u32[]{:S(2)}, u32[]{:S(2)}) collective-permute-start(bf16[256,384]{1,0:T(8,128)(2,1)S(1)} %pad_maximum_fusion.4), channel_id=1, source_target_pairs={{0,2},{1,3},{2,0},{3,1},{4,6},{5,7},{6,4},{7,5},{8,10},{9,11},{10,... | collective-permute-start | bytes 589832 | tf_op jit(solution)/shard_map/ppermute | solution.py:566
  27.9 14.0 %collective-permute-start.4 = (bf16[256,384]{1,0:T(8,128)(2,1)S(1)}, bf16[256,384]{1,0:T(8,128)(2,1)S(1)}, u32[]{:S(2)}, u32[]{:S(2)}) collective-permute-start(bf16[256,384]{1,0:T(8,128)(2,1)S(1)} %pad_maximum_fusion.4), channel_id=1, source_target_pairs={{0,4},{1,5},{2,6},{3,7},{4,0},{5,1},{6,2},{7,3},{8,12},{9,13},{10,... | collective-permute-start | bytes 589832 | tf_op jit(solution)/shard_map/ppermute | solution.py:566
  29.4 12.5 %collective-permute-start.5 = (bf16[256,384]{1,0:T(8,128)(2,1)S(1)}, bf16[256,384]{1,0:T(8,128)(2,1)S(1)}, u32[]{:S(2)}, u32[]{:S(2)}) collective-permute-start(bf16[256,384]{1,0:T(8,128)(2,1)S(1)} %pad_maximum_fusion.4), channel_id=1, source_target_pairs={{0,6},{1,7},{2,4},{3,5},{4,2},{5,3},{6,0},{7,1},{8,14},{9,15},{10,... | collective-permute-start | bytes 589832 | tf_op jit(solution)/shard_map/ppermute | solution.py:566
  50.7 4.7 %collective-permute-start.10 = (f32[40,128]{1,0:T(8,128)S(1)}, f32[40,128]{1,0:T(8,128)S(1)}, u32[]{:S(2)}, u32[]{:S(2)}) collective-permute-start(f32[40,128]{1,0:T(8,128)S(1)} %add.119), channel_id=1, source_target_pairs={{0,6},{1,7},{2,4},{3,5},{4,2},{5,3},{6,0},{7,1},{8,14},{9,15},{10,... | collective-permute-start | bytes 61448 | tf_op jit(solution)/shard_map/ppermute | solution.py:566
  57.7 7.1 %collective-permute-start.11 = (f32[40,128]{1,0:T(8,128)S(1)}, f32[40,128]{1,0:T(8,128)S(1)}, u32[]{:S(2)}, u32[]{:S(2)}) collective-permute-start(f32[40,128]{1,0:T(8,128)S(1)} %add_add_fusion.1), channel_id=1, source_target_pairs={{0,8},{1,9},{2,10},{3,11},{4,12},{5,13},{6,14},{7,15},{8,0},{9,1},... | collective-permute-start | bytes 61448 | tf_op jit(solution)/shard_map/ppermute | solution.py:566
  58.5 6.4 %collective-permute-start.12 = (f32[40,128]{1,0:T(8,128)S(1)}, f32[40,128]{1,0:T(8,128)S(1)}, u32[]{:S(2)}, u32[]{:S(2)}) collective-permute-start(f32[40,128]{1,0:T(8,128)S(1)} %add_add_fusion.1), channel_id=1, source_target_pairs={{0,16},{1,17},{2,18},{3,19},{4,20},{5,21},{6,22},{7,23},{8,24},{9,... | collective-permute-start | bytes 61448 | tf_op jit(solution)/shard_map/ppermute | solution.py:566
  61.9 5.6 %collective-permute-start.13 = (f32[40,128]{1,0:T(8,128)S(1)}, f32[40,128]{1,0:T(8,128)S(1)}, u32[]{:S(2)}, u32[]{:S(2)}) collective-permute-start(f32[40,128]{1,0:T(8,128)S(1)} %add_add_fusion.1), channel_id=1, source_target_pairs={{0,24},{1,25},{2,26},{3,27},{4,28},{5,29},{6,30},{7,31},{8,16},{9,... | collective-permute-start | bytes 61448 | tf_op jit(solution)/shard_map/ppermute | solution.py:566
  73.5 9.8 %collective-permute-start.14 = (bf16[768,384]{1,0:T(8,128)(2,1)}, bf16[768,384]{1,0:T(8,128)(2,1)S(1)}, u32[]{:S(2)}, u32[]{:S(2)}) collective-permute-start(bf16[768,384]{1,0:T(8,128)(2,1)} %get-tuple-element.111), channel_id=1, source_target_pairs={{0,1},{1,0},{2,3},{3,2},{4,5},{5,4},{6,7},{7,6},{8,9},{9,8},{10,11... | collective-permute-start | bytes 1769480 | tf_op jit(solution)/shard_map/ppermute | solution.py:566
  73.5 9.7 %collective-permute-start.16 = (bf16[192,384]{1,0:T(8,128)(2,1)}, bf16[192,384]{1,0:T(8,128)(2,1)S(1)}, u32[]{:S(2)}, u32[]{:S(2)}) collective-permute-start(bf16[192,384]{1,0:T(8,128)(2,1)} %get-tuple-element.115), channel_id=1, source_target_pairs={{0,1},{1,0},{2,3},{3,2},{4,5},{5,4},{6,7},{7,6},{8,9},{9,8},{10,11... | collective-permute-start | bytes 442376 | tf_op jit(solution)/shard_map/ppermute | solution.py:566
  85.9 14.9 %collective-permute-start.17 = (bf16[432,384]{1,0:T(8,128)(2,1)S(1)}, bf16[432,384]{1,0:T(8,128)(2,1)S(1)}, u32[]{:S(2)}, u32[]{:S(2)}) collective-permute-start(bf16[432,384]{1,0:T(8,128)(2,1)S(1)} %get-tuple-element.164), channel_id=1, source_target_pairs={{0,2},{1,3},{2,0},{3,1},{4,6},{5,7},{6,4},{7,5},{8,10},{9,11},{10,... | collective-permute-start | bytes 995336 | tf_op jit(solution)/shard_map/ppermute | solution.py:566
  87.5 16.7 %collective-permute-start.18 = (bf16[432,384]{1,0:T(8,128)(2,1)S(1)}, bf16[432,384]{1,0:T(8,128)(2,1)S(1)}, u32[]{:S(2)}, u32[]{:S(2)}) collective-permute-start(bf16[432,384]{1,0:T(8,128)(2,1)S(1)} %get-tuple-element.163), channel_id=1, source_target_pairs={{0,4},{1,5},{2,6},{3,7},{4,0},{5,1},{6,2},{7,3},{8,12},{9,13},{10,... | collective-permute-start | bytes 995336 | tf_op jit(solution)/shard_map/ppermute | solution.py:566
  88.0 16.2 %collective-permute-start.19 = (bf16[432,384]{1,0:T(8,128)(2,1)S(1)}, bf16[432,384]{1,0:T(8,128)(2,1)S(1)}, u32[]{:S(2)}, u32[]{:S(2)}) collective-permute-start(bf16[432,384]{1,0:T(8,128)(2,1)S(1)} %get-tuple-element.162), channel_id=1, source_target_pairs={{0,6},{1,7},{2,4},{3,5},{4,2},{5,3},{6,0},{7,1},{8,14},{9,15},{10,... | collective-permute-start | bytes 995336 | tf_op jit(solution)/shard_map/ppermute | solution.py:566
  104.4 9.5 %collective-permute-start.20 = (bf16[144,384]{1,0:T(8,128)(2,1)S(1)}, bf16[144,384]{1,0:T(8,128)(2,1)S(1)}, u32[]{:S(2)}, u32[]{:S(2)}) collective-permute-start(bf16[144,384]{1,0:T(8,128)(2,1)S(1)} %get-tuple-element.174), channel_id=1, source_target_pairs={{0,8},{1,9},{2,10},{3,11},{4,12},{5,13},{6,14},{7,15},{8,0},{9,1},... | collective-permute-start | bytes 331784 | tf_op jit(solution)/shard_map/ppermute | solution.py:566
  104.5 10.9 %collective-permute-start.21 = (bf16[144,384]{1,0:T(8,128)(2,1)S(1)}, bf16[144,384]{1,0:T(8,128)(2,1)S(1)}, u32[]{:S(2)}, u32[]{:S(2)}) collective-permute-start(bf16[144,384]{1,0:T(8,128)(2,1)S(1)} %get-tuple-element.173), channel_id=1, source_target_pairs={{0,16},{1,17},{2,18},{3,19},{4,20},{5,21},{6,22},{7,23},{8,24},{9,... | collective-permute-start | bytes 331784 | tf_op jit(solution)/shard_map/ppermute | solution.py:566
  106.0 9.4 %collective-permute-start.22 = (bf16[144,384]{1,0:T(8,128)(2,1)S(1)}, bf16[144,384]{1,0:T(8,128)(2,1)S(1)}, u32[]{:S(2)}, u32[]{:S(2)}) collective-permute-start(bf16[144,384]{1,0:T(8,128)(2,1)S(1)} %concatenate.55), channel_id=1, source_target_pairs={{0,24},{1,25},{2,26},{3,27},{4,28},{5,29},{6,30},{7,31},{8,16},{9,... | collective-permute-start | bytes 331784 | tf_op jit(solution)/shard_map/ppermute | solution.py:566
  115.4 7.7 %collective-permute-start.23 = (bf16[768,384]{1,0:T(8,128)(2,1)}, bf16[768,384]{1,0:T(8,128)(2,1)S(1)}, u32[]{:S(2)}, u32[]{:S(2)}) collective-permute-start(bf16[768,384]{1,0:T(8,128)(2,1)} %get-tuple-element.130), channel_id=1, source_target_pairs={{0,1},{1,0},{2,3},{3,2},{4,5},{5,4},{6,7},{7,6},{8,9},{9,8},{10,11... | collective-permute-start | bytes 1769480 | tf_op jit(solution)/shard_map/ppermute | solution.py:566
  115.5 7.2 %collective-permute-start.27 = (bf16[96,384]{1,0:T(8,128)(2,1)S(1)}, bf16[96,384]{1,0:T(8,128)(2,1)S(1)}, u32[]{:S(2)}, u32[]{:S(2)}) collective-permute-start(bf16[96,384]{1,0:T(8,128)(2,1)S(1)} %slice.84), channel_id=1, source_target_pairs={{0,16},{1,17},{2,18},{3,19},{4,20},{5,21},{6,22},{7,23},{8,24},{9,... | collective-permute-start | bytes 221192 | tf_op jit(solution)/shard_map/ppermute | solution.py:566
  122.7 10.0 %collective-permute-start.28 = (bf16[192,384]{1,0:T(8,128)(2,1)S(1)}, bf16[192,384]{1,0:T(8,128)(2,1)S(1)}, u32[]{:S(2)}, u32[]{:S(2)}) collective-permute-start(bf16[192,384]{1,0:T(8,128)(2,1)S(1)} %pad_maximum_fusion.8), channel_id=1, source_target_pairs={{0,8},{1,9},{2,10},{3,11},{4,12},{5,13},{6,14},{7,15},{8,0},{9,1},... | collective-permute-start | bytes 442376 | tf_op jit(solution)/shard_map/ppermute | solution.py:566
  123.3 9.4 %collective-permute-start.24 = (bf16[192,384]{1,0:T(8,128)(2,1)S(1)}, bf16[192,384]{1,0:T(8,128)(2,1)S(1)}, u32[]{:S(2)}, u32[]{:S(2)}) collective-permute-start(bf16[192,384]{1,0:T(8,128)(2,1)S(1)} %get-tuple-element.167), channel_id=1, source_target_pairs={{0,2},{1,3},{2,0},{3,1},{4,6},{5,7},{6,4},{7,5},{8,10},{9,11},{10,... | collective-permute-start | bytes 442376 | tf_op jit(solution)/shard_map/ppermute | solution.py:566
  123.9 8.8 %collective-permute-start.25 = (bf16[192,384]{1,0:T(8,128)(2,1)S(1)}, bf16[192,384]{1,0:T(8,128)(2,1)S(1)}, u32[]{:S(2)}, u32[]{:S(2)}) collective-permute-start(bf16[192,384]{1,0:T(8,128)(2,1)S(1)} %get-tuple-element.166), channel_id=1, source_target_pairs={{0,4},{1,5},{2,6},{3,7},{4,0},{5,1},{6,2},{7,3},{8,12},{9,13},{10,... | collective-permute-start | bytes 442376 | tf_op jit(solution)/shard_map/ppermute | solution.py:566
  125.3 7.4 %collective-permute-start.26 = (bf16[192,384]{1,0:T(8,128)(2,1)S(1)}, bf16[192,384]{1,0:T(8,128)(2,1)S(1)}, u32[]{:S(2)}, u32[]{:S(2)}) collective-permute-start(bf16[192,384]{1,0:T(8,128)(2,1)S(1)} %get-tuple-element.165), channel_id=1, source_target_pairs={{0,6},{1,7},{2,4},{3,5},{4,2},{5,3},{6,0},{7,1},{8,14},{9,15},{10,... | collective-permute-start | bytes 442376 | tf_op jit(solution)/shard_map/ppermute | solution.py:566
  134.8 7.6 %collective-permute-start.31 = (bf16[432,384]{1,0:T(8,128)(2,1)S(1)}, bf16[432,384]{1,0:T(8,128)(2,1)S(1)}, u32[]{:S(2)}, u32[]{:S(2)}) collective-permute-start(bf16[432,384]{1,0:T(8,128)(2,1)S(1)} %pad_maximum_fusion.3), channel_id=1, source_target_pairs={{0,2},{1,3},{2,0},{3,1},{4,6},{5,7},{6,4},{7,5},{8,10},{9,11},{10,... | collective-permute-start | bytes 995336 | tf_op jit(solution)/shard_map/ppermute | solution.py:566
  135.4 7.1 %collective-permute-start.32 = (bf16[432,384]{1,0:T(8,128)(2,1)S(1)}, bf16[432,384]{1,0:T(8,128)(2,1)S(1)}, u32[]{:S(2)}, u32[]{:S(2)}) collective-permute-start(bf16[432,384]{1,0:T(8,128)(2,1)S(1)} %pad_maximum_fusion.3), channel_id=1, source_target_pairs={{0,4},{1,5},{2,6},{3,7},{4,0},{5,1},{6,2},{7,3},{8,12},{9,13},{10,... | collective-permute-start | bytes 995336 | tf_op jit(solution)/shard_map/ppermute | solution.py:566
  137.4 4.9 %collective-permute-start.30 = (bf16[48,384]{1,0:T(8,128)(2,1)S(1)}, bf16[48,384]{1,0:T(8,128)(2,1)S(1)}, u32[]{:S(2)}, u32[]{:S(2)}) collective-permute-start(bf16[48,384]{1,0:T(8,128)(2,1)S(1)} %slice.88), channel_id=1, source_target_pairs={{0,16},{1,17},{2,18},{3,19},{4,20},{5,21},{6,22},{7,23},{8,24},{9,... | collective-permute-start | bytes 110600 | tf_op jit(solution)/shard_map/ppermute | solution.py:566
  142.5 4.9 %collective-permute-start.34 = (bf16[48,384]{1,0:T(8,128)(2,1)S(1)}, bf16[48,384]{1,0:T(8,128)(2,1)S(1)}, u32[]{:S(2)}, u32[]{:S(2)}) collective-permute-start(bf16[48,384]{1,0:T(8,128)(2,1)S(1)} %add_convert_fusion.6), channel_id=1, source_target_pairs={{0,16},{1,17},{2,18},{3,19},{4,20},{5,21},{6,22},{7,23},{8,24},{9,... | collective-permute-start | bytes 110600 | tf_op jit(solution)/shard_map/ppermute | solution.py:566
  144.6 8.0 %collective-permute-start.33 = (bf16[432,384]{1,0:T(8,128)(2,1)S(1)}, bf16[432,384]{1,0:T(8,128)(2,1)S(1)}, u32[]{:S(2)}, u32[]{:S(2)}) collective-permute-start(bf16[432,384]{1,0:T(8,128)(2,1)S(1)} %pad_maximum_fusion.3), channel_id=1, source_target_pairs={{0,6},{1,7},{2,4},{3,5},{4,2},{5,3},{6,0},{7,1},{8,14},{9,15},{10,... | collective-permute-start | bytes 995336 | tf_op jit(solution)/shard_map/ppermute | solution.py:566
  152.9 8.4 %collective-permute-start.36 = (bf16[192,384]{1,0:T(8,128)(2,1)S(1)}, bf16[192,384]{1,0:T(8,128)(2,1)S(1)}, u32[]{:S(2)}, u32[]{:S(2)}) collective-permute-start(bf16[192,384]{1,0:T(8,128)(2,1)S(1)} %pad_maximum_fusion.9), channel_id=1, source_target_pairs={{0,2},{1,3},{2,0},{3,1},{4,6},{5,7},{6,4},{7,5},{8,10},{9,11},{10,... | collective-permute-start | bytes 442376 | tf_op jit(solution)/shard_map/ppermute | solution.py:566
  153.8 9.1 %collective-permute-start.37 = (bf16[192,384]{1,0:T(8,128)(2,1)S(1)}, bf16[192,384]{1,0:T(8,128)(2,1)S(1)}, u32[]{:S(2)}, u32[]{:S(2)}) collective-permute-start(bf16[192,384]{1,0:T(8,128)(2,1)S(1)} %pad_maximum_fusion.9), channel_id=1, source_target_pairs={{0,4},{1,5},{2,6},{3,7},{4,0},{5,1},{6,2},{7,3},{8,12},{9,13},{10,... | collective-permute-start | bytes 442376 | tf_op jit(solution)/shard_map/ppermute | solution.py:566
  154.9 7.9 %collective-permute-start.38 = (bf16[192,384]{1,0:T(8,128)(2,1)S(1)}, bf16[192,384]{1,0:T(8,128)(2,1)S(1)}, u32[]{:S(2)}, u32[]{:S(2)}) collective-permute-start(bf16[192,384]{1,0:T(8,128)(2,1)S(1)} %pad_maximum_fusion.9), channel_id=1, source_target_pairs={{0,6},{1,7},{2,4},{3,5},{4,2},{5,3},{6,0},{7,1},{8,14},{9,15},{10,... | collective-permute-start | bytes 442376 | tf_op jit(solution)/shard_map/ppermute | solution.py:566
  (20 other events, 108.3 us)

commit v4 on v3

--- a/solution.py
+++ b/solution.py
@@ -638,7 +638,8 @@
     if tuned:
         sums = total_of(sums, [swap(sums, 1)])
         sums = total_of(sums, plane([sums] * 4))
-        sums = total_of(sums, column([sums] * 4))
+        sums = total_of(sums, [swap(sums, 8)])
+        sums = total_of(sums, [swap(sums, 16)])
     else:
         sums = lax.psum(sums, AXES)
     send_d, keep_d, send_p, keep_p, du, dy, loss, temp = simple(
@@ -686,21 +687,23 @@
         got, dqkv = lax.optimization_barrier((got, dqkv))
         m = added(m[0], got)
         m, dqkv = lax.optimization_barrier((m, dqkv))
-        parts = [jnp.concatenate([m[96 * k : 96 * k + 96], m[384:]], 0) for k in (0, 2, 1, 3)]
-        got = column(parts)
+        got = swap(m[192:], 8)
         send_a, keep_a = att_grads(mine, h1, dqkv, o, dxb)
         got, send_a, keep_a = lax.optimization_barrier((got, send_a, keep_a))
-        q = added(parts[0], got)
-        far = swap(q[:96], 16)
+        m = added(joined(m[:192], [m[384:]]), [got])
+        got = swap(m[96:], 16)
         a = added(keep_a, [swap(send_a, 1)]).reshape(4, 192, D)
+        got, a = lax.optimization_barrier((got, a))
+        m = added(joined(m[:96], [m[192:]]), [got])
+        far = swap(m[:96], 16)
         got_a = plane(a)
-        m = joined(q[:96], [far])
-        near = swap(m, 8)
         dqkv, a, m = lax.optimization_barrier((dqkv, a, m))
         grad_tokens = tok_back(text_tokens, dqkv, dx, txt_ln1, txt_qkv)
-        got_a, near, grad_tokens = lax.optimization_barrier((got_a, near, grad_tokens))
+        far, grad_tokens = lax.optimization_barrier((far, grad_tokens))
+        got_a, grad_tokens = lax.optimization_barrier((got_a, grad_tokens))
+        near = joined(m[:96], [far])
+        m = joined(near, [swap(near, 8), m[96:]])
         a = added(a[0], got_a)
-        m = joined(m, [near, q[96:]])
         got_m = plane([m] * 4)
         a = added(a[:96], [swap(a[96:], 8)])
         a = added(a[:48], [swap(a[48:], 16)])

time: 169 us -> 171 us (1.012)
  waiting for transfers between devices: 32.2 us -> 36.2 us
  starting transfers between devices: 46.8 us -> 44 us
    ppermute x41 -> x39, waiting for transfers between devices: 32.2 us -> 36.2 us  [swap(): return lax.ppermute(v, AXES, [(i, i ^ mask) for i in range(32)])]
    ppermute x41 -> x39, starting transfers between devices: 46.8 us -> 44 us  [swap(): return lax.ppermute(v, AXES, [(i, i ^ mask) for i in range(32)])]
  transfers between devices with their start and end apart: 41 -> 39, of which waited for: 18 -> 18; matrix products, arithmetic and copies ran while one was open for 1% -> 1% of each run, Pallas kernels for 35% -> 34%
where the time goes in v4:
time: 171 us; the launch traced here: 170 us
  Pallas kernels  81.1 us (47%)
  starting transfers between devices  44 us (26%)
  waiting for transfers between devices  36.2 us (21%)
  local copies, waits for them, and re-layouts  4.23 us (2%)
  other arithmetic  2.74 us (2%)
  between operations  1.85 us (1%)
    ppermute x39, starting transfers between devices, swap(): return lax.ppermute(v, AXES, [(i, i ^ mask) for i in range(32)])  44 us
    ppermute x39, waiting for transfers between devices, swap(): return lax.ppermute(v, AXES, [(i, i ^ mask) for i in range(32)])  36.2 us
    pallas_call x6, Pallas kernels, call(): pl.pallas_call(kernel, in_specs=[SMEM] * smem + [VMEM] * (len(args) - sme...  23.8 us
    pallas_call x1, Pallas kernels, text_mlp(): pl.pallas_call(text_mlp_kernel, grid=(n // TOK_BLOCK,), in_specs=[token_r...  12.2 us
    pallas_call x1, Pallas kernels, image_tower(): pl.pallas_call(image_kernel, grid=(count // IMG_BLOCK,), in_specs=[pl.Blo...  11.4 us
    pallas_call x1, Pallas kernels, att_core(): pl.pallas_call(att_core_kernel, grid=(n // TOK_BLOCK,), in_specs=[token_r...  11.3 us
    pallas_call x1, Pallas kernels, mlp_back(): pl.pallas_call(mlp_back_kernel, grid=(n // TOK_BLOCK,), in_specs=[SMEM, b...  9.01 us
    pallas_call x1, Pallas kernels, text_att(): pl.pallas_call(text_att_kernel, grid=(blocks,), in_specs=[token_rows(D),...  7.6 us
  transfers between devices with their start and end apart: 39, of which 18 were waited for; matrix products, arithmetic and copies ran while one was open for 1% of the time, Pallas kernels for 34%

profile of v4, /device:TPU:0, one launch (start us, length us, event | category | flops | bytes accessed | tf_op | source)
XLA Modules:
  0.0 170.0 jit_solution(7138255657345189217)
XLA Ops:
  0.7 11.4 %image_tower.1 = bf16[64,384]{1,0:T(8,128)(2,1)} custom-call(bf16[50,64,384]{2,1,0:T(8,128)(2,1)} %bitcast.35, f32[384]{0:T(512)} %g1.5, bf16[384,1152]{1,0:T(8,128)(2,1)} %wqkv.5, bf16[384,384]{1,0:T(8,128)(2,1)} %wout.3, f32[384]{0:T(512)} %g2.4, bf16[384,1536]{1,0:T(8,128)(2,1)} %wup.4, bf16[1536,384]{1,0:T(8,128)(2,1)} %wdown.3, bf16[384,384]{1,0:T(8,128)(2,1)} %wproj.3), custom_call_target="tpu_custom_call" | custom-call | flops 12000000000 | bytes 36000000 | tf_op jit(solution)/shard_map/image_tower/pallas_call | solution.py:129
  12.1 3.1 %collective-permute-start = (bf16[64,384]{1,0:T(8,128)(2,1)}, bf16[64,384]{1,0:T(8,128)(2,1)S(1)}, u32[]{:S(2)}, u32[]{:S(2)}) collective-permute-start(bf16[64,384]{1,0:T(8,128)(2,1)} %image_tower.1), channel_id=1, source_target_pairs={{0,8},{1,9},{2,10},{3,11},{4,12},{5,13},{6,14},{7,15},{8,0},{9,1},... | collective-permute-start | bytes 147464 | tf_op jit(solution)/shard_map/ppermute | solution.py:566
  15.1 2.6 %collective-permute-start.1 = (bf16[64,384]{1,0:T(8,128)(2,1)}, bf16[64,384]{1,0:T(8,128)(2,1)S(1)}, u32[]{:S(2)}, u32[]{:S(2)}) collective-permute-start(bf16[64,384]{1,0:T(8,128)(2,1)} %image_tower.1), channel_id=1, source_target_pairs={{0,16},{1,17},{2,18},{3,19},{4,20},{5,21},{6,22},{7,23},{8,24},{9,... | collective-permute-start | bytes 147464 | tf_op jit(solution)/shard_map/ppermute | solution.py:566
  18.5 7.6 %text_att.1 = (bf16[1024,384]{1,0:T(8,128)(2,1)}, bf16[1024,1152]{1,0:T(8,128)(2,1)}, bf16[8,3,256,128]{3,2,1,0:T(8,128)(2,1)}, bf16[1024,384]{1,0:T(8,128)(2,1)}) custom-call(bf16[1024,384]{1,0:T(8,128)(2,1)} %tok_ref.5, s32[4,1,256]{2,1,0:T(1,128)} %reshape.67.lab_ref, f32[384]{0:T(512)} %g1.7, bf16[384,1152]{1,0:T(8,128)(2,1)} %wqkv.7), custom_call_target="tpu_custom_call" | custom-call | flops 8999999488 | bytes 27000000 | tf_op jit(solution)/shard_map/text_att/pallas_call | solution.py:238
  29.7 12.2 %text_mlp.1 = (bf16[1024,384]{1,0:T(8,128)(2,1)}, f32[1024,384]{1,0:T(8,128)}, bf16[1024,1536]{1,0:T(8,128)(2,1)}, f32[64,1536]{1,0:T(8,128)}, bf16[64,384]{1,0:...) custom-call(bf16[1024,384]{1,0:T(8,128)(2,1)} %tok_ref.5, ...), custom_call_target="tpu_custom_call" | custom-call | flops 11000000512 | bytes 33000000 | tf_op jit(solution)/shard_map/text_mlp/pallas_call | solution.py:259
  45.7 2.9 %cosine.1 = (f32[64,2048]{1,0:T(8,128)}, f32[40,128]{1,0:T(8,128)}) custom-call(f32[1]{0:T(128)S(6)} %copy.44.scale_ref, s32[1]{0:T(128)} %bitcast.mine_ref, bf16[64,384]{1,0:T(8,128)(2,1)} %get-tuple-element.92.emb, bf16[2048,384]{1,0:T(8,128)(2,1)} %copy-done.6, s32[64,1]{1,0:T(8,128)} %copy.29.pair), custom_call_target="tpu_custom_call" | custom-call | flops 3000000000 | bytes 9000000 | tf_op jit(solution)/shard_map/cosine/pallas_call | solution.py:487
  50.7 2.7 %collective-permute-start.10 = (f32[40,128]{1,0:T(8,128)S(1)}, f32[40,128]{1,0:T(8,128)S(1)}, u32[]{:S(2)}, u32[]{:S(2)}) collective-permute-start(f32[40,128]{1,0:T(8,128)S(1)} %add.113), channel_id=1, source_target_pairs={{0,6},{1,7},{2,4},{3,5},{4,2},{5,3},{6,0},{7,1},{8,14},{9,15},{10,... | collective-permute-start | bytes 61448 | tf_op jit(solution)/shard_map/ppermute | solution.py:566
  55.4 1.8 %collective-permute-done.8 = f32[40,128]{1,0:T(8,128)S(1)} collective-permute-done((f32[40,128]{1,0:T(8,128)S(1)}, f32[40,128]{1,0:T(8,128)S(1)}, u32[]{:S(2)}, u32[]{:S(2)}) %collective-permute-start.8) | collective-permute-done | bytes 20512 | tf_op jit(solution)/shard_map/ppermute | solution.py:566
  58.4 3.1 %collective-permute-done.11 = f32[40,128]{1,0:T(8,128)S(1)} collective-permute-done((f32[40,128]{1,0:T(8,128)S(1)}, f32[40,128]{1,0:T(8,128)S(1)}, u32[]{:S(2)}, u32[]{:S(2)}) %collective-permute-start.11) | collective-permute-done | bytes 20512 | tf_op jit(solution)/shard_map/ppermute | solution.py:566
  61.5 2.1 %collective-permute-start.12 = (f32[40,128]{1,0:T(8,128)S(1)}, f32[40,128]{1,0:T(8,128)S(1)}, u32[]{:S(2)}, u32[]{:S(2)}) collective-permute-start(f32[40,128]{1,0:T(8,128)S(1)} %add.117), channel_id=1, source_target_pairs={{0,16},{1,17},{2,18},{3,19},{4,20},{5,21},{6,22},{7,23},{8,24},{9,... | collective-permute-start | bytes 61448 | tf_op jit(solution)/shard_map/ppermute | solution.py:566
  63.7 2.7 %rows.1.dt_row = f32[64,384]{1,0:T(8,128)} custom-call(f32[1]{0:T(128)S(6)} %copy.44.scale_ref, f32[64,2048]{1,0:T(8,128)} %get-tuple-element.98.g_ref, bf16[2048,384]{1,0:T(8,128)(2,1)} %copy-done.6, s32[64,1]{1,0:T(8,128)} %copy.29.pair), custom_call_target="tpu_custom_call" | custom-call | flops 2000000000 | bytes 6000000 | tf_op jit(solution)/shard_map/rows/pallas_call | solution.py:487
  66.9 5.3 %head_back.1 = (bf16[768,384]{1,0:T(8,128)(2,1)}, bf16[768,384]{1,0:T(8,128)(2,1)}, bf16[192,384]{1,0:T(8,128)(2,1)}, bf16[192,384]{1,0:T(8,128)(2,1)}, bf16[4,4...) custom-call(f32[1]{0:T(128)S(6)} %copy.44.scale_ref, s32[1]{0:T(128)} %bitcast.mine_ref, ...), custom_call_target="tpu_custom_call" | custom-call | flops 5000000000 | bytes 15000000 | tf_op jit(solution)/shard_map/head_back/pallas_call | solution.py:487
  72.8 9.0 %mlp_back.1 = (f32[1024,384]{1,0:T(8,128)}, bf16[1024,384]{1,0:T(8,128)(2,1)}, bf16[768,384]{1,0:T(8,128)(2,1)}, bf16[768,384]{1,0:T(8,128)(2,1)}) custom-call(s32[1]{0:T(128)} %bitcast.mine_ref, s32[4,1,256]{2,1,0:T(1,128)} %reshape.67.lab_ref, bf16[1024,384]{1,0:T(8,128)(2,1)} %get-tuple-element.105.h2_ref, bf16[1024,1536]{1,0:T(8,128)(2,1)} %get-tuple-element.106.gp_ref, ...), custom_call_target="tpu_custom_call" | custom-call | flops 8999999488 | bytes 27000000 | tf_op jit(solution)/shard_map/mlp_back/pallas_call | solution.py:510
  82.2 1.9 %collective-permute-done.14 = bf16[768,384]{1,0:T(8,128)(2,1)S(1)} collective-permute-done((bf16[768,384]{1,0:T(8,128)(2,1)}, bf16[768,384]{1,0:T(8,128)(2,1)S(1)}, u32[]{:S(2)}, u32[]{:S(2)}) %collective-permute-start.14) | collective-permute-done | bytes 589856 | tf_op jit(solution)/shard_map/ppermute | solution.py:566
  88.2 11.3 %att_core.1.dqkv_ref = bf16[1024,1152]{1,0:T(8,128)(2,1)} custom-call(bf16[1024,1152]{1,0:T(8,128)(2,1)} %get-tuple-element.118.qkv_ref, bf16[8,3,256,128]{3,2,1,0:T(8,128)(2,1)} %get-tuple-element.119.p_ref, bf16[1024,384]{1,0:T(8,128)(2,1)} %get-tuple-element.120.dxb_ref, bf16[384,384]{1,0:T(8,128)(2,1)} %wout.5), custom_call_target="tpu_custom_call" | custom-call | flops 10000000000 | bytes 30000000 | tf_op jit(solution)/shard_map/att_core/pallas_call | solution.py:527
  99.5 3.4 %collective-permute-done.17 = bf16[432,384]{1,0:T(8,128)(2,1)S(1)} collective-permute-done((bf16[432,384]{1,0:T(8,128)(2,1)S(1)}, bf16[432,384]{1,0:T(8,128)(2,1)S(1)}, u32[]{:S(2)}, u32[]{:S(2)}) %collective-permute-start.17) | collective-permute-done | bytes 331808 | tf_op jit(solution)/shard_map/ppermute | solution.py:566
  103.1 2.1 %collective-permute-start.19 = (bf16[240,384]{1,0:T(8,128)(2,1)S(1)}, bf16[240,384]{1,0:T(8,128)(2,1)S(1)}, u32[]{:S(2)}, u32[]{:S(2)}) collective-permute-start(bf16[240,384]{1,0:T(8,128)(2,1)S(1)} %slice.69), channel_id=1, source_target_pairs={{0,8},{1,9},{2,10},{3,11},{4,12},{5,13},{6,14},{7,15},{8,0},{9,1},... | collective-permute-start | bytes 552968 | tf_op jit(solution)/shard_map/ppermute | solution.py:566
  105.2 5.0 %att_grads.1 = (bf16[768,384]{1,0:T(8,128)(2,1)}, bf16[768,384]{1,0:T(8,128)(2,1)}) custom-call(s32[1]{0:T(128)} %bitcast.mine_ref, bf16[1024,384]{1,0:T(8,128)(2,1)} %get-tuple-element.126.h1_ref, bf16[1024,1152]{1,0:T(8,128)(2,1)} %att_core.1.dqkv_ref, bf16[1024,384]{1,0:T(8,128)(2,1)} %get-tuple-element.90.o_ref, bf16[1024,384]{1,0:T(8,128)(2,1)} %get-tuple-element.120.dxb_ref), custom_call_target="tpu_custom_call" | custom-call | flops 4000000000 | bytes 12000000 | tf_op jit(solution)/shard_map/att_grads/pallas_call | solution.py:487
  110.4 2.1 %collective-permute-start.20 = (bf16[144,384]{1,0:T(8,128)(2,1)S(1)}, bf16[144,384]{1,0:T(8,128)(2,1)S(1)}, u32[]{:S(2)}, u32[]{:S(2)}) collective-permute-start(bf16[144,384]{1,0:T(8,128)(2,1)S(1)} %slice.84), channel_id=1, source_target_pairs={{0,16},{1,17},{2,18},{3,19},{4,20},{5,21},{6,22},{7,23},{8,24},{9,... | collective-permute-start | bytes 331784 | tf_op jit(solution)/shard_map/ppermute | solution.py:566
  112.6 6.5 %collective-permute-done.20 = bf16[144,384]{1,0:T(8,128)(2,1)S(1)} collective-permute-done((bf16[144,384]{1,0:T(8,128)(2,1)S(1)}, bf16[144,384]{1,0:T(8,128)(2,1)S(1)}, u32[]{:S(2)}, u32[]{:S(2)}) %collective-permute-start.20) | collective-permute-done | bytes 110624 | tf_op jit(solution)/shard_map/ppermute | solution.py:566
  122.9 5.8 %tok_back.1 = f32[1024,384]{1,0:T(8,128)} custom-call(bf16[1024,384]{1,0:T(8,128)(2,1)} %tok_ref.5, bf16[1024,1152]{1,0:T(8,128)(2,1)} %att_core.1.dqkv_ref, f32[1024,384]{1,0:T(8,128)} %get-tuple-element.136.dx_ref, f32[384]{0:T(512)} %g1.7, bf16[384,1152]{1,0:T(8,128)(2,1)} %wqkv.7), custom_call_target="tpu_custom_call" | custom-call | flops 4000000000 | bytes 12000000 | tf_op jit(solution)/shard_map/tok_back/pallas_call | solution.py:551
  128.8 2.6 %collective-permute-start.28 = (bf16[192,384]{1,0:T(8,128)(2,1)S(1)}, bf16[192,384]{1,0:T(8,128)(2,1)S(1)}, u32[]{:S(2)}, u32[]{:S(2)}) collective-permute-start(bf16[192,384]{1,0:T(8,128)(2,1)S(1)} %pad_maximum_fusion.5), channel_id=1, source_target_pairs={{0,8},{1,9},{2,10},{3,11},{4,12},{5,13},{6,14},{7,15},{8,0},{9,1},... | collective-permute-start | bytes 442376 | tf_op jit(solution)/shard_map/ppermute | solution.py:566
  131.6 3.2 %collective-permute-done.28 = bf16[192,384]{1,0:T(8,128)(2,1)S(1)} collective-permute-done((bf16[192,384]{1,0:T(8,128)(2,1)S(1)}, bf16[192,384]{1,0:T(8,128)(2,1)S(1)}, u32[]{:S(2)}, u32[]{:S(2)}) %collective-permute-start.28) | collective-permute-done | bytes 147488 | tf_op jit(solution)/shard_map/ppermute | solution.py:566
  137.0 2.0 %collective-permute-start.27 = (bf16[48,384]{1,0:T(8,128)(2,1)S(1)}, bf16[48,384]{1,0:T(8,128)(2,1)S(1)}, u32[]{:S(2)}, u32[]{:S(2)}) collective-permute-start(bf16[48,384]{1,0:T(8,128)(2,1)S(1)} %slice.91), channel_id=1, source_target_pairs={{0,16},{1,17},{2,18},{3,19},{4,20},{5,21},{6,22},{7,23},{8,24},{9,... | collective-permute-start | bytes 110600 | tf_op jit(solution)/shard_map/ppermute | solution.py:566
  139.0 3.0 %collective-permute-done.27 = bf16[48,384]{1,0:T(8,128)(2,1)S(1)} collective-permute-done((bf16[48,384]{1,0:T(8,128)(2,1)S(1)}, bf16[48,384]{1,0:T(8,128)(2,1)S(1)}, u32[]{:S(2)}, u32[]{:S(2)}) %collective-permute-start.27) | collective-permute-done | bytes 36896 | tf_op jit(solution)/shard_map/ppermute | solution.py:566
  142.6 2.4 %collective-permute-start.32 = (bf16[48,384]{1,0:T(8,128)(2,1)S(1)}, bf16[48,384]{1,0:T(8,128)(2,1)S(1)}, u32[]{:S(2)}, u32[]{:S(2)}) collective-permute-start(bf16[48,384]{1,0:T(8,128)(2,1)S(1)} %add_convert_fusion.7), channel_id=1, source_target_pairs={{0,16},{1,17},{2,18},{3,19},{4,20},{5,21},{6,22},{7,23},{8,24},{9,... | collective-permute-start | bytes 110600 | tf_op jit(solution)/shard_map/ppermute | solution.py:566
  147.5 1.8 %collective-permute-start.33 = (bf16[96,384]{1,0:T(8,128)(2,1)S(1)}, bf16[96,384]{1,0:T(8,128)(2,1)S(1)}, u32[]{:S(2)}, u32[]{:S(2)}) collective-permute-start(bf16[96,384]{1,0:T(8,128)(2,1)S(1)} %pad_maximum_fusion.7), channel_id=1, source_target_pairs={{0,8},{1,9},{2,10},{3,11},{4,12},{5,13},{6,14},{7,15},{8,0},{9,1},... | collective-permute-start | bytes 221192 | tf_op jit(solution)/shard_map/ppermute | solution.py:566
  149.3 2.6 %collective-permute-done.33 = bf16[96,384]{1,0:T(8,128)(2,1)S(1)} collective-permute-done((bf16[96,384]{1,0:T(8,128)(2,1)S(1)}, bf16[96,384]{1,0:T(8,128)(2,1)S(1)}, u32[]{:S(2)}, u32[]{:S(2)}) %collective-permute-start.33) | collective-permute-done | bytes 73760 | tf_op jit(solution)/shard_map/ppermute | solution.py:566
  156.9 4.8 %spread_mlp.1 = (f32[1536,384]{1,0:T(8,128)}, f32[384,1536]{1,0:T(8,128)}, f32[384,384]{1,0:T(8,128)}, f32[384]{0:T(512)}) custom-call(s32[1]{0:T(128)} %bitcast.mine_ref, bf16[1728,384]{1,0:T(8,128)(2,1)} %copy-done.8, bf16[1728,384]{1,0:T(8,128)(2,1)} %collective-permute-done.37.other, bf16[384,1536]{1,0:T(8,128)(2,1)} %wup.7, f32[384]{0:T(512)} %g2.7), custom_call_target="tpu_custom_call" | custom-call | flops 4000000000 | bytes 12000000 | tf_op jit(solution)/shard_map/spread_mlp/pallas_call | solution.py:487
  161.7 2.2 %collective-permute-done.35 = bf16[192,384]{1,0:T(8,128)(2,1)S(1)} collective-permute-done((bf16[192,384]{1,0:T(8,128)(2,1)S(1)}, bf16[192,384]{1,0:T(8,128)(2,1)S(1)}, u32[]{:S(2)}, u32[]{:S(2)}) %collective-permute-start.35) | collective-permute-done | bytes 147488 | tf_op jit(solution)/shard_map/ppermute | solution.py:566
  164.1 2.0 %collective-permute-done.38.other = bf16[768,384]{1,0:T(8,128)(2,1)S(1)} collective-permute-done((bf16[768,384]{1,0:T(8,128)(2,1)S(1)}, bf16[768,384]{1,0:T(8,128)(2,1)S(1)}, u32[]{:S(2)}, u32[]{:S(2)}) %collective-permute-start.38) | collective-permute-done | bytes 589856 | tf_op jit(solution)/shard_map/ppermute | solution.py:566
  167.0 3.1 %spread_att.1 = (f32[384,384]{1,0:T(8,128)}, f32[384,1152]{1,0:T(8,128)}, f32[384]{0:T(512)}) custom-call(s32[1]{0:T(128)} %bitcast.mine_ref, bf16[768,384]{1,0:T(8,128)(2,1)} %copy-done.5, bf16[768,384]{1,0:T(8,128)(2,1)} %copy-done.9, bf16[384,1152]{1,0:T(8,128)(2,1)} %wqkv.7, f32[384]{0:T(512)} %g1.7), custom_call_target="tpu_custom_call" | custom-call | flops 4000000000 | bytes 12000000 | tf_op jit(solution)/shard_map/spread_att/pallas_call | solution.py:487
  (134 shorter events, 34.1 us)
Async XLA Ops:
  12.1 14.0 %collective-permute-start = (bf16[64,384]{1,0:T(8,128)(2,1)}, bf16[64,384]{1,0:T(8,128)(2,1)S(1)}, u32[]{:S(2)}, u32[]{:S(2)}) collective-permute-start(bf16[64,384]{1,0:T(8,128)(2,1)} %image_tower.1), channel_id=1, source_target_pairs={{0,8},{1,9},{2,10},{3,11},{4,12},{5,13},{6,14},{7,15},{8,0},{9,1},... | collective-permute-start | bytes 147464 | tf_op jit(solution)/shard_map/ppermute | solution.py:566
  15.1 11.0 %collective-permute-start.1 = (bf16[64,384]{1,0:T(8,128)(2,1)}, bf16[64,384]{1,0:T(8,128)(2,1)S(1)}, u32[]{:S(2)}, u32[]{:S(2)}) collective-permute-start(bf16[64,384]{1,0:T(8,128)(2,1)} %image_tower.1), channel_id=1, source_target_pairs={{0,16},{1,17},{2,18},{3,19},{4,20},{5,21},{6,22},{7,23},{8,24},{9,... | collective-permute-start | bytes 147464 | tf_op jit(solution)/shard_map/ppermute | solution.py:566
  17.7 8.4 %collective-permute-start.2 = (bf16[64,384]{1,0:T(8,128)(2,1)}, bf16[64,384]{1,0:T(8,128)(2,1)S(1)}, u32[]{:S(2)}, u32[]{:S(2)}) collective-permute-start(bf16[64,384]{1,0:T(8,128)(2,1)} %image_tower.1), channel_id=1, source_target_pairs={{0,24},{1,25},{2,26},{3,27},{4,28},{5,29},{6,30},{7,31},{8,16},{9,... | collective-permute-start | bytes 147464 | tf_op jit(solution)/shard_map/ppermute | solution.py:566
  26.2 15.7 %collective-permute-start.3 = (bf16[256,384]{1,0:T(8,128)(2,1)S(1)}, bf16[256,384]{1,0:T(8,128)(2,1)S(1)}, u32[]{:S(2)}, u32[]{:S(2)}) collective-permute-start(bf16[256,384]{1,0:T(8,128)(2,1)S(1)} %pad_maximum_fusion.4), channel_id=1, source_target_pairs={{0,2},{1,3},{2,0},{3,1},{4,6},{5,7},{6,4},{7,5},{8,10},{9,11},{10,... | collective-permute-start | bytes 589832 | tf_op jit(solution)/shard_map/ppermute | solution.py:566
  27.9 14.0 %collective-permute-start.4 = (bf16[256,384]{1,0:T(8,128)(2,1)S(1)}, bf16[256,384]{1,0:T(8,128)(2,1)S(1)}, u32[]{:S(2)}, u32[]{:S(2)}) collective-permute-start(bf16[256,384]{1,0:T(8,128)(2,1)S(1)} %pad_maximum_fusion.4), channel_id=1, source_target_pairs={{0,4},{1,5},{2,6},{3,7},{4,0},{5,1},{6,2},{7,3},{8,12},{9,13},{10,... | collective-permute-start | bytes 589832 | tf_op jit(solution)/shard_map/ppermute | solution.py:566
  29.4 12.5 %collective-permute-start.5 = (bf16[256,384]{1,0:T(8,128)(2,1)S(1)}, bf16[256,384]{1,0:T(8,128)(2,1)S(1)}, u32[]{:S(2)}, u32[]{:S(2)}) collective-permute-start(bf16[256,384]{1,0:T(8,128)(2,1)S(1)} %pad_maximum_fusion.4), channel_id=1, source_target_pairs={{0,6},{1,7},{2,4},{3,5},{4,2},{5,3},{6,0},{7,1},{8,14},{9,15},{10,... | collective-permute-start | bytes 589832 | tf_op jit(solution)/shard_map/ppermute | solution.py:566
  50.7 4.7 %collective-permute-start.10 = (f32[40,128]{1,0:T(8,128)S(1)}, f32[40,128]{1,0:T(8,128)S(1)}, u32[]{:S(2)}, u32[]{:S(2)}) collective-permute-start(f32[40,128]{1,0:T(8,128)S(1)} %add.113), channel_id=1, source_target_pairs={{0,6},{1,7},{2,4},{3,5},{4,2},{5,3},{6,0},{7,1},{8,14},{9,15},{10,... | collective-permute-start | bytes 61448 | tf_op jit(solution)/shard_map/ppermute | solution.py:566
  53.3 3.8 %collective-permute-start.8 = (f32[40,128]{1,0:T(8,128)S(1)}, f32[40,128]{1,0:T(8,128)S(1)}, u32[]{:S(2)}, u32[]{:S(2)}) collective-permute-start(f32[40,128]{1,0:T(8,128)S(1)} %add.113), channel_id=1, source_target_pairs={{0,2},{1,3},{2,0},{3,1},{4,6},{5,7},{6,4},{7,5},{8,10},{9,11},{10,... | collective-permute-start | bytes 61448 | tf_op jit(solution)/shard_map/ppermute | solution.py:566
  57.7 3.8 %collective-permute-start.11 = (f32[40,128]{1,0:T(8,128)S(1)}, f32[40,128]{1,0:T(8,128)S(1)}, u32[]{:S(2)}, u32[]{:S(2)}) collective-permute-start(f32[40,128]{1,0:T(8,128)S(1)} %add_add_fusion), channel_id=1, source_target_pairs={{0,8},{1,9},{2,10},{3,11},{4,12},{5,13},{6,14},{7,15},{8,0},{9,1},... | collective-permute-start | bytes 61448 | tf_op jit(solution)/shard_map/ppermute | solution.py:566
  61.5 4.8 %collective-permute-start.12 = (f32[40,128]{1,0:T(8,128)S(1)}, f32[40,128]{1,0:T(8,128)S(1)}, u32[]{:S(2)}, u32[]{:S(2)}) collective-permute-start(f32[40,128]{1,0:T(8,128)S(1)} %add.117), channel_id=1, source_target_pairs={{0,16},{1,17},{2,18},{3,19},{4,20},{5,21},{6,22},{7,23},{8,24},{9,... | collective-permute-start | bytes 61448 | tf_op jit(solution)/shard_map/ppermute | solution.py:566
  72.2 9.8 %collective-permute-start.13 = (bf16[768,384]{1,0:T(8,128)(2,1)}, bf16[768,384]{1,0:T(8,128)(2,1)S(1)}, u32[]{:S(2)}, u32[]{:S(2)}) collective-permute-start(bf16[768,384]{1,0:T(8,128)(2,1)} %get-tuple-element.112), channel_id=1, source_target_pairs={{0,1},{1,0},{2,3},{3,2},{4,5},{5,4},{6,7},{7,6},{8,9},{9,8},{10,11... | collective-permute-start | bytes 1769480 | tf_op jit(solution)/shard_map/ppermute | solution.py:566
  72.3 9.7 %collective-permute-start.15 = (bf16[192,384]{1,0:T(8,128)(2,1)}, bf16[192,384]{1,0:T(8,128)(2,1)S(1)}, u32[]{:S(2)}, u32[]{:S(2)}) collective-permute-start(bf16[192,384]{1,0:T(8,128)(2,1)} %get-tuple-element.116), channel_id=1, source_target_pairs={{0,1},{1,0},{2,3},{3,2},{4,5},{5,4},{6,7},{7,6},{8,9},{9,8},{10,11... | collective-permute-start | bytes 442376 | tf_op jit(solution)/shard_map/ppermute | solution.py:566
  84.7 14.9 %collective-permute-start.16 = (bf16[432,384]{1,0:T(8,128)(2,1)S(1)}, bf16[432,384]{1,0:T(8,128)(2,1)S(1)}, u32[]{:S(2)}, u32[]{:S(2)}) collective-permute-start(bf16[432,384]{1,0:T(8,128)(2,1)S(1)} %get-tuple-element.166), channel_id=1, source_target_pairs={{0,2},{1,3},{2,0},{3,1},{4,6},{5,7},{6,4},{7,5},{8,10},{9,11},{10,... | collective-permute-start | bytes 995336 | tf_op jit(solution)/shard_map/ppermute | solution.py:566
  86.2 16.7 %collective-permute-start.17 = (bf16[432,384]{1,0:T(8,128)(2,1)S(1)}, bf16[432,384]{1,0:T(8,128)(2,1)S(1)}, u32[]{:S(2)}, u32[]{:S(2)}) collective-permute-start(bf16[432,384]{1,0:T(8,128)(2,1)S(1)} %get-tuple-element.165), channel_id=1, source_target_pairs={{0,4},{1,5},{2,6},{3,7},{4,0},{5,1},{6,2},{7,3},{8,12},{9,13},{10,... | collective-permute-start | bytes 995336 | tf_op jit(solution)/shard_map/ppermute | solution.py:566
  86.7 16.2 %collective-permute-start.18 = (bf16[432,384]{1,0:T(8,128)(2,1)S(1)}, bf16[432,384]{1,0:T(8,128)(2,1)S(1)}, u32[]{:S(2)}, u32[]{:S(2)}) collective-permute-start(bf16[432,384]{1,0:T(8,128)(2,1)S(1)} %get-tuple-element.164), channel_id=1, source_target_pairs={{0,6},{1,7},{2,4},{3,5},{4,2},{5,3},{6,0},{7,1},{8,14},{9,15},{10,... | collective-permute-start | bytes 995336 | tf_op jit(solution)/shard_map/ppermute | solution.py:566
  103.1 7.1 %collective-permute-start.19 = (bf16[240,384]{1,0:T(8,128)(2,1)S(1)}, bf16[240,384]{1,0:T(8,128)(2,1)S(1)}, u32[]{:S(2)}, u32[]{:S(2)}) collective-permute-start(bf16[240,384]{1,0:T(8,128)(2,1)S(1)} %slice.69), channel_id=1, source_target_pairs={{0,8},{1,9},{2,10},{3,11},{4,12},{5,13},{6,14},{7,15},{8,0},{9,1},... | collective-permute-start | bytes 552968 | tf_op jit(solution)/shard_map/ppermute | solution.py:566
  110.4 8.7 %collective-permute-start.20 = (bf16[144,384]{1,0:T(8,128)(2,1)S(1)}, bf16[144,384]{1,0:T(8,128)(2,1)S(1)}, u32[]{:S(2)}, u32[]{:S(2)}) collective-permute-start(bf16[144,384]{1,0:T(8,128)(2,1)S(1)} %slice.84), channel_id=1, source_target_pairs={{0,16},{1,17},{2,18},{3,19},{4,20},{5,21},{6,22},{7,23},{8,24},{9,... | collective-permute-start | bytes 331784 | tf_op jit(solution)/shard_map/ppermute | solution.py:566
  119.2 9.5 %collective-permute-start.25 = (bf16[96,384]{1,0:T(8,128)(2,1)S(1)}, bf16[96,384]{1,0:T(8,128)(2,1)S(1)}, u32[]{:S(2)}, u32[]{:S(2)}) collective-permute-start(bf16[96,384]{1,0:T(8,128)(2,1)S(1)} %slice.87), channel_id=1, source_target_pairs={{0,16},{1,17},{2,18},{3,19},{4,20},{5,21},{6,22},{7,23},{8,24},{9,... | collective-permute-start | bytes 221192 | tf_op jit(solution)/shard_map/ppermute | solution.py:566
  119.3 12.1 %collective-permute-start.22 = (bf16[192,384]{1,0:T(8,128)(2,1)S(1)}, bf16[192,384]{1,0:T(8,128)(2,1)S(1)}, u32[]{:S(2)}, u32[]{:S(2)}) collective-permute-start(bf16[192,384]{1,0:T(8,128)(2,1)S(1)} %get-tuple-element.169), channel_id=1, source_target_pairs={{0,2},{1,3},{2,0},{3,1},{4,6},{5,7},{6,4},{7,5},{8,10},{9,11},{10,... | collective-permute-start | bytes 442376 | tf_op jit(solution)/shard_map/ppermute | solution.py:566
  119.9 11.5 %collective-permute-start.23 = (bf16[192,384]{1,0:T(8,128)(2,1)S(1)}, bf16[192,384]{1,0:T(8,128)(2,1)S(1)}, u32[]{:S(2)}, u32[]{:S(2)}) collective-permute-start(bf16[192,384]{1,0:T(8,128)(2,1)S(1)} %get-tuple-element.168), channel_id=1, source_target_pairs={{0,4},{1,5},{2,6},{3,7},{4,0},{5,1},{6,2},{7,3},{8,12},{9,13},{10,... | collective-permute-start | bytes 442376 | tf_op jit(solution)/shard_map/ppermute | solution.py:566
  121.2 10.2 %collective-permute-start.24 = (bf16[192,384]{1,0:T(8,128)(2,1)S(1)}, bf16[192,384]{1,0:T(8,128)(2,1)S(1)}, u32[]{:S(2)}, u32[]{:S(2)}) collective-permute-start(bf16[192,384]{1,0:T(8,128)(2,1)S(1)} %get-tuple-element.167), channel_id=1, source_target_pairs={{0,6},{1,7},{2,4},{3,5},{4,2},{5,3},{6,0},{7,1},{8,14},{9,15},{10,... | collective-permute-start | bytes 442376 | tf_op jit(solution)/shard_map/ppermute | solution.py:566
  128.8 6.1 %collective-permute-start.28 = (bf16[192,384]{1,0:T(8,128)(2,1)S(1)}, bf16[192,384]{1,0:T(8,128)(2,1)S(1)}, u32[]{:S(2)}, u32[]{:S(2)}) collective-permute-start(bf16[192,384]{1,0:T(8,128)(2,1)S(1)} %pad_maximum_fusion.5), channel_id=1, source_target_pairs={{0,8},{1,9},{2,10},{3,11},{4,12},{5,13},{6,14},{7,15},{8,0},{9,1},... | collective-permute-start | bytes 442376 | tf_op jit(solution)/shard_map/ppermute | solution.py:566
  131.5 5.5 %collective-permute-start.26 = (bf16[96,384]{1,0:T(8,128)(2,1)S(1)}, bf16[96,384]{1,0:T(8,128)(2,1)S(1)}, u32[]{:S(2)}, u32[]{:S(2)}) collective-permute-start(bf16[96,384]{1,0:T(8,128)(2,1)S(1)} %slice.89), channel_id=1, source_target_pairs={{0,8},{1,9},{2,10},{3,11},{4,12},{5,13},{6,14},{7,15},{8,0},{9,1},... | collective-permute-start | bytes 221192 | tf_op jit(solution)/shard_map/ppermute | solution.py:566
  134.9 7.2 %collective-permute-start.29 = (bf16[432,384]{1,0:T(8,128)(2,1)S(1)}, bf16[432,384]{1,0:T(8,128)(2,1)S(1)}, u32[]{:S(2)}, u32[]{:S(2)}) collective-permute-start(bf16[432,384]{1,0:T(8,128)(2,1)S(1)} %pad_maximum_fusion.3), channel_id=1, source_target_pairs={{0,2},{1,3},{2,0},{3,1},{4,6},{5,7},{6,4},{7,5},{8,10},{9,11},{10,... | collective-permute-start | bytes 995336 | tf_op jit(solution)/shard_map/ppermute | solution.py:566
  135.5 7.1 %collective-permute-start.30 = (bf16[432,384]{1,0:T(8,128)(2,1)S(1)}, bf16[432,384]{1,0:T(8,128)(2,1)S(1)}, u32[]{:S(2)}, u32[]{:S(2)}) collective-permute-start(bf16[432,384]{1,0:T(8,128)(2,1)S(1)} %pad_maximum_fusion.3), channel_id=1, source_target_pairs={{0,4},{1,5},{2,6},{3,7},{4,0},{5,1},{6,2},{7,3},{8,12},{9,13},{10,... | collective-permute-start | bytes 995336 | tf_op jit(solution)/shard_map/ppermute | solution.py:566
  137.0 4.9 %collective-permute-start.27 = (bf16[48,384]{1,0:T(8,128)(2,1)S(1)}, bf16[48,384]{1,0:T(8,128)(2,1)S(1)}, u32[]{:S(2)}, u32[]{:S(2)}) collective-permute-start(bf16[48,384]{1,0:T(8,128)(2,1)S(1)} %slice.91), channel_id=1, source_target_pairs={{0,16},{1,17},{2,18},{3,19},{4,20},{5,21},{6,22},{7,23},{8,24},{9,... | collective-permute-start | bytes 110600 | tf_op jit(solution)/shard_map/ppermute | solution.py:566
  142.6 4.9 %collective-permute-start.32 = (bf16[48,384]{1,0:T(8,128)(2,1)S(1)}, bf16[48,384]{1,0:T(8,128)(2,1)S(1)}, u32[]{:S(2)}, u32[]{:S(2)}) collective-permute-start(bf16[48,384]{1,0:T(8,128)(2,1)S(1)} %add_convert_fusion.7), channel_id=1, source_target_pairs={{0,16},{1,17},{2,18},{3,19},{4,20},{5,21},{6,22},{7,23},{8,24},{9,... | collective-permute-start | bytes 110600 | tf_op jit(solution)/shard_map/ppermute | solution.py:566
  145.1 8.0 %collective-permute-start.31 = (bf16[432,384]{1,0:T(8,128)(2,1)S(1)}, bf16[432,384]{1,0:T(8,128)(2,1)S(1)}, u32[]{:S(2)}, u32[]{:S(2)}) collective-permute-start(bf16[432,384]{1,0:T(8,128)(2,1)S(1)} %pad_maximum_fusion.3), channel_id=1, source_target_pairs={{0,6},{1,7},{2,4},{3,5},{4,2},{5,3},{6,0},{7,1},{8,14},{9,15},{10,... | collective-permute-start | bytes 995336 | tf_op jit(solution)/shard_map/ppermute | solution.py:566
  147.5 4.4 %collective-permute-start.33 = (bf16[96,384]{1,0:T(8,128)(2,1)S(1)}, bf16[96,384]{1,0:T(8,128)(2,1)S(1)}, u32[]{:S(2)}, u32[]{:S(2)}) collective-permute-start(bf16[96,384]{1,0:T(8,128)(2,1)S(1)} %pad_maximum_fusion.7), channel_id=1, source_target_pairs={{0,8},{1,9},{2,10},{3,11},{4,12},{5,13},{6,14},{7,15},{8,0},{9,1},... | collective-permute-start | bytes 221192 | tf_op jit(solution)/shard_map/ppermute | solution.py:566
  153.3 8.4 %collective-permute-start.34 = (bf16[192,384]{1,0:T(8,128)(2,1)S(1)}, bf16[192,384]{1,0:T(8,128)(2,1)S(1)}, u32[]{:S(2)}, u32[]{:S(2)}) collective-permute-start(bf16[192,384]{1,0:T(8,128)(2,1)S(1)} %pad_maximum_fusion.6), channel_id=1, source_target_pairs={{0,2},{1,3},{2,0},{3,1},{4,6},{5,7},{6,4},{7,5},{8,10},{9,11},{10,... | collective-permute-start | bytes 442376 | tf_op jit(solution)/shard_map/ppermute | solution.py:566
  154.9 9.1 %collective-permute-start.35 = (bf16[192,384]{1,0:T(8,128)(2,1)S(1)}, bf16[192,384]{1,0:T(8,128)(2,1)S(1)}, u32[]{:S(2)}, u32[]{:S(2)}) collective-permute-start(bf16[192,384]{1,0:T(8,128)(2,1)S(1)} %pad_maximum_fusion.6), channel_id=1, source_target_pairs={{0,4},{1,5},{2,6},{3,7},{4,0},{5,1},{6,2},{7,3},{8,12},{9,13},{10,... | collective-permute-start | bytes 442376 | tf_op jit(solution)/shard_map/ppermute | solution.py:566
  155.5 8.5 %collective-permute-start.36 = (bf16[192,384]{1,0:T(8,128)(2,1)S(1)}, bf16[192,384]{1,0:T(8,128)(2,1)S(1)}, u32[]{:S(2)}, u32[]{:S(2)}) collective-permute-start(bf16[192,384]{1,0:T(8,128)(2,1)S(1)} %pad_maximum_fusion.6), channel_id=1, source_target_pairs={{0,6},{1,7},{2,4},{3,5},{4,2},{5,3},{6,0},{7,1},{8,14},{9,15},{10,... | collective-permute-start | bytes 442376 | tf_op jit(solution)/shard_map/ppermute | solution.py:566
  (18 other events, 91.0 us)

commit v5 on v4

--- a/solution.py
+++ b/solution.py
@@ -22,6 +22,10 @@
 IMG_BLOCK = 16
 IMG_ROWS = IMG_BLOCK * IMG_LEN
 EPS = 1e-06
+
+SMEM = pl.BlockSpec(memory_space=pltpu.SMEM)
+VMEM = pl.BlockSpec(memory_space=pltpu.VMEM)
+ROOM = pltpu.CompilerParams(vmem_limit_bytes=24 * 2**20)
 
 BF = jnp.bfloat16
 F32 = jnp.float32
@@ -146,6 +150,7 @@
             pltpu.VMEM((count, D), F32),
             pltpu.VMEM((count, D), F32),
         ],
+        compiler_params=ROOM,
         cost_estimate=cost(12),
         name="image_tower",
     )(x, g1, wqkv, wout, g2, wup, wdown, wproj)
@@ -157,7 +162,10 @@
     return wide == wide.T
 
 
-def text_att_kernel(tok_ref, lab_ref, g1, wqkv, o_ref, qkv_ref, p_ref, h1_ref):
+def text_att_kernel(tok_ref, lab_ref, g1, wqkv, o_all, qkv_all, p_all, h1_all):
+    step = pl.program_id(0)
+    o_ref, qkv_ref, h1_ref = o_all.at[held_rows()], qkv_all.at[held_rows()], h1_all.at[held_rows()]
+    p_ref = p_all.at[pl.ds(2 * step, 2)]
     x = tok_ref[...].astype(F32)
     h1 = (normalize(x) * g1[...].reshape(1, D)).astype(BF)
     h1_ref[...] = h1
@@ -186,11 +194,12 @@
 
 def text_mlp_kernel(
     tok_ref, o_ref, lab_ref, wout, g2, wup, wdown, wproj,
-    h2_ref, c2_ref, gp_ref, pu_ref, pb_ref, e_ref, emb_ref, cnt_ref, pt, po,
+    h2_all, c2_all, gp_all, pu_ref, pb_ref, e_ref, emb_ref, cnt_ref, pt, po,
 ):
     step = pl.program_id(0)
+    h2_ref, c2_ref, gp_ref = h2_all.at[held_rows()], c2_all.at[held_rows()], gp_all.at[held_rows()]
     tok = tok_ref[...]
-    o = o_ref[...]
+    o = o_ref[held_rows(), :]
     x1 = tok.astype(F32) + mm(o, wout[...])
     c2 = x1 - row_mean(x1)
     c2_ref[...] = c2
@@ -219,6 +228,14 @@
         emb_ref[...] = (e * lax.rsqrt(jnp.sum(e * e, -1, keepdims=True) + EPS)).astype(BF)
 
 
+def near(v):
+    return pltpu.with_memory_space_constraint(v, pltpu.VMEM)
+
+
+def held_rows():
+    return pl.ds(pl.multiple_of(pl.program_id(0) * TOK_BLOCK, TOK_BLOCK), TOK_BLOCK)
+
+
 def token_rows(width):
     return pl.BlockSpec((TOK_BLOCK, width), lambda i: (i, 0))
 
@@ -234,20 +251,16 @@
 def text_att(tok, lab, g1, wqkv):
     n = tok.shape[0]
     blocks = n // TOK_BLOCK
-    shape = jax.ShapeDtypeStruct
+    shape = pltpu.VMEM
     return pl.pallas_call(
         text_att_kernel,
         grid=(blocks,),
         in_specs=[token_rows(D), block_of(1, TOK_BLOCK), const_spec((D,)), const_spec((D, 3 * D))],
-        out_specs=[
-            token_rows(D),
-            token_rows(3 * D),
-            pl.BlockSpec((2, 3, 2 * PAIR, PAIR), lambda i: (i, 0, 0, 0)),
-            token_rows(D),
-        ],
+        out_specs=[VMEM] * 4,
         out_shape=[
             shape((n, D), BF), shape((n, 3 * D), BF), shape((2 * blocks, 3, 2 * PAIR, PAIR), BF), shape((n, D), BF),
         ],
+        compiler_params=ROOM,
         cost_estimate=cost(9),
         name="text_att",
     )(tok, lab, g1, wqkv)
@@ -255,27 +268,25 @@
 
 def text_mlp(tok, o, lab, wout, g2, wup, wdown, wproj):
     n = tok.shape[0]
-    shape = jax.ShapeDtypeStruct
+    shape = pltpu.VMEM
     return pl.pallas_call(
         text_mlp_kernel,
         grid=(n // TOK_BLOCK,),
         in_specs=[
-            token_rows(D), token_rows(D), block_of(1, TOK_BLOCK),
+            token_rows(D), VMEM, block_of(1, TOK_BLOCK),
             const_spec((D, D)), const_spec((D,)), const_spec((D, FF)), const_spec((FF, D)), const_spec((D, D)),
         ],
-        out_specs=[
-            token_rows(D), token_rows(D), token_rows(FF),
-            whole(CAPS, FF), whole(CAPS, D), whole(CAPS, D), whole(CAPS, D), whole(CAPS, 128),
-        ],
+        out_specs=[VMEM] * 8,
         out_shape=[
             shape((n, D), BF), shape((n, D), F32), shape((n, FF), BF),
             shape((CAPS, FF), F32), shape((CAPS, D), BF), shape((CAPS, D), F32),
             shape((CAPS, D), BF), shape((CAPS, 128), F32),
         ],
         scratch_shapes=[pltpu.VMEM((CAPS, D), F32), pltpu.VMEM((CAPS, D), F32)],
+        compiler_params=ROOM,
         cost_estimate=cost(11),
         name="text_mlp",
-    )(tok, o, lab, wout, g2, wup, wdown, wproj)
+    )(tok, near(o), lab, wout, g2, wup, wdown, wproj)
 
 
 def reorder(mine, row):
@@ -371,10 +382,12 @@
 
 
 def mlp_back_kernel(
-    mine_ref, lab_ref, h2_ref, gp_ref, c2_ref, du_ref, dy_ref, g2, wup,
-    dx_ref, dxb_ref, send_ref, keep_ref, acc,
+    mine_ref, lab_ref, h2_all, gp_all, c2_all, du_ref, dy_ref, g2, wup,
+    dx_all, dxb_all, send_ref, keep_ref, acc,
 ):
     step = pl.program_id(0)
+    h2_ref, gp_ref, c2_ref = h2_all.at[held_rows()], gp_all.at[held_rows()], c2_all.at[held_rows()]
+    dx_ref, dxb_ref = dx_all.at[held_rows()], dxb_all.at[held_rows()]
 
     @pl.when(step == 0)
     def _():
@@ -382,9 +395,9 @@
 
     hit = lax.broadcasted_iota(jnp.int32, (3 * CAP_BLOCK, TOK_BLOCK), 0) % CAP_BLOCK == lab_ref[0]
     spread = jnp.where(hit, 1.0, 0.0).astype(BF)
-    du = mm_tn(spread, du_ref[0])
+    du = mm_tn(spread, du_ref[step])
     dz = (du * gp_ref[...].astype(F32)).astype(BF)
-    dy = mm_tn(spread, dy_ref[0])
+    dy = mm_tn(spread, dy_ref[step])
     dh = mm_nt(dz, wup[...])
     c2 = c2_ref[...]
     r = lax.rsqrt(row_mean(c2 * c2) + EPS)
@@ -401,7 +414,10 @@
         halves(mine_ref[0], 192, send_ref, keep_ref, lambda at, k: block(acc, at, 48, k))
 
 
-def att_core_kernel(qkv_ref, p_ref, dxb_ref, wout, dqkv_ref):
+def att_core_kernel(qkv_all, p_all, dxb_all, wout, dqkv_all):
+    step = pl.program_id(0)
+    qkv_ref, dxb_ref, dqkv_ref = qkv_all.at[held_rows()], dxb_all.at[held_rows()], dqkv_all.at[held_rows()]
+    p_ref = p_all.at[pl.ds(2 * step, 2)]
     do = mm_nt(dxb_ref[...], wout[...]).astype(BF)
     low = lax.broadcasted_iota(jnp.int32, (PAIR, PAIR), 1) < HEAD
     zero = jnp.zeros((PAIR, PAIR), BF)
@@ -436,7 +452,8 @@
     halves(mine_ref[0], 192, send_ref, keep_ref, lambda at, k: block(acc, at, 48, k))
 
 
-def tok_back_kernel(tok_ref, dqkv_ref, dx_ref, g1, wqkv, gtok_ref):
+def tok_back_kernel(tok_ref, dqkv_all, dx_all, g1, wqkv, gtok_ref):
+    dqkv_ref, dx_ref = dqkv_all.at[held_rows()], dx_all.at[held_rows()]
     x = tok_ref[...].astype(F32)
     centre = x - row_mean(x)
     r = lax.rsqrt(row_mean(centre * centre) + EPS)
@@ -478,18 +495,16 @@
     gain_ref[...] = gain_of(qkv_ref[...], wqkv[...], g1[...]).reshape(D)
 
 
-SMEM = pl.BlockSpec(memory_space=pltpu.SMEM)
-VMEM = pl.BlockSpec(memory_space=pltpu.VMEM)
-
-
-def simple(kernel, outs, scratch=(), smem=0, us=3, name=None):
+def simple(kernel, outs, scratch=(), smem=0, us=3, name=None, held=(), held_out=True):
     def call(*args):
+        args = [near(v) if i in held else v for i, v in enumerate(args)]
         return pl.pallas_call(
             kernel,
             in_specs=[SMEM] * smem + [VMEM] * (len(args) - smem),
             out_specs=[VMEM] * len(outs),
-            out_shape=[jax.ShapeDtypeStruct(s, t) for s, t in outs],
+            out_shape=[(pltpu.VMEM if held_out else jax.ShapeDtypeStruct)(s, t) for s, t in outs],
             scratch_shapes=list(scratch),
+            compiler_params=ROOM,
             cost_estimate=cost(us),
             name=name,
         )(*args)
@@ -499,27 +514,18 @@
 
 def mlp_back(mine, lab, h2, gp, c2, du, dy, g2, wup):
     n = h2.shape[0]
-
-    def rows(width):
-        return pl.BlockSpec((TOK_BLOCK, width), lambda i: (i, 0))
-
-    def blk(a, b):
-        return pl.BlockSpec((1, a, b), lambda i: (i, 0, 0))
-
-    shape = jax.ShapeDtypeStruct
+    shape = pltpu.VMEM
     return pl.pallas_call(
         mlp_back_kernel,
         grid=(n // TOK_BLOCK,),
-        in_specs=[
-            SMEM, blk(1, TOK_BLOCK), rows(D), rows(FF), rows(D), blk(3 * CAP_BLOCK, FF), blk(3 * CAP_BLOCK, D),
-            const_spec((D,)), const_spec((D, FF)),
-        ],
-        out_specs=[rows(D), rows(D)] + [pl.BlockSpec((768, D), lambda i: (0, 0))] * 2,
+        in_specs=[SMEM, block_of(1, TOK_BLOCK)] + [VMEM] * 5 + [const_spec((D,)), const_spec((D, FF))],
+        out_specs=[VMEM] * 4,
         out_shape=[shape((n, D), F32), shape((n, D), BF), shape((768, D), BF), shape((768, D), BF)],
         scratch_shapes=[pltpu.VMEM((D, FF), F32)],
+        compiler_params=ROOM,
         cost_estimate=cost(9),
         name="mlp_back",
-    )(mine, lab, h2, gp, c2, du, dy, g2, wup)
+    )(mine, lab, near(h2), near(gp), near(c2), near(du), near(dy), g2, wup)
 
 
 def att_core(qkv, p, dxb, wout):
@@ -527,23 +533,19 @@
     return pl.pallas_call(
         att_core_kernel,
         grid=(n // TOK_BLOCK,),
-        in_specs=[
-            token_rows(3 * D),
-            pl.BlockSpec((2, 3, 2 * PAIR, PAIR), lambda i: (i, 0, 0, 0)),
-            token_rows(D),
-            const_spec((D, D)),
-        ],
-        out_specs=token_rows(3 * D),
-        out_shape=jax.ShapeDtypeStruct((n, 3 * D), BF),
+        in_specs=[VMEM, VMEM, VMEM, const_spec((D, D))],
+        out_specs=VMEM,
+        out_shape=pltpu.VMEM((n, 3 * D), BF),
+        compiler_params=ROOM,
         cost_estimate=cost(10),
         name="att_core",
-    )(qkv, p, dxb, wout)
+    )(near(qkv), near(p), near(dxb), wout)
 
 
 def att_grads(mine, h1, dqkv, o, dxb):
     outs = [((768, D), BF)] * 2
     scratch = [pltpu.VMEM((D, 4 * D), F32)]
-    return simple(att_grads_kernel, outs, scratch, smem=1, us=4, name="att_grads")(mine, h1, dqkv, o, dxb)
+    return simple(att_grads_kernel, outs, scratch, smem=1, us=4, name="att_grads", held=(1, 2, 3, 4))(mine, h1, dqkv, o, dxb)
 
 
 def tok_back(tok, dqkv, dx, g1, wqkv):
@@ -551,12 +553,13 @@
     return pl.pallas_call(
         tok_back_kernel,
         grid=(n // TOK_BLOCK,),
-        in_specs=[token_rows(D), token_rows(3 * D), token_rows(D), const_spec((D,)), const_spec((D, 3 * D))],
+        in_specs=[token_rows(D), VMEM, VMEM, const_spec((D,)), const_spec((D, 3 * D))],
         out_specs=token_rows(D),
         out_shape=jax.ShapeDtypeStruct((n, D), F32),
+        compiler_params=ROOM,
         cost_estimate=cost(4),
         name="tok_back",
-    )(tok, dqkv, dx, g1, wqkv)
+    )(tok, near(dqkv), near(dx), g1, wqkv)
 
 
 AXES = ("dp", "replica")
@@ -631,8 +634,9 @@
         smem=2,
         us=3,
         name="cosine",
+        held=(3,),
     )(log_scale, mine, temb, images, pair)
-    (dt_row,) = simple(functools.partial(rows_kernel, denom), [((CAPS, D), F32)], smem=1, us=2, name="rows")(
+    (dt_row,) = simple(functools.partial(rows_kernel, denom), [((CAPS, D), F32)], smem=1, us=2, name="rows", held=(2,))(
         log_scale, g, images, pair
     )
     if tuned:
@@ -652,6 +656,7 @@
         smem=2,
         us=5,
         name="head_back",
+        held=(3, 4),
     )(log_scale, mine, g, images, sums, dt_row, e, pb, cnt, pu, txt_proj, txt_down)
     dx, dxb, send_u, keep_u = mlp_back(mine, lab, h2, gp, c2, du, dy, txt_ln2, txt_up)
 
@@ -661,11 +666,11 @@
 
     def spread_mlp(own, other):
         outs = [((FF, D), F32), ((D, FF), F32), ((D, D), F32), ((D,), F32)]
-        return simple(spread_mlp_kernel, outs, smem=1, us=4, name="spread_mlp")(mine, own, other, txt_up, txt_ln2)
+        return simple(spread_mlp_kernel, outs, smem=1, us=4, name="spread_mlp", held=(1, 2), held_out=False)(mine, own, other, txt_up, txt_ln2)
 
     def spread_att(own, other):
         outs = [((D, D), F32), ((D, 3 * D), F32), ((D,), F32)]
-        return simple(spread_att_kernel, outs, smem=1, us=4, name="spread_att")(mine, own, other, txt_qkv, txt_ln1)
+        return simple(spread_att_kernel, outs, smem=1, us=4, name="spread_att", held=(1, 2), held_out=False)(mine, own, other, txt_qkv, txt_ln1)
 
     if not tuned:
         dqkv = att_core(qkv, p, dxb, txt_out)
@@ -701,8 +706,8 @@
         grad_tokens = tok_back(text_tokens, dqkv, dx, txt_ln1, txt_qkv)
         far, grad_tokens = lax.optimization_barrier((far, grad_tokens))
         got_a, grad_tokens = lax.optimization_barrier((got_a, grad_tokens))
-        near = joined(m[:96], [far])
-        m = joined(near, [swap(near, 8), m[96:]])
+        m = joined(m[:96], [far, m[96:]])
+        m = joined(m[:192], [swap(m[:192], 8), m[192:]])
         a = added(a[0], got_a)
         got_m = plane([m] * 4)
         a = added(a[:96], [swap(a[96:], 8)])

time: 171 us -> 171 us (level)
  Pallas kernels: 81.1 us -> 50.3 us
  local copies, waits for them, and re-layouts: 4.23 us -> 22.2 us
  waiting for transfers between devices: 36.2 us -> 46.4 us
  between operations: 1.85 us -> 4.31 us
    unnamed x35 -> x95, local copies, waits for them, and re-layouts: 2.36 us -> 20.4 us
    pallas_call x6, Pallas kernels: 23.8 us -> 9.3 us  [call(): pl.pallas_call(kernel, in_specs=[SMEM] * smem + [VMEM] * (len(args) - sme...]
    ppermute x39, waiting for transfers between devices: 36.2 us -> 46.4 us  [swap(): return lax.ppermute(v, AXES, [(i, i ^ mask) for i in range(32)])]
    pallas_call x1, Pallas kernels: 9.01 us -> 5.35 us  [mlp_back(): pl.pallas_call(mlp_back_kernel, grid=(n // TOK_BLOCK,), in_specs=[SMEM, b...]
    pallas_call x1, Pallas kernels: 12.2 us -> 8.86 us  [text_mlp(): pl.pallas_call(text_mlp_kernel, grid=(n // TOK_BLOCK,), in_specs=[token_r...]
    pallas_call x1, Pallas kernels: 11.4 us -> 8.66 us  [image_tower(): pl.pallas_call(image_kernel, grid=(count // IMG_BLOCK,), in_specs=[pl.Blo...]
    pallas_call x1, Pallas kernels: 5.85 us -> 3.43 us  [tok_back(): pl.pallas_call(tok_back_kernel, grid=(n // TOK_BLOCK,), in_specs=[token_r...]
    pallas_call x1, Pallas kernels: 11.3 us -> 9.2 us  [att_core(): pl.pallas_call(att_core_kernel, grid=(n // TOK_BLOCK,), in_specs=[VMEM, V...]
  transfers between devices with their start and end apart: 39 -> 39, of which waited for: 18 -> 19; matrix products, arithmetic and copies ran while one was open for 1% -> 3% of each run, Pallas kernels for 34% -> 22%
where the time goes in v5:
time: 171 us
  Pallas kernels  50.3 us (29%)
  waiting for transfers between devices  46.4 us (27%)
  starting transfers between devices  44.9 us (26%)
  local copies, waits for them, and re-layouts  22.2 us (13%)
  between operations  4.31 us (3%)
  other arithmetic  2.43 us (1%)
    ppermute x39, waiting for transfers between devices, swap(): return lax.ppermute(v, AXES, [(i, i ^ mask) for i in range(32)])  46.4 us
    ppermute x39, starting transfers between devices, swap(): return lax.ppermute(v, AXES, [(i, i ^ mask) for i in range(32)])  44.9 us
    unnamed x95, local copies, waits for them, and re-layouts  20.4 us
    pallas_call x6, Pallas kernels, call(): pl.pallas_call(kernel, in_specs=[SMEM] * smem + [VMEM] * (len(args) - sme...  9.3 us
    pallas_call x1, Pallas kernels, att_core(): pl.pallas_call(att_core_kernel, grid=(n // TOK_BLOCK,), in_specs=[VMEM, V...  9.2 us
    pallas_call x1, Pallas kernels, text_mlp(): pl.pallas_call(text_mlp_kernel, grid=(n // TOK_BLOCK,), in_specs=[token_r...  8.86 us
    pallas_call x1, Pallas kernels, image_tower(): pl.pallas_call(image_kernel, grid=(count // IMG_BLOCK,), in_specs=[pl.Blo...  8.66 us
    pallas_call x1, Pallas kernels, text_att(): pl.pallas_call(text_att_kernel, grid=(blocks,), in_specs=[token_rows(D),...  5.54 us
  transfers between devices with their start and end apart: 39, of which 19 were waited for; matrix products, arithmetic and copies ran while one was open for 3% of the time, Pallas kernels for 22%

profile of v5, /device:TPU:0, one launch (start us, length us, event | category | flops | bytes accessed | tf_op | source)
XLA Modules:
  0.0 170.5 jit_solution(505025296658945166)
XLA Ops:
  9.4 8.7 %image_tower.1 = bf16[64,384]{1,0:T(8,128)(2,1)S(1)} custom-call(bf16[50,64,384]{2,1,0:T(8,128)(2,1)S(1)} %bitcast.29, f32[384]{0:T(512)S(1)} %copy-done.15, bf16[384,1152]{1,0:T(8,128)(2,1)S(1)} %copy-done.5, bf16[384,384]{1,0:T(8,128)(2,1)S(1)} %copy-done.9, f32[384]{0:T(512)S(1)} %copy-done.16, bf16[384,1536]{1,0:T(8,128)(2,1)S(1)} %copy-done.1, ...), custom_call_target="tpu_custom_call" | custom-call | flops 12000000000 | bytes 36000000 | tf_op jit(solution)/shard_map/image_tower/pallas_call | solution.py:133
  18.0 3.1 %collective-permute-start = (bf16[64,384]{1,0:T(8,128)(2,1)S(1)}, bf16[64,384]{1,0:T(8,128)(2,1)S(1)}, u32[]{:S(2)}, u32[]{:S(2)}) collective-permute-start(bf16[64,384]{1,0:T(8,128)(2,1)S(1)} %image_tower.1), channel_id=1, source_target_pairs={{0,8},{1,9},{2,10},{3,11},{4,12},{5,13},{6,14},{7,15},{8,0},{9,1},... | collective-permute-start | bytes 147464 | tf_op jit(solution)/shard_map/ppermute | solution.py:569
  21.1 2.6 %collective-permute-start.1 = (bf16[64,384]{1,0:T(8,128)(2,1)S(1)}, bf16[64,384]{1,0:T(8,128)(2,1)S(1)}, u32[]{:S(2)}, u32[]{:S(2)}) collective-permute-start(bf16[64,384]{1,0:T(8,128)(2,1)S(1)} %image_tower.1), channel_id=1, source_target_pairs={{0,16},{1,17},{2,18},{3,19},{4,20},{5,21},{6,22},{7,23},{8,24},{9,... | collective-permute-start | bytes 147464 | tf_op jit(solution)/shard_map/ppermute | solution.py:569
  25.1 5.5 %text_att.1 = (bf16[1024,384]{1,0:T(8,128)(2,1)S(1)}, bf16[1024,1152]{1,0:T(8,128)(2,1)S(1)}, bf16[8,3,256,128]{3,2,1,0:T(8,128)(2,1)S(1)}, bf16[1024,384]{1,0:T(8,128)(2,1)S(1)}) custom-call(bf16[1024,384]{1,0:T(8,128)(2,1)S(1)} %copy-done.7, s32[4,1,256]{2,1,0:T(1,128)S(1)} %reshape.67.lab_ref, f32[384]{0:T(512)S(1)} %copy-done.18, ...), custom_call_target="tpu_custom_call" | custom-call | flops 8999999488 | bytes 27000000 | tf_op jit(solution)/shard_map/text_att/pallas_call | solution.py:255
  33.3 1.8 %collective-permute-start.3 = (bf16[256,384]{1,0:T(8,128)(2,1)S(1)}, bf16[256,384]{1,0:T(8,128)(2,1)S(1)}, u32[]{:S(2)}, u32[]{:S(2)}) collective-permute-start(bf16[256,384]{1,0:T(8,128)(2,1)S(1)} %pad_maximum_fusion.4), channel_id=1, source_target_pairs={{0,2},{1,3},{2,0},{3,1},{4,6},{5,7},{6,4},{7,5},{8,10},{9,11},{10,... | collective-permute-start | bytes 589832 | tf_op jit(solution)/shard_map/ppermute | solution.py:569
  36.8 8.9 %text_mlp.1 = (bf16[1024,384]{1,0:T(8,128)(2,1)S(1)}, f32[1024,384]{1,0:T(8,128)S(1)}, bf16[1024,1536]{1,0:T(8,128)(2,1)S(1)}, f32[64,1536]{1,0:T(8,128)S(1)}, b...) custom-call(bf16[1024,384]{1,0:T(8,128)(2,1)S(1)} %copy-done.7, ...), custom_call_target="tpu_custom_call" | custom-call | flops 11000000512 | bytes 33000000 | tf_op jit(solution)/shard_map/text_mlp/pallas_call | solution.py:272
  58.7 2.7 %collective-permute-start.10 = (f32[40,128]{1,0:T(8,128)S(1)}, f32[40,128]{1,0:T(8,128)S(1)}, u32[]{:S(2)}, u32[]{:S(2)}) collective-permute-start(f32[40,128]{1,0:T(8,128)S(1)} %add.113), channel_id=1, source_target_pairs={{0,6},{1,7},{2,4},{3,5},{4,2},{5,3},{6,0},{7,1},{8,14},{9,15},{10,... | collective-permute-start | bytes 61448 | tf_op jit(solution)/shard_map/ppermute | solution.py:569
  63.4 1.8 %collective-permute-done.8 = f32[40,128]{1,0:T(8,128)S(1)} collective-permute-done((f32[40,128]{1,0:T(8,128)S(1)}, f32[40,128]{1,0:T(8,128)S(1)}, u32[]{:S(2)}, u32[]{:S(2)}) %collective-permute-start.8) | collective-permute-done | bytes 20512 | tf_op jit(solution)/shard_map/ppermute | solution.py:569
  66.4 3.1 %collective-permute-done.11 = f32[40,128]{1,0:T(8,128)S(1)} collective-permute-done((f32[40,128]{1,0:T(8,128)S(1)}, f32[40,128]{1,0:T(8,128)S(1)}, u32[]{:S(2)}, u32[]{:S(2)}) %collective-permute-start.11) | collective-permute-done | bytes 20512 | tf_op jit(solution)/shard_map/ppermute | solution.py:569
  69.5 2.1 %collective-permute-start.12 = (f32[40,128]{1,0:T(8,128)S(1)}, f32[40,128]{1,0:T(8,128)S(1)}, u32[]{:S(2)}, u32[]{:S(2)}) collective-permute-start(f32[40,128]{1,0:T(8,128)S(1)} %add.117), channel_id=1, source_target_pairs={{0,16},{1,17},{2,18},{3,19},{4,20},{5,21},{6,22},{7,23},{8,24},{9,... | collective-permute-start | bytes 61448 | tf_op jit(solution)/shard_map/ppermute | solution.py:569
  72.2 2.0 %collective-permute-done.12 = f32[40,128]{1,0:T(8,128)S(1)} collective-permute-done((f32[40,128]{1,0:T(8,128)S(1)}, f32[40,128]{1,0:T(8,128)S(1)}, u32[]{:S(2)}, u32[]{:S(2)}) %collective-permute-start.12) | collective-permute-done | bytes 20512 | tf_op jit(solution)/shard_map/ppermute | solution.py:569
  74.2 1.8 %head_back.1 = (bf16[768,384]{1,0:T(8,128)(2,1)S(1)}, bf16[768,384]{1,0:T(8,128)(2,1)S(1)}, bf16[192,384]{1,0:T(8,128)(2,1)S(1)}, bf16[192,384]{1,0:T(8,128)(2,1...) custom-call(f32[1]{0:T(128)S(6)} %copy.46.scale_ref, ...), custom_call_target="tpu_custom_call" | custom-call | flops 5000000000 | bytes 15000000 | tf_op jit(solution)/shard_map/head_back/pallas_call | solution.py:501
  76.8 5.4 %mlp_back.1 = (f32[1024,384]{1,0:T(8,128)S(1)}, bf16[1024,384]{1,0:T(8,128)(2,1)S(1)}, bf16[768,384]{1,0:T(8,128)(2,1)S(1)}, bf16[768,384]{1,0:T(8,128)(2,1)S(1)}) custom-call(s32[1]{0:T(128)} %bitcast.mine_ref, s32[4,1,256]{2,1,0:T(1,128)S(1)} %reshape.67.lab_ref, bf16[1024,384]{1,0:T(8,128)(2,1)S(1)} %copy-done.34, bf16[1024,1536]{1,0:T(8,128)(2,1)S(1)} %copy-done.24, ...), custom_call_target="tpu_custom_call" | custom-call | flops 8999999488 | bytes 27000000 | tf_op jit(solution)/shard_map/mlp_back/pallas_call | solution.py:518
  82.4 1.8 %collective-permute-done.14 = bf16[768,384]{1,0:T(8,128)(2,1)S(1)} collective-permute-done((bf16[768,384]{1,0:T(8,128)(2,1)S(1)}, bf16[768,384]{1,0:T(8,128)(2,1)S(1)}, u32[]{:S(2)}, u32[]{:S(2)}) %collective-permute-start.14) | collective-permute-done | bytes 589856 | tf_op jit(solution)/shard_map/ppermute | solution.py:569
  88.3 9.2 %att_core.1.dqkv_ref.dqkv_all = bf16[1024,1152]{1,0:T(8,128)(2,1)S(1)} custom-call(bf16[1024,1152]{1,0:T(8,128)(2,1)S(1)} %copy-done.26, bf16[8,3,256,128]{3,2,1,0:T(8,128)(2,1)S(1)} %copy-done.32, bf16[1024,384]{1,0:T(8,128)(2,1)S(1)} %get-tuple-element.120.dxb_all.dxb_ref, bf16[384,384]{1,0:T(8,128)(2,1)S(1)} %copy-done.14), custom_call_target="tpu_custom_call" | custom-call | flops 10000000000 | bytes 30000000 | tf_op jit(solution)/shard_map/att_core/pallas_call | solution.py:533
  97.6 5.4 %collective-permute-done.17 = bf16[432,384]{1,0:T(8,128)(2,1)S(1)} collective-permute-done((bf16[432,384]{1,0:T(8,128)(2,1)S(1)}, bf16[432,384]{1,0:T(8,128)(2,1)S(1)}, u32[]{:S(2)}, u32[]{:S(2)}) %collective-permute-start.17) | collective-permute-done | bytes 331808 | tf_op jit(solution)/shard_map/ppermute | solution.py:569
  104.5 1.8 %att_grads.1 = (bf16[768,384]{1,0:T(8,128)(2,1)S(1)}, bf16[768,384]{1,0:T(8,128)(2,1)S(1)}) custom-call(s32[1]{0:T(128)} %bitcast.mine_ref, bf16[1024,384]{1,0:T(8,128)(2,1)S(1)} %copy-done.22, bf16[1024,1152]{1,0:T(8,128)(2,1)S(1)} %att_core.1.dqkv_ref.dqkv_all, bf16[1024,384]{1,0:T(8,128)(2,1)S(1)} %copy-done.20, ...), custom_call_target="tpu_custom_call" | custom-call | flops 4000000000 | bytes 12000000 | tf_op jit(solution)/shard_map/att_grads/pallas_call | solution.py:501
  106.3 2.5 %collective-permute-done.19 = bf16[240,384]{1,0:T(8,128)(2,1)S(1)} collective-permute-done((bf16[240,384]{1,0:T(8,128)(2,1)S(1)}, bf16[240,384]{1,0:T(8,128)(2,1)S(1)}, u32[]{:S(2)}, u32[]{:S(2)}) %collective-permute-start.19) | collective-permute-done | bytes 184352 | tf_op jit(solution)/shard_map/ppermute | solution.py:569
  109.0 2.5 %collective-permute-start.20 = (bf16[144,384]{1,0:T(8,128)(2,1)S(1)}, bf16[144,384]{1,0:T(8,128)(2,1)S(1)}, u32[]{:S(2)}, u32[]{:S(2)}) collective-permute-start(bf16[144,384]{1,0:T(8,128)(2,1)S(1)} %slice.87), channel_id=1, source_target_pairs={{0,16},{1,17},{2,18},{3,19},{4,20},{5,21},{6,22},{7,23},{8,24},{9,... | collective-permute-start | bytes 331784 | tf_op jit(solution)/shard_map/ppermute | solution.py:569
  111.6 6.1 %collective-permute-done.20 = bf16[144,384]{1,0:T(8,128)(2,1)S(1)} collective-permute-done((bf16[144,384]{1,0:T(8,128)(2,1)S(1)}, bf16[144,384]{1,0:T(8,128)(2,1)S(1)}, u32[]{:S(2)}, u32[]{:S(2)}) %collective-permute-start.20) | collective-permute-done | bytes 110624 | tf_op jit(solution)/shard_map/ppermute | solution.py:569
  121.7 3.4 %tok_back.1 = f32[1024,384]{1,0:T(8,128)} custom-call(bf16[1024,384]{1,0:T(8,128)(2,1)S(1)} %copy-done.8, bf16[1024,1152]{1,0:T(8,128)(2,1)S(1)} %att_core.1.dqkv_ref.dqkv_all, f32[1024,384]{1,0:T(8,128)S(1)} %get-tuple-element.136.dx_all, f32[384]{0:T(512)S(1)} %copy-done.18, bf16[384,1152]{1,0:T(8,128)(2,1)S(1)} %copy-done.6), custom_call_target="tpu_custom_call" | custom-call | flops 4000000000 | bytes 12000000 | tf_op jit(solution)/shard_map/tok_back/pallas_call | solution.py:553
  125.1 3.8 %collective-permute-start.28 = (bf16[192,384]{1,0:T(8,128)(2,1)S(1)}, bf16[192,384]{1,0:T(8,128)(2,1)S(1)}, u32[]{:S(2)}, u32[]{:S(2)}) collective-permute-start(bf16[192,384]{1,0:T(8,128)(2,1)S(1)} %pad_maximum_fusion.5), channel_id=1, source_target_pairs={{0,8},{1,9},{2,10},{3,11},{4,12},{5,13},{6,14},{7,15},{8,0},{9,1},... | collective-permute-start | bytes 442376 | tf_op jit(solution)/shard_map/ppermute | solution.py:569
  129.1 2.0 %collective-permute-start.26 = (bf16[96,384]{1,0:T(8,128)(2,1)S(1)}, bf16[96,384]{1,0:T(8,128)(2,1)S(1)}, u32[]{:S(2)}, u32[]{:S(2)}) collective-permute-start(bf16[96,384]{1,0:T(8,128)(2,1)S(1)} %slice.92), channel_id=1, source_target_pairs={{0,8},{1,9},{2,10},{3,11},{4,12},{5,13},{6,14},{7,15},{8,0},{9,1},... | collective-permute-start | bytes 221192 | tf_op jit(solution)/shard_map/ppermute | solution.py:569
  131.1 1.8 %collective-permute-done.28 = bf16[192,384]{1,0:T(8,128)(2,1)S(1)} collective-permute-done((bf16[192,384]{1,0:T(8,128)(2,1)S(1)}, bf16[192,384]{1,0:T(8,128)(2,1)S(1)}, u32[]{:S(2)}, u32[]{:S(2)}) %collective-permute-start.28) | collective-permute-done | bytes 147488 | tf_op jit(solution)/shard_map/ppermute | solution.py:569
  136.0 4.0 %collective-permute-done.27 = bf16[48,384]{1,0:T(8,128)(2,1)S(1)} collective-permute-done((bf16[48,384]{1,0:T(8,128)(2,1)S(1)}, bf16[48,384]{1,0:T(8,128)(2,1)S(1)}, u32[]{:S(2)}, u32[]{:S(2)}) %collective-permute-start.27) | collective-permute-done | bytes 36896 | tf_op jit(solution)/shard_map/ppermute | solution.py:569
  140.1 3.1 %collective-permute-done.30 = bf16[432,384]{1,0:T(8,128)(2,1)S(1)} collective-permute-done((bf16[432,384]{1,0:T(8,128)(2,1)S(1)}, bf16[432,384]{1,0:T(8,128)(2,1)S(1)}, u32[]{:S(2)}, u32[]{:S(2)}) %collective-permute-start.30) | collective-permute-done | bytes 331808 | tf_op jit(solution)/shard_map/ppermute | solution.py:569
  144.7 3.4 %collective-permute-done.32 = bf16[48,384]{1,0:T(8,128)(2,1)S(1)} collective-permute-done((bf16[48,384]{1,0:T(8,128)(2,1)S(1)}, bf16[48,384]{1,0:T(8,128)(2,1)S(1)}, u32[]{:S(2)}, u32[]{:S(2)}) %collective-permute-start.32) | collective-permute-done | bytes 36896 | tf_op jit(solution)/shard_map/ppermute | solution.py:569
  148.1 3.0 %collective-permute-start.33 = (bf16[96,384]{1,0:T(8,128)(2,1)S(1)}, bf16[96,384]{1,0:T(8,128)(2,1)S(1)}, u32[]{:S(2)}, u32[]{:S(2)}) collective-permute-start(bf16[96,384]{1,0:T(8,128)(2,1)S(1)} %pad_maximum_fusion.7), channel_id=1, source_target_pairs={{0,8},{1,9},{2,10},{3,11},{4,12},{5,13},{6,14},{7,15},{8,0},{9,1},... | collective-permute-start | bytes 221192 | tf_op jit(solution)/shard_map/ppermute | solution.py:569
  151.2 2.3 %collective-permute-done.33 = bf16[96,384]{1,0:T(8,128)(2,1)S(1)} collective-permute-done((bf16[96,384]{1,0:T(8,128)(2,1)S(1)}, bf16[96,384]{1,0:T(8,128)(2,1)S(1)}, u32[]{:S(2)}, u32[]{:S(2)}) %collective-permute-start.33) | collective-permute-done | bytes 73760 | tf_op jit(solution)/shard_map/ppermute | solution.py:569
  157.4 2.7 %spread_mlp.1 = (f32[1536,384]{1,0:T(8,128)}, f32[384,1536]{1,0:T(8,128)}, f32[384,384]{1,0:T(8,128)}, f32[384]{0:T(512)}) custom-call(s32[1]{0:T(128)} %bitcast.mine_ref, bf16[1728,384]{1,0:T(8,128)(2,1)S(1)} %constant_dynamic-update-slice_fusion.5.own, bf16[1728,384]{1,0:T(8,128)(2,1)S(1)} %collective-permute-done.37.other, ...), custom_call_target="tpu_custom_call" | custom-call | flops 4000000000 | bytes 12000000 | tf_op jit(solution)/shard_map/spread_mlp/pallas_call | solution.py:501
  160.6 3.8 %collective-permute-done.35 = bf16[192,384]{1,0:T(8,128)(2,1)S(1)} collective-permute-done((bf16[192,384]{1,0:T(8,128)(2,1)S(1)}, bf16[192,384]{1,0:T(8,128)(2,1)S(1)}, u32[]{:S(2)}, u32[]{:S(2)}) %collective-permute-start.35) | collective-permute-done | bytes 147488 | tf_op jit(solution)/shard_map/ppermute | solution.py:569
  164.7 1.9 %collective-permute-done.38.other = bf16[768,384]{1,0:T(8,128)(2,1)S(1)} collective-permute-done((bf16[768,384]{1,0:T(8,128)(2,1)S(1)}, bf16[768,384]{1,0:T(8,128)(2,1)S(1)}, u32[]{:S(2)}, u32[]{:S(2)}) %collective-permute-start.38) | collective-permute-done | bytes 589856 | tf_op jit(solution)/shard_map/ppermute | solution.py:569
  (194 shorter events, 52.1 us)
Async XLA Ops:
  18.0 15.2 %collective-permute-start = (bf16[64,384]{1,0:T(8,128)(2,1)S(1)}, bf16[64,384]{1,0:T(8,128)(2,1)S(1)}, u32[]{:S(2)}, u32[]{:S(2)}) collective-permute-start(bf16[64,384]{1,0:T(8,128)(2,1)S(1)} %image_tower.1), channel_id=1, source_target_pairs={{0,8},{1,9},{2,10},{3,11},{4,12},{5,13},{6,14},{7,15},{8,0},{9,1},... | collective-permute-start | bytes 147464 | tf_op jit(solution)/shard_map/ppermute | solution.py:569
  21.1 12.1 %collective-permute-start.1 = (bf16[64,384]{1,0:T(8,128)(2,1)S(1)}, bf16[64,384]{1,0:T(8,128)(2,1)S(1)}, u32[]{:S(2)}, u32[]{:S(2)}) collective-permute-start(bf16[64,384]{1,0:T(8,128)(2,1)S(1)} %image_tower.1), channel_id=1, source_target_pairs={{0,16},{1,17},{2,18},{3,19},{4,20},{5,21},{6,22},{7,23},{8,24},{9,... | collective-permute-start | bytes 147464 | tf_op jit(solution)/shard_map/ppermute | solution.py:569
  23.7 9.5 %collective-permute-start.2 = (bf16[64,384]{1,0:T(8,128)(2,1)S(1)}, bf16[64,384]{1,0:T(8,128)(2,1)S(1)}, u32[]{:S(2)}, u32[]{:S(2)}) collective-permute-start(bf16[64,384]{1,0:T(8,128)(2,1)S(1)} %image_tower.1), channel_id=1, source_target_pairs={{0,24},{1,25},{2,26},{3,27},{4,28},{5,29},{6,30},{7,31},{8,16},{9,... | collective-permute-start | bytes 147464 | tf_op jit(solution)/shard_map/ppermute | solution.py:569
  33.3 15.7 %collective-permute-start.3 = (bf16[256,384]{1,0:T(8,128)(2,1)S(1)}, bf16[256,384]{1,0:T(8,128)(2,1)S(1)}, u32[]{:S(2)}, u32[]{:S(2)}) collective-permute-start(bf16[256,384]{1,0:T(8,128)(2,1)S(1)} %pad_maximum_fusion.4), channel_id=1, source_target_pairs={{0,2},{1,3},{2,0},{3,1},{4,6},{5,7},{6,4},{7,5},{8,10},{9,11},{10,... | collective-permute-start | bytes 589832 | tf_op jit(solution)/shard_map/ppermute | solution.py:569
  35.0 14.0 %collective-permute-start.4 = (bf16[256,384]{1,0:T(8,128)(2,1)S(1)}, bf16[256,384]{1,0:T(8,128)(2,1)S(1)}, u32[]{:S(2)}, u32[]{:S(2)}) collective-permute-start(bf16[256,384]{1,0:T(8,128)(2,1)S(1)} %pad_maximum_fusion.4), channel_id=1, source_target_pairs={{0,4},{1,5},{2,6},{3,7},{4,0},{5,1},{6,2},{7,3},{8,12},{9,13},{10,... | collective-permute-start | bytes 589832 | tf_op jit(solution)/shard_map/ppermute | solution.py:569
  36.6 12.5 %collective-permute-start.5 = (bf16[256,384]{1,0:T(8,128)(2,1)S(1)}, bf16[256,384]{1,0:T(8,128)(2,1)S(1)}, u32[]{:S(2)}, u32[]{:S(2)}) collective-permute-start(bf16[256,384]{1,0:T(8,128)(2,1)S(1)} %pad_maximum_fusion.4), channel_id=1, source_target_pairs={{0,6},{1,7},{2,4},{3,5},{4,2},{5,3},{6,0},{7,1},{8,14},{9,15},{10,... | collective-permute-start | bytes 589832 | tf_op jit(solution)/shard_map/ppermute | solution.py:569
  50.6 4.6 %collective-permute-start.6 = (bf16[1024,384]{1,0:T(8,128)(2,1)}, bf16[1024,384]{1,0:T(8,128)(2,1)}, u32[]{:S(2)}, u32[]{:S(2)}) collective-permute-start(bf16[1024,384]{1,0:T(8,128)(2,1)} %pad_maximum_fusion.2), channel_id=1, source_target_pairs={{0,1},{1,0},{2,3},{3,2},{4,5},{5,4},{6,7},{7,6},{8,9},{9,8},{10,11... | collective-permute-start | bytes 2359304 | tf_op jit(solution)/shard_map/ppermute | solution.py:569
  58.7 4.7 %collective-permute-start.10 = (f32[40,128]{1,0:T(8,128)S(1)}, f32[40,128]{1,0:T(8,128)S(1)}, u32[]{:S(2)}, u32[]{:S(2)}) collective-permute-start(f32[40,128]{1,0:T(8,128)S(1)} %add.113), channel_id=1, source_target_pairs={{0,6},{1,7},{2,4},{3,5},{4,2},{5,3},{6,0},{7,1},{8,14},{9,15},{10,... | collective-permute-start | bytes 61448 | tf_op jit(solution)/shard_map/ppermute | solution.py:569
  65.7 3.8 %collective-permute-start.11 = (f32[40,128]{1,0:T(8,128)S(1)}, f32[40,128]{1,0:T(8,128)S(1)}, u32[]{:S(2)}, u32[]{:S(2)}) collective-permute-start(f32[40,128]{1,0:T(8,128)S(1)} %add_add_fusion), channel_id=1, source_target_pairs={{0,8},{1,9},{2,10},{3,11},{4,12},{5,13},{6,14},{7,15},{8,0},{9,1},... | collective-permute-start | bytes 61448 | tf_op jit(solution)/shard_map/ppermute | solution.py:569
  69.5 4.7 %collective-permute-start.12 = (f32[40,128]{1,0:T(8,128)S(1)}, f32[40,128]{1,0:T(8,128)S(1)}, u32[]{:S(2)}, u32[]{:S(2)}) collective-permute-start(f32[40,128]{1,0:T(8,128)S(1)} %add.117), channel_id=1, source_target_pairs={{0,16},{1,17},{2,18},{3,19},{4,20},{5,21},{6,22},{7,23},{8,24},{9,... | collective-permute-start | bytes 61448 | tf_op jit(solution)/shard_map/ppermute | solution.py:569
  76.1 6.2 %collective-permute-start.13 = (bf16[768,384]{1,0:T(8,128)(2,1)S(1)}, bf16[768,384]{1,0:T(8,128)(2,1)S(1)}, u32[]{:S(2)}, u32[]{:S(2)}) collective-permute-start(bf16[768,384]{1,0:T(8,128)(2,1)S(1)} %get-tuple-element.112), channel_id=1, source_target_pairs={{0,1},{1,0},{2,3},{3,2},{4,5},{5,4},{6,7},{7,6},{8,9},{9,8},{10,11... | collective-permute-start | bytes 1769480 | tf_op jit(solution)/shard_map/ppermute | solution.py:569
  76.1 6.1 %collective-permute-start.15 = (bf16[192,384]{1,0:T(8,128)(2,1)S(1)}, bf16[192,384]{1,0:T(8,128)(2,1)S(1)}, u32[]{:S(2)}, u32[]{:S(2)}) collective-permute-start(bf16[192,384]{1,0:T(8,128)(2,1)S(1)} %get-tuple-element.116), channel_id=1, source_target_pairs={{0,1},{1,0},{2,3},{3,2},{4,5},{5,4},{6,7},{7,6},{8,9},{9,8},{10,11... | collective-permute-start | bytes 442376 | tf_op jit(solution)/shard_map/ppermute | solution.py:569
  84.8 12.8 %collective-permute-start.16 = (bf16[432,384]{1,0:T(8,128)(2,1)S(1)}, bf16[432,384]{1,0:T(8,128)(2,1)S(1)}, u32[]{:S(2)}, u32[]{:S(2)}) collective-permute-start(bf16[432,384]{1,0:T(8,128)(2,1)S(1)} %get-tuple-element.166), channel_id=1, source_target_pairs={{0,2},{1,3},{2,0},{3,1},{4,6},{5,7},{6,4},{7,5},{8,10},{9,11},{10,... | collective-permute-start | bytes 995336 | tf_op jit(solution)/shard_map/ppermute | solution.py:569
  86.3 16.7 %collective-permute-start.17 = (bf16[432,384]{1,0:T(8,128)(2,1)S(1)}, bf16[432,384]{1,0:T(8,128)(2,1)S(1)}, u32[]{:S(2)}, u32[]{:S(2)}) collective-permute-start(bf16[432,384]{1,0:T(8,128)(2,1)S(1)} %get-tuple-element.165), channel_id=1, source_target_pairs={{0,4},{1,5},{2,6},{3,7},{4,0},{5,1},{6,2},{7,3},{8,12},{9,13},{10,... | collective-permute-start | bytes 995336 | tf_op jit(solution)/shard_map/ppermute | solution.py:569
  86.8 16.2 %collective-permute-start.18 = (bf16[432,384]{1,0:T(8,128)(2,1)S(1)}, bf16[432,384]{1,0:T(8,128)(2,1)S(1)}, u32[]{:S(2)}, u32[]{:S(2)}) collective-permute-start(bf16[432,384]{1,0:T(8,128)(2,1)S(1)} %get-tuple-element.164), channel_id=1, source_target_pairs={{0,6},{1,7},{2,4},{3,5},{4,2},{5,3},{6,0},{7,1},{8,14},{9,15},{10,... | collective-permute-start | bytes 995336 | tf_op jit(solution)/shard_map/ppermute | solution.py:569
  103.2 5.6 %collective-permute-start.19 = (bf16[240,384]{1,0:T(8,128)(2,1)S(1)}, bf16[240,384]{1,0:T(8,128)(2,1)S(1)}, u32[]{:S(2)}, u32[]{:S(2)}) collective-permute-start(bf16[240,384]{1,0:T(8,128)(2,1)S(1)} %slice.72), channel_id=1, source_target_pairs={{0,8},{1,9},{2,10},{3,11},{4,12},{5,13},{6,14},{7,15},{8,0},{9,1},... | collective-permute-start | bytes 552968 | tf_op jit(solution)/shard_map/ppermute | solution.py:569
  109.0 8.8 %collective-permute-start.20 = (bf16[144,384]{1,0:T(8,128)(2,1)S(1)}, bf16[144,384]{1,0:T(8,128)(2,1)S(1)}, u32[]{:S(2)}, u32[]{:S(2)}) collective-permute-start(bf16[144,384]{1,0:T(8,128)(2,1)S(1)} %slice.87), channel_id=1, source_target_pairs={{0,16},{1,17},{2,18},{3,19},{4,20},{5,21},{6,22},{7,23},{8,24},{9,... | collective-permute-start | bytes 331784 | tf_op jit(solution)/shard_map/ppermute | solution.py:569
  117.9 7.2 %collective-permute-start.25 = (bf16[96,384]{1,0:T(8,128)(2,1)S(1)}, bf16[96,384]{1,0:T(8,128)(2,1)S(1)}, u32[]{:S(2)}, u32[]{:S(2)}) collective-permute-start(bf16[96,384]{1,0:T(8,128)(2,1)S(1)} %slice.90), channel_id=1, source_target_pairs={{0,16},{1,17},{2,18},{3,19},{4,20},{5,21},{6,22},{7,23},{8,24},{9,... | collective-permute-start | bytes 221192 | tf_op jit(solution)/shard_map/ppermute | solution.py:569
  118.1 10.8 %collective-permute-start.22 = (bf16[192,384]{1,0:T(8,128)(2,1)S(1)}, bf16[192,384]{1,0:T(8,128)(2,1)S(1)}, u32[]{:S(2)}, u32[]{:S(2)}) collective-permute-start(bf16[192,384]{1,0:T(8,128)(2,1)S(1)} %get-tuple-element.169), channel_id=1, source_target_pairs={{0,2},{1,3},{2,0},{3,1},{4,6},{5,7},{6,4},{7,5},{8,10},{9,11},{10,... | collective-permute-start | bytes 442376 | tf_op jit(solution)/shard_map/ppermute | solution.py:569
  118.7 10.2 %collective-permute-start.23 = (bf16[192,384]{1,0:T(8,128)(2,1)S(1)}, bf16[192,384]{1,0:T(8,128)(2,1)S(1)}, u32[]{:S(2)}, u32[]{:S(2)}) collective-permute-start(bf16[192,384]{1,0:T(8,128)(2,1)S(1)} %get-tuple-element.168), channel_id=1, source_target_pairs={{0,4},{1,5},{2,6},{3,7},{4,0},{5,1},{6,2},{7,3},{8,12},{9,13},{10,... | collective-permute-start | bytes 442376 | tf_op jit(solution)/shard_map/ppermute | solution.py:569
  120.2 8.8 %collective-permute-start.24 = (bf16[192,384]{1,0:T(8,128)(2,1)S(1)}, bf16[192,384]{1,0:T(8,128)(2,1)S(1)}, u32[]{:S(2)}, u32[]{:S(2)}) collective-permute-start(bf16[192,384]{1,0:T(8,128)(2,1)S(1)} %get-tuple-element.167), channel_id=1, source_target_pairs={{0,6},{1,7},{2,4},{3,5},{4,2},{5,3},{6,0},{7,1},{8,14},{9,15},{10,... | collective-permute-start | bytes 442376 | tf_op jit(solution)/shard_map/ppermute | solution.py:569
  125.1 7.7 %collective-permute-start.28 = (bf16[192,384]{1,0:T(8,128)(2,1)S(1)}, bf16[192,384]{1,0:T(8,128)(2,1)S(1)}, u32[]{:S(2)}, u32[]{:S(2)}) collective-permute-start(bf16[192,384]{1,0:T(8,128)(2,1)S(1)} %pad_maximum_fusion.5), channel_id=1, source_target_pairs={{0,8},{1,9},{2,10},{3,11},{4,12},{5,13},{6,14},{7,15},{8,0},{9,1},... | collective-permute-start | bytes 442376 | tf_op jit(solution)/shard_map/ppermute | solution.py:569
  129.1 5.9 %collective-permute-start.26 = (bf16[96,384]{1,0:T(8,128)(2,1)S(1)}, bf16[96,384]{1,0:T(8,128)(2,1)S(1)}, u32[]{:S(2)}, u32[]{:S(2)}) collective-permute-start(bf16[96,384]{1,0:T(8,128)(2,1)S(1)} %slice.92), channel_id=1, source_target_pairs={{0,8},{1,9},{2,10},{3,11},{4,12},{5,13},{6,14},{7,15},{8,0},{9,1},... | collective-permute-start | bytes 221192 | tf_op jit(solution)/shard_map/ppermute | solution.py:569
  132.9 7.2 %collective-permute-start.29 = (bf16[432,384]{1,0:T(8,128)(2,1)S(1)}, bf16[432,384]{1,0:T(8,128)(2,1)S(1)}, u32[]{:S(2)}, u32[]{:S(2)}) collective-permute-start(bf16[432,384]{1,0:T(8,128)(2,1)S(1)} %pad_maximum_fusion.3), channel_id=1, source_target_pairs={{0,2},{1,3},{2,0},{3,1},{4,6},{5,7},{6,4},{7,5},{8,10},{9,11},{10,... | collective-permute-start | bytes 995336 | tf_op jit(solution)/shard_map/ppermute | solution.py:569
  133.3 10.0 %collective-permute-start.30 = (bf16[432,384]{1,0:T(8,128)(2,1)S(1)}, bf16[432,384]{1,0:T(8,128)(2,1)S(1)}, u32[]{:S(2)}, u32[]{:S(2)}) collective-permute-start(bf16[432,384]{1,0:T(8,128)(2,1)S(1)} %pad_maximum_fusion.3), channel_id=1, source_target_pairs={{0,4},{1,5},{2,6},{3,7},{4,0},{5,1},{6,2},{7,3},{8,12},{9,13},{10,... | collective-permute-start | bytes 995336 | tf_op jit(solution)/shard_map/ppermute | solution.py:569
  135.1 4.9 %collective-permute-start.27 = (bf16[48,384]{1,0:T(8,128)(2,1)S(1)}, bf16[48,384]{1,0:T(8,128)(2,1)S(1)}, u32[]{:S(2)}, u32[]{:S(2)}) collective-permute-start(bf16[48,384]{1,0:T(8,128)(2,1)S(1)} %slice.94), channel_id=1, source_target_pairs={{0,16},{1,17},{2,18},{3,19},{4,20},{5,21},{6,22},{7,23},{8,24},{9,... | collective-permute-start | bytes 110600 | tf_op jit(solution)/shard_map/ppermute | solution.py:569
  143.3 4.9 %collective-permute-start.32 = (bf16[48,384]{1,0:T(8,128)(2,1)S(1)}, bf16[48,384]{1,0:T(8,128)(2,1)S(1)}, u32[]{:S(2)}, u32[]{:S(2)}) collective-permute-start(bf16[48,384]{1,0:T(8,128)(2,1)S(1)} %add_convert_fusion.7), channel_id=1, source_target_pairs={{0,16},{1,17},{2,18},{3,19},{4,20},{5,21},{6,22},{7,23},{8,24},{9,... | collective-permute-start | bytes 110600 | tf_op jit(solution)/shard_map/ppermute | solution.py:569
  143.3 10.3 %collective-permute-start.31 = (bf16[432,384]{1,0:T(8,128)(2,1)S(1)}, bf16[432,384]{1,0:T(8,128)(2,1)S(1)}, u32[]{:S(2)}, u32[]{:S(2)}) collective-permute-start(bf16[432,384]{1,0:T(8,128)(2,1)S(1)} %pad_maximum_fusion.3), channel_id=1, source_target_pairs={{0,6},{1,7},{2,4},{3,5},{4,2},{5,3},{6,0},{7,1},{8,14},{9,15},{10,... | collective-permute-start | bytes 995336 | tf_op jit(solution)/shard_map/ppermute | solution.py:569
  148.1 5.4 %collective-permute-start.33 = (bf16[96,384]{1,0:T(8,128)(2,1)S(1)}, bf16[96,384]{1,0:T(8,128)(2,1)S(1)}, u32[]{:S(2)}, u32[]{:S(2)}) collective-permute-start(bf16[96,384]{1,0:T(8,128)(2,1)S(1)} %pad_maximum_fusion.7), channel_id=1, source_target_pairs={{0,8},{1,9},{2,10},{3,11},{4,12},{5,13},{6,14},{7,15},{8,0},{9,1},... | collective-permute-start | bytes 221192 | tf_op jit(solution)/shard_map/ppermute | solution.py:569
  153.8 6.8 %collective-permute-start.34 = (bf16[192,384]{1,0:T(8,128)(2,1)S(1)}, bf16[192,384]{1,0:T(8,128)(2,1)S(1)}, u32[]{:S(2)}, u32[]{:S(2)}) collective-permute-start(bf16[192,384]{1,0:T(8,128)(2,1)S(1)} %pad_maximum_fusion.6), channel_id=1, source_target_pairs={{0,2},{1,3},{2,0},{3,1},{4,6},{5,7},{6,4},{7,5},{8,10},{9,11},{10,... | collective-permute-start | bytes 442376 | tf_op jit(solution)/shard_map/ppermute | solution.py:569
  155.4 9.1 %collective-permute-start.35 = (bf16[192,384]{1,0:T(8,128)(2,1)S(1)}, bf16[192,384]{1,0:T(8,128)(2,1)S(1)}, u32[]{:S(2)}, u32[]{:S(2)}) collective-permute-start(bf16[192,384]{1,0:T(8,128)(2,1)S(1)} %pad_maximum_fusion.6), channel_id=1, source_target_pairs={{0,4},{1,5},{2,6},{3,7},{4,0},{5,1},{6,2},{7,3},{8,12},{9,13},{10,... | collective-permute-start | bytes 442376 | tf_op jit(solution)/shard_map/ppermute | solution.py:569
  155.9 8.5 %collective-permute-start.36 = (bf16[192,384]{1,0:T(8,128)(2,1)S(1)}, bf16[192,384]{1,0:T(8,128)(2,1)S(1)}, u32[]{:S(2)}, u32[]{:S(2)}) collective-permute-start(bf16[192,384]{1,0:T(8,128)(2,1)S(1)} %pad_maximum_fusion.6), channel_id=1, source_target_pairs={{0,6},{1,7},{2,4},{3,5},{4,2},{5,3},{6,0},{7,1},{8,14},{9,15},{10,... | collective-permute-start | bytes 442376 | tf_op jit(solution)/shard_map/ppermute | solution.py:569
  (48 other events, 248.9 us)

commit v6 on v5

--- a/solution.py
+++ b/solution.py
@@ -119,6 +119,14 @@
         emb_ref[...] = (e * lax.rsqrt(jnp.sum(e * e, -1, keepdims=True) + EPS)).astype(BF)
 
 
+def near(v):
+    return pltpu.with_memory_space_constraint(v, pltpu.VMEM)
+
+
+def away(v):
+    return pltpu.with_memory_space_constraint(v, pltpu.HBM)
+
+
 def cost(us):
     return pl.CostEstimate(flops=int(us * 1e9), bytes_accessed=int(us * 3e6), transcendentals=0)
 
@@ -153,7 +161,7 @@
         compiler_params=ROOM,
         cost_estimate=cost(12),
         name="image_tower",
-    )(x, g1, wqkv, wout, g2, wup, wdown, wproj)
+    )(*[away(v) for v in (x, g1, wqkv, wout, g2, wup, wdown, wproj)])
 
 
 def pair_mask(lab_ref, pair):
@@ -162,10 +170,7 @@
     return wide == wide.T
 
 
-def text_att_kernel(tok_ref, lab_ref, g1, wqkv, o_all, qkv_all, p_all, h1_all):
-    step = pl.program_id(0)
-    o_ref, qkv_ref, h1_ref = o_all.at[held_rows()], qkv_all.at[held_rows()], h1_all.at[held_rows()]
-    p_ref = p_all.at[pl.ds(2 * step, 2)]
+def text_att_kernel(tok_ref, lab_ref, g1, wqkv, o_all, o_ref, qkv_ref, p_ref, h1_ref):
     x = tok_ref[...].astype(F32)
     h1 = (normalize(x) * g1[...].reshape(1, D)).astype(BF)
     h1_ref[...] = h1
@@ -190,14 +195,14 @@
             v22 = jnp.concatenate([jnp.where(low, v2, zero), jnp.where(low, zero, v2)], 0)
             o = mm(jnp.concatenate([p[:PAIR], p[PAIR:]], 1), v22)
             o_ref[rows, cols] = o.astype(BF)
+    o_all[held_rows(), :] = o_ref[...]
 
 
 def text_mlp_kernel(
     tok_ref, o_ref, lab_ref, wout, g2, wup, wdown, wproj,
-    h2_all, c2_all, gp_all, pu_ref, pb_ref, e_ref, emb_ref, cnt_ref, pt, po,
+    h2_ref, c2_ref, gp_ref, pu_ref, pb_ref, e_ref, emb_ref, cnt_ref, pt, po,
 ):
     step = pl.program_id(0)
-    h2_ref, c2_ref, gp_ref = h2_all.at[held_rows()], c2_all.at[held_rows()], gp_all.at[held_rows()]
     tok = tok_ref[...]
     o = o_ref[held_rows(), :]
     x1 = tok.astype(F32) + mm(o, wout[...])
@@ -228,10 +233,6 @@
         emb_ref[...] = (e * lax.rsqrt(jnp.sum(e * e, -1, keepdims=True) + EPS)).astype(BF)
 
 
-def near(v):
-    return pltpu.with_memory_space_constraint(v, pltpu.VMEM)
-
-
 def held_rows():
     return pl.ds(pl.multiple_of(pl.program_id(0) * TOK_BLOCK, TOK_BLOCK), TOK_BLOCK)
 
@@ -251,19 +252,26 @@
 def text_att(tok, lab, g1, wqkv):
     n = tok.shape[0]
     blocks = n // TOK_BLOCK
-    shape = pltpu.VMEM
+    shape = pltpu.HBM
     return pl.pallas_call(
         text_att_kernel,
         grid=(blocks,),
         in_specs=[token_rows(D), block_of(1, TOK_BLOCK), const_spec((D,)), const_spec((D, 3 * D))],
-        out_specs=[VMEM] * 4,
+        out_specs=[
+            VMEM,
+            token_rows(D),
+            token_rows(3 * D),
+            pl.BlockSpec((2, 3, 2 * PAIR, PAIR), lambda i: (i, 0, 0, 0)),
+            token_rows(D),
+        ],
         out_shape=[
-            shape((n, D), BF), shape((n, 3 * D), BF), shape((2 * blocks, 3, 2 * PAIR, PAIR), BF), shape((n, D), BF),
+            pltpu.VMEM((n, D), BF), shape((n, D), BF), shape((n, 3 * D), BF),
+            shape((2 * blocks, 3, 2 * PAIR, PAIR), BF), shape((n, D), BF),
         ],
         compiler_params=ROOM,
         cost_estimate=cost(9),
         name="text_att",
-    )(tok, lab, g1, wqkv)
+    )(away(tok), lab, g1, away(wqkv))
 
 
 def text_mlp(tok, o, lab, wout, g2, wup, wdown, wproj):
@@ -276,9 +284,9 @@
             token_rows(D), VMEM, block_of(1, TOK_BLOCK),
             const_spec((D, D)), const_spec((D,)), const_spec((D, FF)), const_spec((FF, D)), const_spec((D, D)),
         ],
-        out_specs=[VMEM] * 8,
+        out_specs=[token_rows(D), token_rows(D), token_rows(FF)] + [VMEM] * 5,
         out_shape=[
-            shape((n, D), BF), shape((n, D), F32), shape((n, FF), BF),
+            pltpu.HBM((n, D), BF), pltpu.HBM((n, D), F32), pltpu.HBM((n, FF), BF),
             shape((CAPS, FF), F32), shape((CAPS, D), BF), shape((CAPS, D), F32),
             shape((CAPS, D), BF), shape((CAPS, 128), F32),
         ],
@@ -293,10 +301,10 @@
     return jnp.where(mine & 1 == 1, pltpu.roll(row, 64, 1), row)
 
 
-def cosine_kernel(denom, scale_ref, mine_ref, emb, images, pair, g_ref, sum_ref):
+def cosine_kernel(denom, scale_ref, mine_ref, emb, own, other, pair, g_ref, sum_ref):
     mine = mine_ref[0]
     scale = jnp.exp(jnp.full((1, 1), scale_ref[0], F32))
-    g = mm_nt(emb[...], images[...])
+    g = jnp.concatenate([mm_nt(emb[...], own[...]), mm_nt(emb[...], other[...])], 1)
     g_ref[...] = g
     e = jnp.exp(g * scale)
     eg = e * g
@@ -313,14 +321,19 @@
     sum_ref[2 * n :, :] = jnp.where(lane == 0, loss, jnp.where(lane == 1, temp, 0.0))
 
 
-def rows_kernel(denom, scale_ref, g_ref, images, pair, dt_ref):
+def times_images(dl, own, other):
+    half = dl.shape[1] // 2
+    return mm(dl[:, :half], own[...]) + mm(dl[:, half:], other[...])
+
+
+def rows_kernel(denom, scale_ref, g_ref, own, other, pair, dt_ref):
     scale = jnp.exp(jnp.full((1, 1), scale_ref[0], F32))
     g = g_ref[...]
     e = jnp.exp(g * scale)
     hit = lax.broadcasted_iota(jnp.int32, g.shape, 1) == pair[...]
     p = e * (1.0 / jnp.sum(e, -1, keepdims=True))
     dl = jnp.where(hit, p - 2.0, p) * (scale * (1.0 / denom))
-    dt_ref[...] = mm(dl.astype(BF), images[...])
+    dt_ref[...] = times_images(dl.astype(BF), own, other)
 
 
 def quarter(mine, base, k, rows=48):
@@ -344,7 +357,7 @@
 
 
 def head_kernel(
-    denom, scale_ref, mine_ref, g_ref, images, sums, dt_row, e_ref, pb, cnt, pu, wproj, wdown,
+    denom, scale_ref, mine_ref, g_ref, own, other, sums, dt_row, e_ref, pb, cnt, pu, wproj, wdown,
     sd_ref, kd_ref, sp_ref, kp_ref, du_ref, dy_ref, loss_out, temp_out, down, proj,
 ):
     mine = mine_ref[0]
@@ -360,7 +373,7 @@
     temp_out[...] = (sums[2 * n : 2 * n + 1, 1:2] + temp) * (scale * (1.0 / denom))
     inverse = 1.0 / columns(0)
     dl = jnp.exp(g_ref[...] * scale) * (inverse * (scale * (1.0 / denom)))
-    dt = dt_row[...] + mm(dl.astype(BF), images[...])
+    dt = dt_row[...] + times_images(dl.astype(BF), own, other)
     e = e_ref[...]
     r = lax.rsqrt(jnp.sum(e * e, -1, keepdims=True) + EPS)
     de = (dt - e * (r * r * jnp.sum(dt * e, -1, keepdims=True))) * r
@@ -615,18 +628,18 @@
     )
     if tuned:
         near = joined(emb, column([emb] * 4))
-        o, qkv, p, h1 = text_att(text_tokens, lab, txt_ln1, txt_qkv)
-        o, near = lax.optimization_barrier((o, near))
+        o_now, o, qkv, p, h1 = text_att(text_tokens, lab, txt_ln1, txt_qkv)
+        o_now, near = lax.optimization_barrier((o_now, near))
         got = plane([near] * 4)
     else:
-        o, qkv, p, h1 = text_att(text_tokens, lab, txt_ln1, txt_qkv)
-    h2, c2, gp, pu, pb, e, temb, cnt = text_mlp(text_tokens, o, lab, txt_out, txt_ln2, txt_up, txt_down, txt_proj)
+        o_now, o, qkv, p, h1 = text_att(text_tokens, lab, txt_ln1, txt_qkv)
+    h2, c2, gp, pu, pb, e, temb, cnt = text_mlp(text_tokens, o_now, lab, txt_out, txt_ln2, txt_up, txt_down, txt_proj)
     if tuned:
         near, got, temb = lax.optimization_barrier((near, got, temb))
         near = joined(near, got)
-        images = joined(near, [swap(near, 1)])
+        own, other = near, swap(near, 1)
     else:
-        images = lax.all_gather(emb, AXES, axis=0, tiled=True)
+        own, other = jnp.split(lax.all_gather(emb, AXES, axis=0, tiled=True), 2)
     lines = total // 128
     g, sums = simple(
         functools.partial(cosine_kernel, denom),
@@ -634,10 +647,10 @@
         smem=2,
         us=3,
         name="cosine",
-        held=(3,),
-    )(log_scale, mine, temb, images, pair)
-    (dt_row,) = simple(functools.partial(rows_kernel, denom), [((CAPS, D), F32)], smem=1, us=2, name="rows", held=(2,))(
-        log_scale, g, images, pair
+        held=(3, 4),
+    )(log_scale, mine, temb, own, other, pair)
+    (dt_row,) = simple(functools.partial(rows_kernel, denom), [((CAPS, D), F32)], smem=1, us=2, name="rows", held=(2, 3))(
+        log_scale, g, own, other, pair
     )
     if tuned:
         sums = total_of(sums, [swap(sums, 1)])
@@ -656,8 +669,8 @@
         smem=2,
         us=5,
         name="head_back",
-        held=(3, 4),
-    )(log_scale, mine, g, images, sums, dt_row, e, pb, cnt, pu, txt_proj, txt_down)
+        held=(3, 4, 5),
+    )(log_scale, mine, g, own, other, sums, dt_row, e, pb, cnt, pu, txt_proj, txt_down)
     dx, dxb, send_u, keep_u = mlp_back(mine, lab, h2, gp, c2, du, dy, txt_ln2, txt_up)
 
     def mlp_parts(d, u, p):

time: 171 us -> 159 us (0.930)
  local copies, waits for them, and re-layouts: 22.2 us -> 1.58 us
  Pallas kernels: 50.3 us -> 59.5 us
  waiting for transfers between devices: 46.4 us -> 48.3 us
    unnamed x95 -> x66, local copies, waits for them, and re-layouts: 20.4 us -> 1.05 us
    pallas_call x6, Pallas kernels: 9.3 us -> 12.9 us  [call(): pl.pallas_call(kernel, in_specs=[SMEM] * smem + [VMEM] * (len(args) - sme...]
    pallas_call x1, Pallas kernels: 5.54 us -> 7.86 us  [text_att(): pl.pallas_call(text_att_kernel, grid=(blocks,), in_specs=[token_rows(D),...]
    pallas_call x1, Pallas kernels: 8.66 us -> 10.8 us  [image_tower(): pl.pallas_call(image_kernel, grid=(count // IMG_BLOCK,), in_specs=[pl.Blo...]
    ppermute x39, waiting for transfers between devices: 46.4 us -> 48.3 us  [swap(): return lax.ppermute(v, AXES, [(i, i ^ mask) for i in range(32)])]
  transfers between devices with their start and end apart: 39 -> 39, of which waited for: 19 -> 20; matrix products, arithmetic and copies ran while one was open for 3% -> 1% of each run, Pallas kernels for 22% -> 27%
where the time goes in v6:
time: 159 us; the launch traced here: 158 us
  Pallas kernels  59.5 us (37%)
  waiting for transfers between devices  48.3 us (30%)
  starting transfers between devices  43.3 us (27%)
  between operations  4.32 us (3%)
    ppermute x39, waiting for transfers between devices, swap(): return lax.ppermute(v, AXES, [(i, i ^ mask) for i in range(32)])  48.3 us
    ppermute x39, starting transfers between devices, swap(): return lax.ppermute(v, AXES, [(i, i ^ mask) for i in range(32)])  43.3 us
    pallas_call x6, Pallas kernels, call(): pl.pallas_call(kernel, in_specs=[SMEM] * smem + [VMEM] * (len(args) - sme...  12.9 us
    pallas_call x1, Pallas kernels, image_tower(): pl.pallas_call(image_kernel, grid=(count // IMG_BLOCK,), in_specs=[pl.Blo...  10.8 us
    pallas_call x1, Pallas kernels, text_mlp(): pl.pallas_call(text_mlp_kernel, grid=(n // TOK_BLOCK,), in_specs=[token_r...  10 us
    pallas_call x1, Pallas kernels, att_core(): pl.pallas_call(att_core_kernel, grid=(n // TOK_BLOCK,), in_specs=[VMEM, V...  9.2 us
    pallas_call x1, Pallas kernels, text_att(): pl.pallas_call(text_att_kernel, grid=(blocks,), in_specs=[token_rows(D),...  7.86 us
    pallas_call x1, Pallas kernels, mlp_back(): pl.pallas_call(mlp_back_kernel, grid=(n // TOK_BLOCK,), in_specs=[SMEM, b...  5.36 us
  transfers between devices with their start and end apart: 39, of which 20 were waited for; matrix products, arithmetic and copies ran while one was open for 1% of the time, Pallas kernels for 27%

profile of v6, /device:TPU:0, one launch (start us, length us, event | category | flops | bytes accessed | tf_op | source)
XLA Modules:
  0.0 158.4 jit_solution(15380737290718524454)
XLA Ops:
  0.7 10.8 %image_tower.1 = bf16[64,384]{1,0:T(8,128)(2,1)S(1)} custom-call(bf16[50,64,384]{2,1,0:T(8,128)(2,1)} %bitcast.35, f32[384]{0:T(512)} %g1.5, bf16[384,1152]{1,0:T(8,128)(2,1)} %wqkv.5, bf16[384,384]{1,0:T(8,128)(2,1)} %wout.3, f32[384]{0:T(512)} %g2.4, bf16[384,1536]{1,0:T(8,128)(2,1)} %wup.4, bf16[1536,384]{1,0:T(8,128)(2,1)} %wdown.3, bf16[384,384]{1,0:T(8,128)(2,1)} %wproj.3), custom_call_target="tpu_custom_call" | custom-call | flops 12000000000 | bytes 36000000 | tf_op jit(solution)/shard_map/image_tower/pallas_call | solution.py:141
  11.5 3.1 %collective-permute-start = (bf16[64,384]{1,0:T(8,128)(2,1)S(1)}, bf16[64,384]{1,0:T(8,128)(2,1)S(1)}, u32[]{:S(2)}, u32[]{:S(2)}) collective-permute-start(bf16[64,384]{1,0:T(8,128)(2,1)S(1)} %image_tower.1), channel_id=1, source_target_pairs={{0,8},{1,9},{2,10},{3,11},{4,12},{5,13},{6,14},{7,15},{8,0},{9,1},... | collective-permute-start | bytes 147464 | tf_op jit(solution)/shard_map/ppermute | solution.py:582
  14.6 2.6 %collective-permute-start.1 = (bf16[64,384]{1,0:T(8,128)(2,1)S(1)}, bf16[64,384]{1,0:T(8,128)(2,1)S(1)}, u32[]{:S(2)}, u32[]{:S(2)}) collective-permute-start(bf16[64,384]{1,0:T(8,128)(2,1)S(1)} %image_tower.1), channel_id=1, source_target_pairs={{0,16},{1,17},{2,18},{3,19},{4,20},{5,21},{6,22},{7,23},{8,24},{9,... | collective-permute-start | bytes 147464 | tf_op jit(solution)/shard_map/ppermute | solution.py:582
  17.4 7.9 %text_att.1 = (bf16[1024,384]{1,0:T(8,128)(2,1)S(1)}, bf16[1024,384]{1,0:T(8,128)(2,1)}, bf16[1024,1152]{1,0:T(8,128)(2,1)}, bf16[8,3,256,128]{3,2,1,0:T(8,128)(2,1)}, bf16[1024,384]{1,0:T(8,128)(2,1)}) custom-call(bf16[1024,384]{1,0:T(8,128)(2,1)} %tok_ref.5, s32[4,1,256]{2,1,0:T(1,128)S(1)} %reshape.67.lab_ref, f32[384]{0:T(512)S(1)} %copy-done.9, ...), custom_call_target="tpu_custom_call" | custom-call | flops 8999999488 | bytes 27000000 | tf_op jit(solution)/shard_map/text_att/pallas_call | solution.py:256
  25.3 1.8 %collective-permute-start.3 = (bf16[256,384]{1,0:T(8,128)(2,1)S(1)}, bf16[256,384]{1,0:T(8,128)(2,1)S(1)}, u32[]{:S(2)}, u32[]{:S(2)}) collective-permute-start(bf16[256,384]{1,0:T(8,128)(2,1)S(1)} %pad_maximum_fusion.3), channel_id=1, source_target_pairs={{0,2},{1,3},{2,0},{3,1},{4,6},{5,7},{6,4},{7,5},{8,10},{9,11},{10,... | collective-permute-start | bytes 589832 | tf_op jit(solution)/shard_map/ppermute | solution.py:582
  28.9 10.0 %text_mlp.1 = (bf16[1024,384]{1,0:T(8,128)(2,1)}, f32[1024,384]{1,0:T(8,128)}, bf16[1024,1536]{1,0:T(8,128)(2,1)}, f32[64,1536]{1,0:T(8,128)S(1)}, bf16[64,384]{...) custom-call(bf16[1024,384]{1,0:T(8,128)(2,1)S(1)} %copy-done.3, ...), custom_call_target="tpu_custom_call" | custom-call | flops 11000000512 | bytes 33000000 | tf_op jit(solution)/shard_map/text_mlp/pallas_call | solution.py:280
  42.2 1.9 %cosine.1 = (f32[64,2048]{1,0:T(8,128)S(1)}, f32[40,128]{1,0:T(8,128)S(1)}) custom-call(f32[1]{0:T(128)S(6)} %copy.45.scale_ref, s32[1]{0:T(128)} %bitcast.mine_ref, bf16[64,384]{1,0:T(8,128)(2,1)S(1)} %get-tuple-element.93.emb, bf16[1024,384]{1,0:T(8,128)(2,1)S(1)} %constant_dynamic-update-slice_fusion.own, bf16[1024,384]{1,0:T(8,128)(2,1)} %collective-permute-done.6.other, ...), custom_call_target="tpu_custom_call" | custom-call | flops 3000000000 | bytes 9000000 | tf_op jit(solution)/shard_map/cosine/pallas_call | solution.py:514
  45.3 2.7 %collective-permute-start.10 = (f32[40,128]{1,0:T(8,128)S(1)}, f32[40,128]{1,0:T(8,128)S(1)}, u32[]{:S(2)}, u32[]{:S(2)}) collective-permute-start(f32[40,128]{1,0:T(8,128)S(1)} %add.113), channel_id=1, source_target_pairs={{0,6},{1,7},{2,4},{3,5},{4,2},{5,3},{6,0},{7,1},{8,14},{9,15},{10,... | collective-permute-start | bytes 61448 | tf_op jit(solution)/shard_map/ppermute | solution.py:582
  50.0 1.8 %collective-permute-done.8 = f32[40,128]{1,0:T(8,128)S(1)} collective-permute-done((f32[40,128]{1,0:T(8,128)S(1)}, f32[40,128]{1,0:T(8,128)S(1)}, u32[]{:S(2)}, u32[]{:S(2)}) %collective-permute-start.8) | collective-permute-done | bytes 20512 | tf_op jit(solution)/shard_map/ppermute | solution.py:582
  53.1 3.1 %collective-permute-done.11 = f32[40,128]{1,0:T(8,128)S(1)} collective-permute-done((f32[40,128]{1,0:T(8,128)S(1)}, f32[40,128]{1,0:T(8,128)S(1)}, u32[]{:S(2)}, u32[]{:S(2)}) %collective-permute-start.11) | collective-permute-done | bytes 20512 | tf_op jit(solution)/shard_map/ppermute | solution.py:582
  56.1 2.2 %collective-permute-start.12 = (f32[40,128]{1,0:T(8,128)S(1)}, f32[40,128]{1,0:T(8,128)S(1)}, u32[]{:S(2)}, u32[]{:S(2)}) collective-permute-start(f32[40,128]{1,0:T(8,128)S(1)} %add.117), channel_id=1, source_target_pairs={{0,16},{1,17},{2,18},{3,19},{4,20},{5,21},{6,22},{7,23},{8,24},{9,... | collective-permute-start | bytes 61448 | tf_op jit(solution)/shard_map/ppermute | solution.py:582
  60.9 3.1 %head_back.1 = (bf16[768,384]{1,0:T(8,128)(2,1)S(1)}, bf16[768,384]{1,0:T(8,128)(2,1)S(1)}, bf16[192,384]{1,0:T(8,128)(2,1)S(1)}, bf16[192,384]{1,0:T(8,128)(2,1...) custom-call(f32[1]{0:T(128)S(6)} %copy.45.scale_ref, ...), custom_call_target="tpu_custom_call" | custom-call | flops 5000000000 | bytes 15000000 | tf_op jit(solution)/shard_map/head_back/pallas_call | solution.py:514
  64.6 5.4 %mlp_back.1 = (f32[1024,384]{1,0:T(8,128)S(1)}, bf16[1024,384]{1,0:T(8,128)(2,1)S(1)}, bf16[768,384]{1,0:T(8,128)(2,1)S(1)}, bf16[768,384]{1,0:T(8,128)(2,1)S(1)}) custom-call(s32[1]{0:T(128)} %bitcast.mine_ref, s32[4,1,256]{2,1,0:T(1,128)S(1)} %reshape.67.lab_ref, bf16[1024,384]{1,0:T(8,128)(2,1)S(1)} %copy-done.18, bf16[1024,1536]{1,0:T(8,128)(2,1)S(1)} %copy-done.12, ...), custom_call_target="tpu_custom_call" | custom-call | flops 8999999488 | bytes 27000000 | tf_op jit(solution)/shard_map/mlp_back/pallas_call | solution.py:531
  76.2 9.2 %att_core.1.dqkv_ref.dqkv_all = bf16[1024,1152]{1,0:T(8,128)(2,1)S(1)} custom-call(bf16[1024,1152]{1,0:T(8,128)(2,1)S(1)} %copy-done.13, bf16[8,3,256,128]{3,2,1,0:T(8,128)(2,1)S(1)} %copy-done.17, bf16[1024,384]{1,0:T(8,128)(2,1)S(1)} %get-tuple-element.121.dxb_all.dxb_ref, bf16[384,384]{1,0:T(8,128)(2,1)S(1)} %copy-done.7), custom_call_target="tpu_custom_call" | custom-call | flops 10000000000 | bytes 30000000 | tf_op jit(solution)/shard_map/att_core/pallas_call | solution.py:546
  85.4 5.4 %collective-permute-done.17 = bf16[432,384]{1,0:T(8,128)(2,1)S(1)} collective-permute-done((bf16[432,384]{1,0:T(8,128)(2,1)S(1)}, bf16[432,384]{1,0:T(8,128)(2,1)S(1)}, u32[]{:S(2)}, u32[]{:S(2)}) %collective-permute-start.17) | collective-permute-done | bytes 331808 | tf_op jit(solution)/shard_map/ppermute | solution.py:582
  92.4 1.8 %att_grads.1 = (bf16[768,384]{1,0:T(8,128)(2,1)S(1)}, bf16[768,384]{1,0:T(8,128)(2,1)S(1)}) custom-call(s32[1]{0:T(128)} %bitcast.mine_ref, bf16[1024,384]{1,0:T(8,128)(2,1)S(1)} %copy-done.11, bf16[1024,1152]{1,0:T(8,128)(2,1)S(1)} %att_core.1.dqkv_ref.dqkv_all, bf16[1024,384]{1,0:T(8,128)(2,1)S(1)} %copy-done.10, ...), custom_call_target="tpu_custom_call" | custom-call | flops 4000000000 | bytes 12000000 | tf_op jit(solution)/shard_map/att_grads/pallas_call | solution.py:514
  94.2 2.5 %collective-permute-done.19 = bf16[240,384]{1,0:T(8,128)(2,1)S(1)} collective-permute-done((bf16[240,384]{1,0:T(8,128)(2,1)S(1)}, bf16[240,384]{1,0:T(8,128)(2,1)S(1)}, u32[]{:S(2)}, u32[]{:S(2)}) %collective-permute-start.19) | collective-permute-done | bytes 184352 | tf_op jit(solution)/shard_map/ppermute | solution.py:582
  96.8 2.5 %collective-permute-start.20 = (bf16[144,384]{1,0:T(8,128)(2,1)S(1)}, bf16[144,384]{1,0:T(8,128)(2,1)S(1)}, u32[]{:S(2)}, u32[]{:S(2)}) collective-permute-start(bf16[144,384]{1,0:T(8,128)(2,1)S(1)} %slice.87), channel_id=1, source_target_pairs={{0,16},{1,17},{2,18},{3,19},{4,20},{5,21},{6,22},{7,23},{8,24},{9,... | collective-permute-start | bytes 331784 | tf_op jit(solution)/shard_map/ppermute | solution.py:582
  99.5 6.1 %collective-permute-done.20 = bf16[144,384]{1,0:T(8,128)(2,1)S(1)} collective-permute-done((bf16[144,384]{1,0:T(8,128)(2,1)S(1)}, bf16[144,384]{1,0:T(8,128)(2,1)S(1)}, u32[]{:S(2)}, u32[]{:S(2)}) %collective-permute-start.20) | collective-permute-done | bytes 110624 | tf_op jit(solution)/shard_map/ppermute | solution.py:582
  109.5 3.4 %tok_back.1 = f32[1024,384]{1,0:T(8,128)} custom-call(bf16[1024,384]{1,0:T(8,128)(2,1)S(1)} %copy-done.4, bf16[1024,1152]{1,0:T(8,128)(2,1)S(1)} %att_core.1.dqkv_ref.dqkv_all, f32[1024,384]{1,0:T(8,128)S(1)} %get-tuple-element.138.dx_all, f32[384]{0:T(512)S(1)} %copy-done.9, bf16[384,1152]{1,0:T(8,128)(2,1)S(1)} %copy-done.2), custom_call_target="tpu_custom_call" | custom-call | flops 4000000000 | bytes 12000000 | tf_op jit(solution)/shard_map/tok_back/pallas_call | solution.py:566
  113.0 3.8 %collective-permute-start.28 = (bf16[192,384]{1,0:T(8,128)(2,1)S(1)}, bf16[192,384]{1,0:T(8,128)(2,1)S(1)}, u32[]{:S(2)}, u32[]{:S(2)}) collective-permute-start(bf16[192,384]{1,0:T(8,128)(2,1)S(1)} %pad_maximum_fusion.4), channel_id=1, source_target_pairs={{0,8},{1,9},{2,10},{3,11},{4,12},{5,13},{6,14},{7,15},{8,0},{9,1},... | collective-permute-start | bytes 442376 | tf_op jit(solution)/shard_map/ppermute | solution.py:582
  116.9 2.0 %collective-permute-start.26 = (bf16[96,384]{1,0:T(8,128)(2,1)S(1)}, bf16[96,384]{1,0:T(8,128)(2,1)S(1)}, u32[]{:S(2)}, u32[]{:S(2)}) collective-permute-start(bf16[96,384]{1,0:T(8,128)(2,1)S(1)} %slice.92), channel_id=1, source_target_pairs={{0,8},{1,9},{2,10},{3,11},{4,12},{5,13},{6,14},{7,15},{8,0},{9,1},... | collective-permute-start | bytes 221192 | tf_op jit(solution)/shard_map/ppermute | solution.py:582
  118.9 1.8 %collective-permute-done.28 = bf16[192,384]{1,0:T(8,128)(2,1)S(1)} collective-permute-done((bf16[192,384]{1,0:T(8,128)(2,1)S(1)}, bf16[192,384]{1,0:T(8,128)(2,1)S(1)}, u32[]{:S(2)}, u32[]{:S(2)}) %collective-permute-start.28) | collective-permute-done | bytes 147488 | tf_op jit(solution)/shard_map/ppermute | solution.py:582
  121.2 1.7 %collective-permute-start.30 = (bf16[432,384]{1,0:T(8,128)(2,1)S(1)}, bf16[432,384]{1,0:T(8,128)(2,1)S(1)}, u32[]{:S(2)}, u32[]{:S(2)}) collective-permute-start(bf16[432,384]{1,0:T(8,128)(2,1)S(1)} %pad_maximum_fusion.2), channel_id=1, source_target_pairs={{0,4},{1,5},{2,6},{3,7},{4,0},{5,1},{6,2},{7,3},{8,12},{9,13},{10,... | collective-permute-start | bytes 995336 | tf_op jit(solution)/shard_map/ppermute | solution.py:582
  123.8 4.0 %collective-permute-done.27 = bf16[48,384]{1,0:T(8,128)(2,1)S(1)} collective-permute-done((bf16[48,384]{1,0:T(8,128)(2,1)S(1)}, bf16[48,384]{1,0:T(8,128)(2,1)S(1)}, u32[]{:S(2)}, u32[]{:S(2)}) %collective-permute-start.27) | collective-permute-done | bytes 36896 | tf_op jit(solution)/shard_map/ppermute | solution.py:582
  128.0 3.1 %collective-permute-done.30 = bf16[432,384]{1,0:T(8,128)(2,1)S(1)} collective-permute-done((bf16[432,384]{1,0:T(8,128)(2,1)S(1)}, bf16[432,384]{1,0:T(8,128)(2,1)S(1)}, u32[]{:S(2)}, u32[]{:S(2)}) %collective-permute-start.30) | collective-permute-done | bytes 331808 | tf_op jit(solution)/shard_map/ppermute | solution.py:582
  131.1 4.9 %collective-permute-done.32 = bf16[48,384]{1,0:T(8,128)(2,1)S(1)} collective-permute-done((bf16[48,384]{1,0:T(8,128)(2,1)S(1)}, bf16[48,384]{1,0:T(8,128)(2,1)S(1)}, u32[]{:S(2)}, u32[]{:S(2)}) %collective-permute-start.32) | collective-permute-done | bytes 36896 | tf_op jit(solution)/shard_map/ppermute | solution.py:582
  136.0 3.0 %collective-permute-start.33 = (bf16[96,384]{1,0:T(8,128)(2,1)S(1)}, bf16[96,384]{1,0:T(8,128)(2,1)S(1)}, u32[]{:S(2)}, u32[]{:S(2)}) collective-permute-start(bf16[96,384]{1,0:T(8,128)(2,1)S(1)} %pad_maximum_fusion.6), channel_id=1, source_target_pairs={{0,8},{1,9},{2,10},{3,11},{4,12},{5,13},{6,14},{7,15},{8,0},{9,1},... | collective-permute-start | bytes 221192 | tf_op jit(solution)/shard_map/ppermute | solution.py:582
  139.0 2.3 %collective-permute-done.33 = bf16[96,384]{1,0:T(8,128)(2,1)S(1)} collective-permute-done((bf16[96,384]{1,0:T(8,128)(2,1)S(1)}, bf16[96,384]{1,0:T(8,128)(2,1)S(1)}, u32[]{:S(2)}, u32[]{:S(2)}) %collective-permute-start.33) | collective-permute-done | bytes 73760 | tf_op jit(solution)/shard_map/ppermute | solution.py:582
  145.2 2.7 %spread_mlp.1 = (f32[1536,384]{1,0:T(8,128)}, f32[384,1536]{1,0:T(8,128)}, f32[384,384]{1,0:T(8,128)}, f32[384]{0:T(512)}) custom-call(s32[1]{0:T(128)} %bitcast.mine_ref, bf16[1728,384]{1,0:T(8,128)(2,1)S(1)} %constant_dynamic-update-slice_fusion.4.own, bf16[1728,384]{1,0:T(8,128)(2,1)S(1)} %collective-permute-done.37.other, ...), custom_call_target="tpu_custom_call" | custom-call | flops 4000000000 | bytes 12000000 | tf_op jit(solution)/shard_map/spread_mlp/pallas_call | solution.py:514
  148.4 3.8 %collective-permute-done.35 = bf16[192,384]{1,0:T(8,128)(2,1)S(1)} collective-permute-done((bf16[192,384]{1,0:T(8,128)(2,1)S(1)}, bf16[192,384]{1,0:T(8,128)(2,1)S(1)}, u32[]{:S(2)}, u32[]{:S(2)}) %collective-permute-start.35) | collective-permute-done | bytes 147488 | tf_op jit(solution)/shard_map/ppermute | solution.py:582
  152.5 1.9 %collective-permute-done.38.other = bf16[768,384]{1,0:T(8,128)(2,1)S(1)} collective-permute-done((bf16[768,384]{1,0:T(8,128)(2,1)S(1)}, bf16[768,384]{1,0:T(8,128)(2,1)S(1)}, u32[]{:S(2)}, u32[]{:S(2)}) %collective-permute-start.38) | collective-permute-done | bytes 589856 | tf_op jit(solution)/shard_map/ppermute | solution.py:582
  (164 shorter events, 31.8 us)
Async XLA Ops:
  11.5 13.8 %collective-permute-start = (bf16[64,384]{1,0:T(8,128)(2,1)S(1)}, bf16[64,384]{1,0:T(8,128)(2,1)S(1)}, u32[]{:S(2)}, u32[]{:S(2)}) collective-permute-start(bf16[64,384]{1,0:T(8,128)(2,1)S(1)} %image_tower.1), channel_id=1, source_target_pairs={{0,8},{1,9},{2,10},{3,11},{4,12},{5,13},{6,14},{7,15},{8,0},{9,1},... | collective-permute-start | bytes 147464 | tf_op jit(solution)/shard_map/ppermute | solution.py:582
  14.6 10.7 %collective-permute-start.1 = (bf16[64,384]{1,0:T(8,128)(2,1)S(1)}, bf16[64,384]{1,0:T(8,128)(2,1)S(1)}, u32[]{:S(2)}, u32[]{:S(2)}) collective-permute-start(bf16[64,384]{1,0:T(8,128)(2,1)S(1)} %image_tower.1), channel_id=1, source_target_pairs={{0,16},{1,17},{2,18},{3,19},{4,20},{5,21},{6,22},{7,23},{8,24},{9,... | collective-permute-start | bytes 147464 | tf_op jit(solution)/shard_map/ppermute | solution.py:582
  17.2 8.2 %collective-permute-start.2 = (bf16[64,384]{1,0:T(8,128)(2,1)S(1)}, bf16[64,384]{1,0:T(8,128)(2,1)S(1)}, u32[]{:S(2)}, u32[]{:S(2)}) collective-permute-start(bf16[64,384]{1,0:T(8,128)(2,1)S(1)} %image_tower.1), channel_id=1, source_target_pairs={{0,24},{1,25},{2,26},{3,27},{4,28},{5,29},{6,30},{7,31},{8,16},{9,... | collective-permute-start | bytes 147464 | tf_op jit(solution)/shard_map/ppermute | solution.py:582
  25.3 13.6 %collective-permute-start.3 = (bf16[256,384]{1,0:T(8,128)(2,1)S(1)}, bf16[256,384]{1,0:T(8,128)(2,1)S(1)}, u32[]{:S(2)}, u32[]{:S(2)}) collective-permute-start(bf16[256,384]{1,0:T(8,128)(2,1)S(1)} %pad_maximum_fusion.3), channel_id=1, source_target_pairs={{0,2},{1,3},{2,0},{3,1},{4,6},{5,7},{6,4},{7,5},{8,10},{9,11},{10,... | collective-permute-start | bytes 589832 | tf_op jit(solution)/shard_map/ppermute | solution.py:582
  27.1 11.8 %collective-permute-start.4 = (bf16[256,384]{1,0:T(8,128)(2,1)S(1)}, bf16[256,384]{1,0:T(8,128)(2,1)S(1)}, u32[]{:S(2)}, u32[]{:S(2)}) collective-permute-start(bf16[256,384]{1,0:T(8,128)(2,1)S(1)} %pad_maximum_fusion.3), channel_id=1, source_target_pairs={{0,4},{1,5},{2,6},{3,7},{4,0},{5,1},{6,2},{7,3},{8,12},{9,13},{10,... | collective-permute-start | bytes 589832 | tf_op jit(solution)/shard_map/ppermute | solution.py:582
  28.6 10.3 %collective-permute-start.5 = (bf16[256,384]{1,0:T(8,128)(2,1)S(1)}, bf16[256,384]{1,0:T(8,128)(2,1)S(1)}, u32[]{:S(2)}, u32[]{:S(2)}) collective-permute-start(bf16[256,384]{1,0:T(8,128)(2,1)S(1)} %pad_maximum_fusion.3), channel_id=1, source_target_pairs={{0,6},{1,7},{2,4},{3,5},{4,2},{5,3},{6,0},{7,1},{8,14},{9,15},{10,... | collective-permute-start | bytes 589832 | tf_op jit(solution)/shard_map/ppermute | solution.py:582
  45.3 4.7 %collective-permute-start.10 = (f32[40,128]{1,0:T(8,128)S(1)}, f32[40,128]{1,0:T(8,128)S(1)}, u32[]{:S(2)}, u32[]{:S(2)}) collective-permute-start(f32[40,128]{1,0:T(8,128)S(1)} %add.113), channel_id=1, source_target_pairs={{0,6},{1,7},{2,4},{3,5},{4,2},{5,3},{6,0},{7,1},{8,14},{9,15},{10,... | collective-permute-start | bytes 61448 | tf_op jit(solution)/shard_map/ppermute | solution.py:582
  48.5 3.8 %collective-permute-start.9 = (f32[40,128]{1,0:T(8,128)S(1)}, f32[40,128]{1,0:T(8,128)S(1)}, u32[]{:S(2)}, u32[]{:S(2)}) collective-permute-start(f32[40,128]{1,0:T(8,128)S(1)} %add.113), channel_id=1, source_target_pairs={{0,4},{1,5},{2,6},{3,7},{4,0},{5,1},{6,2},{7,3},{8,12},{9,13},{10,... | collective-permute-start | bytes 61448 | tf_op jit(solution)/shard_map/ppermute | solution.py:582
  52.3 3.8 %collective-permute-start.11 = (f32[40,128]{1,0:T(8,128)S(1)}, f32[40,128]{1,0:T(8,128)S(1)}, u32[]{:S(2)}, u32[]{:S(2)}) collective-permute-start(f32[40,128]{1,0:T(8,128)S(1)} %add_add_fusion), channel_id=1, source_target_pairs={{0,8},{1,9},{2,10},{3,11},{4,12},{5,13},{6,14},{7,15},{8,0},{9,1},... | collective-permute-start | bytes 61448 | tf_op jit(solution)/shard_map/ppermute | solution.py:582
  56.1 4.7 %collective-permute-start.12 = (f32[40,128]{1,0:T(8,128)S(1)}, f32[40,128]{1,0:T(8,128)S(1)}, u32[]{:S(2)}, u32[]{:S(2)}) collective-permute-start(f32[40,128]{1,0:T(8,128)S(1)} %add.117), channel_id=1, source_target_pairs={{0,16},{1,17},{2,18},{3,19},{4,20},{5,21},{6,22},{7,23},{8,24},{9,... | collective-permute-start | bytes 61448 | tf_op jit(solution)/shard_map/ppermute | solution.py:582
  64.0 6.1 %collective-permute-start.13 = (bf16[768,384]{1,0:T(8,128)(2,1)S(1)}, bf16[768,384]{1,0:T(8,128)(2,1)S(1)}, u32[]{:S(2)}, u32[]{:S(2)}) collective-permute-start(bf16[768,384]{1,0:T(8,128)(2,1)S(1)} %get-tuple-element.113), channel_id=1, source_target_pairs={{0,1},{1,0},{2,3},{3,2},{4,5},{5,4},{6,7},{7,6},{8,9},{9,8},{10,11... | collective-permute-start | bytes 1769480 | tf_op jit(solution)/shard_map/ppermute | solution.py:582
  64.1 6.0 %collective-permute-start.15 = (bf16[192,384]{1,0:T(8,128)(2,1)S(1)}, bf16[192,384]{1,0:T(8,128)(2,1)S(1)}, u32[]{:S(2)}, u32[]{:S(2)}) collective-permute-start(bf16[192,384]{1,0:T(8,128)(2,1)S(1)} %get-tuple-element.117), channel_id=1, source_target_pairs={{0,1},{1,0},{2,3},{3,2},{4,5},{5,4},{6,7},{7,6},{8,9},{9,8},{10,11... | collective-permute-start | bytes 442376 | tf_op jit(solution)/shard_map/ppermute | solution.py:582
  72.6 12.8 %collective-permute-start.16 = (bf16[432,384]{1,0:T(8,128)(2,1)S(1)}, bf16[432,384]{1,0:T(8,128)(2,1)S(1)}, u32[]{:S(2)}, u32[]{:S(2)}) collective-permute-start(bf16[432,384]{1,0:T(8,128)(2,1)S(1)} %get-tuple-element.168), channel_id=1, source_target_pairs={{0,2},{1,3},{2,0},{3,1},{4,6},{5,7},{6,4},{7,5},{8,10},{9,11},{10,... | collective-permute-start | bytes 995336 | tf_op jit(solution)/shard_map/ppermute | solution.py:582
  74.2 16.7 %collective-permute-start.17 = (bf16[432,384]{1,0:T(8,128)(2,1)S(1)}, bf16[432,384]{1,0:T(8,128)(2,1)S(1)}, u32[]{:S(2)}, u32[]{:S(2)}) collective-permute-start(bf16[432,384]{1,0:T(8,128)(2,1)S(1)} %get-tuple-element.167), channel_id=1, source_target_pairs={{0,4},{1,5},{2,6},{3,7},{4,0},{5,1},{6,2},{7,3},{8,12},{9,13},{10,... | collective-permute-start | bytes 995336 | tf_op jit(solution)/shard_map/ppermute | solution.py:582
  74.7 16.2 %collective-permute-start.18 = (bf16[432,384]{1,0:T(8,128)(2,1)S(1)}, bf16[432,384]{1,0:T(8,128)(2,1)S(1)}, u32[]{:S(2)}, u32[]{:S(2)}) collective-permute-start(bf16[432,384]{1,0:T(8,128)(2,1)S(1)} %get-tuple-element.166), channel_id=1, source_target_pairs={{0,6},{1,7},{2,4},{3,5},{4,2},{5,3},{6,0},{7,1},{8,14},{9,15},{10,... | collective-permute-start | bytes 995336 | tf_op jit(solution)/shard_map/ppermute | solution.py:582
  91.1 5.6 %collective-permute-start.19 = (bf16[240,384]{1,0:T(8,128)(2,1)S(1)}, bf16[240,384]{1,0:T(8,128)(2,1)S(1)}, u32[]{:S(2)}, u32[]{:S(2)}) collective-permute-start(bf16[240,384]{1,0:T(8,128)(2,1)S(1)} %slice.72), channel_id=1, source_target_pairs={{0,8},{1,9},{2,10},{3,11},{4,12},{5,13},{6,14},{7,15},{8,0},{9,1},... | collective-permute-start | bytes 552968 | tf_op jit(solution)/shard_map/ppermute | solution.py:582
  96.8 8.8 %collective-permute-start.20 = (bf16[144,384]{1,0:T(8,128)(2,1)S(1)}, bf16[144,384]{1,0:T(8,128)(2,1)S(1)}, u32[]{:S(2)}, u32[]{:S(2)}) collective-permute-start(bf16[144,384]{1,0:T(8,128)(2,1)S(1)} %slice.87), channel_id=1, source_target_pairs={{0,16},{1,17},{2,18},{3,19},{4,20},{5,21},{6,22},{7,23},{8,24},{9,... | collective-permute-start | bytes 331784 | tf_op jit(solution)/shard_map/ppermute | solution.py:582
  105.7 7.2 %collective-permute-start.25 = (bf16[96,384]{1,0:T(8,128)(2,1)S(1)}, bf16[96,384]{1,0:T(8,128)(2,1)S(1)}, u32[]{:S(2)}, u32[]{:S(2)}) collective-permute-start(bf16[96,384]{1,0:T(8,128)(2,1)S(1)} %slice.90), channel_id=1, source_target_pairs={{0,16},{1,17},{2,18},{3,19},{4,20},{5,21},{6,22},{7,23},{8,24},{9,... | collective-permute-start | bytes 221192 | tf_op jit(solution)/shard_map/ppermute | solution.py:582
  106.0 10.8 %collective-permute-start.22 = (bf16[192,384]{1,0:T(8,128)(2,1)S(1)}, bf16[192,384]{1,0:T(8,128)(2,1)S(1)}, u32[]{:S(2)}, u32[]{:S(2)}) collective-permute-start(bf16[192,384]{1,0:T(8,128)(2,1)S(1)} %get-tuple-element.171), channel_id=1, source_target_pairs={{0,2},{1,3},{2,0},{3,1},{4,6},{5,7},{6,4},{7,5},{8,10},{9,11},{10,... | collective-permute-start | bytes 442376 | tf_op jit(solution)/shard_map/ppermute | solution.py:582
  106.6 10.2 %collective-permute-start.23 = (bf16[192,384]{1,0:T(8,128)(2,1)S(1)}, bf16[192,384]{1,0:T(8,128)(2,1)S(1)}, u32[]{:S(2)}, u32[]{:S(2)}) collective-permute-start(bf16[192,384]{1,0:T(8,128)(2,1)S(1)} %get-tuple-element.170), channel_id=1, source_target_pairs={{0,4},{1,5},{2,6},{3,7},{4,0},{5,1},{6,2},{7,3},{8,12},{9,13},{10,... | collective-permute-start | bytes 442376 | tf_op jit(solution)/shard_map/ppermute | solution.py:582
  108.1 8.7 %collective-permute-start.24 = (bf16[192,384]{1,0:T(8,128)(2,1)S(1)}, bf16[192,384]{1,0:T(8,128)(2,1)S(1)}, u32[]{:S(2)}, u32[]{:S(2)}) collective-permute-start(bf16[192,384]{1,0:T(8,128)(2,1)S(1)} %get-tuple-element.169), channel_id=1, source_target_pairs={{0,6},{1,7},{2,4},{3,5},{4,2},{5,3},{6,0},{7,1},{8,14},{9,15},{10,... | collective-permute-start | bytes 442376 | tf_op jit(solution)/shard_map/ppermute | solution.py:582
  113.0 7.7 %collective-permute-start.28 = (bf16[192,384]{1,0:T(8,128)(2,1)S(1)}, bf16[192,384]{1,0:T(8,128)(2,1)S(1)}, u32[]{:S(2)}, u32[]{:S(2)}) collective-permute-start(bf16[192,384]{1,0:T(8,128)(2,1)S(1)} %pad_maximum_fusion.4), channel_id=1, source_target_pairs={{0,8},{1,9},{2,10},{3,11},{4,12},{5,13},{6,14},{7,15},{8,0},{9,1},... | collective-permute-start | bytes 442376 | tf_op jit(solution)/shard_map/ppermute | solution.py:582
  116.9 6.0 %collective-permute-start.26 = (bf16[96,384]{1,0:T(8,128)(2,1)S(1)}, bf16[96,384]{1,0:T(8,128)(2,1)S(1)}, u32[]{:S(2)}, u32[]{:S(2)}) collective-permute-start(bf16[96,384]{1,0:T(8,128)(2,1)S(1)} %slice.92), channel_id=1, source_target_pairs={{0,8},{1,9},{2,10},{3,11},{4,12},{5,13},{6,14},{7,15},{8,0},{9,1},... | collective-permute-start | bytes 221192 | tf_op jit(solution)/shard_map/ppermute | solution.py:582
  120.8 7.2 %collective-permute-start.29 = (bf16[432,384]{1,0:T(8,128)(2,1)S(1)}, bf16[432,384]{1,0:T(8,128)(2,1)S(1)}, u32[]{:S(2)}, u32[]{:S(2)}) collective-permute-start(bf16[432,384]{1,0:T(8,128)(2,1)S(1)} %pad_maximum_fusion.2), channel_id=1, source_target_pairs={{0,2},{1,3},{2,0},{3,1},{4,6},{5,7},{6,4},{7,5},{8,10},{9,11},{10,... | collective-permute-start | bytes 995336 | tf_op jit(solution)/shard_map/ppermute | solution.py:582
  121.2 10.0 %collective-permute-start.30 = (bf16[432,384]{1,0:T(8,128)(2,1)S(1)}, bf16[432,384]{1,0:T(8,128)(2,1)S(1)}, u32[]{:S(2)}, u32[]{:S(2)}) collective-permute-start(bf16[432,384]{1,0:T(8,128)(2,1)S(1)} %pad_maximum_fusion.2), channel_id=1, source_target_pairs={{0,4},{1,5},{2,6},{3,7},{4,0},{5,1},{6,2},{7,3},{8,12},{9,13},{10,... | collective-permute-start | bytes 995336 | tf_op jit(solution)/shard_map/ppermute | solution.py:582
  122.9 4.9 %collective-permute-start.27 = (bf16[48,384]{1,0:T(8,128)(2,1)S(1)}, bf16[48,384]{1,0:T(8,128)(2,1)S(1)}, u32[]{:S(2)}, u32[]{:S(2)}) collective-permute-start(bf16[48,384]{1,0:T(8,128)(2,1)S(1)} %slice.94), channel_id=1, source_target_pairs={{0,16},{1,17},{2,18},{3,19},{4,20},{5,21},{6,22},{7,23},{8,24},{9,... | collective-permute-start | bytes 110600 | tf_op jit(solution)/shard_map/ppermute | solution.py:582
  131.1 4.9 %collective-permute-start.32 = (bf16[48,384]{1,0:T(8,128)(2,1)S(1)}, bf16[48,384]{1,0:T(8,128)(2,1)S(1)}, u32[]{:S(2)}, u32[]{:S(2)}) collective-permute-start(bf16[48,384]{1,0:T(8,128)(2,1)S(1)} %add_convert_fusion.7), channel_id=1, source_target_pairs={{0,16},{1,17},{2,18},{3,19},{4,20},{5,21},{6,22},{7,23},{8,24},{9,... | collective-permute-start | bytes 110600 | tf_op jit(solution)/shard_map/ppermute | solution.py:582
  131.1 10.3 %collective-permute-start.31 = (bf16[432,384]{1,0:T(8,128)(2,1)S(1)}, bf16[432,384]{1,0:T(8,128)(2,1)S(1)}, u32[]{:S(2)}, u32[]{:S(2)}) collective-permute-start(bf16[432,384]{1,0:T(8,128)(2,1)S(1)} %pad_maximum_fusion.2), channel_id=1, source_target_pairs={{0,6},{1,7},{2,4},{3,5},{4,2},{5,3},{6,0},{7,1},{8,14},{9,15},{10,... | collective-permute-start | bytes 995336 | tf_op jit(solution)/shard_map/ppermute | solution.py:582
  136.0 5.4 %collective-permute-start.33 = (bf16[96,384]{1,0:T(8,128)(2,1)S(1)}, bf16[96,384]{1,0:T(8,128)(2,1)S(1)}, u32[]{:S(2)}, u32[]{:S(2)}) collective-permute-start(bf16[96,384]{1,0:T(8,128)(2,1)S(1)} %pad_maximum_fusion.6), channel_id=1, source_target_pairs={{0,8},{1,9},{2,10},{3,11},{4,12},{5,13},{6,14},{7,15},{8,0},{9,1},... | collective-permute-start | bytes 221192 | tf_op jit(solution)/shard_map/ppermute | solution.py:582
  141.7 6.8 %collective-permute-start.34 = (bf16[192,384]{1,0:T(8,128)(2,1)S(1)}, bf16[192,384]{1,0:T(8,128)(2,1)S(1)}, u32[]{:S(2)}, u32[]{:S(2)}) collective-permute-start(bf16[192,384]{1,0:T(8,128)(2,1)S(1)} %pad_maximum_fusion.5), channel_id=1, source_target_pairs={{0,2},{1,3},{2,0},{3,1},{4,6},{5,7},{6,4},{7,5},{8,10},{9,11},{10,... | collective-permute-start | bytes 442376 | tf_op jit(solution)/shard_map/ppermute | solution.py:582
  143.2 9.1 %collective-permute-start.35 = (bf16[192,384]{1,0:T(8,128)(2,1)S(1)}, bf16[192,384]{1,0:T(8,128)(2,1)S(1)}, u32[]{:S(2)}, u32[]{:S(2)}) collective-permute-start(bf16[192,384]{1,0:T(8,128)(2,1)S(1)} %pad_maximum_fusion.5), channel_id=1, source_target_pairs={{0,4},{1,5},{2,6},{3,7},{4,0},{5,1},{6,2},{7,3},{8,12},{9,13},{10,... | collective-permute-start | bytes 442376 | tf_op jit(solution)/shard_map/ppermute | solution.py:582
  143.8 8.4 %collective-permute-start.36 = (bf16[192,384]{1,0:T(8,128)(2,1)S(1)}, bf16[192,384]{1,0:T(8,128)(2,1)S(1)}, u32[]{:S(2)}, u32[]{:S(2)}) collective-permute-start(bf16[192,384]{1,0:T(8,128)(2,1)S(1)} %pad_maximum_fusion.5), channel_id=1, source_target_pairs={{0,6},{1,7},{2,4},{3,5},{4,2},{5,3},{6,0},{7,1},{8,14},{9,15},{10,... | collective-permute-start | bytes 442376 | tf_op jit(solution)/shard_map/ppermute | solution.py:582
  (34 other events, 211.8 us)

commit v7 on v6

--- a/solution.py
+++ b/solution.py
@@ -427,7 +427,10 @@
         halves(mine_ref[0], 192, send_ref, keep_ref, lambda at, k: block(acc, at, 48, k))
 
 
-def att_core_kernel(qkv_all, p_all, dxb_all, wout, dqkv_all):
+def att_back_kernel(
+    mine_ref, qkv_all, p_all, dxb_all, dx_all, h1_ref, o_ref, tok_ref, wout, g1, wqkv,
+    gtok_ref, send_ref, keep_ref, dqkv_all, acc,
+):
     step = pl.program_id(0)
     qkv_ref, dxb_ref, dqkv_ref = qkv_all.at[held_rows()], dxb_all.at[held_rows()], dqkv_all.at[held_rows()]
     p_ref = p_all.at[pl.ds(2 * step, 2)]
@@ -457,22 +460,18 @@
             dqkv_ref[rows, PAIR * j : PAIR * j + PAIR] = dq.astype(BF)
             dqkv_ref[rows, D + PAIR * j : D + PAIR * j + PAIR] = dk.astype(BF)
             dqkv_ref[rows, 2 * D + PAIR * j : 2 * D + PAIR * j + PAIR] = dv.astype(BF)
-
-
-def att_grads_kernel(mine_ref, h1_ref, dqkv_ref, o_ref, dxb_ref, send_ref, keep_ref, acc):
-    acc[:, :D] = mm_tn(o_ref[...], dxb_ref[...])
-    acc[:, D:] = mm_tn(h1_ref[...], dqkv_ref[...])
-    halves(mine_ref[0], 192, send_ref, keep_ref, lambda at, k: block(acc, at, 48, k))
-
-
-def tok_back_kernel(tok_ref, dqkv_all, dx_all, g1, wqkv, gtok_ref):
-    dqkv_ref, dx_ref = dqkv_all.at[held_rows()], dx_all.at[held_rows()]
     x = tok_ref[...].astype(F32)
     centre = x - row_mean(x)
     r = lax.rsqrt(row_mean(centre * centre) + EPS)
     unit = centre * r
     dn = mm_nt(dqkv_ref[...], wqkv[...]) * g1[...].reshape(1, D)
-    gtok_ref[...] = dx_ref[...] + r * (dn - row_mean(dn) - unit * row_mean(dn * unit))
+    gtok_ref[...] = dx_all[held_rows(), :] + r * (dn - row_mean(dn) - unit * row_mean(dn * unit))
+
+    @pl.when(step == pl.num_programs(0) - 1)
+    def _():
+        acc[:, :D] = mm_tn(o_ref[...], dxb_all[...])
+        acc[:, D:] = mm_tn(h1_ref[...], dqkv_all[...])
+        halves(mine_ref[0], 192, send_ref, keep_ref, lambda at, k: block(acc, at, 48, k))
 
 
 def gain_of(grad, weight, gain):
@@ -541,38 +540,19 @@
     )(mine, lab, near(h2), near(gp), near(c2), near(du), near(dy), g2, wup)
 
 
-def att_core(qkv, p, dxb, wout):
+def att_back(mine, qkv, p, dxb, dx, h1, o, tok, wout, g1, wqkv):
     n = dxb.shape[0]
     return pl.pallas_call(
-        att_core_kernel,
+        att_back_kernel,
         grid=(n // TOK_BLOCK,),
-        in_specs=[VMEM, VMEM, VMEM, const_spec((D, D))],
-        out_specs=VMEM,
-        out_shape=pltpu.VMEM((n, 3 * D), BF),
+        in_specs=[SMEM] + [VMEM] * 6 + [token_rows(D), const_spec((D, D)), const_spec((D,)), const_spec((D, 3 * D))],
+        out_specs=[token_rows(D), VMEM, VMEM],
+        out_shape=[pltpu.HBM((n, D), F32), pltpu.VMEM((768, D), BF), pltpu.VMEM((768, D), BF)],
+        scratch_shapes=[pltpu.VMEM((n, 3 * D), BF), pltpu.VMEM((D, 4 * D), F32)],
         compiler_params=ROOM,
-        cost_estimate=cost(10),
-        name="att_core",
-    )(near(qkv), near(p), near(dxb), wout)
-
-
-def att_grads(mine, h1, dqkv, o, dxb):
-    outs = [((768, D), BF)] * 2
-    scratch = [pltpu.VMEM((D, 4 * D), F32)]
-    return simple(att_grads_kernel, outs, scratch, smem=1, us=4, name="att_grads", held=(1, 2, 3, 4))(mine, h1, dqkv, o, dxb)
-
-
-def tok_back(tok, dqkv, dx, g1, wqkv):
-    n = tok.shape[0]
-    return pl.pallas_call(
-        tok_back_kernel,
-        grid=(n // TOK_BLOCK,),
-        in_specs=[token_rows(D), VMEM, VMEM, const_spec((D,)), const_spec((D, 3 * D))],
-        out_specs=token_rows(D),
-        out_shape=jax.ShapeDtypeStruct((n, D), F32),
-        compiler_params=ROOM,
-        cost_estimate=cost(4),
-        name="tok_back",
-    )(tok, near(dqkv), near(dx), g1, wqkv)
+        cost_estimate=cost(14),
+        name="att_back",
+    )(mine, *[near(v) for v in (qkv, p, dxb, dx, h1, o)], tok, wout, g1, wqkv)
 
 
 AXES = ("dp", "replica")
@@ -686,9 +666,9 @@
         return simple(spread_att_kernel, outs, smem=1, us=4, name="spread_att", held=(1, 2), held_out=False)(mine, own, other, txt_qkv, txt_ln1)
 
     if not tuned:
-        dqkv = att_core(qkv, p, dxb, txt_out)
-        send_a, keep_a = att_grads(mine, h1, dqkv, o, dxb)
-        grad_tokens = tok_back(text_tokens, dqkv, dx, txt_ln1, txt_qkv)
+        grad_tokens, send_a, keep_a = att_back(
+            mine, qkv, p, dxb, dx, h1, o, text_tokens, txt_out, txt_ln1, txt_qkv
+        )
         sums = [keep_d, send_d, keep_u, send_u, keep_a, send_a, keep_p, send_p]
         d, d2, u, u2, a, a2, p, p2 = [v.astype(BF) for v in lax.psum([v.astype(F32) for v in sums], AXES)]
         grad_down, grad_up, grad_proj, gain2 = spread_mlp(
@@ -701,35 +681,34 @@
         m = mlp_parts(d, added(keep_u, [swap(send_u, 1)]), pr)
         dxb, m = lax.optimization_barrier((dxb, m))
         got = plane(m)
-        dqkv = att_core(qkv, p, dxb, txt_out)
-        got, dqkv = lax.optimization_barrier((got, dqkv))
+        grad_tokens, send_a, keep_a = att_back(
+            mine, qkv, p, dxb, dx, h1, o, text_tokens, txt_out, txt_ln1, txt_qkv
+        )
+        other = swap(send_a, 1)
+        got, keep_a = lax.optimization_barrier((got, keep_a))
         m = added(m[0], got)
-        m, dqkv = lax.optimization_barrier((m, dqkv))
         got = swap(m[192:], 8)
-        send_a, keep_a = att_grads(mine, h1, dqkv, o, dxb)
-        got, send_a, keep_a = lax.optimization_barrier((got, send_a, keep_a))
+        a = added(keep_a, [other]).reshape(4, 192, D)
+        got_a = plane(a)
+        got, got_a[0], got_a[1] = lax.optimization_barrier((got, got_a[0], got_a[1]))
         m = added(joined(m[:192], [m[384:]]), [got])
         got = swap(m[96:], 16)
-        a = added(keep_a, [swap(send_a, 1)]).reshape(4, 192, D)
-        got, a = lax.optimization_barrier((got, a))
+        got, got_a = lax.optimization_barrier((got, got_a))
+        a = added(a[0], got_a)
+        got_a = swap(a[96:], 8)
         m = added(joined(m[:96], [m[192:]]), [got])
         far = swap(m[:96], 16)
-        got_a = plane(a)
-        dqkv, a, m = lax.optimization_barrier((dqkv, a, m))
-        grad_tokens = tok_back(text_tokens, dqkv, dx, txt_ln1, txt_qkv)
-        far, grad_tokens = lax.optimization_barrier((far, grad_tokens))
-        got_a, grad_tokens = lax.optimization_barrier((got_a, grad_tokens))
+        a = added(a[:96], [got_a])
+        got_a = swap(a[48:], 16)
         m = joined(m[:96], [far, m[96:]])
         m = joined(m[:192], [swap(m[:192], 8), m[192:]])
-        a = added(a[0], got_a)
         got_m = plane([m] * 4)
-        a = added(a[:96], [swap(a[96:], 8)])
-        a = added(a[:48], [swap(a[48:], 16)])
-        a, got_m[0], got_m[1] = lax.optimization_barrier((a, got_m[0], got_m[1]))
+        a = added(a[:48], [got_a])
         a = joined(a, [swap(a, 16)])
         a = joined(a, [swap(a, 8)])
-        got_m, a = lax.optimization_barrier((got_m, a))
+        got_m[0], got_m[1], a = lax.optimization_barrier((got_m[0], got_m[1], a))
         got_a = plane([a] * 4)
+        got_m[2], got_a[0], got_a[1] = lax.optimization_barrier((got_m[2], got_a[0], got_a[1]))
         m = joined(m, got_m)
         grad_down, grad_up, grad_proj, gain2 = spread_mlp(m, swap(m, 1))
         got_a, grad_up = lax.optimization_barrier((got_a, grad_up))

time: 159 us -> 157 us (0.987)
  waiting for transfers between devices: 48.3 us -> 40.1 us
  starting transfers between devices: 43.3 us -> 50.5 us
    ppermute x39, waiting for transfers between devices: 48.3 us -> 40.1 us  [swap(): return lax.ppermute(v, AXES, [(i, i ^ mask) for i in range(32)])]
    ppermute x39, starting transfers between devices: 43.3 us -> 50.5 us  [swap(): return lax.ppermute(v, AXES, [(i, i ^ mask) for i in range(32)])]
    pallas_call x6 -> x5, Pallas kernels: 12.9 us -> 11.1 us  [call(): pl.pallas_call(kernel, in_specs=[SMEM] * smem + [VMEM] * (len(args) - sme...]
    pallas_call x2 -> x1, Pallas kernels: 12.6 us -> 13.7 us  [att_back(): pl.pallas_call(att_back_kernel, grid=(n // TOK_BLOCK,), in_specs=[SMEM] +...]
  transfers between devices with their start and end apart: 39 -> 39, of which waited for: 20 -> 24; matrix products, arithmetic and copies ran while one was open for 1% -> 1% of each run, Pallas kernels for 27% -> 26%
where the time goes in v7:
time: 157 us
  Pallas kernels  58.8 us (37%)
  starting transfers between devices  50.5 us (32%)
  waiting for transfers between devices  40.1 us (26%)
  between operations  4.26 us (3%)
  local copies, waits for them, and re-layouts  1.57 us (1%)
    ppermute x39, starting transfers between devices, swap(): return lax.ppermute(v, AXES, [(i, i ^ mask) for i in range(32)])  50.5 us
    ppermute x39, waiting for transfers between devices, swap(): return lax.ppermute(v, AXES, [(i, i ^ mask) for i in range(32)])  40.1 us
    pallas_call x1, Pallas kernels, att_back(): pl.pallas_call(att_back_kernel, grid=(n // TOK_BLOCK,), in_specs=[SMEM] +...  13.7 us
    pallas_call x5, Pallas kernels, call(): pl.pallas_call(kernel, in_specs=[SMEM] * smem + [VMEM] * (len(args) - sme...  11.1 us
    pallas_call x1, Pallas kernels, image_tower(): pl.pallas_call(image_kernel, grid=(count // IMG_BLOCK,), in_specs=[pl.Blo...  10.8 us
    pallas_call x1, Pallas kernels, text_mlp(): pl.pallas_call(text_mlp_kernel, grid=(n // TOK_BLOCK,), in_specs=[token_r...  10 us
    pallas_call x1, Pallas kernels, text_att(): pl.pallas_call(text_att_kernel, grid=(blocks,), in_specs=[token_rows(D),...  7.86 us
    pallas_call x1, Pallas kernels, mlp_back(): pl.pallas_call(mlp_back_kernel, grid=(n // TOK_BLOCK,), in_specs=[SMEM, b...  5.36 us
  transfers between devices with their start and end apart: 39, of which 24 were waited for; matrix products, arithmetic and copies ran while one was open for 1% of the time, Pallas kernels for 26%

profile of v7, /device:TPU:0, one launch (start us, length us, event | category | flops | bytes accessed | tf_op | source)
XLA Modules:
  0.0 156.7 jit_solution(3950749310932020314)
XLA Ops:
  0.7 10.8 %image_tower.1 = bf16[64,384]{1,0:T(8,128)(2,1)S(1)} custom-call(bf16[50,64,384]{2,1,0:T(8,128)(2,1)} %bitcast.23, f32[384]{0:T(512)} %g1.5, bf16[384,1152]{1,0:T(8,128)(2,1)} %wqkv.5, bf16[384,384]{1,0:T(8,128)(2,1)} %wout.3, f32[384]{0:T(512)} %g2.4, bf16[384,1536]{1,0:T(8,128)(2,1)} %wup.4, bf16[1536,384]{1,0:T(8,128)(2,1)} %wdown.3, bf16[384,384]{1,0:T(8,128)(2,1)} %wproj.3), custom_call_target="tpu_custom_call" | custom-call | flops 12000000000 | bytes 36000000 | tf_op jit(solution)/shard_map/image_tower/pallas_call | solution.py:141
  11.5 3.1 %collective-permute-start = (bf16[64,384]{1,0:T(8,128)(2,1)S(1)}, bf16[64,384]{1,0:T(8,128)(2,1)S(1)}, u32[]{:S(2)}, u32[]{:S(2)}) collective-permute-start(bf16[64,384]{1,0:T(8,128)(2,1)S(1)} %image_tower.1), channel_id=1, source_target_pairs={{0,8},{1,9},{2,10},{3,11},{4,12},{5,13},{6,14},{7,15},{8,0},{9,1},... | collective-permute-start | bytes 147464 | tf_op jit(solution)/shard_map/ppermute | solution.py:562
  14.6 2.6 %collective-permute-start.1 = (bf16[64,384]{1,0:T(8,128)(2,1)S(1)}, bf16[64,384]{1,0:T(8,128)(2,1)S(1)}, u32[]{:S(2)}, u32[]{:S(2)}) collective-permute-start(bf16[64,384]{1,0:T(8,128)(2,1)S(1)} %image_tower.1), channel_id=1, source_target_pairs={{0,16},{1,17},{2,18},{3,19},{4,20},{5,21},{6,22},{7,23},{8,24},{9,... | collective-permute-start | bytes 147464 | tf_op jit(solution)/shard_map/ppermute | solution.py:562
  17.4 7.9 %text_att.1 = (bf16[1024,384]{1,0:T(8,128)(2,1)S(1)}, bf16[1024,384]{1,0:T(8,128)(2,1)}, bf16[1024,1152]{1,0:T(8,128)(2,1)}, bf16[8,3,256,128]{3,2,1,0:T(8,128)(2,1)}, bf16[1024,384]{1,0:T(8,128)(2,1)}) custom-call(bf16[1024,384]{1,0:T(8,128)(2,1)} %tok_ref.5, s32[4,1,256]{2,1,0:T(1,128)S(1)} %reshape.71.lab_ref, f32[384]{0:T(512)S(1)} %copy-done.9, ...), custom_call_target="tpu_custom_call" | custom-call | flops 8999999488 | bytes 27000000 | tf_op jit(solution)/shard_map/text_att/pallas_call | solution.py:256
  25.3 1.8 %collective-permute-start.3 = (bf16[256,384]{1,0:T(8,128)(2,1)S(1)}, bf16[256,384]{1,0:T(8,128)(2,1)S(1)}, u32[]{:S(2)}, u32[]{:S(2)}) collective-permute-start(bf16[256,384]{1,0:T(8,128)(2,1)S(1)} %pad_maximum_fusion.3), channel_id=1, source_target_pairs={{0,2},{1,3},{2,0},{3,1},{4,6},{5,7},{6,4},{7,5},{8,10},{9,11},{10,... | collective-permute-start | bytes 589832 | tf_op jit(solution)/shard_map/ppermute | solution.py:562
  28.9 10.0 %text_mlp.1 = (bf16[1024,384]{1,0:T(8,128)(2,1)}, f32[1024,384]{1,0:T(8,128)}, bf16[1024,1536]{1,0:T(8,128)(2,1)}, f32[64,1536]{1,0:T(8,128)S(1)}, bf16[64,384]{...) custom-call(bf16[1024,384]{1,0:T(8,128)(2,1)S(1)} %copy-done.3, ...), custom_call_target="tpu_custom_call" | custom-call | flops 11000000512 | bytes 33000000 | tf_op jit(solution)/shard_map/text_mlp/pallas_call | solution.py:280
  42.2 1.9 %cosine.1 = (f32[64,2048]{1,0:T(8,128)S(1)}, f32[40,128]{1,0:T(8,128)S(1)}) custom-call(f32[1]{0:T(128)S(6)} %copy.45.scale_ref, s32[1]{0:T(128)} %bitcast.mine_ref, bf16[64,384]{1,0:T(8,128)(2,1)S(1)} %get-tuple-element.84.emb, bf16[1024,384]{1,0:T(8,128)(2,1)S(1)} %constant_dynamic-update-slice_fusion.own, bf16[1024,384]{1,0:T(8,128)(2,1)} %collective-permute-done.6.other, ...), custom_call_target="tpu_custom_call" | custom-call | flops 3000000000 | bytes 9000000 | tf_op jit(solution)/shard_map/cosine/pallas_call | solution.py:513
  45.3 2.7 %collective-permute-start.10 = (f32[40,128]{1,0:T(8,128)S(1)}, f32[40,128]{1,0:T(8,128)S(1)}, u32[]{:S(2)}, u32[]{:S(2)}) collective-permute-start(f32[40,128]{1,0:T(8,128)S(1)} %add.113), channel_id=1, source_target_pairs={{0,6},{1,7},{2,4},{3,5},{4,2},{5,3},{6,0},{7,1},{8,14},{9,15},{10,... | collective-permute-start | bytes 61448 | tf_op jit(solution)/shard_map/ppermute | solution.py:562
  50.0 1.8 %collective-permute-done.8 = f32[40,128]{1,0:T(8,128)S(1)} collective-permute-done((f32[40,128]{1,0:T(8,128)S(1)}, f32[40,128]{1,0:T(8,128)S(1)}, u32[]{:S(2)}, u32[]{:S(2)}) %collective-permute-start.8) | collective-permute-done | bytes 20512 | tf_op jit(solution)/shard_map/ppermute | solution.py:562
  53.1 3.1 %collective-permute-done.11 = f32[40,128]{1,0:T(8,128)S(1)} collective-permute-done((f32[40,128]{1,0:T(8,128)S(1)}, f32[40,128]{1,0:T(8,128)S(1)}, u32[]{:S(2)}, u32[]{:S(2)}) %collective-permute-start.11) | collective-permute-done | bytes 20512 | tf_op jit(solution)/shard_map/ppermute | solution.py:562
  56.1 2.2 %collective-permute-start.12 = (f32[40,128]{1,0:T(8,128)S(1)}, f32[40,128]{1,0:T(8,128)S(1)}, u32[]{:S(2)}, u32[]{:S(2)}) collective-permute-start(f32[40,128]{1,0:T(8,128)S(1)} %add.117), channel_id=1, source_target_pairs={{0,16},{1,17},{2,18},{3,19},{4,20},{5,21},{6,22},{7,23},{8,24},{9,... | collective-permute-start | bytes 61448 | tf_op jit(solution)/shard_map/ppermute | solution.py:562
  58.4 1.7 %rows.1.dt_row = f32[64,384]{1,0:T(8,128)S(1)} custom-call(f32[1]{0:T(128)S(6)} %copy.45.scale_ref, f32[64,2048]{1,0:T(8,128)S(1)} %get-tuple-element.90.g_ref, bf16[1024,384]{1,0:T(8,128)(2,1)S(1)} %constant_dynamic-update-slice_fusion.own, bf16[1024,384]{1,0:T(8,128)(2,1)} %collective-permute-done.6.other, s32[64,1]{1,0:T(8,128)S(1)} %copy.29.pair), custom_call_target="tpu_custom_call" | custom-call | flops 2000000000 | bytes 6000000 | tf_op jit(solution)/shard_map/rows/pallas_call | solution.py:513
  60.9 3.1 %head_back.1 = (bf16[768,384]{1,0:T(8,128)(2,1)S(1)}, bf16[768,384]{1,0:T(8,128)(2,1)S(1)}, bf16[192,384]{1,0:T(8,128)(2,1)S(1)}, bf16[192,384]{1,0:T(8,128)(2,1...) custom-call(f32[1]{0:T(128)S(6)} %copy.45.scale_ref, ...), custom_call_target="tpu_custom_call" | custom-call | flops 5000000000 | bytes 15000000 | tf_op jit(solution)/shard_map/head_back/pallas_call | solution.py:513
  64.6 5.4 %mlp_back.1 = (f32[1024,384]{1,0:T(8,128)S(1)}, bf16[1024,384]{1,0:T(8,128)(2,1)S(1)}, bf16[768,384]{1,0:T(8,128)(2,1)S(1)}, bf16[768,384]{1,0:T(8,128)(2,1)S(1)}) custom-call(s32[1]{0:T(128)} %bitcast.mine_ref, s32[4,1,256]{2,1,0:T(1,128)S(1)} %reshape.71.lab_ref, bf16[1024,384]{1,0:T(8,128)(2,1)S(1)} %copy-done.16, bf16[1024,1536]{1,0:T(8,128)(2,1)S(1)} %copy-done.10, ...), custom_call_target="tpu_custom_call" | custom-call | flops 8999999488 | bytes 27000000 | tf_op jit(solution)/shard_map/mlp_back/pallas_call | solution.py:530
  70.3 1.7 %collective-permute-done.14 = bf16[768,384]{1,0:T(8,128)(2,1)S(1)} collective-permute-done((bf16[768,384]{1,0:T(8,128)(2,1)S(1)}, bf16[768,384]{1,0:T(8,128)(2,1)S(1)}, u32[]{:S(2)}, u32[]{:S(2)}) %collective-permute-start.14) | collective-permute-done | bytes 589856 | tf_op jit(solution)/shard_map/ppermute | solution.py:562
  76.2 13.7 %att_back.1 = (f32[1024,384]{1,0:T(8,128)}, bf16[768,384]{1,0:T(8,128)(2,1)S(1)}, bf16[768,384]{1,0:T(8,128)(2,1)S(1)}) custom-call(s32[1]{0:T(128)} %bitcast.mine_ref, bf16[1024,1152]{1,0:T(8,128)(2,1)S(1)} %copy-done.11, bf16[8,3,256,128]{3,2,1,0:T(8,128)(2,1)S(1)} %copy-done.15, bf16[1024,384]{1,0:T(8,128)(2,1)S(1)} %get-tuple-element.111.dxb_all, ...), custom_call_target="tpu_custom_call" | custom-call | flops 14000000000 | bytes 42000000 | tf_op jit(solution)/shard_map/att_back/pallas_call | solution.py:545
  94.5 1.8 %collective-permute-start.24 = (bf16[192,384]{1,0:T(8,128)(2,1)S(1)}, bf16[192,384]{1,0:T(8,128)(2,1)S(1)}, u32[]{:S(2)}, u32[]{:S(2)}) collective-permute-start(bf16[192,384]{1,0:T(8,128)(2,1)S(1)} %get-tuple-element.151), channel_id=1, source_target_pairs={{0,6},{1,7},{2,4},{3,5},{4,2},{5,3},{6,0},{7,1},{8,14},{9,15},{10,... | collective-permute-start | bytes 442376 | tf_op jit(solution)/shard_map/ppermute | solution.py:562
  98.7 3.7 %collective-permute-done.22 = bf16[192,384]{1,0:T(8,128)(2,1)S(1)} collective-permute-done((bf16[192,384]{1,0:T(8,128)(2,1)S(1)}, bf16[192,384]{1,0:T(8,128)(2,1)S(1)}, u32[]{:S(2)}, u32[]{:S(2)}) %collective-permute-start.22) | collective-permute-done | bytes 147488 | tf_op jit(solution)/shard_map/ppermute | solution.py:562
  102.6 2.6 %collective-permute-start.23 = (bf16[144,384]{1,0:T(8,128)(2,1)S(1)}, bf16[144,384]{1,0:T(8,128)(2,1)S(1)}, u32[]{:S(2)}, u32[]{:S(2)}) collective-permute-start(bf16[144,384]{1,0:T(8,128)(2,1)S(1)} %slice.95), channel_id=1, source_target_pairs={{0,16},{1,17},{2,18},{3,19},{4,20},{5,21},{6,22},{7,23},{8,24},{9,... | collective-permute-start | bytes 331784 | tf_op jit(solution)/shard_map/ppermute | solution.py:562
  105.2 4.6 %collective-permute-done.23 = bf16[144,384]{1,0:T(8,128)(2,1)S(1)} collective-permute-done((bf16[144,384]{1,0:T(8,128)(2,1)S(1)}, bf16[144,384]{1,0:T(8,128)(2,1)S(1)}, u32[]{:S(2)}, u32[]{:S(2)}) %collective-permute-start.23) | collective-permute-done | bytes 110624 | tf_op jit(solution)/shard_map/ppermute | solution.py:562
  110.8 3.4 %collective-permute-start.25 = (bf16[96,384]{1,0:T(8,128)(2,1)S(1)}, bf16[96,384]{1,0:T(8,128)(2,1)S(1)}, u32[]{:S(2)}, u32[]{:S(2)}) collective-permute-start(bf16[96,384]{1,0:T(8,128)(2,1)S(1)} %get-tuple-element.157), channel_id=1, source_target_pairs={{0,16},{1,17},{2,18},{3,19},{4,20},{5,21},{6,22},{7,23},{8,24},{9,... | collective-permute-start | bytes 221192 | tf_op jit(solution)/shard_map/ppermute | solution.py:562
  114.9 1.8 %collective-permute-start.30 = (bf16[48,384]{1,0:T(8,128)(2,1)S(1)}, bf16[48,384]{1,0:T(8,128)(2,1)S(1)}, u32[]{:S(2)}, u32[]{:S(2)}) collective-permute-start(bf16[48,384]{1,0:T(8,128)(2,1)S(1)} %slice.103), channel_id=1, source_target_pairs={{0,16},{1,17},{2,18},{3,19},{4,20},{5,21},{6,22},{7,23},{8,24},{9,... | collective-permute-start | bytes 110600 | tf_op jit(solution)/shard_map/ppermute | solution.py:562
  119.9 2.1 %collective-permute-start.31 = (bf16[48,384]{1,0:T(8,128)(2,1)S(1)}, bf16[48,384]{1,0:T(8,128)(2,1)S(1)}, u32[]{:S(2)}, u32[]{:S(2)}) collective-permute-start(bf16[48,384]{1,0:T(8,128)(2,1)S(1)} %add_convert_fusion.8), channel_id=1, source_target_pairs={{0,16},{1,17},{2,18},{3,19},{4,20},{5,21},{6,22},{7,23},{8,24},{9,... | collective-permute-start | bytes 110600 | tf_op jit(solution)/shard_map/ppermute | solution.py:562
  122.1 1.7 %collective-permute-done.26 = bf16[192,384]{1,0:T(8,128)(2,1)S(1)} collective-permute-done((bf16[192,384]{1,0:T(8,128)(2,1)S(1)}, bf16[192,384]{1,0:T(8,128)(2,1)S(1)}, u32[]{:S(2)}, u32[]{:S(2)}) %collective-permute-start.26) | collective-permute-done | bytes 147488 | tf_op jit(solution)/shard_map/ppermute | solution.py:562
  125.7 2.5 %collective-permute-start.32 = (bf16[96,384]{1,0:T(8,128)(2,1)S(1)}, bf16[96,384]{1,0:T(8,128)(2,1)S(1)}, u32[]{:S(2)}, u32[]{:S(2)}) collective-permute-start(bf16[96,384]{1,0:T(8,128)(2,1)S(1)} %pad_maximum_fusion.6), channel_id=1, source_target_pairs={{0,8},{1,9},{2,10},{3,11},{4,12},{5,13},{6,14},{7,15},{8,0},{9,1},... | collective-permute-start | bytes 221192 | tf_op jit(solution)/shard_map/ppermute | solution.py:562
  130.6 2.9 %collective-permute-done.27 = bf16[432,384]{1,0:T(8,128)(2,1)S(1)} collective-permute-done((bf16[432,384]{1,0:T(8,128)(2,1)S(1)}, bf16[432,384]{1,0:T(8,128)(2,1)S(1)}, u32[]{:S(2)}, u32[]{:S(2)}) %collective-permute-start.27) | collective-permute-done | bytes 331808 | tf_op jit(solution)/shard_map/ppermute | solution.py:562
  133.5 3.6 %collective-permute-start.34 = (bf16[192,384]{1,0:T(8,128)(2,1)S(1)}, bf16[192,384]{1,0:T(8,128)(2,1)S(1)}, u32[]{:S(2)}, u32[]{:S(2)}) collective-permute-start(bf16[192,384]{1,0:T(8,128)(2,1)S(1)} %pad_maximum_fusion.5), channel_id=1, source_target_pairs={{0,2},{1,3},{2,0},{3,1},{4,6},{5,7},{6,4},{7,5},{8,10},{9,11},{10,... | collective-permute-start | bytes 442376 | tf_op jit(solution)/shard_map/ppermute | solution.py:562
  137.1 3.0 %collective-permute-start.35 = (bf16[192,384]{1,0:T(8,128)(2,1)S(1)}, bf16[192,384]{1,0:T(8,128)(2,1)S(1)}, u32[]{:S(2)}, u32[]{:S(2)}) collective-permute-start(bf16[192,384]{1,0:T(8,128)(2,1)S(1)} %pad_maximum_fusion.5), channel_id=1, source_target_pairs={{0,4},{1,5},{2,6},{3,7},{4,0},{5,1},{6,2},{7,3},{8,12},{9,13},{10,... | collective-permute-start | bytes 442376 | tf_op jit(solution)/shard_map/ppermute | solution.py:562
  140.3 3.0 %collective-permute-done.35 = bf16[192,384]{1,0:T(8,128)(2,1)S(1)} collective-permute-done((bf16[192,384]{1,0:T(8,128)(2,1)S(1)}, bf16[192,384]{1,0:T(8,128)(2,1)S(1)}, u32[]{:S(2)}, u32[]{:S(2)}) %collective-permute-start.35) | collective-permute-done | bytes 147488 | tf_op jit(solution)/shard_map/ppermute | solution.py:562
  146.4 2.7 %spread_mlp.1 = (f32[1536,384]{1,0:T(8,128)}, f32[384,1536]{1,0:T(8,128)}, f32[384,384]{1,0:T(8,128)}, f32[384]{0:T(512)}) custom-call(s32[1]{0:T(128)} %bitcast.mine_ref, bf16[1728,384]{1,0:T(8,128)(2,1)S(1)} %constant_dynamic-update-slice_fusion.4.own, bf16[1728,384]{1,0:T(8,128)(2,1)S(1)} %collective-permute-done.37.other, ...), custom_call_target="tpu_custom_call" | custom-call | flops 4000000000 | bytes 12000000 | tf_op jit(solution)/shard_map/spread_mlp/pallas_call | solution.py:513
  150.8 1.9 %collective-permute-done.38.other = bf16[768,384]{1,0:T(8,128)(2,1)S(1)} collective-permute-done((bf16[768,384]{1,0:T(8,128)(2,1)S(1)}, bf16[768,384]{1,0:T(8,128)(2,1)S(1)}, u32[]{:S(2)}, u32[]{:S(2)}) %collective-permute-start.38) | collective-permute-done | bytes 589856 | tf_op jit(solution)/shard_map/ppermute | solution.py:562
  152.7 1.7 %spread_att.1 = (f32[384,384]{1,0:T(8,128)}, f32[384,1152]{1,0:T(8,128)}, f32[384]{0:T(512)}) custom-call(s32[1]{0:T(128)} %bitcast.mine_ref, bf16[768,384]{1,0:T(8,128)(2,1)S(1)} %constant_dynamic-update-slice_fusion.11.own, bf16[768,384]{1,0:T(8,128)(2,1)S(1)} %collective-permute-done.38.other, bf16[384,1152]{1,0:T(8,128)(2,1)S(1)} %copy-done.2, ...), custom_call_target="tpu_custom_call" | custom-call | flops 4000000000 | bytes 12000000 | tf_op jit(solution)/shard_map/spread_att/pallas_call | solution.py:513
  (161 shorter events, 35.9 us)
Async XLA Ops:
  11.5 13.8 %collective-permute-start = (bf16[64,384]{1,0:T(8,128)(2,1)S(1)}, bf16[64,384]{1,0:T(8,128)(2,1)S(1)}, u32[]{:S(2)}, u32[]{:S(2)}) collective-permute-start(bf16[64,384]{1,0:T(8,128)(2,1)S(1)} %image_tower.1), channel_id=1, source_target_pairs={{0,8},{1,9},{2,10},{3,11},{4,12},{5,13},{6,14},{7,15},{8,0},{9,1},... | collective-permute-start | bytes 147464 | tf_op jit(solution)/shard_map/ppermute | solution.py:562
  14.6 10.7 %collective-permute-start.1 = (bf16[64,384]{1,0:T(8,128)(2,1)S(1)}, bf16[64,384]{1,0:T(8,128)(2,1)S(1)}, u32[]{:S(2)}, u32[]{:S(2)}) collective-permute-start(bf16[64,384]{1,0:T(8,128)(2,1)S(1)} %image_tower.1), channel_id=1, source_target_pairs={{0,16},{1,17},{2,18},{3,19},{4,20},{5,21},{6,22},{7,23},{8,24},{9,... | collective-permute-start | bytes 147464 | tf_op jit(solution)/shard_map/ppermute | solution.py:562
  17.2 8.2 %collective-permute-start.2 = (bf16[64,384]{1,0:T(8,128)(2,1)S(1)}, bf16[64,384]{1,0:T(8,128)(2,1)S(1)}, u32[]{:S(2)}, u32[]{:S(2)}) collective-permute-start(bf16[64,384]{1,0:T(8,128)(2,1)S(1)} %image_tower.1), channel_id=1, source_target_pairs={{0,24},{1,25},{2,26},{3,27},{4,28},{5,29},{6,30},{7,31},{8,16},{9,... | collective-permute-start | bytes 147464 | tf_op jit(solution)/shard_map/ppermute | solution.py:562
  25.3 13.6 %collective-permute-start.3 = (bf16[256,384]{1,0:T(8,128)(2,1)S(1)}, bf16[256,384]{1,0:T(8,128)(2,1)S(1)}, u32[]{:S(2)}, u32[]{:S(2)}) collective-permute-start(bf16[256,384]{1,0:T(8,128)(2,1)S(1)} %pad_maximum_fusion.3), channel_id=1, source_target_pairs={{0,2},{1,3},{2,0},{3,1},{4,6},{5,7},{6,4},{7,5},{8,10},{9,11},{10,... | collective-permute-start | bytes 589832 | tf_op jit(solution)/shard_map/ppermute | solution.py:562
  27.1 11.8 %collective-permute-start.4 = (bf16[256,384]{1,0:T(8,128)(2,1)S(1)}, bf16[256,384]{1,0:T(8,128)(2,1)S(1)}, u32[]{:S(2)}, u32[]{:S(2)}) collective-permute-start(bf16[256,384]{1,0:T(8,128)(2,1)S(1)} %pad_maximum_fusion.3), channel_id=1, source_target_pairs={{0,4},{1,5},{2,6},{3,7},{4,0},{5,1},{6,2},{7,3},{8,12},{9,13},{10,... | collective-permute-start | bytes 589832 | tf_op jit(solution)/shard_map/ppermute | solution.py:562
  28.6 10.3 %collective-permute-start.5 = (bf16[256,384]{1,0:T(8,128)(2,1)S(1)}, bf16[256,384]{1,0:T(8,128)(2,1)S(1)}, u32[]{:S(2)}, u32[]{:S(2)}) collective-permute-start(bf16[256,384]{1,0:T(8,128)(2,1)S(1)} %pad_maximum_fusion.3), channel_id=1, source_target_pairs={{0,6},{1,7},{2,4},{3,5},{4,2},{5,3},{6,0},{7,1},{8,14},{9,15},{10,... | collective-permute-start | bytes 589832 | tf_op jit(solution)/shard_map/ppermute | solution.py:562
  45.3 4.7 %collective-permute-start.10 = (f32[40,128]{1,0:T(8,128)S(1)}, f32[40,128]{1,0:T(8,128)S(1)}, u32[]{:S(2)}, u32[]{:S(2)}) collective-permute-start(f32[40,128]{1,0:T(8,128)S(1)} %add.113), channel_id=1, source_target_pairs={{0,6},{1,7},{2,4},{3,5},{4,2},{5,3},{6,0},{7,1},{8,14},{9,15},{10,... | collective-permute-start | bytes 61448 | tf_op jit(solution)/shard_map/ppermute | solution.py:562
  48.5 3.8 %collective-permute-start.9 = (f32[40,128]{1,0:T(8,128)S(1)}, f32[40,128]{1,0:T(8,128)S(1)}, u32[]{:S(2)}, u32[]{:S(2)}) collective-permute-start(f32[40,128]{1,0:T(8,128)S(1)} %add.113), channel_id=1, source_target_pairs={{0,4},{1,5},{2,6},{3,7},{4,0},{5,1},{6,2},{7,3},{8,12},{9,13},{10,... | collective-permute-start | bytes 61448 | tf_op jit(solution)/shard_map/ppermute | solution.py:562
  52.3 3.8 %collective-permute-start.11 = (f32[40,128]{1,0:T(8,128)S(1)}, f32[40,128]{1,0:T(8,128)S(1)}, u32[]{:S(2)}, u32[]{:S(2)}) collective-permute-start(f32[40,128]{1,0:T(8,128)S(1)} %add_add_fusion), channel_id=1, source_target_pairs={{0,8},{1,9},{2,10},{3,11},{4,12},{5,13},{6,14},{7,15},{8,0},{9,1},... | collective-permute-start | bytes 61448 | tf_op jit(solution)/shard_map/ppermute | solution.py:562
  56.1 4.7 %collective-permute-start.12 = (f32[40,128]{1,0:T(8,128)S(1)}, f32[40,128]{1,0:T(8,128)S(1)}, u32[]{:S(2)}, u32[]{:S(2)}) collective-permute-start(f32[40,128]{1,0:T(8,128)S(1)} %add.117), channel_id=1, source_target_pairs={{0,16},{1,17},{2,18},{3,19},{4,20},{5,21},{6,22},{7,23},{8,24},{9,... | collective-permute-start | bytes 61448 | tf_op jit(solution)/shard_map/ppermute | solution.py:562
  64.0 6.1 %collective-permute-start.13 = (bf16[768,384]{1,0:T(8,128)(2,1)S(1)}, bf16[768,384]{1,0:T(8,128)(2,1)S(1)}, u32[]{:S(2)}, u32[]{:S(2)}) collective-permute-start(bf16[768,384]{1,0:T(8,128)(2,1)S(1)} %get-tuple-element.106), channel_id=1, source_target_pairs={{0,1},{1,0},{2,3},{3,2},{4,5},{5,4},{6,7},{7,6},{8,9},{9,8},{10,11... | collective-permute-start | bytes 1769480 | tf_op jit(solution)/shard_map/ppermute | solution.py:562
  64.1 6.0 %collective-permute-start.15 = (bf16[192,384]{1,0:T(8,128)(2,1)S(1)}, bf16[192,384]{1,0:T(8,128)(2,1)S(1)}, u32[]{:S(2)}, u32[]{:S(2)}) collective-permute-start(bf16[192,384]{1,0:T(8,128)(2,1)S(1)} %get-tuple-element.110), channel_id=1, source_target_pairs={{0,1},{1,0},{2,3},{3,2},{4,5},{5,4},{6,7},{7,6},{8,9},{9,8},{10,11... | collective-permute-start | bytes 442376 | tf_op jit(solution)/shard_map/ppermute | solution.py:562
  72.6 17.3 %collective-permute-start.16 = (bf16[432,384]{1,0:T(8,128)(2,1)S(1)}, bf16[432,384]{1,0:T(8,128)(2,1)S(1)}, u32[]{:S(2)}, u32[]{:S(2)}) collective-permute-start(bf16[432,384]{1,0:T(8,128)(2,1)S(1)} %get-tuple-element.150), channel_id=1, source_target_pairs={{0,2},{1,3},{2,0},{3,1},{4,6},{5,7},{6,4},{7,5},{8,10},{9,11},{10,... | collective-permute-start | bytes 995336 | tf_op jit(solution)/shard_map/ppermute | solution.py:562
  74.2 16.7 %collective-permute-start.17 = (bf16[432,384]{1,0:T(8,128)(2,1)S(1)}, bf16[432,384]{1,0:T(8,128)(2,1)S(1)}, u32[]{:S(2)}, u32[]{:S(2)}) collective-permute-start(bf16[432,384]{1,0:T(8,128)(2,1)S(1)} %get-tuple-element.149), channel_id=1, source_target_pairs={{0,4},{1,5},{2,6},{3,7},{4,0},{5,1},{6,2},{7,3},{8,12},{9,13},{10,... | collective-permute-start | bytes 995336 | tf_op jit(solution)/shard_map/ppermute | solution.py:562
  74.7 16.2 %collective-permute-start.18 = (bf16[432,384]{1,0:T(8,128)(2,1)S(1)}, bf16[432,384]{1,0:T(8,128)(2,1)S(1)}, u32[]{:S(2)}, u32[]{:S(2)}) collective-permute-start(bf16[432,384]{1,0:T(8,128)(2,1)S(1)} %get-tuple-element.148), channel_id=1, source_target_pairs={{0,6},{1,7},{2,4},{3,5},{4,2},{5,3},{6,0},{7,1},{8,14},{9,15},{10,... | collective-permute-start | bytes 995336 | tf_op jit(solution)/shard_map/ppermute | solution.py:562
  91.1 6.2 %collective-permute-start.19 = (bf16[240,384]{1,0:T(8,128)(2,1)S(1)}, bf16[240,384]{1,0:T(8,128)(2,1)S(1)}, u32[]{:S(2)}, u32[]{:S(2)}) collective-permute-start(bf16[240,384]{1,0:T(8,128)(2,1)S(1)} %slice.90), channel_id=1, source_target_pairs={{0,8},{1,9},{2,10},{3,11},{4,12},{5,13},{6,14},{7,15},{8,0},{9,1},... | collective-permute-start | bytes 552968 | tf_op jit(solution)/shard_map/ppermute | solution.py:562
  92.6 6.1 %collective-permute-start.21 = (bf16[192,384]{1,0:T(8,128)(2,1)S(1)}, bf16[192,384]{1,0:T(8,128)(2,1)S(1)}, u32[]{:S(2)}, u32[]{:S(2)}) collective-permute-start(bf16[192,384]{1,0:T(8,128)(2,1)S(1)} %get-tuple-element.153), channel_id=1, source_target_pairs={{0,2},{1,3},{2,0},{3,1},{4,6},{5,7},{6,4},{7,5},{8,10},{9,11},{10,... | collective-permute-start | bytes 442376 | tf_op jit(solution)/shard_map/ppermute | solution.py:562
  93.7 8.8 %collective-permute-start.22 = (bf16[192,384]{1,0:T(8,128)(2,1)S(1)}, bf16[192,384]{1,0:T(8,128)(2,1)S(1)}, u32[]{:S(2)}, u32[]{:S(2)}) collective-permute-start(bf16[192,384]{1,0:T(8,128)(2,1)S(1)} %get-tuple-element.152), channel_id=1, source_target_pairs={{0,4},{1,5},{2,6},{3,7},{4,0},{5,1},{6,2},{7,3},{8,12},{9,13},{10,... | collective-permute-start | bytes 442376 | tf_op jit(solution)/shard_map/ppermute | solution.py:562
  94.5 10.7 %collective-permute-start.24 = (bf16[192,384]{1,0:T(8,128)(2,1)S(1)}, bf16[192,384]{1,0:T(8,128)(2,1)S(1)}, u32[]{:S(2)}, u32[]{:S(2)}) collective-permute-start(bf16[192,384]{1,0:T(8,128)(2,1)S(1)} %get-tuple-element.151), channel_id=1, source_target_pairs={{0,6},{1,7},{2,4},{3,5},{4,2},{5,3},{6,0},{7,1},{8,14},{9,15},{10,... | collective-permute-start | bytes 442376 | tf_op jit(solution)/shard_map/ppermute | solution.py:562
  102.6 7.3 %collective-permute-start.23 = (bf16[144,384]{1,0:T(8,128)(2,1)S(1)}, bf16[144,384]{1,0:T(8,128)(2,1)S(1)}, u32[]{:S(2)}, u32[]{:S(2)}) collective-permute-start(bf16[144,384]{1,0:T(8,128)(2,1)S(1)} %slice.95), channel_id=1, source_target_pairs={{0,16},{1,17},{2,18},{3,19},{4,20},{5,21},{6,22},{7,23},{8,24},{9,... | collective-permute-start | bytes 331784 | tf_op jit(solution)/shard_map/ppermute | solution.py:562
  110.0 4.9 %collective-permute-start.29 = (bf16[96,384]{1,0:T(8,128)(2,1)S(1)}, bf16[96,384]{1,0:T(8,128)(2,1)S(1)}, u32[]{:S(2)}, u32[]{:S(2)}) collective-permute-start(bf16[96,384]{1,0:T(8,128)(2,1)S(1)} %slice.101), channel_id=1, source_target_pairs={{0,8},{1,9},{2,10},{3,11},{4,12},{5,13},{6,14},{7,15},{8,0},{9,1},... | collective-permute-start | bytes 221192 | tf_op jit(solution)/shard_map/ppermute | solution.py:562
  110.8 7.4 %collective-permute-start.25 = (bf16[96,384]{1,0:T(8,128)(2,1)S(1)}, bf16[96,384]{1,0:T(8,128)(2,1)S(1)}, u32[]{:S(2)}, u32[]{:S(2)}) collective-permute-start(bf16[96,384]{1,0:T(8,128)(2,1)S(1)} %get-tuple-element.157), channel_id=1, source_target_pairs={{0,16},{1,17},{2,18},{3,19},{4,20},{5,21},{6,22},{7,23},{8,24},{9,... | collective-permute-start | bytes 221192 | tf_op jit(solution)/shard_map/ppermute | solution.py:562
  114.9 5.0 %collective-permute-start.30 = (bf16[48,384]{1,0:T(8,128)(2,1)S(1)}, bf16[48,384]{1,0:T(8,128)(2,1)S(1)}, u32[]{:S(2)}, u32[]{:S(2)}) collective-permute-start(bf16[48,384]{1,0:T(8,128)(2,1)S(1)} %slice.103), channel_id=1, source_target_pairs={{0,16},{1,17},{2,18},{3,19},{4,20},{5,21},{6,22},{7,23},{8,24},{9,... | collective-permute-start | bytes 110600 | tf_op jit(solution)/shard_map/ppermute | solution.py:562
  118.2 5.6 %collective-permute-start.26 = (bf16[192,384]{1,0:T(8,128)(2,1)S(1)}, bf16[192,384]{1,0:T(8,128)(2,1)S(1)}, u32[]{:S(2)}, u32[]{:S(2)}) collective-permute-start(bf16[192,384]{1,0:T(8,128)(2,1)S(1)} %pad_maximum_fusion.4), channel_id=1, source_target_pairs={{0,8},{1,9},{2,10},{3,11},{4,12},{5,13},{6,14},{7,15},{8,0},{9,1},... | collective-permute-start | bytes 442376 | tf_op jit(solution)/shard_map/ppermute | solution.py:562
  119.9 5.8 %collective-permute-start.31 = (bf16[48,384]{1,0:T(8,128)(2,1)S(1)}, bf16[48,384]{1,0:T(8,128)(2,1)S(1)}, u32[]{:S(2)}, u32[]{:S(2)}) collective-permute-start(bf16[48,384]{1,0:T(8,128)(2,1)S(1)} %add_convert_fusion.8), channel_id=1, source_target_pairs={{0,16},{1,17},{2,18},{3,19},{4,20},{5,21},{6,22},{7,23},{8,24},{9,... | collective-permute-start | bytes 110600 | tf_op jit(solution)/shard_map/ppermute | solution.py:562
  123.9 9.6 %collective-permute-start.27 = (bf16[432,384]{1,0:T(8,128)(2,1)S(1)}, bf16[432,384]{1,0:T(8,128)(2,1)S(1)}, u32[]{:S(2)}, u32[]{:S(2)}) collective-permute-start(bf16[432,384]{1,0:T(8,128)(2,1)S(1)} %pad_maximum_fusion.2), channel_id=1, source_target_pairs={{0,2},{1,3},{2,0},{3,1},{4,6},{5,7},{6,4},{7,5},{8,10},{9,11},{10,... | collective-permute-start | bytes 995336 | tf_op jit(solution)/shard_map/ppermute | solution.py:562
  124.5 9.1 %collective-permute-start.28 = (bf16[432,384]{1,0:T(8,128)(2,1)S(1)}, bf16[432,384]{1,0:T(8,128)(2,1)S(1)}, u32[]{:S(2)}, u32[]{:S(2)}) collective-permute-start(bf16[432,384]{1,0:T(8,128)(2,1)S(1)} %pad_maximum_fusion.2), channel_id=1, source_target_pairs={{0,4},{1,5},{2,6},{3,7},{4,0},{5,1},{6,2},{7,3},{8,12},{9,13},{10,... | collective-permute-start | bytes 995336 | tf_op jit(solution)/shard_map/ppermute | solution.py:562
  125.7 4.8 %collective-permute-start.32 = (bf16[96,384]{1,0:T(8,128)(2,1)S(1)}, bf16[96,384]{1,0:T(8,128)(2,1)S(1)}, u32[]{:S(2)}, u32[]{:S(2)}) collective-permute-start(bf16[96,384]{1,0:T(8,128)(2,1)S(1)} %pad_maximum_fusion.6), channel_id=1, source_target_pairs={{0,8},{1,9},{2,10},{3,11},{4,12},{5,13},{6,14},{7,15},{8,0},{9,1},... | collective-permute-start | bytes 221192 | tf_op jit(solution)/shard_map/ppermute | solution.py:562
  128.2 12.0 %collective-permute-start.33 = (bf16[432,384]{1,0:T(8,128)(2,1)S(1)}, bf16[432,384]{1,0:T(8,128)(2,1)S(1)}, u32[]{:S(2)}, u32[]{:S(2)}) collective-permute-start(bf16[432,384]{1,0:T(8,128)(2,1)S(1)} %pad_maximum_fusion.2), channel_id=1, source_target_pairs={{0,6},{1,7},{2,4},{3,5},{4,2},{5,3},{6,0},{7,1},{8,14},{9,15},{10,... | collective-permute-start | bytes 995336 | tf_op jit(solution)/shard_map/ppermute | solution.py:562
  133.5 6.7 %collective-permute-start.34 = (bf16[192,384]{1,0:T(8,128)(2,1)S(1)}, bf16[192,384]{1,0:T(8,128)(2,1)S(1)}, u32[]{:S(2)}, u32[]{:S(2)}) collective-permute-start(bf16[192,384]{1,0:T(8,128)(2,1)S(1)} %pad_maximum_fusion.5), channel_id=1, source_target_pairs={{0,2},{1,3},{2,0},{3,1},{4,6},{5,7},{6,4},{7,5},{8,10},{9,11},{10,... | collective-permute-start | bytes 442376 | tf_op jit(solution)/shard_map/ppermute | solution.py:562
  137.1 6.1 %collective-permute-start.35 = (bf16[192,384]{1,0:T(8,128)(2,1)S(1)}, bf16[192,384]{1,0:T(8,128)(2,1)S(1)}, u32[]{:S(2)}, u32[]{:S(2)}) collective-permute-start(bf16[192,384]{1,0:T(8,128)(2,1)S(1)} %pad_maximum_fusion.5), channel_id=1, source_target_pairs={{0,4},{1,5},{2,6},{3,7},{4,0},{5,1},{6,2},{7,3},{8,12},{9,13},{10,... | collective-permute-start | bytes 442376 | tf_op jit(solution)/shard_map/ppermute | solution.py:562
  143.4 7.1 %collective-permute-start.36 = (bf16[192,384]{1,0:T(8,128)(2,1)S(1)}, bf16[192,384]{1,0:T(8,128)(2,1)S(1)}, u32[]{:S(2)}, u32[]{:S(2)}) collective-permute-start(bf16[192,384]{1,0:T(8,128)(2,1)S(1)} %pad_maximum_fusion.5), channel_id=1, source_target_pairs={{0,6},{1,7},{2,4},{3,5},{4,2},{5,3},{6,0},{7,1},{8,14},{9,15},{10,... | collective-permute-start | bytes 442376 | tf_op jit(solution)/shard_map/ppermute | solution.py:562
  (34 other events, 187.7 us)

commit v8 on v7

--- a/solution.py
+++ b/solution.py
@@ -690,10 +690,10 @@
         got = swap(m[192:], 8)
         a = added(keep_a, [other]).reshape(4, 192, D)
         got_a = plane(a)
-        got, got_a[0], got_a[1] = lax.optimization_barrier((got, got_a[0], got_a[1]))
+        got, got_a[0] = lax.optimization_barrier((got, got_a[0]))
         m = added(joined(m[:192], [m[384:]]), [got])
         got = swap(m[96:], 16)
-        got, got_a = lax.optimization_barrier((got, got_a))
+        got, got_a[1], got_a[2] = lax.optimization_barrier((got, got_a[1], got_a[2]))
         a = added(a[0], got_a)
         got_a = swap(a[96:], 8)
         m = added(joined(m[:96], [m[192:]]), [got])
@@ -706,8 +706,8 @@
         a = added(a[:48], [got_a])
         a = joined(a, [swap(a, 16)])
         a = joined(a, [swap(a, 8)])
-        got_m[0], got_m[1], a = lax.optimization_barrier((got_m[0], got_m[1], a))
-        got_a = plane([a] * 4)
+        last, got_m[0], got_m[1] = lax.optimization_barrier((a, got_m[0], got_m[1]))
+        got_a = plane([a, a, a, last])
         got_m[2], got_a[0], got_a[1] = lax.optimization_barrier((got_m[2], got_a[0], got_a[1]))
         m = joined(m, got_m)
         grad_down, grad_up, grad_proj, gain2 = spread_mlp(m, swap(m, 1))

time: 157 us -> 152 us (0.968)
  starting transfers between devices: 50.5 us -> 47.7 us
  waiting for transfers between devices: 40.1 us -> 38 us
    ppermute x39, starting transfers between devices: 50.5 us -> 47.7 us  [swap(): return lax.ppermute(v, AXES, [(i, i ^ mask) for i in range(32)])]
    ppermute x39, waiting for transfers between devices: 40.1 us -> 38 us  [swap(): return lax.ppermute(v, AXES, [(i, i ^ mask) for i in range(32)])]
  transfers between devices with their start and end apart: 39 -> 39, of which waited for: 24 -> 22; matrix products, arithmetic and copies ran while one was open for 1% -> 1% of each run, Pallas kernels for 26% -> 27%
where the time goes in v8:
time: 152 us
  Pallas kernels  58.9 us (39%)
  starting transfers between devices  47.7 us (31%)
  waiting for transfers between devices  38 us (25%)
  between operations  4.26 us (3%)
  local copies, waits for them, and re-layouts  1.58 us (1%)
    ppermute x39, starting transfers between devices, swap(): return lax.ppermute(v, AXES, [(i, i ^ mask) for i in range(32)])  47.7 us
    ppermute x39, waiting for transfers between devices, swap(): return lax.ppermute(v, AXES, [(i, i ^ mask) for i in range(32)])  38 us
    pallas_call x1, Pallas kernels, att_back(): pl.pallas_call(att_back_kernel, grid=(n // TOK_BLOCK,), in_specs=[SMEM] +...  13.7 us
    pallas_call x5, Pallas kernels, call(): pl.pallas_call(kernel, in_specs=[SMEM] * smem + [VMEM] * (len(args) - sme...  11.2 us
    pallas_call x1, Pallas kernels, image_tower(): pl.pallas_call(image_kernel, grid=(count // IMG_BLOCK,), in_specs=[pl.Blo...  10.8 us
    pallas_call x1, Pallas kernels, text_mlp(): pl.pallas_call(text_mlp_kernel, grid=(n // TOK_BLOCK,), in_specs=[token_r...  10 us
    pallas_call x1, Pallas kernels, text_att(): pl.pallas_call(text_att_kernel, grid=(blocks,), in_specs=[token_rows(D),...  7.86 us
    pallas_call x1, Pallas kernels, mlp_back(): pl.pallas_call(mlp_back_kernel, grid=(n // TOK_BLOCK,), in_specs=[SMEM, b...  5.36 us
  transfers between devices with their start and end apart: 39, of which 22 were waited for; matrix products, arithmetic and copies ran while one was open for 1% of the time, Pallas kernels for 27%

profile of v8, /device:TPU:0, one launch (start us, length us, event | category | flops | bytes accessed | tf_op | source)
XLA Modules:
  0.0 151.7 jit_solution(4438123383060981552)
XLA Ops:
  0.7 10.8 %image_tower.1 = bf16[64,384]{1,0:T(8,128)(2,1)S(1)} custom-call(bf16[50,64,384]{2,1,0:T(8,128)(2,1)} %bitcast.23, f32[384]{0:T(512)} %g1.5, bf16[384,1152]{1,0:T(8,128)(2,1)} %wqkv.5, bf16[384,384]{1,0:T(8,128)(2,1)} %wout.3, f32[384]{0:T(512)} %g2.4, bf16[384,1536]{1,0:T(8,128)(2,1)} %wup.4, bf16[1536,384]{1,0:T(8,128)(2,1)} %wdown.3, bf16[384,384]{1,0:T(8,128)(2,1)} %wproj.3), custom_call_target="tpu_custom_call" | custom-call | flops 12000000000 | bytes 36000000 | tf_op jit(solution)/shard_map/image_tower/pallas_call | solution.py:141
  11.5 3.1 %collective-permute-start = (bf16[64,384]{1,0:T(8,128)(2,1)S(1)}, bf16[64,384]{1,0:T(8,128)(2,1)S(1)}, u32[]{:S(2)}, u32[]{:S(2)}) collective-permute-start(bf16[64,384]{1,0:T(8,128)(2,1)S(1)} %image_tower.1), channel_id=1, source_target_pairs={{0,8},{1,9},{2,10},{3,11},{4,12},{5,13},{6,14},{7,15},{8,0},{9,1},... | collective-permute-start | bytes 147464 | tf_op jit(solution)/shard_map/ppermute | solution.py:562
  14.6 2.6 %collective-permute-start.1 = (bf16[64,384]{1,0:T(8,128)(2,1)S(1)}, bf16[64,384]{1,0:T(8,128)(2,1)S(1)}, u32[]{:S(2)}, u32[]{:S(2)}) collective-permute-start(bf16[64,384]{1,0:T(8,128)(2,1)S(1)} %image_tower.1), channel_id=1, source_target_pairs={{0,16},{1,17},{2,18},{3,19},{4,20},{5,21},{6,22},{7,23},{8,24},{9,... | collective-permute-start | bytes 147464 | tf_op jit(solution)/shard_map/ppermute | solution.py:562
  17.4 7.9 %text_att.1 = (bf16[1024,384]{1,0:T(8,128)(2,1)S(1)}, bf16[1024,384]{1,0:T(8,128)(2,1)}, bf16[1024,1152]{1,0:T(8,128)(2,1)}, bf16[8,3,256,128]{3,2,1,0:T(8,128)(2,1)}, bf16[1024,384]{1,0:T(8,128)(2,1)}) custom-call(bf16[1024,384]{1,0:T(8,128)(2,1)} %tok_ref.5, s32[4,1,256]{2,1,0:T(1,128)S(1)} %reshape.71.lab_ref, f32[384]{0:T(512)S(1)} %copy-done.9, ...), custom_call_target="tpu_custom_call" | custom-call | flops 8999999488 | bytes 27000000 | tf_op jit(solution)/shard_map/text_att/pallas_call | solution.py:256
  25.3 1.8 %collective-permute-start.3 = (bf16[256,384]{1,0:T(8,128)(2,1)S(1)}, bf16[256,384]{1,0:T(8,128)(2,1)S(1)}, u32[]{:S(2)}, u32[]{:S(2)}) collective-permute-start(bf16[256,384]{1,0:T(8,128)(2,1)S(1)} %pad_maximum_fusion.3), channel_id=1, source_target_pairs={{0,2},{1,3},{2,0},{3,1},{4,6},{5,7},{6,4},{7,5},{8,10},{9,11},{10,... | collective-permute-start | bytes 589832 | tf_op jit(solution)/shard_map/ppermute | solution.py:562
  28.9 10.0 %text_mlp.1 = (bf16[1024,384]{1,0:T(8,128)(2,1)}, f32[1024,384]{1,0:T(8,128)}, bf16[1024,1536]{1,0:T(8,128)(2,1)}, f32[64,1536]{1,0:T(8,128)S(1)}, bf16[64,384]{...) custom-call(bf16[1024,384]{1,0:T(8,128)(2,1)S(1)} %copy-done.3, ...), custom_call_target="tpu_custom_call" | custom-call | flops 11000000512 | bytes 33000000 | tf_op jit(solution)/shard_map/text_mlp/pallas_call | solution.py:280
  40.5 1.7 %collective-permute-done.6.other = bf16[1024,384]{1,0:T(8,128)(2,1)} collective-permute-done((bf16[1024,384]{1,0:T(8,128)(2,1)S(1)}, bf16[1024,384]{1,0:T(8,128)(2,1)}, u32[]{:S(2)}, u32[]{:S(2)}) %collective-permute-start.6) | collective-permute-done | bytes 786464 | tf_op jit(solution)/shard_map/ppermute | solution.py:562
  42.2 1.9 %cosine.1 = (f32[64,2048]{1,0:T(8,128)S(1)}, f32[40,128]{1,0:T(8,128)S(1)}) custom-call(f32[1]{0:T(128)S(6)} %copy.47.scale_ref, s32[1]{0:T(128)} %bitcast.mine_ref, bf16[64,384]{1,0:T(8,128)(2,1)S(1)} %get-tuple-element.82.emb, bf16[1024,384]{1,0:T(8,128)(2,1)S(1)} %constant_dynamic-update-slice_fusion.own, bf16[1024,384]{1,0:T(8,128)(2,1)} %collective-permute-done.6.other, ...), custom_call_target="tpu_custom_call" | custom-call | flops 3000000000 | bytes 9000000 | tf_op jit(solution)/shard_map/cosine/pallas_call | solution.py:513
  45.3 2.7 %collective-permute-start.10 = (f32[40,128]{1,0:T(8,128)S(1)}, f32[40,128]{1,0:T(8,128)S(1)}, u32[]{:S(2)}, u32[]{:S(2)}) collective-permute-start(f32[40,128]{1,0:T(8,128)S(1)} %add.113), channel_id=1, source_target_pairs={{0,6},{1,7},{2,4},{3,5},{4,2},{5,3},{6,0},{7,1},{8,14},{9,15},{10,... | collective-permute-start | bytes 61448 | tf_op jit(solution)/shard_map/ppermute | solution.py:562
  50.0 1.8 %collective-permute-done.8 = f32[40,128]{1,0:T(8,128)S(1)} collective-permute-done((f32[40,128]{1,0:T(8,128)S(1)}, f32[40,128]{1,0:T(8,128)S(1)}, u32[]{:S(2)}, u32[]{:S(2)}) %collective-permute-start.8) | collective-permute-done | bytes 20512 | tf_op jit(solution)/shard_map/ppermute | solution.py:562
  53.1 3.1 %collective-permute-done.11 = f32[40,128]{1,0:T(8,128)S(1)} collective-permute-done((f32[40,128]{1,0:T(8,128)S(1)}, f32[40,128]{1,0:T(8,128)S(1)}, u32[]{:S(2)}, u32[]{:S(2)}) %collective-permute-start.11) | collective-permute-done | bytes 20512 | tf_op jit(solution)/shard_map/ppermute | solution.py:562
  56.1 2.2 %collective-permute-start.12 = (f32[40,128]{1,0:T(8,128)S(1)}, f32[40,128]{1,0:T(8,128)S(1)}, u32[]{:S(2)}, u32[]{:S(2)}) collective-permute-start(f32[40,128]{1,0:T(8,128)S(1)} %add.117), channel_id=1, source_target_pairs={{0,16},{1,17},{2,18},{3,19},{4,20},{5,21},{6,22},{7,23},{8,24},{9,... | collective-permute-start | bytes 61448 | tf_op jit(solution)/shard_map/ppermute | solution.py:562
  58.4 1.7 %rows.1.dt_row = f32[64,384]{1,0:T(8,128)S(1)} custom-call(f32[1]{0:T(128)S(6)} %copy.47.scale_ref, f32[64,2048]{1,0:T(8,128)S(1)} %get-tuple-element.88.g_ref, bf16[1024,384]{1,0:T(8,128)(2,1)S(1)} %constant_dynamic-update-slice_fusion.own, bf16[1024,384]{1,0:T(8,128)(2,1)} %collective-permute-done.6.other, s32[64,1]{1,0:T(8,128)S(1)} %copy.29.pair), custom_call_target="tpu_custom_call" | custom-call | flops 2000000000 | bytes 6000000 | tf_op jit(solution)/shard_map/rows/pallas_call | solution.py:513
  60.9 3.1 %head_back.1 = (bf16[768,384]{1,0:T(8,128)(2,1)S(1)}, bf16[768,384]{1,0:T(8,128)(2,1)S(1)}, bf16[192,384]{1,0:T(8,128)(2,1)S(1)}, bf16[192,384]{1,0:T(8,128)(2,1...) custom-call(f32[1]{0:T(128)S(6)} %copy.47.scale_ref, ...), custom_call_target="tpu_custom_call" | custom-call | flops 5000000000 | bytes 15000000 | tf_op jit(solution)/shard_map/head_back/pallas_call | solution.py:513
  64.6 5.4 %mlp_back.1 = (f32[1024,384]{1,0:T(8,128)S(1)}, bf16[1024,384]{1,0:T(8,128)(2,1)S(1)}, bf16[768,384]{1,0:T(8,128)(2,1)S(1)}, bf16[768,384]{1,0:T(8,128)(2,1)S(1)}) custom-call(s32[1]{0:T(128)} %bitcast.mine_ref, s32[4,1,256]{2,1,0:T(1,128)S(1)} %reshape.71.lab_ref, bf16[1024,384]{1,0:T(8,128)(2,1)S(1)} %copy-done.16, bf16[1024,1536]{1,0:T(8,128)(2,1)S(1)} %copy-done.10, ...), custom_call_target="tpu_custom_call" | custom-call | flops 8999999488 | bytes 27000000 | tf_op jit(solution)/shard_map/mlp_back/pallas_call | solution.py:530
  70.3 1.7 %collective-permute-done.14 = bf16[768,384]{1,0:T(8,128)(2,1)S(1)} collective-permute-done((bf16[768,384]{1,0:T(8,128)(2,1)S(1)}, bf16[768,384]{1,0:T(8,128)(2,1)S(1)}, u32[]{:S(2)}, u32[]{:S(2)}) %collective-permute-start.14) | collective-permute-done | bytes 589856 | tf_op jit(solution)/shard_map/ppermute | solution.py:562
  76.2 13.7 %att_back.1 = (f32[1024,384]{1,0:T(8,128)}, bf16[768,384]{1,0:T(8,128)(2,1)S(1)}, bf16[768,384]{1,0:T(8,128)(2,1)S(1)}) custom-call(s32[1]{0:T(128)} %bitcast.mine_ref, bf16[1024,1152]{1,0:T(8,128)(2,1)S(1)} %copy-done.11, bf16[8,3,256,128]{3,2,1,0:T(8,128)(2,1)S(1)} %copy-done.15, bf16[1024,384]{1,0:T(8,128)(2,1)S(1)} %get-tuple-element.109.dxb_all, ...), custom_call_target="tpu_custom_call" | custom-call | flops 14000000000 | bytes 42000000 | tf_op jit(solution)/shard_map/att_back/pallas_call | solution.py:545
  94.5 1.8 %collective-permute-start.24 = (bf16[192,384]{1,0:T(8,128)(2,1)S(1)}, bf16[192,384]{1,0:T(8,128)(2,1)S(1)}, u32[]{:S(2)}, u32[]{:S(2)}) collective-permute-start(bf16[192,384]{1,0:T(8,128)(2,1)S(1)} %get-tuple-element.149), channel_id=1, source_target_pairs={{0,6},{1,7},{2,4},{3,5},{4,2},{5,3},{6,0},{7,1},{8,14},{9,15},{10,... | collective-permute-start | bytes 442376 | tf_op jit(solution)/shard_map/ppermute | solution.py:562
  98.8 2.8 %collective-permute-start.22 = (bf16[144,384]{1,0:T(8,128)(2,1)S(1)}, bf16[144,384]{1,0:T(8,128)(2,1)S(1)}, u32[]{:S(2)}, u32[]{:S(2)}) collective-permute-start(bf16[144,384]{1,0:T(8,128)(2,1)S(1)} %slice.93), channel_id=1, source_target_pairs={{0,16},{1,17},{2,18},{3,19},{4,20},{5,21},{6,22},{7,23},{8,24},{9,... | collective-permute-start | bytes 331784 | tf_op jit(solution)/shard_map/ppermute | solution.py:562
  102.6 3.1 %collective-permute-done.22 = bf16[144,384]{1,0:T(8,128)(2,1)S(1)} collective-permute-done((bf16[144,384]{1,0:T(8,128)(2,1)S(1)}, bf16[144,384]{1,0:T(8,128)(2,1)S(1)}, u32[]{:S(2)}, u32[]{:S(2)}) %collective-permute-start.22) | collective-permute-done | bytes 110624 | tf_op jit(solution)/shard_map/ppermute | solution.py:562
  106.8 3.5 %collective-permute-start.29 = (bf16[96,384]{1,0:T(8,128)(2,1)S(1)}, bf16[96,384]{1,0:T(8,128)(2,1)S(1)}, u32[]{:S(2)}, u32[]{:S(2)}) collective-permute-start(bf16[96,384]{1,0:T(8,128)(2,1)S(1)} %get-tuple-element.155), channel_id=1, source_target_pairs={{0,16},{1,17},{2,18},{3,19},{4,20},{5,21},{6,22},{7,23},{8,24},{9,... | collective-permute-start | bytes 221192 | tf_op jit(solution)/shard_map/ppermute | solution.py:562
  110.4 2.5 %collective-permute-start.26 = (bf16[48,384]{1,0:T(8,128)(2,1)S(1)}, bf16[48,384]{1,0:T(8,128)(2,1)S(1)}, u32[]{:S(2)}, u32[]{:S(2)}) collective-permute-start(bf16[48,384]{1,0:T(8,128)(2,1)S(1)} %slice.99), channel_id=1, source_target_pairs={{0,16},{1,17},{2,18},{3,19},{4,20},{5,21},{6,22},{7,23},{8,24},{9,... | collective-permute-start | bytes 110600 | tf_op jit(solution)/shard_map/ppermute | solution.py:562
  113.9 2.4 %collective-permute-start.30 = (bf16[192,384]{1,0:T(8,128)(2,1)S(1)}, bf16[192,384]{1,0:T(8,128)(2,1)S(1)}, u32[]{:S(2)}, u32[]{:S(2)}) collective-permute-start(bf16[192,384]{1,0:T(8,128)(2,1)S(1)} %pad_maximum_fusion.4), channel_id=1, source_target_pairs={{0,8},{1,9},{2,10},{3,11},{4,12},{5,13},{6,14},{7,15},{8,0},{9,1},... | collective-permute-start | bytes 442376 | tf_op jit(solution)/shard_map/ppermute | solution.py:562
  116.3 1.7 %collective-permute-start.27 = (bf16[48,384]{1,0:T(8,128)(2,1)S(1)}, bf16[48,384]{1,0:T(8,128)(2,1)S(1)}, u32[]{:S(2)}, u32[]{:S(2)}) collective-permute-start(bf16[48,384]{1,0:T(8,128)(2,1)S(1)} %get-tuple-element.145), channel_id=1, source_target_pairs={{0,16},{1,17},{2,18},{3,19},{4,20},{5,21},{6,22},{7,23},{8,24},{9,... | collective-permute-start | bytes 110600 | tf_op jit(solution)/shard_map/ppermute | solution.py:562
  118.0 3.2 %collective-permute-done.27 = bf16[48,384]{1,0:T(8,128)(2,1)S(1)} collective-permute-done((bf16[48,384]{1,0:T(8,128)(2,1)S(1)}, bf16[48,384]{1,0:T(8,128)(2,1)S(1)}, u32[]{:S(2)}, u32[]{:S(2)}) %collective-permute-start.27) | collective-permute-done | bytes 36896 | tf_op jit(solution)/shard_map/ppermute | solution.py:562
  121.3 2.0 %collective-permute-start.28 = (bf16[96,384]{1,0:T(8,128)(2,1)S(1)}, bf16[96,384]{1,0:T(8,128)(2,1)S(1)}, u32[]{:S(2)}, u32[]{:S(2)}) collective-permute-start(bf16[96,384]{1,0:T(8,128)(2,1)S(1)} %pad_maximum_fusion.6), channel_id=1, source_target_pairs={{0,8},{1,9},{2,10},{3,11},{4,12},{5,13},{6,14},{7,15},{8,0},{9,1},... | collective-permute-start | bytes 221192 | tf_op jit(solution)/shard_map/ppermute | solution.py:562
  129.5 2.4 %collective-permute-done.34 = bf16[432,384]{1,0:T(8,128)(2,1)S(1)} collective-permute-done((bf16[432,384]{1,0:T(8,128)(2,1)S(1)}, bf16[432,384]{1,0:T(8,128)(2,1)S(1)}, u32[]{:S(2)}, u32[]{:S(2)}) %collective-permute-start.34) | collective-permute-done | bytes 331808 | tf_op jit(solution)/shard_map/ppermute | solution.py:562
  131.9 4.7 %collective-permute-done.35 = bf16[432,384]{1,0:T(8,128)(2,1)S(1)} collective-permute-done((bf16[432,384]{1,0:T(8,128)(2,1)S(1)}, bf16[432,384]{1,0:T(8,128)(2,1)S(1)}, u32[]{:S(2)}, u32[]{:S(2)}) %collective-permute-start.35) | collective-permute-done | bytes 331808 | tf_op jit(solution)/shard_map/ppermute | solution.py:562
  139.0 2.5 %collective-permute-done.37.other = bf16[1728,384]{1,0:T(8,128)(2,1)S(1)} collective-permute-done((bf16[1728,384]{1,0:T(8,128)(2,1)S(1)}, bf16[1728,384]{1,0:T(8,128)(2,1)S(1)}, u32[]{:S(2)}, u32[]{:S(2)}) %collective-permute-start.37) | collective-permute-done | bytes 1327136 | tf_op jit(solution)/shard_map/ppermute | solution.py:562
  141.4 2.7 %spread_mlp.1 = (f32[1536,384]{1,0:T(8,128)}, f32[384,1536]{1,0:T(8,128)}, f32[384,384]{1,0:T(8,128)}, f32[384]{0:T(512)}) custom-call(s32[1]{0:T(128)} %bitcast.mine_ref, bf16[1728,384]{1,0:T(8,128)(2,1)S(1)} %constant_dynamic-update-slice_fusion.4.own, bf16[1728,384]{1,0:T(8,128)(2,1)S(1)} %collective-permute-done.37.other, ...), custom_call_target="tpu_custom_call" | custom-call | flops 4000000000 | bytes 12000000 | tf_op jit(solution)/shard_map/spread_mlp/pallas_call | solution.py:513
  145.9 1.9 %collective-permute-done.38.other = bf16[768,384]{1,0:T(8,128)(2,1)S(1)} collective-permute-done((bf16[768,384]{1,0:T(8,128)(2,1)S(1)}, bf16[768,384]{1,0:T(8,128)(2,1)S(1)}, u32[]{:S(2)}, u32[]{:S(2)}) %collective-permute-start.38) | collective-permute-done | bytes 589856 | tf_op jit(solution)/shard_map/ppermute | solution.py:562
  147.8 1.7 %spread_att.1 = (f32[384,384]{1,0:T(8,128)}, f32[384,1152]{1,0:T(8,128)}, f32[384]{0:T(512)}) custom-call(s32[1]{0:T(128)} %bitcast.mine_ref, bf16[768,384]{1,0:T(8,128)(2,1)S(1)} %constant_dynamic-update-slice_fusion.11.own, bf16[768,384]{1,0:T(8,128)(2,1)S(1)} %collective-permute-done.38.other, bf16[384,1152]{1,0:T(8,128)(2,1)S(1)} %copy-done.2, ...), custom_call_target="tpu_custom_call" | custom-call | flops 4000000000 | bytes 12000000 | tf_op jit(solution)/shard_map/spread_att/pallas_call | solution.py:513
  (162 shorter events, 33.7 us)
Async XLA Ops:
  11.5 13.8 %collective-permute-start = (bf16[64,384]{1,0:T(8,128)(2,1)S(1)}, bf16[64,384]{1,0:T(8,128)(2,1)S(1)}, u32[]{:S(2)}, u32[]{:S(2)}) collective-permute-start(bf16[64,384]{1,0:T(8,128)(2,1)S(1)} %image_tower.1), channel_id=1, source_target_pairs={{0,8},{1,9},{2,10},{3,11},{4,12},{5,13},{6,14},{7,15},{8,0},{9,1},... | collective-permute-start | bytes 147464 | tf_op jit(solution)/shard_map/ppermute | solution.py:562
  14.6 10.7 %collective-permute-start.1 = (bf16[64,384]{1,0:T(8,128)(2,1)S(1)}, bf16[64,384]{1,0:T(8,128)(2,1)S(1)}, u32[]{:S(2)}, u32[]{:S(2)}) collective-permute-start(bf16[64,384]{1,0:T(8,128)(2,1)S(1)} %image_tower.1), channel_id=1, source_target_pairs={{0,16},{1,17},{2,18},{3,19},{4,20},{5,21},{6,22},{7,23},{8,24},{9,... | collective-permute-start | bytes 147464 | tf_op jit(solution)/shard_map/ppermute | solution.py:562
  17.2 8.2 %collective-permute-start.2 = (bf16[64,384]{1,0:T(8,128)(2,1)S(1)}, bf16[64,384]{1,0:T(8,128)(2,1)S(1)}, u32[]{:S(2)}, u32[]{:S(2)}) collective-permute-start(bf16[64,384]{1,0:T(8,128)(2,1)S(1)} %image_tower.1), channel_id=1, source_target_pairs={{0,24},{1,25},{2,26},{3,27},{4,28},{5,29},{6,30},{7,31},{8,16},{9,... | collective-permute-start | bytes 147464 | tf_op jit(solution)/shard_map/ppermute | solution.py:562
  25.3 13.6 %collective-permute-start.3 = (bf16[256,384]{1,0:T(8,128)(2,1)S(1)}, bf16[256,384]{1,0:T(8,128)(2,1)S(1)}, u32[]{:S(2)}, u32[]{:S(2)}) collective-permute-start(bf16[256,384]{1,0:T(8,128)(2,1)S(1)} %pad_maximum_fusion.3), channel_id=1, source_target_pairs={{0,2},{1,3},{2,0},{3,1},{4,6},{5,7},{6,4},{7,5},{8,10},{9,11},{10,... | collective-permute-start | bytes 589832 | tf_op jit(solution)/shard_map/ppermute | solution.py:562
  27.1 11.8 %collective-permute-start.4 = (bf16[256,384]{1,0:T(8,128)(2,1)S(1)}, bf16[256,384]{1,0:T(8,128)(2,1)S(1)}, u32[]{:S(2)}, u32[]{:S(2)}) collective-permute-start(bf16[256,384]{1,0:T(8,128)(2,1)S(1)} %pad_maximum_fusion.3), channel_id=1, source_target_pairs={{0,4},{1,5},{2,6},{3,7},{4,0},{5,1},{6,2},{7,3},{8,12},{9,13},{10,... | collective-permute-start | bytes 589832 | tf_op jit(solution)/shard_map/ppermute | solution.py:562
  28.6 10.3 %collective-permute-start.5 = (bf16[256,384]{1,0:T(8,128)(2,1)S(1)}, bf16[256,384]{1,0:T(8,128)(2,1)S(1)}, u32[]{:S(2)}, u32[]{:S(2)}) collective-permute-start(bf16[256,384]{1,0:T(8,128)(2,1)S(1)} %pad_maximum_fusion.3), channel_id=1, source_target_pairs={{0,6},{1,7},{2,4},{3,5},{4,2},{5,3},{6,0},{7,1},{8,14},{9,15},{10,... | collective-permute-start | bytes 589832 | tf_op jit(solution)/shard_map/ppermute | solution.py:562
  45.3 4.7 %collective-permute-start.10 = (f32[40,128]{1,0:T(8,128)S(1)}, f32[40,128]{1,0:T(8,128)S(1)}, u32[]{:S(2)}, u32[]{:S(2)}) collective-permute-start(f32[40,128]{1,0:T(8,128)S(1)} %add.113), channel_id=1, source_target_pairs={{0,6},{1,7},{2,4},{3,5},{4,2},{5,3},{6,0},{7,1},{8,14},{9,15},{10,... | collective-permute-start | bytes 61448 | tf_op jit(solution)/shard_map/ppermute | solution.py:562
  48.0 3.8 %collective-permute-start.8 = (f32[40,128]{1,0:T(8,128)S(1)}, f32[40,128]{1,0:T(8,128)S(1)}, u32[]{:S(2)}, u32[]{:S(2)}) collective-permute-start(f32[40,128]{1,0:T(8,128)S(1)} %add.113), channel_id=1, source_target_pairs={{0,2},{1,3},{2,0},{3,1},{4,6},{5,7},{6,4},{7,5},{8,10},{9,11},{10,... | collective-permute-start | bytes 61448 | tf_op jit(solution)/shard_map/ppermute | solution.py:562
  52.3 3.8 %collective-permute-start.11 = (f32[40,128]{1,0:T(8,128)S(1)}, f32[40,128]{1,0:T(8,128)S(1)}, u32[]{:S(2)}, u32[]{:S(2)}) collective-permute-start(f32[40,128]{1,0:T(8,128)S(1)} %add_add_fusion), channel_id=1, source_target_pairs={{0,8},{1,9},{2,10},{3,11},{4,12},{5,13},{6,14},{7,15},{8,0},{9,1},... | collective-permute-start | bytes 61448 | tf_op jit(solution)/shard_map/ppermute | solution.py:562
  56.1 4.7 %collective-permute-start.12 = (f32[40,128]{1,0:T(8,128)S(1)}, f32[40,128]{1,0:T(8,128)S(1)}, u32[]{:S(2)}, u32[]{:S(2)}) collective-permute-start(f32[40,128]{1,0:T(8,128)S(1)} %add.117), channel_id=1, source_target_pairs={{0,16},{1,17},{2,18},{3,19},{4,20},{5,21},{6,22},{7,23},{8,24},{9,... | collective-permute-start | bytes 61448 | tf_op jit(solution)/shard_map/ppermute | solution.py:562
  64.0 6.1 %collective-permute-start.13 = (bf16[768,384]{1,0:T(8,128)(2,1)S(1)}, bf16[768,384]{1,0:T(8,128)(2,1)S(1)}, u32[]{:S(2)}, u32[]{:S(2)}) collective-permute-start(bf16[768,384]{1,0:T(8,128)(2,1)S(1)} %get-tuple-element.104), channel_id=1, source_target_pairs={{0,1},{1,0},{2,3},{3,2},{4,5},{5,4},{6,7},{7,6},{8,9},{9,8},{10,11... | collective-permute-start | bytes 1769480 | tf_op jit(solution)/shard_map/ppermute | solution.py:562
  64.1 6.0 %collective-permute-start.15 = (bf16[192,384]{1,0:T(8,128)(2,1)S(1)}, bf16[192,384]{1,0:T(8,128)(2,1)S(1)}, u32[]{:S(2)}, u32[]{:S(2)}) collective-permute-start(bf16[192,384]{1,0:T(8,128)(2,1)S(1)} %get-tuple-element.108), channel_id=1, source_target_pairs={{0,1},{1,0},{2,3},{3,2},{4,5},{5,4},{6,7},{7,6},{8,9},{9,8},{10,11... | collective-permute-start | bytes 442376 | tf_op jit(solution)/shard_map/ppermute | solution.py:562
  72.6 17.3 %collective-permute-start.16 = (bf16[432,384]{1,0:T(8,128)(2,1)S(1)}, bf16[432,384]{1,0:T(8,128)(2,1)S(1)}, u32[]{:S(2)}, u32[]{:S(2)}) collective-permute-start(bf16[432,384]{1,0:T(8,128)(2,1)S(1)} %get-tuple-element.148), channel_id=1, source_target_pairs={{0,2},{1,3},{2,0},{3,1},{4,6},{5,7},{6,4},{7,5},{8,10},{9,11},{10,... | collective-permute-start | bytes 995336 | tf_op jit(solution)/shard_map/ppermute | solution.py:562
  74.2 16.7 %collective-permute-start.17 = (bf16[432,384]{1,0:T(8,128)(2,1)S(1)}, bf16[432,384]{1,0:T(8,128)(2,1)S(1)}, u32[]{:S(2)}, u32[]{:S(2)}) collective-permute-start(bf16[432,384]{1,0:T(8,128)(2,1)S(1)} %get-tuple-element.147), channel_id=1, source_target_pairs={{0,4},{1,5},{2,6},{3,7},{4,0},{5,1},{6,2},{7,3},{8,12},{9,13},{10,... | collective-permute-start | bytes 995336 | tf_op jit(solution)/shard_map/ppermute | solution.py:562
  74.7 16.2 %collective-permute-start.18 = (bf16[432,384]{1,0:T(8,128)(2,1)S(1)}, bf16[432,384]{1,0:T(8,128)(2,1)S(1)}, u32[]{:S(2)}, u32[]{:S(2)}) collective-permute-start(bf16[432,384]{1,0:T(8,128)(2,1)S(1)} %get-tuple-element.146), channel_id=1, source_target_pairs={{0,6},{1,7},{2,4},{3,5},{4,2},{5,3},{6,0},{7,1},{8,14},{9,15},{10,... | collective-permute-start | bytes 995336 | tf_op jit(solution)/shard_map/ppermute | solution.py:562
  91.1 6.2 %collective-permute-start.20 = (bf16[240,384]{1,0:T(8,128)(2,1)S(1)}, bf16[240,384]{1,0:T(8,128)(2,1)S(1)}, u32[]{:S(2)}, u32[]{:S(2)}) collective-permute-start(bf16[240,384]{1,0:T(8,128)(2,1)S(1)} %slice.89), channel_id=1, source_target_pairs={{0,8},{1,9},{2,10},{3,11},{4,12},{5,13},{6,14},{7,15},{8,0},{9,1},... | collective-permute-start | bytes 552968 | tf_op jit(solution)/shard_map/ppermute | solution.py:562
  92.6 6.1 %collective-permute-start.21 = (bf16[192,384]{1,0:T(8,128)(2,1)S(1)}, bf16[192,384]{1,0:T(8,128)(2,1)S(1)}, u32[]{:S(2)}, u32[]{:S(2)}) collective-permute-start(bf16[192,384]{1,0:T(8,128)(2,1)S(1)} %get-tuple-element.151), channel_id=1, source_target_pairs={{0,2},{1,3},{2,0},{3,1},{4,6},{5,7},{6,4},{7,5},{8,10},{9,11},{10,... | collective-permute-start | bytes 442376 | tf_op jit(solution)/shard_map/ppermute | solution.py:562
  93.7 8.8 %collective-permute-start.23 = (bf16[192,384]{1,0:T(8,128)(2,1)S(1)}, bf16[192,384]{1,0:T(8,128)(2,1)S(1)}, u32[]{:S(2)}, u32[]{:S(2)}) collective-permute-start(bf16[192,384]{1,0:T(8,128)(2,1)S(1)} %get-tuple-element.150), channel_id=1, source_target_pairs={{0,4},{1,5},{2,6},{3,7},{4,0},{5,1},{6,2},{7,3},{8,12},{9,13},{10,... | collective-permute-start | bytes 442376 | tf_op jit(solution)/shard_map/ppermute | solution.py:562
  94.5 8.1 %collective-permute-start.24 = (bf16[192,384]{1,0:T(8,128)(2,1)S(1)}, bf16[192,384]{1,0:T(8,128)(2,1)S(1)}, u32[]{:S(2)}, u32[]{:S(2)}) collective-permute-start(bf16[192,384]{1,0:T(8,128)(2,1)S(1)} %get-tuple-element.149), channel_id=1, source_target_pairs={{0,6},{1,7},{2,4},{3,5},{4,2},{5,3},{6,0},{7,1},{8,14},{9,15},{10,... | collective-permute-start | bytes 442376 | tf_op jit(solution)/shard_map/ppermute | solution.py:562
  98.8 6.9 %collective-permute-start.22 = (bf16[144,384]{1,0:T(8,128)(2,1)S(1)}, bf16[144,384]{1,0:T(8,128)(2,1)S(1)}, u32[]{:S(2)}, u32[]{:S(2)}) collective-permute-start(bf16[144,384]{1,0:T(8,128)(2,1)S(1)} %slice.93), channel_id=1, source_target_pairs={{0,16},{1,17},{2,18},{3,19},{4,20},{5,21},{6,22},{7,23},{8,24},{9,... | collective-permute-start | bytes 331784 | tf_op jit(solution)/shard_map/ppermute | solution.py:562
  105.8 4.5 %collective-permute-start.25 = (bf16[96,384]{1,0:T(8,128)(2,1)S(1)}, bf16[96,384]{1,0:T(8,128)(2,1)S(1)}, u32[]{:S(2)}, u32[]{:S(2)}) collective-permute-start(bf16[96,384]{1,0:T(8,128)(2,1)S(1)} %slice.97), channel_id=1, source_target_pairs={{0,8},{1,9},{2,10},{3,11},{4,12},{5,13},{6,14},{7,15},{8,0},{9,1},... | collective-permute-start | bytes 221192 | tf_op jit(solution)/shard_map/ppermute | solution.py:562
  106.8 7.1 %collective-permute-start.29 = (bf16[96,384]{1,0:T(8,128)(2,1)S(1)}, bf16[96,384]{1,0:T(8,128)(2,1)S(1)}, u32[]{:S(2)}, u32[]{:S(2)}) collective-permute-start(bf16[96,384]{1,0:T(8,128)(2,1)S(1)} %get-tuple-element.155), channel_id=1, source_target_pairs={{0,16},{1,17},{2,18},{3,19},{4,20},{5,21},{6,22},{7,23},{8,24},{9,... | collective-permute-start | bytes 221192 | tf_op jit(solution)/shard_map/ppermute | solution.py:562
  110.4 5.9 %collective-permute-start.26 = (bf16[48,384]{1,0:T(8,128)(2,1)S(1)}, bf16[48,384]{1,0:T(8,128)(2,1)S(1)}, u32[]{:S(2)}, u32[]{:S(2)}) collective-permute-start(bf16[48,384]{1,0:T(8,128)(2,1)S(1)} %slice.99), channel_id=1, source_target_pairs={{0,16},{1,17},{2,18},{3,19},{4,20},{5,21},{6,22},{7,23},{8,24},{9,... | collective-permute-start | bytes 110600 | tf_op jit(solution)/shard_map/ppermute | solution.py:562
  113.9 9.4 %collective-permute-start.30 = (bf16[192,384]{1,0:T(8,128)(2,1)S(1)}, bf16[192,384]{1,0:T(8,128)(2,1)S(1)}, u32[]{:S(2)}, u32[]{:S(2)}) collective-permute-start(bf16[192,384]{1,0:T(8,128)(2,1)S(1)} %pad_maximum_fusion.4), channel_id=1, source_target_pairs={{0,8},{1,9},{2,10},{3,11},{4,12},{5,13},{6,14},{7,15},{8,0},{9,1},... | collective-permute-start | bytes 442376 | tf_op jit(solution)/shard_map/ppermute | solution.py:562
  116.3 4.9 %collective-permute-start.27 = (bf16[48,384]{1,0:T(8,128)(2,1)S(1)}, bf16[48,384]{1,0:T(8,128)(2,1)S(1)}, u32[]{:S(2)}, u32[]{:S(2)}) collective-permute-start(bf16[48,384]{1,0:T(8,128)(2,1)S(1)} %get-tuple-element.145), channel_id=1, source_target_pairs={{0,16},{1,17},{2,18},{3,19},{4,20},{5,21},{6,22},{7,23},{8,24},{9,... | collective-permute-start | bytes 110600 | tf_op jit(solution)/shard_map/ppermute | solution.py:562
  121.3 5.7 %collective-permute-start.28 = (bf16[96,384]{1,0:T(8,128)(2,1)S(1)}, bf16[96,384]{1,0:T(8,128)(2,1)S(1)}, u32[]{:S(2)}, u32[]{:S(2)}) collective-permute-start(bf16[96,384]{1,0:T(8,128)(2,1)S(1)} %pad_maximum_fusion.6), channel_id=1, source_target_pairs={{0,8},{1,9},{2,10},{3,11},{4,12},{5,13},{6,14},{7,15},{8,0},{9,1},... | collective-permute-start | bytes 221192 | tf_op jit(solution)/shard_map/ppermute | solution.py:562
  123.4 8.5 %collective-permute-start.34 = (bf16[432,384]{1,0:T(8,128)(2,1)S(1)}, bf16[432,384]{1,0:T(8,128)(2,1)S(1)}, u32[]{:S(2)}, u32[]{:S(2)}) collective-permute-start(bf16[432,384]{1,0:T(8,128)(2,1)S(1)} %pad_maximum_fusion.2), channel_id=1, source_target_pairs={{0,2},{1,3},{2,0},{3,1},{4,6},{5,7},{6,4},{7,5},{8,10},{9,11},{10,... | collective-permute-start | bytes 995336 | tf_op jit(solution)/shard_map/ppermute | solution.py:562
  124.3 12.2 %collective-permute-start.35 = (bf16[432,384]{1,0:T(8,128)(2,1)S(1)}, bf16[432,384]{1,0:T(8,128)(2,1)S(1)}, u32[]{:S(2)}, u32[]{:S(2)}) collective-permute-start(bf16[432,384]{1,0:T(8,128)(2,1)S(1)} %pad_maximum_fusion.2), channel_id=1, source_target_pairs={{0,4},{1,5},{2,6},{3,7},{4,0},{5,1},{6,2},{7,3},{8,12},{9,13},{10,... | collective-permute-start | bytes 995336 | tf_op jit(solution)/shard_map/ppermute | solution.py:562
  125.9 12.2 %collective-permute-start.31 = (bf16[432,384]{1,0:T(8,128)(2,1)S(1)}, bf16[432,384]{1,0:T(8,128)(2,1)S(1)}, u32[]{:S(2)}, u32[]{:S(2)}) collective-permute-start(bf16[432,384]{1,0:T(8,128)(2,1)S(1)} %pad_maximum_fusion.2), channel_id=1, source_target_pairs={{0,6},{1,7},{2,4},{3,5},{4,2},{5,3},{6,0},{7,1},{8,14},{9,15},{10,... | collective-permute-start | bytes 995336 | tf_op jit(solution)/shard_map/ppermute | solution.py:562
  126.9 10.1 %collective-permute-start.32 = (bf16[192,384]{1,0:T(8,128)(2,1)S(1)}, bf16[192,384]{1,0:T(8,128)(2,1)S(1)}, u32[]{:S(2)}, u32[]{:S(2)}) collective-permute-start(bf16[192,384]{1,0:T(8,128)(2,1)S(1)} %pad_maximum_fusion.5), channel_id=1, source_target_pairs={{0,2},{1,3},{2,0},{3,1},{4,6},{5,7},{6,4},{7,5},{8,10},{9,11},{10,... | collective-permute-start | bytes 442376 | tf_op jit(solution)/shard_map/ppermute | solution.py:562
  127.9 10.2 %collective-permute-start.33 = (bf16[192,384]{1,0:T(8,128)(2,1)S(1)}, bf16[192,384]{1,0:T(8,128)(2,1)S(1)}, u32[]{:S(2)}, u32[]{:S(2)}) collective-permute-start(bf16[192,384]{1,0:T(8,128)(2,1)S(1)} %pad_maximum_fusion.5), channel_id=1, source_target_pairs={{0,4},{1,5},{2,6},{3,7},{4,0},{5,1},{6,2},{7,3},{8,12},{9,13},{10,... | collective-permute-start | bytes 442376 | tf_op jit(solution)/shard_map/ppermute | solution.py:562
  138.4 7.2 %collective-permute-start.36 = (bf16[192,384]{1,0:T(8,128)(2,1)S(1)}, bf16[192,384]{1,0:T(8,128)(2,1)S(1)}, u32[]{:S(2)}, u32[]{:S(2)}) collective-permute-start(bf16[192,384]{1,0:T(8,128)(2,1)S(1)} %pad_maximum_fusion.5), channel_id=1, source_target_pairs={{0,6},{1,7},{2,4},{3,5},{4,2},{5,3},{6,0},{7,1},{8,14},{9,15},{10,... | collective-permute-start | bytes 442376 | tf_op jit(solution)/shard_map/ppermute | solution.py:562
  (34 other events, 187.7 us)

commit v9 on v8

--- a/solution.py
+++ b/solution.py
@@ -703,7 +703,7 @@
         m = joined(m[:96], [far, m[96:]])
         m = joined(m[:192], [swap(m[:192], 8), m[192:]])
         got_m = plane([m] * 4)
-        a = added(a[:48], [got_a])
+        a, m = lax.optimization_barrier((added(a[:48], [got_a]), m))
         a = joined(a, [swap(a, 16)])
         a = joined(a, [swap(a, 8)])
         last, got_m[0], got_m[1] = lax.optimization_barrier((a, got_m[0], got_m[1]))

time: 152 us -> 151 us (level)
  no operation moved by 1% of the time
where the time goes in v9:
time: 151 us
  Pallas kernels  58.9 us (39%)
  starting transfers between devices  47.4 us (31%)
  waiting for transfers between devices  37.5 us (25%)
  between operations  4.25 us (3%)
  local copies, waits for them, and re-layouts  1.58 us (1%)
    ppermute x39, starting transfers between devices, swap(): return lax.ppermute(v, AXES, [(i, i ^ mask) for i in range(32)])  47.4 us
    ppermute x39, waiting for transfers between devices, swap(): return lax.ppermute(v, AXES, [(i, i ^ mask) for i in range(32)])  37.5 us
    pallas_call x1, Pallas kernels, att_back(): pl.pallas_call(att_back_kernel, grid=(n // TOK_BLOCK,), in_specs=[SMEM] +...  13.7 us
    pallas_call x5, Pallas kernels, call(): pl.pallas_call(kernel, in_specs=[SMEM] * smem + [VMEM] * (len(args) - sme...  11.2 us
    pallas_call x1, Pallas kernels, image_tower(): pl.pallas_call(image_kernel, grid=(count // IMG_BLOCK,), in_specs=[pl.Blo...  10.8 us
    pallas_call x1, Pallas kernels, text_mlp(): pl.pallas_call(text_mlp_kernel, grid=(n // TOK_BLOCK,), in_specs=[token_r...  10 us
    pallas_call x1, Pallas kernels, text_att(): pl.pallas_call(text_att_kernel, grid=(blocks,), in_specs=[token_rows(D),...  7.86 us
    pallas_call x1, Pallas kernels, mlp_back(): pl.pallas_call(mlp_back_kernel, grid=(n // TOK_BLOCK,), in_specs=[SMEM, b...  5.36 us
  transfers between devices with their start and end apart: 39, of which 22 were waited for; matrix products, arithmetic and copies ran while one was open for 1% of the time, Pallas kernels for 27%

profile of v9, /device:TPU:0, one launch (start us, length us, event | category | flops | bytes accessed | tf_op | source)
XLA Modules:
  0.0 150.9 jit_solution(12608369156469816094)
XLA Ops:
  0.7 10.8 %image_tower.1 = bf16[64,384]{1,0:T(8,128)(2,1)S(1)} custom-call(bf16[50,64,384]{2,1,0:T(8,128)(2,1)} %bitcast.23, f32[384]{0:T(512)} %g1.5, bf16[384,1152]{1,0:T(8,128)(2,1)} %wqkv.5, bf16[384,384]{1,0:T(8,128)(2,1)} %wout.3, f32[384]{0:T(512)} %g2.4, bf16[384,1536]{1,0:T(8,128)(2,1)} %wup.4, bf16[1536,384]{1,0:T(8,128)(2,1)} %wdown.3, bf16[384,384]{1,0:T(8,128)(2,1)} %wproj.3), custom_call_target="tpu_custom_call" | custom-call | flops 12000000000 | bytes 36000000 | tf_op jit(solution)/shard_map/image_tower/pallas_call | solution.py:141
  11.5 3.1 %collective-permute-start = (bf16[64,384]{1,0:T(8,128)(2,1)S(1)}, bf16[64,384]{1,0:T(8,128)(2,1)S(1)}, u32[]{:S(2)}, u32[]{:S(2)}) collective-permute-start(bf16[64,384]{1,0:T(8,128)(2,1)S(1)} %image_tower.1), channel_id=1, source_target_pairs={{0,8},{1,9},{2,10},{3,11},{4,12},{5,13},{6,14},{7,15},{8,0},{9,1},... | collective-permute-start | bytes 147464 | tf_op jit(solution)/shard_map/ppermute | solution.py:562
  14.6 2.6 %collective-permute-start.1 = (bf16[64,384]{1,0:T(8,128)(2,1)S(1)}, bf16[64,384]{1,0:T(8,128)(2,1)S(1)}, u32[]{:S(2)}, u32[]{:S(2)}) collective-permute-start(bf16[64,384]{1,0:T(8,128)(2,1)S(1)} %image_tower.1), channel_id=1, source_target_pairs={{0,16},{1,17},{2,18},{3,19},{4,20},{5,21},{6,22},{7,23},{8,24},{9,... | collective-permute-start | bytes 147464 | tf_op jit(solution)/shard_map/ppermute | solution.py:562
  17.4 7.9 %text_att.1 = (bf16[1024,384]{1,0:T(8,128)(2,1)S(1)}, bf16[1024,384]{1,0:T(8,128)(2,1)}, bf16[1024,1152]{1,0:T(8,128)(2,1)}, bf16[8,3,256,128]{3,2,1,0:T(8,128)(2,1)}, bf16[1024,384]{1,0:T(8,128)(2,1)}) custom-call(bf16[1024,384]{1,0:T(8,128)(2,1)} %tok_ref.5, s32[4,1,256]{2,1,0:T(1,128)S(1)} %reshape.71.lab_ref, f32[384]{0:T(512)S(1)} %copy-done.9, ...), custom_call_target="tpu_custom_call" | custom-call | flops 8999999488 | bytes 27000000 | tf_op jit(solution)/shard_map/text_att/pallas_call | solution.py:256
  25.3 1.8 %collective-permute-start.3 = (bf16[256,384]{1,0:T(8,128)(2,1)S(1)}, bf16[256,384]{1,0:T(8,128)(2,1)S(1)}, u32[]{:S(2)}, u32[]{:S(2)}) collective-permute-start(bf16[256,384]{1,0:T(8,128)(2,1)S(1)} %pad_maximum_fusion.3), channel_id=1, source_target_pairs={{0,2},{1,3},{2,0},{3,1},{4,6},{5,7},{6,4},{7,5},{8,10},{9,11},{10,... | collective-permute-start | bytes 589832 | tf_op jit(solution)/shard_map/ppermute | solution.py:562
  28.9 10.0 %text_mlp.1 = (bf16[1024,384]{1,0:T(8,128)(2,1)}, f32[1024,384]{1,0:T(8,128)}, bf16[1024,1536]{1,0:T(8,128)(2,1)}, f32[64,1536]{1,0:T(8,128)S(1)}, bf16[64,384]{...) custom-call(bf16[1024,384]{1,0:T(8,128)(2,1)S(1)} %copy-done.3, ...), custom_call_target="tpu_custom_call" | custom-call | flops 11000000512 | bytes 33000000 | tf_op jit(solution)/shard_map/text_mlp/pallas_call | solution.py:280
  40.5 1.7 %collective-permute-done.6.other = bf16[1024,384]{1,0:T(8,128)(2,1)} collective-permute-done((bf16[1024,384]{1,0:T(8,128)(2,1)S(1)}, bf16[1024,384]{1,0:T(8,128)(2,1)}, u32[]{:S(2)}, u32[]{:S(2)}) %collective-permute-start.6) | collective-permute-done | bytes 786464 | tf_op jit(solution)/shard_map/ppermute | solution.py:562
  42.2 1.9 %cosine.1 = (f32[64,2048]{1,0:T(8,128)S(1)}, f32[40,128]{1,0:T(8,128)S(1)}) custom-call(f32[1]{0:T(128)S(6)} %copy.46.scale_ref, s32[1]{0:T(128)} %bitcast.mine_ref, bf16[64,384]{1,0:T(8,128)(2,1)S(1)} %get-tuple-element.84.emb, bf16[1024,384]{1,0:T(8,128)(2,1)S(1)} %constant_dynamic-update-slice_fusion.own, bf16[1024,384]{1,0:T(8,128)(2,1)} %collective-permute-done.6.other, ...), custom_call_target="tpu_custom_call" | custom-call | flops 3000000000 | bytes 9000000 | tf_op jit(solution)/shard_map/cosine/pallas_call | solution.py:513
  45.3 2.7 %collective-permute-start.10 = (f32[40,128]{1,0:T(8,128)S(1)}, f32[40,128]{1,0:T(8,128)S(1)}, u32[]{:S(2)}, u32[]{:S(2)}) collective-permute-start(f32[40,128]{1,0:T(8,128)S(1)} %add.113), channel_id=1, source_target_pairs={{0,6},{1,7},{2,4},{3,5},{4,2},{5,3},{6,0},{7,1},{8,14},{9,15},{10,... | collective-permute-start | bytes 61448 | tf_op jit(solution)/shard_map/ppermute | solution.py:562
  50.0 1.8 %collective-permute-done.8 = f32[40,128]{1,0:T(8,128)S(1)} collective-permute-done((f32[40,128]{1,0:T(8,128)S(1)}, f32[40,128]{1,0:T(8,128)S(1)}, u32[]{:S(2)}, u32[]{:S(2)}) %collective-permute-start.8) | collective-permute-done | bytes 20512 | tf_op jit(solution)/shard_map/ppermute | solution.py:562
  53.1 3.1 %collective-permute-done.11 = f32[40,128]{1,0:T(8,128)S(1)} collective-permute-done((f32[40,128]{1,0:T(8,128)S(1)}, f32[40,128]{1,0:T(8,128)S(1)}, u32[]{:S(2)}, u32[]{:S(2)}) %collective-permute-start.11) | collective-permute-done | bytes 20512 | tf_op jit(solution)/shard_map/ppermute | solution.py:562
  56.1 2.2 %collective-permute-start.12 = (f32[40,128]{1,0:T(8,128)S(1)}, f32[40,128]{1,0:T(8,128)S(1)}, u32[]{:S(2)}, u32[]{:S(2)}) collective-permute-start(f32[40,128]{1,0:T(8,128)S(1)} %add.117), channel_id=1, source_target_pairs={{0,16},{1,17},{2,18},{3,19},{4,20},{5,21},{6,22},{7,23},{8,24},{9,... | collective-permute-start | bytes 61448 | tf_op jit(solution)/shard_map/ppermute | solution.py:562
  58.4 1.7 %rows.1.dt_row = f32[64,384]{1,0:T(8,128)S(1)} custom-call(f32[1]{0:T(128)S(6)} %copy.46.scale_ref, f32[64,2048]{1,0:T(8,128)S(1)} %get-tuple-element.90.g_ref, bf16[1024,384]{1,0:T(8,128)(2,1)S(1)} %constant_dynamic-update-slice_fusion.own, bf16[1024,384]{1,0:T(8,128)(2,1)} %collective-permute-done.6.other, s32[64,1]{1,0:T(8,128)S(1)} %copy.29.pair), custom_call_target="tpu_custom_call" | custom-call | flops 2000000000 | bytes 6000000 | tf_op jit(solution)/shard_map/rows/pallas_call | solution.py:513
  60.9 3.1 %head_back.1 = (bf16[768,384]{1,0:T(8,128)(2,1)S(1)}, bf16[768,384]{1,0:T(8,128)(2,1)S(1)}, bf16[192,384]{1,0:T(8,128)(2,1)S(1)}, bf16[192,384]{1,0:T(8,128)(2,1...) custom-call(f32[1]{0:T(128)S(6)} %copy.46.scale_ref, ...), custom_call_target="tpu_custom_call" | custom-call | flops 5000000000 | bytes 15000000 | tf_op jit(solution)/shard_map/head_back/pallas_call | solution.py:513
  64.6 5.4 %mlp_back.1 = (f32[1024,384]{1,0:T(8,128)S(1)}, bf16[1024,384]{1,0:T(8,128)(2,1)S(1)}, bf16[768,384]{1,0:T(8,128)(2,1)S(1)}, bf16[768,384]{1,0:T(8,128)(2,1)S(1)}) custom-call(s32[1]{0:T(128)} %bitcast.mine_ref, s32[4,1,256]{2,1,0:T(1,128)S(1)} %reshape.71.lab_ref, bf16[1024,384]{1,0:T(8,128)(2,1)S(1)} %copy-done.16, bf16[1024,1536]{1,0:T(8,128)(2,1)S(1)} %copy-done.10, ...), custom_call_target="tpu_custom_call" | custom-call | flops 8999999488 | bytes 27000000 | tf_op jit(solution)/shard_map/mlp_back/pallas_call | solution.py:530
  70.3 1.7 %collective-permute-done.14 = bf16[768,384]{1,0:T(8,128)(2,1)S(1)} collective-permute-done((bf16[768,384]{1,0:T(8,128)(2,1)S(1)}, bf16[768,384]{1,0:T(8,128)(2,1)S(1)}, u32[]{:S(2)}, u32[]{:S(2)}) %collective-permute-start.14) | collective-permute-done | bytes 589856 | tf_op jit(solution)/shard_map/ppermute | solution.py:562
  72.6 1.6 %collective-permute-start.16 = (bf16[432,384]{1,0:T(8,128)(2,1)S(1)}, bf16[432,384]{1,0:T(8,128)(2,1)S(1)}, u32[]{:S(2)}, u32[]{:S(2)}) collective-permute-start(bf16[432,384]{1,0:T(8,128)(2,1)S(1)} %get-tuple-element.150), channel_id=1, source_target_pairs={{0,2},{1,3},{2,0},{3,1},{4,6},{5,7},{6,4},{7,5},{8,10},{9,11},{10,... | collective-permute-start | bytes 995336 | tf_op jit(solution)/shard_map/ppermute | solution.py:562
  76.2 13.7 %att_back.1 = (f32[1024,384]{1,0:T(8,128)}, bf16[768,384]{1,0:T(8,128)(2,1)S(1)}, bf16[768,384]{1,0:T(8,128)(2,1)S(1)}) custom-call(s32[1]{0:T(128)} %bitcast.mine_ref, bf16[1024,1152]{1,0:T(8,128)(2,1)S(1)} %copy-done.11, bf16[8,3,256,128]{3,2,1,0:T(8,128)(2,1)S(1)} %copy-done.15, bf16[1024,384]{1,0:T(8,128)(2,1)S(1)} %get-tuple-element.111.dxb_all, ...), custom_call_target="tpu_custom_call" | custom-call | flops 14000000000 | bytes 42000000 | tf_op jit(solution)/shard_map/att_back/pallas_call | solution.py:545
  94.5 1.8 %collective-permute-start.24 = (bf16[192,384]{1,0:T(8,128)(2,1)S(1)}, bf16[192,384]{1,0:T(8,128)(2,1)S(1)}, u32[]{:S(2)}, u32[]{:S(2)}) collective-permute-start(bf16[192,384]{1,0:T(8,128)(2,1)S(1)} %get-tuple-element.151), channel_id=1, source_target_pairs={{0,6},{1,7},{2,4},{3,5},{4,2},{5,3},{6,0},{7,1},{8,14},{9,15},{10,... | collective-permute-start | bytes 442376 | tf_op jit(solution)/shard_map/ppermute | solution.py:562
  98.8 2.8 %collective-permute-start.22 = (bf16[144,384]{1,0:T(8,128)(2,1)S(1)}, bf16[144,384]{1,0:T(8,128)(2,1)S(1)}, u32[]{:S(2)}, u32[]{:S(2)}) collective-permute-start(bf16[144,384]{1,0:T(8,128)(2,1)S(1)} %slice.93), channel_id=1, source_target_pairs={{0,16},{1,17},{2,18},{3,19},{4,20},{5,21},{6,22},{7,23},{8,24},{9,... | collective-permute-start | bytes 331784 | tf_op jit(solution)/shard_map/ppermute | solution.py:562
  102.6 3.1 %collective-permute-done.22 = bf16[144,384]{1,0:T(8,128)(2,1)S(1)} collective-permute-done((bf16[144,384]{1,0:T(8,128)(2,1)S(1)}, bf16[144,384]{1,0:T(8,128)(2,1)S(1)}, u32[]{:S(2)}, u32[]{:S(2)}) %collective-permute-start.22) | collective-permute-done | bytes 110624 | tf_op jit(solution)/shard_map/ppermute | solution.py:562
  106.8 3.5 %collective-permute-start.27 = (bf16[96,384]{1,0:T(8,128)(2,1)S(1)}, bf16[96,384]{1,0:T(8,128)(2,1)S(1)}, u32[]{:S(2)}, u32[]{:S(2)}) collective-permute-start(bf16[96,384]{1,0:T(8,128)(2,1)S(1)} %slice.102), channel_id=1, source_target_pairs={{0,16},{1,17},{2,18},{3,19},{4,20},{5,21},{6,22},{7,23},{8,24},{9,... | collective-permute-start | bytes 221192 | tf_op jit(solution)/shard_map/ppermute | solution.py:562
  110.4 2.5 %collective-permute-start.26 = (bf16[48,384]{1,0:T(8,128)(2,1)S(1)}, bf16[48,384]{1,0:T(8,128)(2,1)S(1)}, u32[]{:S(2)}, u32[]{:S(2)}) collective-permute-start(bf16[48,384]{1,0:T(8,128)(2,1)S(1)} %slice.99), channel_id=1, source_target_pairs={{0,16},{1,17},{2,18},{3,19},{4,20},{5,21},{6,22},{7,23},{8,24},{9,... | collective-permute-start | bytes 110600 | tf_op jit(solution)/shard_map/ppermute | solution.py:562
  113.9 2.4 %collective-permute-start.28 = (bf16[192,384]{1,0:T(8,128)(2,1)S(1)}, bf16[192,384]{1,0:T(8,128)(2,1)S(1)}, u32[]{:S(2)}, u32[]{:S(2)}) collective-permute-start(bf16[192,384]{1,0:T(8,128)(2,1)S(1)} %pad_maximum_fusion.4), channel_id=1, source_target_pairs={{0,8},{1,9},{2,10},{3,11},{4,12},{5,13},{6,14},{7,15},{8,0},{9,1},... | collective-permute-start | bytes 442376 | tf_op jit(solution)/shard_map/ppermute | solution.py:562
  116.3 3.4 %collective-permute-done.28 = bf16[192,384]{1,0:T(8,128)(2,1)S(1)} collective-permute-done((bf16[192,384]{1,0:T(8,128)(2,1)S(1)}, bf16[192,384]{1,0:T(8,128)(2,1)S(1)}, u32[]{:S(2)}, u32[]{:S(2)}) %collective-permute-start.28) | collective-permute-done | bytes 147488 | tf_op jit(solution)/shard_map/ppermute | solution.py:562
  119.8 1.9 %collective-permute-start.29 = (bf16[48,384]{1,0:T(8,128)(2,1)S(1)}, bf16[48,384]{1,0:T(8,128)(2,1)S(1)}, u32[]{:S(2)}, u32[]{:S(2)}) collective-permute-start(bf16[48,384]{1,0:T(8,128)(2,1)S(1)} %add_convert_fusion.8), channel_id=1, source_target_pairs={{0,16},{1,17},{2,18},{3,19},{4,20},{5,21},{6,22},{7,23},{8,24},{9,... | collective-permute-start | bytes 110600 | tf_op jit(solution)/shard_map/ppermute | solution.py:562
  126.5 3.2 %collective-permute-done.30 = bf16[96,384]{1,0:T(8,128)(2,1)S(1)} collective-permute-done((bf16[96,384]{1,0:T(8,128)(2,1)S(1)}, bf16[96,384]{1,0:T(8,128)(2,1)S(1)}, u32[]{:S(2)}, u32[]{:S(2)}) %collective-permute-start.30) | collective-permute-done | bytes 73760 | tf_op jit(solution)/shard_map/ppermute | solution.py:562
  132.0 3.8 %collective-permute-done.35 = bf16[432,384]{1,0:T(8,128)(2,1)S(1)} collective-permute-done((bf16[432,384]{1,0:T(8,128)(2,1)S(1)}, bf16[432,384]{1,0:T(8,128)(2,1)S(1)}, u32[]{:S(2)}, u32[]{:S(2)}) %collective-permute-start.35) | collective-permute-done | bytes 331808 | tf_op jit(solution)/shard_map/ppermute | solution.py:562
  138.9 1.8 %collective-permute-done.37.other = bf16[1728,384]{1,0:T(8,128)(2,1)S(1)} collective-permute-done((bf16[1728,384]{1,0:T(8,128)(2,1)S(1)}, bf16[1728,384]{1,0:T(8,128)(2,1)S(1)}, u32[]{:S(2)}, u32[]{:S(2)}) %collective-permute-start.37) | collective-permute-done | bytes 1327136 | tf_op jit(solution)/shard_map/ppermute | solution.py:562
  140.7 2.7 %spread_mlp.1 = (f32[1536,384]{1,0:T(8,128)}, f32[384,1536]{1,0:T(8,128)}, f32[384,384]{1,0:T(8,128)}, f32[384]{0:T(512)}) custom-call(s32[1]{0:T(128)} %bitcast.mine_ref, bf16[1728,384]{1,0:T(8,128)(2,1)S(1)} %constant_dynamic-update-slice_fusion.7.own, bf16[1728,384]{1,0:T(8,128)(2,1)S(1)} %collective-permute-done.37.other, ...), custom_call_target="tpu_custom_call" | custom-call | flops 4000000000 | bytes 12000000 | tf_op jit(solution)/shard_map/spread_mlp/pallas_call | solution.py:513
  145.0 1.9 %collective-permute-done.38.other = bf16[768,384]{1,0:T(8,128)(2,1)S(1)} collective-permute-done((bf16[768,384]{1,0:T(8,128)(2,1)S(1)}, bf16[768,384]{1,0:T(8,128)(2,1)S(1)}, u32[]{:S(2)}, u32[]{:S(2)}) %collective-permute-start.38) | collective-permute-done | bytes 589856 | tf_op jit(solution)/shard_map/ppermute | solution.py:562
  147.0 1.7 %spread_att.1 = (f32[384,384]{1,0:T(8,128)}, f32[384,1152]{1,0:T(8,128)}, f32[384]{0:T(512)}) custom-call(s32[1]{0:T(128)} %bitcast.mine_ref, bf16[768,384]{1,0:T(8,128)(2,1)S(1)} %constant_dynamic-update-slice_fusion.11.own, bf16[768,384]{1,0:T(8,128)(2,1)S(1)} %collective-permute-done.38.other, bf16[384,1152]{1,0:T(8,128)(2,1)S(1)} %copy-done.2, ...), custom_call_target="tpu_custom_call" | custom-call | flops 4000000000 | bytes 12000000 | tf_op jit(solution)/shard_map/spread_att/pallas_call | solution.py:513
  (161 shorter events, 33.5 us)
Async XLA Ops:
  11.5 13.8 %collective-permute-start = (bf16[64,384]{1,0:T(8,128)(2,1)S(1)}, bf16[64,384]{1,0:T(8,128)(2,1)S(1)}, u32[]{:S(2)}, u32[]{:S(2)}) collective-permute-start(bf16[64,384]{1,0:T(8,128)(2,1)S(1)} %image_tower.1), channel_id=1, source_target_pairs={{0,8},{1,9},{2,10},{3,11},{4,12},{5,13},{6,14},{7,15},{8,0},{9,1},... | collective-permute-start | bytes 147464 | tf_op jit(solution)/shard_map/ppermute | solution.py:562
  14.6 10.7 %collective-permute-start.1 = (bf16[64,384]{1,0:T(8,128)(2,1)S(1)}, bf16[64,384]{1,0:T(8,128)(2,1)S(1)}, u32[]{:S(2)}, u32[]{:S(2)}) collective-permute-start(bf16[64,384]{1,0:T(8,128)(2,1)S(1)} %image_tower.1), channel_id=1, source_target_pairs={{0,16},{1,17},{2,18},{3,19},{4,20},{5,21},{6,22},{7,23},{8,24},{9,... | collective-permute-start | bytes 147464 | tf_op jit(solution)/shard_map/ppermute | solution.py:562
  17.2 8.2 %collective-permute-start.2 = (bf16[64,384]{1,0:T(8,128)(2,1)S(1)}, bf16[64,384]{1,0:T(8,128)(2,1)S(1)}, u32[]{:S(2)}, u32[]{:S(2)}) collective-permute-start(bf16[64,384]{1,0:T(8,128)(2,1)S(1)} %image_tower.1), channel_id=1, source_target_pairs={{0,24},{1,25},{2,26},{3,27},{4,28},{5,29},{6,30},{7,31},{8,16},{9,... | collective-permute-start | bytes 147464 | tf_op jit(solution)/shard_map/ppermute | solution.py:562
  25.3 13.6 %collective-permute-start.3 = (bf16[256,384]{1,0:T(8,128)(2,1)S(1)}, bf16[256,384]{1,0:T(8,128)(2,1)S(1)}, u32[]{:S(2)}, u32[]{:S(2)}) collective-permute-start(bf16[256,384]{1,0:T(8,128)(2,1)S(1)} %pad_maximum_fusion.3), channel_id=1, source_target_pairs={{0,2},{1,3},{2,0},{3,1},{4,6},{5,7},{6,4},{7,5},{8,10},{9,11},{10,... | collective-permute-start | bytes 589832 | tf_op jit(solution)/shard_map/ppermute | solution.py:562
  27.1 11.8 %collective-permute-start.4 = (bf16[256,384]{1,0:T(8,128)(2,1)S(1)}, bf16[256,384]{1,0:T(8,128)(2,1)S(1)}, u32[]{:S(2)}, u32[]{:S(2)}) collective-permute-start(bf16[256,384]{1,0:T(8,128)(2,1)S(1)} %pad_maximum_fusion.3), channel_id=1, source_target_pairs={{0,4},{1,5},{2,6},{3,7},{4,0},{5,1},{6,2},{7,3},{8,12},{9,13},{10,... | collective-permute-start | bytes 589832 | tf_op jit(solution)/shard_map/ppermute | solution.py:562
  28.6 10.3 %collective-permute-start.5 = (bf16[256,384]{1,0:T(8,128)(2,1)S(1)}, bf16[256,384]{1,0:T(8,128)(2,1)S(1)}, u32[]{:S(2)}, u32[]{:S(2)}) collective-permute-start(bf16[256,384]{1,0:T(8,128)(2,1)S(1)} %pad_maximum_fusion.3), channel_id=1, source_target_pairs={{0,6},{1,7},{2,4},{3,5},{4,2},{5,3},{6,0},{7,1},{8,14},{9,15},{10,... | collective-permute-start | bytes 589832 | tf_op jit(solution)/shard_map/ppermute | solution.py:562
  45.3 4.7 %collective-permute-start.10 = (f32[40,128]{1,0:T(8,128)S(1)}, f32[40,128]{1,0:T(8,128)S(1)}, u32[]{:S(2)}, u32[]{:S(2)}) collective-permute-start(f32[40,128]{1,0:T(8,128)S(1)} %add.113), channel_id=1, source_target_pairs={{0,6},{1,7},{2,4},{3,5},{4,2},{5,3},{6,0},{7,1},{8,14},{9,15},{10,... | collective-permute-start | bytes 61448 | tf_op jit(solution)/shard_map/ppermute | solution.py:562
  48.0 3.8 %collective-permute-start.8 = (f32[40,128]{1,0:T(8,128)S(1)}, f32[40,128]{1,0:T(8,128)S(1)}, u32[]{:S(2)}, u32[]{:S(2)}) collective-permute-start(f32[40,128]{1,0:T(8,128)S(1)} %add.113), channel_id=1, source_target_pairs={{0,2},{1,3},{2,0},{3,1},{4,6},{5,7},{6,4},{7,5},{8,10},{9,11},{10,... | collective-permute-start | bytes 61448 | tf_op jit(solution)/shard_map/ppermute | solution.py:562
  52.3 3.8 %collective-permute-start.11 = (f32[40,128]{1,0:T(8,128)S(1)}, f32[40,128]{1,0:T(8,128)S(1)}, u32[]{:S(2)}, u32[]{:S(2)}) collective-permute-start(f32[40,128]{1,0:T(8,128)S(1)} %add_add_fusion), channel_id=1, source_target_pairs={{0,8},{1,9},{2,10},{3,11},{4,12},{5,13},{6,14},{7,15},{8,0},{9,1},... | collective-permute-start | bytes 61448 | tf_op jit(solution)/shard_map/ppermute | solution.py:562
  56.1 4.7 %collective-permute-start.12 = (f32[40,128]{1,0:T(8,128)S(1)}, f32[40,128]{1,0:T(8,128)S(1)}, u32[]{:S(2)}, u32[]{:S(2)}) collective-permute-start(f32[40,128]{1,0:T(8,128)S(1)} %add.117), channel_id=1, source_target_pairs={{0,16},{1,17},{2,18},{3,19},{4,20},{5,21},{6,22},{7,23},{8,24},{9,... | collective-permute-start | bytes 61448 | tf_op jit(solution)/shard_map/ppermute | solution.py:562
  64.0 6.1 %collective-permute-start.13 = (bf16[768,384]{1,0:T(8,128)(2,1)S(1)}, bf16[768,384]{1,0:T(8,128)(2,1)S(1)}, u32[]{:S(2)}, u32[]{:S(2)}) collective-permute-start(bf16[768,384]{1,0:T(8,128)(2,1)S(1)} %get-tuple-element.106), channel_id=1, source_target_pairs={{0,1},{1,0},{2,3},{3,2},{4,5},{5,4},{6,7},{7,6},{8,9},{9,8},{10,11... | collective-permute-start | bytes 1769480 | tf_op jit(solution)/shard_map/ppermute | solution.py:562
  64.1 6.0 %collective-permute-start.15 = (bf16[192,384]{1,0:T(8,128)(2,1)S(1)}, bf16[192,384]{1,0:T(8,128)(2,1)S(1)}, u32[]{:S(2)}, u32[]{:S(2)}) collective-permute-start(bf16[192,384]{1,0:T(8,128)(2,1)S(1)} %get-tuple-element.110), channel_id=1, source_target_pairs={{0,1},{1,0},{2,3},{3,2},{4,5},{5,4},{6,7},{7,6},{8,9},{9,8},{10,11... | collective-permute-start | bytes 442376 | tf_op jit(solution)/shard_map/ppermute | solution.py:562
  72.6 17.3 %collective-permute-start.16 = (bf16[432,384]{1,0:T(8,128)(2,1)S(1)}, bf16[432,384]{1,0:T(8,128)(2,1)S(1)}, u32[]{:S(2)}, u32[]{:S(2)}) collective-permute-start(bf16[432,384]{1,0:T(8,128)(2,1)S(1)} %get-tuple-element.150), channel_id=1, source_target_pairs={{0,2},{1,3},{2,0},{3,1},{4,6},{5,7},{6,4},{7,5},{8,10},{9,11},{10,... | collective-permute-start | bytes 995336 | tf_op jit(solution)/shard_map/ppermute | solution.py:562
  74.2 16.7 %collective-permute-start.17 = (bf16[432,384]{1,0:T(8,128)(2,1)S(1)}, bf16[432,384]{1,0:T(8,128)(2,1)S(1)}, u32[]{:S(2)}, u32[]{:S(2)}) collective-permute-start(bf16[432,384]{1,0:T(8,128)(2,1)S(1)} %get-tuple-element.149), channel_id=1, source_target_pairs={{0,4},{1,5},{2,6},{3,7},{4,0},{5,1},{6,2},{7,3},{8,12},{9,13},{10,... | collective-permute-start | bytes 995336 | tf_op jit(solution)/shard_map/ppermute | solution.py:562
  74.7 16.2 %collective-permute-start.18 = (bf16[432,384]{1,0:T(8,128)(2,1)S(1)}, bf16[432,384]{1,0:T(8,128)(2,1)S(1)}, u32[]{:S(2)}, u32[]{:S(2)}) collective-permute-start(bf16[432,384]{1,0:T(8,128)(2,1)S(1)} %get-tuple-element.148), channel_id=1, source_target_pairs={{0,6},{1,7},{2,4},{3,5},{4,2},{5,3},{6,0},{7,1},{8,14},{9,15},{10,... | collective-permute-start | bytes 995336 | tf_op jit(solution)/shard_map/ppermute | solution.py:562
  91.1 6.2 %collective-permute-start.20 = (bf16[240,384]{1,0:T(8,128)(2,1)S(1)}, bf16[240,384]{1,0:T(8,128)(2,1)S(1)}, u32[]{:S(2)}, u32[]{:S(2)}) collective-permute-start(bf16[240,384]{1,0:T(8,128)(2,1)S(1)} %slice.89), channel_id=1, source_target_pairs={{0,8},{1,9},{2,10},{3,11},{4,12},{5,13},{6,14},{7,15},{8,0},{9,1},... | collective-permute-start | bytes 552968 | tf_op jit(solution)/shard_map/ppermute | solution.py:562
  92.6 6.1 %collective-permute-start.21 = (bf16[192,384]{1,0:T(8,128)(2,1)S(1)}, bf16[192,384]{1,0:T(8,128)(2,1)S(1)}, u32[]{:S(2)}, u32[]{:S(2)}) collective-permute-start(bf16[192,384]{1,0:T(8,128)(2,1)S(1)} %get-tuple-element.153), channel_id=1, source_target_pairs={{0,2},{1,3},{2,0},{3,1},{4,6},{5,7},{6,4},{7,5},{8,10},{9,11},{10,... | collective-permute-start | bytes 442376 | tf_op jit(solution)/shard_map/ppermute | solution.py:562
  93.7 8.8 %collective-permute-start.23 = (bf16[192,384]{1,0:T(8,128)(2,1)S(1)}, bf16[192,384]{1,0:T(8,128)(2,1)S(1)}, u32[]{:S(2)}, u32[]{:S(2)}) collective-permute-start(bf16[192,384]{1,0:T(8,128)(2,1)S(1)} %get-tuple-element.152), channel_id=1, source_target_pairs={{0,4},{1,5},{2,6},{3,7},{4,0},{5,1},{6,2},{7,3},{8,12},{9,13},{10,... | collective-permute-start | bytes 442376 | tf_op jit(solution)/shard_map/ppermute | solution.py:562
  94.5 8.1 %collective-permute-start.24 = (bf16[192,384]{1,0:T(8,128)(2,1)S(1)}, bf16[192,384]{1,0:T(8,128)(2,1)S(1)}, u32[]{:S(2)}, u32[]{:S(2)}) collective-permute-start(bf16[192,384]{1,0:T(8,128)(2,1)S(1)} %get-tuple-element.151), channel_id=1, source_target_pairs={{0,6},{1,7},{2,4},{3,5},{4,2},{5,3},{6,0},{7,1},{8,14},{9,15},{10,... | collective-permute-start | bytes 442376 | tf_op jit(solution)/shard_map/ppermute | solution.py:562
  98.8 6.9 %collective-permute-start.22 = (bf16[144,384]{1,0:T(8,128)(2,1)S(1)}, bf16[144,384]{1,0:T(8,128)(2,1)S(1)}, u32[]{:S(2)}, u32[]{:S(2)}) collective-permute-start(bf16[144,384]{1,0:T(8,128)(2,1)S(1)} %slice.93), channel_id=1, source_target_pairs={{0,16},{1,17},{2,18},{3,19},{4,20},{5,21},{6,22},{7,23},{8,24},{9,... | collective-permute-start | bytes 331784 | tf_op jit(solution)/shard_map/ppermute | solution.py:562
  105.8 4.5 %collective-permute-start.25 = (bf16[96,384]{1,0:T(8,128)(2,1)S(1)}, bf16[96,384]{1,0:T(8,128)(2,1)S(1)}, u32[]{:S(2)}, u32[]{:S(2)}) collective-permute-start(bf16[96,384]{1,0:T(8,128)(2,1)S(1)} %slice.97), channel_id=1, source_target_pairs={{0,8},{1,9},{2,10},{3,11},{4,12},{5,13},{6,14},{7,15},{8,0},{9,1},... | collective-permute-start | bytes 221192 | tf_op jit(solution)/shard_map/ppermute | solution.py:562
  106.8 7.1 %collective-permute-start.27 = (bf16[96,384]{1,0:T(8,128)(2,1)S(1)}, bf16[96,384]{1,0:T(8,128)(2,1)S(1)}, u32[]{:S(2)}, u32[]{:S(2)}) collective-permute-start(bf16[96,384]{1,0:T(8,128)(2,1)S(1)} %slice.102), channel_id=1, source_target_pairs={{0,16},{1,17},{2,18},{3,19},{4,20},{5,21},{6,22},{7,23},{8,24},{9,... | collective-permute-start | bytes 221192 | tf_op jit(solution)/shard_map/ppermute | solution.py:562
  110.4 5.9 %collective-permute-start.26 = (bf16[48,384]{1,0:T(8,128)(2,1)S(1)}, bf16[48,384]{1,0:T(8,128)(2,1)S(1)}, u32[]{:S(2)}, u32[]{:S(2)}) collective-permute-start(bf16[48,384]{1,0:T(8,128)(2,1)S(1)} %slice.99), channel_id=1, source_target_pairs={{0,16},{1,17},{2,18},{3,19},{4,20},{5,21},{6,22},{7,23},{8,24},{9,... | collective-permute-start | bytes 110600 | tf_op jit(solution)/shard_map/ppermute | solution.py:562
  113.9 5.9 %collective-permute-start.28 = (bf16[192,384]{1,0:T(8,128)(2,1)S(1)}, bf16[192,384]{1,0:T(8,128)(2,1)S(1)}, u32[]{:S(2)}, u32[]{:S(2)}) collective-permute-start(bf16[192,384]{1,0:T(8,128)(2,1)S(1)} %pad_maximum_fusion.4), channel_id=1, source_target_pairs={{0,8},{1,9},{2,10},{3,11},{4,12},{5,13},{6,14},{7,15},{8,0},{9,1},... | collective-permute-start | bytes 442376 | tf_op jit(solution)/shard_map/ppermute | solution.py:562
  119.8 5.5 %collective-permute-start.29 = (bf16[48,384]{1,0:T(8,128)(2,1)S(1)}, bf16[48,384]{1,0:T(8,128)(2,1)S(1)}, u32[]{:S(2)}, u32[]{:S(2)}) collective-permute-start(bf16[48,384]{1,0:T(8,128)(2,1)S(1)} %add_convert_fusion.8), channel_id=1, source_target_pairs={{0,16},{1,17},{2,18},{3,19},{4,20},{5,21},{6,22},{7,23},{8,24},{9,... | collective-permute-start | bytes 110600 | tf_op jit(solution)/shard_map/ppermute | solution.py:562
  121.7 10.2 %collective-permute-start.34 = (bf16[432,384]{1,0:T(8,128)(2,1)S(1)}, bf16[432,384]{1,0:T(8,128)(2,1)S(1)}, u32[]{:S(2)}, u32[]{:S(2)}) collective-permute-start(bf16[432,384]{1,0:T(8,128)(2,1)S(1)} %pad_maximum_fusion.2), channel_id=1, source_target_pairs={{0,2},{1,3},{2,0},{3,1},{4,6},{5,7},{6,4},{7,5},{8,10},{9,11},{10,... | collective-permute-start | bytes 995336 | tf_op jit(solution)/shard_map/ppermute | solution.py:562
  123.1 12.7 %collective-permute-start.35 = (bf16[432,384]{1,0:T(8,128)(2,1)S(1)}, bf16[432,384]{1,0:T(8,128)(2,1)S(1)}, u32[]{:S(2)}, u32[]{:S(2)}) collective-permute-start(bf16[432,384]{1,0:T(8,128)(2,1)S(1)} %pad_maximum_fusion.2), channel_id=1, source_target_pairs={{0,4},{1,5},{2,6},{3,7},{4,0},{5,1},{6,2},{7,3},{8,12},{9,13},{10,... | collective-permute-start | bytes 995336 | tf_op jit(solution)/shard_map/ppermute | solution.py:562
  123.9 13.5 %collective-permute-start.31 = (bf16[432,384]{1,0:T(8,128)(2,1)S(1)}, bf16[432,384]{1,0:T(8,128)(2,1)S(1)}, u32[]{:S(2)}, u32[]{:S(2)}) collective-permute-start(bf16[432,384]{1,0:T(8,128)(2,1)S(1)} %pad_maximum_fusion.2), channel_id=1, source_target_pairs={{0,6},{1,7},{2,4},{3,5},{4,2},{5,3},{6,0},{7,1},{8,14},{9,15},{10,... | collective-permute-start | bytes 995336 | tf_op jit(solution)/shard_map/ppermute | solution.py:562
  125.3 4.4 %collective-permute-start.30 = (bf16[96,384]{1,0:T(8,128)(2,1)S(1)}, bf16[96,384]{1,0:T(8,128)(2,1)S(1)}, u32[]{:S(2)}, u32[]{:S(2)}) collective-permute-start(bf16[96,384]{1,0:T(8,128)(2,1)S(1)} %pad_maximum_fusion.5), channel_id=1, source_target_pairs={{0,8},{1,9},{2,10},{3,11},{4,12},{5,13},{6,14},{7,15},{8,0},{9,1},... | collective-permute-start | bytes 221192 | tf_op jit(solution)/shard_map/ppermute | solution.py:562
  129.8 6.3 %collective-permute-start.32 = (bf16[192,384]{1,0:T(8,128)(2,1)S(1)}, bf16[192,384]{1,0:T(8,128)(2,1)S(1)}, u32[]{:S(2)}, u32[]{:S(2)}) collective-permute-start(bf16[192,384]{1,0:T(8,128)(2,1)S(1)} %get-tuple-element.131), channel_id=1, source_target_pairs={{0,2},{1,3},{2,0},{3,1},{4,6},{5,7},{6,4},{7,5},{8,10},{9,11},{10,... | collective-permute-start | bytes 442376 | tf_op jit(solution)/shard_map/ppermute | solution.py:562
  131.1 6.3 %collective-permute-start.33 = (bf16[192,384]{1,0:T(8,128)(2,1)S(1)}, bf16[192,384]{1,0:T(8,128)(2,1)S(1)}, u32[]{:S(2)}, u32[]{:S(2)}) collective-permute-start(bf16[192,384]{1,0:T(8,128)(2,1)S(1)} %get-tuple-element.131), channel_id=1, source_target_pairs={{0,4},{1,5},{2,6},{3,7},{4,0},{5,1},{6,2},{7,3},{8,12},{9,13},{10,... | collective-permute-start | bytes 442376 | tf_op jit(solution)/shard_map/ppermute | solution.py:562
  137.6 7.1 %collective-permute-start.36 = (bf16[192,384]{1,0:T(8,128)(2,1)S(1)}, bf16[192,384]{1,0:T(8,128)(2,1)S(1)}, u32[]{:S(2)}, u32[]{:S(2)}) collective-permute-start(bf16[192,384]{1,0:T(8,128)(2,1)S(1)} %get-tuple-element.131), channel_id=1, source_target_pairs={{0,6},{1,7},{2,4},{3,5},{4,2},{5,3},{6,0},{7,1},{8,14},{9,15},{10,... | collective-permute-start | bytes 442376 | tf_op jit(solution)/shard_map/ppermute | solution.py:562
  (34 other events, 187.7 us)

commit v10 on v9

--- a/solution.py
+++ b/solution.py
@@ -707,8 +707,8 @@
         a = joined(a, [swap(a, 16)])
         a = joined(a, [swap(a, 8)])
         last, got_m[0], got_m[1] = lax.optimization_barrier((a, got_m[0], got_m[1]))
-        got_a = plane([a, a, a, last])
-        got_m[2], got_a[0], got_a[1] = lax.optimization_barrier((got_m[2], got_a[0], got_a[1]))
+        got_a = plane([a, a, last, a])
+        got_m[2], got_a[0], got_a[2] = lax.optimization_barrier((got_m[2], got_a[0], got_a[2]))
         m = joined(m, got_m)
         grad_down, grad_up, grad_proj, gain2 = spread_mlp(m, swap(m, 1))
         got_a, grad_up = lax.optimization_barrier((got_a, grad_up))

time: 151 us -> 152 us (level)
  transfers between devices with their start and end apart: 39 -> 39, of which waited for: 22 -> 23; matrix products, arithmetic and copies ran while one was open for 1% -> 1% of each run, Pallas kernels for 27% -> 27%
where the time goes in v10:
time: 152 us; the launch traced here: 151 us
  Pallas kernels  58.9 us (39%)
  starting transfers between devices  48 us (32%)
  waiting for transfers between devices  37.4 us (25%)
  between operations  4.24 us (3%)
  local copies, waits for them, and re-layouts  1.58 us (1%)
    ppermute x39, starting transfers between devices, swap(): return lax.ppermute(v, AXES, [(i, i ^ mask) for i in range(32)])  48 us
    ppermute x39, waiting for transfers between devices, swap(): return lax.ppermute(v, AXES, [(i, i ^ mask) for i in range(32)])  37.4 us
    pallas_call x1, Pallas kernels, att_back(): pl.pallas_call(att_back_kernel, grid=(n // TOK_BLOCK,), in_specs=[SMEM] +...  13.7 us
    pallas_call x5, Pallas kernels, call(): pl.pallas_call(kernel, in_specs=[SMEM] * smem + [VMEM] * (len(args) - sme...  11.2 us
    pallas_call x1, Pallas kernels, image_tower(): pl.pallas_call(image_kernel, grid=(count // IMG_BLOCK,), in_specs=[pl.Blo...  10.8 us
    pallas_call x1, Pallas kernels, text_mlp(): pl.pallas_call(text_mlp_kernel, grid=(n // TOK_BLOCK,), in_specs=[token_r...  10 us
    pallas_call x1, Pallas kernels, text_att(): pl.pallas_call(text_att_kernel, grid=(blocks,), in_specs=[token_rows(D),...  7.86 us
    pallas_call x1, Pallas kernels, mlp_back(): pl.pallas_call(mlp_back_kernel, grid=(n // TOK_BLOCK,), in_specs=[SMEM, b...  5.36 us
  transfers between devices with their start and end apart: 39, of which 23 were waited for; matrix products, arithmetic and copies ran while one was open for 1% of the time, Pallas kernels for 27%

profile of v10, /device:TPU:0, one launch (start us, length us, event | category | flops | bytes accessed | tf_op | source)
XLA Modules:
  0.0 151.5 jit_solution(8648234334545145685)
XLA Ops:
  0.7 10.8 %image_tower.1 = bf16[64,384]{1,0:T(8,128)(2,1)S(1)} custom-call(bf16[50,64,384]{2,1,0:T(8,128)(2,1)} %bitcast.23, f32[384]{0:T(512)} %g1.5, bf16[384,1152]{1,0:T(8,128)(2,1)} %wqkv.5, bf16[384,384]{1,0:T(8,128)(2,1)} %wout.3, f32[384]{0:T(512)} %g2.4, bf16[384,1536]{1,0:T(8,128)(2,1)} %wup.4, bf16[1536,384]{1,0:T(8,128)(2,1)} %wdown.3, bf16[384,384]{1,0:T(8,128)(2,1)} %wproj.3), custom_call_target="tpu_custom_call" | custom-call | flops 12000000000 | bytes 36000000 | tf_op jit(solution)/shard_map/image_tower/pallas_call | solution.py:141
  11.5 3.1 %collective-permute-start = (bf16[64,384]{1,0:T(8,128)(2,1)S(1)}, bf16[64,384]{1,0:T(8,128)(2,1)S(1)}, u32[]{:S(2)}, u32[]{:S(2)}) collective-permute-start(bf16[64,384]{1,0:T(8,128)(2,1)S(1)} %image_tower.1), channel_id=1, source_target_pairs={{0,8},{1,9},{2,10},{3,11},{4,12},{5,13},{6,14},{7,15},{8,0},{9,1},... | collective-permute-start | bytes 147464 | tf_op jit(solution)/shard_map/ppermute | solution.py:562
  14.6 2.6 %collective-permute-start.1 = (bf16[64,384]{1,0:T(8,128)(2,1)S(1)}, bf16[64,384]{1,0:T(8,128)(2,1)S(1)}, u32[]{:S(2)}, u32[]{:S(2)}) collective-permute-start(bf16[64,384]{1,0:T(8,128)(2,1)S(1)} %image_tower.1), channel_id=1, source_target_pairs={{0,16},{1,17},{2,18},{3,19},{4,20},{5,21},{6,22},{7,23},{8,24},{9,... | collective-permute-start | bytes 147464 | tf_op jit(solution)/shard_map/ppermute | solution.py:562
  17.4 7.9 %text_att.1 = (bf16[1024,384]{1,0:T(8,128)(2,1)S(1)}, bf16[1024,384]{1,0:T(8,128)(2,1)}, bf16[1024,1152]{1,0:T(8,128)(2,1)}, bf16[8,3,256,128]{3,2,1,0:T(8,128)(2,1)}, bf16[1024,384]{1,0:T(8,128)(2,1)}) custom-call(bf16[1024,384]{1,0:T(8,128)(2,1)} %tok_ref.5, s32[4,1,256]{2,1,0:T(1,128)S(1)} %reshape.71.lab_ref, f32[384]{0:T(512)S(1)} %copy-done.9, ...), custom_call_target="tpu_custom_call" | custom-call | flops 8999999488 | bytes 27000000 | tf_op jit(solution)/shard_map/text_att/pallas_call | solution.py:256
  25.3 1.8 %collective-permute-start.3 = (bf16[256,384]{1,0:T(8,128)(2,1)S(1)}, bf16[256,384]{1,0:T(8,128)(2,1)S(1)}, u32[]{:S(2)}, u32[]{:S(2)}) collective-permute-start(bf16[256,384]{1,0:T(8,128)(2,1)S(1)} %pad_maximum_fusion.3), channel_id=1, source_target_pairs={{0,2},{1,3},{2,0},{3,1},{4,6},{5,7},{6,4},{7,5},{8,10},{9,11},{10,... | collective-permute-start | bytes 589832 | tf_op jit(solution)/shard_map/ppermute | solution.py:562
  28.9 10.0 %text_mlp.1 = (bf16[1024,384]{1,0:T(8,128)(2,1)}, f32[1024,384]{1,0:T(8,128)}, bf16[1024,1536]{1,0:T(8,128)(2,1)}, f32[64,1536]{1,0:T(8,128)S(1)}, bf16[64,384]{...) custom-call(bf16[1024,384]{1,0:T(8,128)(2,1)S(1)} %copy-done.3, ...), custom_call_target="tpu_custom_call" | custom-call | flops 11000000512 | bytes 33000000 | tf_op jit(solution)/shard_map/text_mlp/pallas_call | solution.py:280
  40.5 1.7 %collective-permute-done.6.other = bf16[1024,384]{1,0:T(8,128)(2,1)} collective-permute-done((bf16[1024,384]{1,0:T(8,128)(2,1)S(1)}, bf16[1024,384]{1,0:T(8,128)(2,1)}, u32[]{:S(2)}, u32[]{:S(2)}) %collective-permute-start.6) | collective-permute-done | bytes 786464 | tf_op jit(solution)/shard_map/ppermute | solution.py:562
  42.2 1.9 %cosine.1 = (f32[64,2048]{1,0:T(8,128)S(1)}, f32[40,128]{1,0:T(8,128)S(1)}) custom-call(f32[1]{0:T(128)S(6)} %copy.46.scale_ref, s32[1]{0:T(128)} %bitcast.mine_ref, bf16[64,384]{1,0:T(8,128)(2,1)S(1)} %get-tuple-element.84.emb, bf16[1024,384]{1,0:T(8,128)(2,1)S(1)} %constant_dynamic-update-slice_fusion.own, bf16[1024,384]{1,0:T(8,128)(2,1)} %collective-permute-done.6.other, ...), custom_call_target="tpu_custom_call" | custom-call | flops 3000000000 | bytes 9000000 | tf_op jit(solution)/shard_map/cosine/pallas_call | solution.py:513
  45.3 2.7 %collective-permute-start.10 = (f32[40,128]{1,0:T(8,128)S(1)}, f32[40,128]{1,0:T(8,128)S(1)}, u32[]{:S(2)}, u32[]{:S(2)}) collective-permute-start(f32[40,128]{1,0:T(8,128)S(1)} %add.113), channel_id=1, source_target_pairs={{0,6},{1,7},{2,4},{3,5},{4,2},{5,3},{6,0},{7,1},{8,14},{9,15},{10,... | collective-permute-start | bytes 61448 | tf_op jit(solution)/shard_map/ppermute | solution.py:562
  50.0 1.8 %collective-permute-done.8 = f32[40,128]{1,0:T(8,128)S(1)} collective-permute-done((f32[40,128]{1,0:T(8,128)S(1)}, f32[40,128]{1,0:T(8,128)S(1)}, u32[]{:S(2)}, u32[]{:S(2)}) %collective-permute-start.8) | collective-permute-done | bytes 20512 | tf_op jit(solution)/shard_map/ppermute | solution.py:562
  53.1 3.1 %collective-permute-done.11 = f32[40,128]{1,0:T(8,128)S(1)} collective-permute-done((f32[40,128]{1,0:T(8,128)S(1)}, f32[40,128]{1,0:T(8,128)S(1)}, u32[]{:S(2)}, u32[]{:S(2)}) %collective-permute-start.11) | collective-permute-done | bytes 20512 | tf_op jit(solution)/shard_map/ppermute | solution.py:562
  56.1 2.2 %collective-permute-start.12 = (f32[40,128]{1,0:T(8,128)S(1)}, f32[40,128]{1,0:T(8,128)S(1)}, u32[]{:S(2)}, u32[]{:S(2)}) collective-permute-start(f32[40,128]{1,0:T(8,128)S(1)} %add.117), channel_id=1, source_target_pairs={{0,16},{1,17},{2,18},{3,19},{4,20},{5,21},{6,22},{7,23},{8,24},{9,... | collective-permute-start | bytes 61448 | tf_op jit(solution)/shard_map/ppermute | solution.py:562
  58.4 1.7 %rows.1.dt_row = f32[64,384]{1,0:T(8,128)S(1)} custom-call(f32[1]{0:T(128)S(6)} %copy.46.scale_ref, f32[64,2048]{1,0:T(8,128)S(1)} %get-tuple-element.90.g_ref, bf16[1024,384]{1,0:T(8,128)(2,1)S(1)} %constant_dynamic-update-slice_fusion.own, bf16[1024,384]{1,0:T(8,128)(2,1)} %collective-permute-done.6.other, s32[64,1]{1,0:T(8,128)S(1)} %copy.29.pair), custom_call_target="tpu_custom_call" | custom-call | flops 2000000000 | bytes 6000000 | tf_op jit(solution)/shard_map/rows/pallas_call | solution.py:513
  60.9 3.1 %head_back.1 = (bf16[768,384]{1,0:T(8,128)(2,1)S(1)}, bf16[768,384]{1,0:T(8,128)(2,1)S(1)}, bf16[192,384]{1,0:T(8,128)(2,1)S(1)}, bf16[192,384]{1,0:T(8,128)(2,1...) custom-call(f32[1]{0:T(128)S(6)} %copy.46.scale_ref, ...), custom_call_target="tpu_custom_call" | custom-call | flops 5000000000 | bytes 15000000 | tf_op jit(solution)/shard_map/head_back/pallas_call | solution.py:513
  64.6 5.4 %mlp_back.1 = (f32[1024,384]{1,0:T(8,128)S(1)}, bf16[1024,384]{1,0:T(8,128)(2,1)S(1)}, bf16[768,384]{1,0:T(8,128)(2,1)S(1)}, bf16[768,384]{1,0:T(8,128)(2,1)S(1)}) custom-call(s32[1]{0:T(128)} %bitcast.mine_ref, s32[4,1,256]{2,1,0:T(1,128)S(1)} %reshape.71.lab_ref, bf16[1024,384]{1,0:T(8,128)(2,1)S(1)} %copy-done.16, bf16[1024,1536]{1,0:T(8,128)(2,1)S(1)} %copy-done.10, ...), custom_call_target="tpu_custom_call" | custom-call | flops 8999999488 | bytes 27000000 | tf_op jit(solution)/shard_map/mlp_back/pallas_call | solution.py:530
  70.3 1.7 %collective-permute-done.14 = bf16[768,384]{1,0:T(8,128)(2,1)S(1)} collective-permute-done((bf16[768,384]{1,0:T(8,128)(2,1)S(1)}, bf16[768,384]{1,0:T(8,128)(2,1)S(1)}, u32[]{:S(2)}, u32[]{:S(2)}) %collective-permute-start.14) | collective-permute-done | bytes 589856 | tf_op jit(solution)/shard_map/ppermute | solution.py:562
  76.2 13.7 %att_back.1 = (f32[1024,384]{1,0:T(8,128)}, bf16[768,384]{1,0:T(8,128)(2,1)S(1)}, bf16[768,384]{1,0:T(8,128)(2,1)S(1)}) custom-call(s32[1]{0:T(128)} %bitcast.mine_ref, bf16[1024,1152]{1,0:T(8,128)(2,1)S(1)} %copy-done.11, bf16[8,3,256,128]{3,2,1,0:T(8,128)(2,1)S(1)} %copy-done.15, bf16[1024,384]{1,0:T(8,128)(2,1)S(1)} %get-tuple-element.111.dxb_all, ...), custom_call_target="tpu_custom_call" | custom-call | flops 14000000000 | bytes 42000000 | tf_op jit(solution)/shard_map/att_back/pallas_call | solution.py:545
  94.5 1.8 %collective-permute-start.24 = (bf16[192,384]{1,0:T(8,128)(2,1)S(1)}, bf16[192,384]{1,0:T(8,128)(2,1)S(1)}, u32[]{:S(2)}, u32[]{:S(2)}) collective-permute-start(bf16[192,384]{1,0:T(8,128)(2,1)S(1)} %get-tuple-element.151), channel_id=1, source_target_pairs={{0,6},{1,7},{2,4},{3,5},{4,2},{5,3},{6,0},{7,1},{8,14},{9,15},{10,... | collective-permute-start | bytes 442376 | tf_op jit(solution)/shard_map/ppermute | solution.py:562
  98.8 2.8 %collective-permute-start.22 = (bf16[144,384]{1,0:T(8,128)(2,1)S(1)}, bf16[144,384]{1,0:T(8,128)(2,1)S(1)}, u32[]{:S(2)}, u32[]{:S(2)}) collective-permute-start(bf16[144,384]{1,0:T(8,128)(2,1)S(1)} %slice.93), channel_id=1, source_target_pairs={{0,16},{1,17},{2,18},{3,19},{4,20},{5,21},{6,22},{7,23},{8,24},{9,... | collective-permute-start | bytes 331784 | tf_op jit(solution)/shard_map/ppermute | solution.py:562
  102.6 3.1 %collective-permute-done.22 = bf16[144,384]{1,0:T(8,128)(2,1)S(1)} collective-permute-done((bf16[144,384]{1,0:T(8,128)(2,1)S(1)}, bf16[144,384]{1,0:T(8,128)(2,1)S(1)}, u32[]{:S(2)}, u32[]{:S(2)}) %collective-permute-start.22) | collective-permute-done | bytes 110624 | tf_op jit(solution)/shard_map/ppermute | solution.py:562
  106.8 3.5 %collective-permute-start.27 = (bf16[96,384]{1,0:T(8,128)(2,1)S(1)}, bf16[96,384]{1,0:T(8,128)(2,1)S(1)}, u32[]{:S(2)}, u32[]{:S(2)}) collective-permute-start(bf16[96,384]{1,0:T(8,128)(2,1)S(1)} %slice.102), channel_id=1, source_target_pairs={{0,16},{1,17},{2,18},{3,19},{4,20},{5,21},{6,22},{7,23},{8,24},{9,... | collective-permute-start | bytes 221192 | tf_op jit(solution)/shard_map/ppermute | solution.py:562
  110.4 2.5 %collective-permute-start.26 = (bf16[48,384]{1,0:T(8,128)(2,1)S(1)}, bf16[48,384]{1,0:T(8,128)(2,1)S(1)}, u32[]{:S(2)}, u32[]{:S(2)}) collective-permute-start(bf16[48,384]{1,0:T(8,128)(2,1)S(1)} %slice.99), channel_id=1, source_target_pairs={{0,16},{1,17},{2,18},{3,19},{4,20},{5,21},{6,22},{7,23},{8,24},{9,... | collective-permute-start | bytes 110600 | tf_op jit(solution)/shard_map/ppermute | solution.py:562
  113.9 2.4 %collective-permute-start.28 = (bf16[192,384]{1,0:T(8,128)(2,1)S(1)}, bf16[192,384]{1,0:T(8,128)(2,1)S(1)}, u32[]{:S(2)}, u32[]{:S(2)}) collective-permute-start(bf16[192,384]{1,0:T(8,128)(2,1)S(1)} %pad_maximum_fusion.4), channel_id=1, source_target_pairs={{0,8},{1,9},{2,10},{3,11},{4,12},{5,13},{6,14},{7,15},{8,0},{9,1},... | collective-permute-start | bytes 442376 | tf_op jit(solution)/shard_map/ppermute | solution.py:562
  116.3 3.4 %collective-permute-done.28 = bf16[192,384]{1,0:T(8,128)(2,1)S(1)} collective-permute-done((bf16[192,384]{1,0:T(8,128)(2,1)S(1)}, bf16[192,384]{1,0:T(8,128)(2,1)S(1)}, u32[]{:S(2)}, u32[]{:S(2)}) %collective-permute-start.28) | collective-permute-done | bytes 147488 | tf_op jit(solution)/shard_map/ppermute | solution.py:562
  119.8 1.9 %collective-permute-start.29 = (bf16[48,384]{1,0:T(8,128)(2,1)S(1)}, bf16[48,384]{1,0:T(8,128)(2,1)S(1)}, u32[]{:S(2)}, u32[]{:S(2)}) collective-permute-start(bf16[48,384]{1,0:T(8,128)(2,1)S(1)} %add_convert_fusion.8), channel_id=1, source_target_pairs={{0,16},{1,17},{2,18},{3,19},{4,20},{5,21},{6,22},{7,23},{8,24},{9,... | collective-permute-start | bytes 110600 | tf_op jit(solution)/shard_map/ppermute | solution.py:562
  126.5 3.2 %collective-permute-done.30 = bf16[96,384]{1,0:T(8,128)(2,1)S(1)} collective-permute-done((bf16[96,384]{1,0:T(8,128)(2,1)S(1)}, bf16[96,384]{1,0:T(8,128)(2,1)S(1)}, u32[]{:S(2)}, u32[]{:S(2)}) %collective-permute-start.30) | collective-permute-done | bytes 73760 | tf_op jit(solution)/shard_map/ppermute | solution.py:562
  132.4 3.4 %collective-permute-done.35 = bf16[432,384]{1,0:T(8,128)(2,1)S(1)} collective-permute-done((bf16[432,384]{1,0:T(8,128)(2,1)S(1)}, bf16[432,384]{1,0:T(8,128)(2,1)S(1)}, u32[]{:S(2)}, u32[]{:S(2)}) %collective-permute-start.35) | collective-permute-done | bytes 331808 | tf_op jit(solution)/shard_map/ppermute | solution.py:562
  135.8 1.7 %collective-permute-done.32 = bf16[192,384]{1,0:T(8,128)(2,1)S(1)} collective-permute-done((bf16[192,384]{1,0:T(8,128)(2,1)S(1)}, bf16[192,384]{1,0:T(8,128)(2,1)S(1)}, u32[]{:S(2)}, u32[]{:S(2)}) %collective-permute-start.32) | collective-permute-done | bytes 147488 | tf_op jit(solution)/shard_map/ppermute | solution.py:562
  138.9 2.0 %collective-permute-start.36 = (bf16[192,384]{1,0:T(8,128)(2,1)S(1)}, bf16[192,384]{1,0:T(8,128)(2,1)S(1)}, u32[]{:S(2)}, u32[]{:S(2)}) collective-permute-start(bf16[192,384]{1,0:T(8,128)(2,1)S(1)} %get-tuple-element.130), channel_id=1, source_target_pairs={{0,4},{1,5},{2,6},{3,7},{4,0},{5,1},{6,2},{7,3},{8,12},{9,13},{10,... | collective-permute-start | bytes 442376 | tf_op jit(solution)/shard_map/ppermute | solution.py:562
  141.9 2.7 %spread_mlp.1 = (f32[1536,384]{1,0:T(8,128)}, f32[384,1536]{1,0:T(8,128)}, f32[384,384]{1,0:T(8,128)}, f32[384]{0:T(512)}) custom-call(s32[1]{0:T(128)} %bitcast.mine_ref, bf16[1728,384]{1,0:T(8,128)(2,1)S(1)} %constant_dynamic-update-slice_fusion.7.own, bf16[1728,384]{1,0:T(8,128)(2,1)S(1)} %collective-permute-done.37.other, ...), custom_call_target="tpu_custom_call" | custom-call | flops 4000000000 | bytes 12000000 | tf_op jit(solution)/shard_map/spread_mlp/pallas_call | solution.py:513
  145.6 1.9 %collective-permute-done.38.other = bf16[768,384]{1,0:T(8,128)(2,1)S(1)} collective-permute-done((bf16[768,384]{1,0:T(8,128)(2,1)S(1)}, bf16[768,384]{1,0:T(8,128)(2,1)S(1)}, u32[]{:S(2)}, u32[]{:S(2)}) %collective-permute-start.38) | collective-permute-done | bytes 589856 | tf_op jit(solution)/shard_map/ppermute | solution.py:562
  147.5 1.7 %spread_att.1 = (f32[384,384]{1,0:T(8,128)}, f32[384,1152]{1,0:T(8,128)}, f32[384]{0:T(512)}) custom-call(s32[1]{0:T(128)} %bitcast.mine_ref, bf16[768,384]{1,0:T(8,128)(2,1)S(1)} %constant_dynamic-update-slice_fusion.11.own, bf16[768,384]{1,0:T(8,128)(2,1)S(1)} %collective-permute-done.38.other, bf16[384,1152]{1,0:T(8,128)(2,1)S(1)} %copy-done.2, ...), custom_call_target="tpu_custom_call" | custom-call | flops 4000000000 | bytes 12000000 | tf_op jit(solution)/shard_map/spread_att/pallas_call | solution.py:513
  (161 shorter events, 34.1 us)
Async XLA Ops:
  11.5 13.8 %collective-permute-start = (bf16[64,384]{1,0:T(8,128)(2,1)S(1)}, bf16[64,384]{1,0:T(8,128)(2,1)S(1)}, u32[]{:S(2)}, u32[]{:S(2)}) collective-permute-start(bf16[64,384]{1,0:T(8,128)(2,1)S(1)} %image_tower.1), channel_id=1, source_target_pairs={{0,8},{1,9},{2,10},{3,11},{4,12},{5,13},{6,14},{7,15},{8,0},{9,1},... | collective-permute-start | bytes 147464 | tf_op jit(solution)/shard_map/ppermute | solution.py:562
  14.6 10.7 %collective-permute-start.1 = (bf16[64,384]{1,0:T(8,128)(2,1)S(1)}, bf16[64,384]{1,0:T(8,128)(2,1)S(1)}, u32[]{:S(2)}, u32[]{:S(2)}) collective-permute-start(bf16[64,384]{1,0:T(8,128)(2,1)S(1)} %image_tower.1), channel_id=1, source_target_pairs={{0,16},{1,17},{2,18},{3,19},{4,20},{5,21},{6,22},{7,23},{8,24},{9,... | collective-permute-start | bytes 147464 | tf_op jit(solution)/shard_map/ppermute | solution.py:562
  17.2 8.2 %collective-permute-start.2 = (bf16[64,384]{1,0:T(8,128)(2,1)S(1)}, bf16[64,384]{1,0:T(8,128)(2,1)S(1)}, u32[]{:S(2)}, u32[]{:S(2)}) collective-permute-start(bf16[64,384]{1,0:T(8,128)(2,1)S(1)} %image_tower.1), channel_id=1, source_target_pairs={{0,24},{1,25},{2,26},{3,27},{4,28},{5,29},{6,30},{7,31},{8,16},{9,... | collective-permute-start | bytes 147464 | tf_op jit(solution)/shard_map/ppermute | solution.py:562
  25.3 13.6 %collective-permute-start.3 = (bf16[256,384]{1,0:T(8,128)(2,1)S(1)}, bf16[256,384]{1,0:T(8,128)(2,1)S(1)}, u32[]{:S(2)}, u32[]{:S(2)}) collective-permute-start(bf16[256,384]{1,0:T(8,128)(2,1)S(1)} %pad_maximum_fusion.3), channel_id=1, source_target_pairs={{0,2},{1,3},{2,0},{3,1},{4,6},{5,7},{6,4},{7,5},{8,10},{9,11},{10,... | collective-permute-start | bytes 589832 | tf_op jit(solution)/shard_map/ppermute | solution.py:562
  27.1 11.8 %collective-permute-start.4 = (bf16[256,384]{1,0:T(8,128)(2,1)S(1)}, bf16[256,384]{1,0:T(8,128)(2,1)S(1)}, u32[]{:S(2)}, u32[]{:S(2)}) collective-permute-start(bf16[256,384]{1,0:T(8,128)(2,1)S(1)} %pad_maximum_fusion.3), channel_id=1, source_target_pairs={{0,4},{1,5},{2,6},{3,7},{4,0},{5,1},{6,2},{7,3},{8,12},{9,13},{10,... | collective-permute-start | bytes 589832 | tf_op jit(solution)/shard_map/ppermute | solution.py:562
  28.6 10.3 %collective-permute-start.5 = (bf16[256,384]{1,0:T(8,128)(2,1)S(1)}, bf16[256,384]{1,0:T(8,128)(2,1)S(1)}, u32[]{:S(2)}, u32[]{:S(2)}) collective-permute-start(bf16[256,384]{1,0:T(8,128)(2,1)S(1)} %pad_maximum_fusion.3), channel_id=1, source_target_pairs={{0,6},{1,7},{2,4},{3,5},{4,2},{5,3},{6,0},{7,1},{8,14},{9,15},{10,... | collective-permute-start | bytes 589832 | tf_op jit(solution)/shard_map/ppermute | solution.py:562
  45.3 4.7 %collective-permute-start.10 = (f32[40,128]{1,0:T(8,128)S(1)}, f32[40,128]{1,0:T(8,128)S(1)}, u32[]{:S(2)}, u32[]{:S(2)}) collective-permute-start(f32[40,128]{1,0:T(8,128)S(1)} %add.113), channel_id=1, source_target_pairs={{0,6},{1,7},{2,4},{3,5},{4,2},{5,3},{6,0},{7,1},{8,14},{9,15},{10,... | collective-permute-start | bytes 61448 | tf_op jit(solution)/shard_map/ppermute | solution.py:562
  48.0 3.8 %collective-permute-start.8 = (f32[40,128]{1,0:T(8,128)S(1)}, f32[40,128]{1,0:T(8,128)S(1)}, u32[]{:S(2)}, u32[]{:S(2)}) collective-permute-start(f32[40,128]{1,0:T(8,128)S(1)} %add.113), channel_id=1, source_target_pairs={{0,2},{1,3},{2,0},{3,1},{4,6},{5,7},{6,4},{7,5},{8,10},{9,11},{10,... | collective-permute-start | bytes 61448 | tf_op jit(solution)/shard_map/ppermute | solution.py:562
  52.3 3.8 %collective-permute-start.11 = (f32[40,128]{1,0:T(8,128)S(1)}, f32[40,128]{1,0:T(8,128)S(1)}, u32[]{:S(2)}, u32[]{:S(2)}) collective-permute-start(f32[40,128]{1,0:T(8,128)S(1)} %add_add_fusion), channel_id=1, source_target_pairs={{0,8},{1,9},{2,10},{3,11},{4,12},{5,13},{6,14},{7,15},{8,0},{9,1},... | collective-permute-start | bytes 61448 | tf_op jit(solution)/shard_map/ppermute | solution.py:562
  56.1 4.7 %collective-permute-start.12 = (f32[40,128]{1,0:T(8,128)S(1)}, f32[40,128]{1,0:T(8,128)S(1)}, u32[]{:S(2)}, u32[]{:S(2)}) collective-permute-start(f32[40,128]{1,0:T(8,128)S(1)} %add.117), channel_id=1, source_target_pairs={{0,16},{1,17},{2,18},{3,19},{4,20},{5,21},{6,22},{7,23},{8,24},{9,... | collective-permute-start | bytes 61448 | tf_op jit(solution)/shard_map/ppermute | solution.py:562
  64.0 6.1 %collective-permute-start.13 = (bf16[768,384]{1,0:T(8,128)(2,1)S(1)}, bf16[768,384]{1,0:T(8,128)(2,1)S(1)}, u32[]{:S(2)}, u32[]{:S(2)}) collective-permute-start(bf16[768,384]{1,0:T(8,128)(2,1)S(1)} %get-tuple-element.106), channel_id=1, source_target_pairs={{0,1},{1,0},{2,3},{3,2},{4,5},{5,4},{6,7},{7,6},{8,9},{9,8},{10,11... | collective-permute-start | bytes 1769480 | tf_op jit(solution)/shard_map/ppermute | solution.py:562
  64.1 6.0 %collective-permute-start.15 = (bf16[192,384]{1,0:T(8,128)(2,1)S(1)}, bf16[192,384]{1,0:T(8,128)(2,1)S(1)}, u32[]{:S(2)}, u32[]{:S(2)}) collective-permute-start(bf16[192,384]{1,0:T(8,128)(2,1)S(1)} %get-tuple-element.110), channel_id=1, source_target_pairs={{0,1},{1,0},{2,3},{3,2},{4,5},{5,4},{6,7},{7,6},{8,9},{9,8},{10,11... | collective-permute-start | bytes 442376 | tf_op jit(solution)/shard_map/ppermute | solution.py:562
  72.6 17.3 %collective-permute-start.16 = (bf16[432,384]{1,0:T(8,128)(2,1)S(1)}, bf16[432,384]{1,0:T(8,128)(2,1)S(1)}, u32[]{:S(2)}, u32[]{:S(2)}) collective-permute-start(bf16[432,384]{1,0:T(8,128)(2,1)S(1)} %get-tuple-element.150), channel_id=1, source_target_pairs={{0,2},{1,3},{2,0},{3,1},{4,6},{5,7},{6,4},{7,5},{8,10},{9,11},{10,... | collective-permute-start | bytes 995336 | tf_op jit(solution)/shard_map/ppermute | solution.py:562
  74.2 16.7 %collective-permute-start.17 = (bf16[432,384]{1,0:T(8,128)(2,1)S(1)}, bf16[432,384]{1,0:T(8,128)(2,1)S(1)}, u32[]{:S(2)}, u32[]{:S(2)}) collective-permute-start(bf16[432,384]{1,0:T(8,128)(2,1)S(1)} %get-tuple-element.149), channel_id=1, source_target_pairs={{0,4},{1,5},{2,6},{3,7},{4,0},{5,1},{6,2},{7,3},{8,12},{9,13},{10,... | collective-permute-start | bytes 995336 | tf_op jit(solution)/shard_map/ppermute | solution.py:562
  74.7 16.2 %collective-permute-start.18 = (bf16[432,384]{1,0:T(8,128)(2,1)S(1)}, bf16[432,384]{1,0:T(8,128)(2,1)S(1)}, u32[]{:S(2)}, u32[]{:S(2)}) collective-permute-start(bf16[432,384]{1,0:T(8,128)(2,1)S(1)} %get-tuple-element.148), channel_id=1, source_target_pairs={{0,6},{1,7},{2,4},{3,5},{4,2},{5,3},{6,0},{7,1},{8,14},{9,15},{10,... | collective-permute-start | bytes 995336 | tf_op jit(solution)/shard_map/ppermute | solution.py:562
  91.1 6.2 %collective-permute-start.20 = (bf16[240,384]{1,0:T(8,128)(2,1)S(1)}, bf16[240,384]{1,0:T(8,128)(2,1)S(1)}, u32[]{:S(2)}, u32[]{:S(2)}) collective-permute-start(bf16[240,384]{1,0:T(8,128)(2,1)S(1)} %slice.89), channel_id=1, source_target_pairs={{0,8},{1,9},{2,10},{3,11},{4,12},{5,13},{6,14},{7,15},{8,0},{9,1},... | collective-permute-start | bytes 552968 | tf_op jit(solution)/shard_map/ppermute | solution.py:562
  92.6 6.1 %collective-permute-start.21 = (bf16[192,384]{1,0:T(8,128)(2,1)S(1)}, bf16[192,384]{1,0:T(8,128)(2,1)S(1)}, u32[]{:S(2)}, u32[]{:S(2)}) collective-permute-start(bf16[192,384]{1,0:T(8,128)(2,1)S(1)} %get-tuple-element.153), channel_id=1, source_target_pairs={{0,2},{1,3},{2,0},{3,1},{4,6},{5,7},{6,4},{7,5},{8,10},{9,11},{10,... | collective-permute-start | bytes 442376 | tf_op jit(solution)/shard_map/ppermute | solution.py:562
  93.7 8.8 %collective-permute-start.23 = (bf16[192,384]{1,0:T(8,128)(2,1)S(1)}, bf16[192,384]{1,0:T(8,128)(2,1)S(1)}, u32[]{:S(2)}, u32[]{:S(2)}) collective-permute-start(bf16[192,384]{1,0:T(8,128)(2,1)S(1)} %get-tuple-element.152), channel_id=1, source_target_pairs={{0,4},{1,5},{2,6},{3,7},{4,0},{5,1},{6,2},{7,3},{8,12},{9,13},{10,... | collective-permute-start | bytes 442376 | tf_op jit(solution)/shard_map/ppermute | solution.py:562
  94.5 8.1 %collective-permute-start.24 = (bf16[192,384]{1,0:T(8,128)(2,1)S(1)}, bf16[192,384]{1,0:T(8,128)(2,1)S(1)}, u32[]{:S(2)}, u32[]{:S(2)}) collective-permute-start(bf16[192,384]{1,0:T(8,128)(2,1)S(1)} %get-tuple-element.151), channel_id=1, source_target_pairs={{0,6},{1,7},{2,4},{3,5},{4,2},{5,3},{6,0},{7,1},{8,14},{9,15},{10,... | collective-permute-start | bytes 442376 | tf_op jit(solution)/shard_map/ppermute | solution.py:562
  98.8 6.9 %collective-permute-start.22 = (bf16[144,384]{1,0:T(8,128)(2,1)S(1)}, bf16[144,384]{1,0:T(8,128)(2,1)S(1)}, u32[]{:S(2)}, u32[]{:S(2)}) collective-permute-start(bf16[144,384]{1,0:T(8,128)(2,1)S(1)} %slice.93), channel_id=1, source_target_pairs={{0,16},{1,17},{2,18},{3,19},{4,20},{5,21},{6,22},{7,23},{8,24},{9,... | collective-permute-start | bytes 331784 | tf_op jit(solution)/shard_map/ppermute | solution.py:562
  105.8 4.5 %collective-permute-start.25 = (bf16[96,384]{1,0:T(8,128)(2,1)S(1)}, bf16[96,384]{1,0:T(8,128)(2,1)S(1)}, u32[]{:S(2)}, u32[]{:S(2)}) collective-permute-start(bf16[96,384]{1,0:T(8,128)(2,1)S(1)} %slice.97), channel_id=1, source_target_pairs={{0,8},{1,9},{2,10},{3,11},{4,12},{5,13},{6,14},{7,15},{8,0},{9,1},... | collective-permute-start | bytes 221192 | tf_op jit(solution)/shard_map/ppermute | solution.py:562
  106.8 7.1 %collective-permute-start.27 = (bf16[96,384]{1,0:T(8,128)(2,1)S(1)}, bf16[96,384]{1,0:T(8,128)(2,1)S(1)}, u32[]{:S(2)}, u32[]{:S(2)}) collective-permute-start(bf16[96,384]{1,0:T(8,128)(2,1)S(1)} %slice.102), channel_id=1, source_target_pairs={{0,16},{1,17},{2,18},{3,19},{4,20},{5,21},{6,22},{7,23},{8,24},{9,... | collective-permute-start | bytes 221192 | tf_op jit(solution)/shard_map/ppermute | solution.py:562
  110.4 5.9 %collective-permute-start.26 = (bf16[48,384]{1,0:T(8,128)(2,1)S(1)}, bf16[48,384]{1,0:T(8,128)(2,1)S(1)}, u32[]{:S(2)}, u32[]{:S(2)}) collective-permute-start(bf16[48,384]{1,0:T(8,128)(2,1)S(1)} %slice.99), channel_id=1, source_target_pairs={{0,16},{1,17},{2,18},{3,19},{4,20},{5,21},{6,22},{7,23},{8,24},{9,... | collective-permute-start | bytes 110600 | tf_op jit(solution)/shard_map/ppermute | solution.py:562
  113.9 5.9 %collective-permute-start.28 = (bf16[192,384]{1,0:T(8,128)(2,1)S(1)}, bf16[192,384]{1,0:T(8,128)(2,1)S(1)}, u32[]{:S(2)}, u32[]{:S(2)}) collective-permute-start(bf16[192,384]{1,0:T(8,128)(2,1)S(1)} %pad_maximum_fusion.4), channel_id=1, source_target_pairs={{0,8},{1,9},{2,10},{3,11},{4,12},{5,13},{6,14},{7,15},{8,0},{9,1},... | collective-permute-start | bytes 442376 | tf_op jit(solution)/shard_map/ppermute | solution.py:562
  119.8 5.5 %collective-permute-start.29 = (bf16[48,384]{1,0:T(8,128)(2,1)S(1)}, bf16[48,384]{1,0:T(8,128)(2,1)S(1)}, u32[]{:S(2)}, u32[]{:S(2)}) collective-permute-start(bf16[48,384]{1,0:T(8,128)(2,1)S(1)} %add_convert_fusion.8), channel_id=1, source_target_pairs={{0,16},{1,17},{2,18},{3,19},{4,20},{5,21},{6,22},{7,23},{8,24},{9,... | collective-permute-start | bytes 110600 | tf_op jit(solution)/shard_map/ppermute | solution.py:562
  121.7 10.7 %collective-permute-start.34 = (bf16[432,384]{1,0:T(8,128)(2,1)S(1)}, bf16[432,384]{1,0:T(8,128)(2,1)S(1)}, u32[]{:S(2)}, u32[]{:S(2)}) collective-permute-start(bf16[432,384]{1,0:T(8,128)(2,1)S(1)} %pad_maximum_fusion.2), channel_id=1, source_target_pairs={{0,2},{1,3},{2,0},{3,1},{4,6},{5,7},{6,4},{7,5},{8,10},{9,11},{10,... | collective-permute-start | bytes 995336 | tf_op jit(solution)/shard_map/ppermute | solution.py:562
  123.1 12.7 %collective-permute-start.35 = (bf16[432,384]{1,0:T(8,128)(2,1)S(1)}, bf16[432,384]{1,0:T(8,128)(2,1)S(1)}, u32[]{:S(2)}, u32[]{:S(2)}) collective-permute-start(bf16[432,384]{1,0:T(8,128)(2,1)S(1)} %pad_maximum_fusion.2), channel_id=1, source_target_pairs={{0,4},{1,5},{2,6},{3,7},{4,0},{5,1},{6,2},{7,3},{8,12},{9,13},{10,... | collective-permute-start | bytes 995336 | tf_op jit(solution)/shard_map/ppermute | solution.py:562
  123.9 14.7 %collective-permute-start.31 = (bf16[432,384]{1,0:T(8,128)(2,1)S(1)}, bf16[432,384]{1,0:T(8,128)(2,1)S(1)}, u32[]{:S(2)}, u32[]{:S(2)}) collective-permute-start(bf16[432,384]{1,0:T(8,128)(2,1)S(1)} %pad_maximum_fusion.2), channel_id=1, source_target_pairs={{0,6},{1,7},{2,4},{3,5},{4,2},{5,3},{6,0},{7,1},{8,14},{9,15},{10,... | collective-permute-start | bytes 995336 | tf_op jit(solution)/shard_map/ppermute | solution.py:562
  125.3 4.4 %collective-permute-start.30 = (bf16[96,384]{1,0:T(8,128)(2,1)S(1)}, bf16[96,384]{1,0:T(8,128)(2,1)S(1)}, u32[]{:S(2)}, u32[]{:S(2)}) collective-permute-start(bf16[96,384]{1,0:T(8,128)(2,1)S(1)} %pad_maximum_fusion.5), channel_id=1, source_target_pairs={{0,8},{1,9},{2,10},{3,11},{4,12},{5,13},{6,14},{7,15},{8,0},{9,1},... | collective-permute-start | bytes 221192 | tf_op jit(solution)/shard_map/ppermute | solution.py:562
  129.8 7.8 %collective-permute-start.32 = (bf16[192,384]{1,0:T(8,128)(2,1)S(1)}, bf16[192,384]{1,0:T(8,128)(2,1)S(1)}, u32[]{:S(2)}, u32[]{:S(2)}) collective-permute-start(bf16[192,384]{1,0:T(8,128)(2,1)S(1)} %get-tuple-element.130), channel_id=1, source_target_pairs={{0,2},{1,3},{2,0},{3,1},{4,6},{5,7},{6,4},{7,5},{8,10},{9,11},{10,... | collective-permute-start | bytes 442376 | tf_op jit(solution)/shard_map/ppermute | solution.py:562
  131.1 7.5 %collective-permute-start.33 = (bf16[192,384]{1,0:T(8,128)(2,1)S(1)}, bf16[192,384]{1,0:T(8,128)(2,1)S(1)}, u32[]{:S(2)}, u32[]{:S(2)}) collective-permute-start(bf16[192,384]{1,0:T(8,128)(2,1)S(1)} %get-tuple-element.130), channel_id=1, source_target_pairs={{0,6},{1,7},{2,4},{3,5},{4,2},{5,3},{6,0},{7,1},{8,14},{9,15},{10,... | collective-permute-start | bytes 442376 | tf_op jit(solution)/shard_map/ppermute | solution.py:562
  138.9 6.5 %collective-permute-start.36 = (bf16[192,384]{1,0:T(8,128)(2,1)S(1)}, bf16[192,384]{1,0:T(8,128)(2,1)S(1)}, u32[]{:S(2)}, u32[]{:S(2)}) collective-permute-start(bf16[192,384]{1,0:T(8,128)(2,1)S(1)} %get-tuple-element.130), channel_id=1, source_target_pairs={{0,4},{1,5},{2,6},{3,7},{4,0},{5,1},{6,2},{7,3},{8,12},{9,13},{10,... | collective-permute-start | bytes 442376 | tf_op jit(solution)/shard_map/ppermute | solution.py:562
  (34 other events, 187.7 us)
